TPU v7x, 32 devices: a whole 2x2x4 slice. The times are simulated.
32 devices in a mesh: shard: 2 (over core), ctx: 4 (over y, x), tp: 4 (over z).
Axes of the slice: x: 2, y: 2, z: 4, core: 2. Of those that a mesh axis runs over, the one named last changes fastest.
Arguments:
- layer_input: bfloat16 [8, 1024, 2048], P('shard', 'ctx'), may hold values from -6 to 6
- output_gradient: bfloat16 [8, 1024, 2048], P('shard', 'ctx'), may hold values from -6 to 6
- picture_piece_starts: int32 [8, 2], P('shard'), may hold values from 0 to 768, as said below
- sequence_adapter_index: int32 [8], P('shard'), may hold values from 0 to 7
- attention_norm_gain: float32 [2048], replicated, may hold values from 0.5 to 1.5
- attention_norm_bias: float32 [2048], replicated, may hold values from -1 to 1
- feedforward_norm_gain: float32 [2048], replicated, may hold values from 0.5 to 1.5
- feedforward_norm_bias: float32 [2048], replicated, may hold values from -1 to 1
- query_key_value_weight: bfloat16 [2048, 3, 2048], P('shard', None, 'tp'), may hold values from -0.125 to 0.125
- attention_output_weight: bfloat16 [2048, 2048], P('tp', 'shard'), may hold values from -0.375 to 0.375
- up_projection_weight: bfloat16 [2048, 8192], P('shard', 'tp'), may hold values from -0.125 to 0.125
- down_projection_weight: bfloat16 [8192, 2048], P('tp', 'shard'), may hold values from -0.09375 to 0.09375
- adapter_projection_first: bfloat16 [8, 2048, 16], replicated, may hold values from -0.125 to 0.125
- adapter_projection_second: bfloat16 [8, 16, 3, 2048], P(None, None, None, 'tp'), may hold values from -0.75 to 0.75
- adapter_heads_first: bfloat16 [8, 2048, 16], P(None, 'tp'), may hold values from -0.375 to 0.375
- adapter_heads_second: bfloat16 [8, 16, 2048], replicated, may hold values from -0.75 to 0.75
- adapter_up_first: bfloat16 [8, 2048, 16], replicated, may hold values from -0.125 to 0.125
- adapter_up_second: bfloat16 [8, 16, 8192], P(None, None, 'tp'), may hold values from -0.75 to 0.75
- adapter_down_first: bfloat16 [8, 8192, 16], P(None, 'tp'), may hold values from -0.09375 to 0.09375
- adapter_down_second: bfloat16 [8, 16, 2048], replicated, may hold values from -0.75 to 0.75
Outputs:
- layer_out: bfloat16 [8, 1024, 2048], P('shard', 'ctx')
- input_grad: bfloat16 [8, 1024, 2048], P('shard', 'ctx')
- qkv_in_grad: float32 [8, 2048, 16], replicated
- qkv_out_grad: float32 [8, 16, 3, 2048], P(None, None, None, 'tp')
- heads_in_grad: float32 [8, 2048, 16], P(None, 'tp')
- heads_out_grad: float32 [8, 16, 2048], replicated
- up_in_grad: float32 [8, 2048, 16], replicated
- up_out_grad: float32 [8, 16, 8192], P(None, None, 'tp')
- down_in_grad: float32 [8, 8192, 16], P(None, 'tp')
- down_out_grad: float32 [8, 16, 2048], replicated
Inputs may be any that keep to these rules, and one draw needn't show every extreme that they name: `picture_piece_starts`: piece c of a sequence starts within positions c * 512 to (c + 1) * 512 - 256, so pieces never meet; in some sequence a piece starts at 0, in some sequence a piece ends at 1024.
All inputs are finite; a program needn't handle non-finite values.
Results may differ from a plain program's by a relative error of at most 0.019.
Values may be sent and summed in bfloat16 or wider, within the bound.
A program may use at most 320 MiB of HBM per device.

v0:
```python
import jax
import jax.numpy as jnp
from jax import lax
from jax.sharding import PartitionSpec as P

HD = 128
PIC = 256


NORM_EPS = 1e-05


def layer_norm(inputs, gains, biases):
    average = jnp.mean(inputs, axis=-1, keepdims=True)
    centred = inputs - average
    spread = jnp.mean(centred * centred, axis=-1, keepdims=True)
    return centred * lax.rsqrt(spread + NORM_EPS) * gains + biases


def gelu_tanh(inputs):
    return (
        0.5
        * inputs
        * (1.0 + jnp.tanh(0.7978845608028654 * (inputs + 0.044715 * inputs * inputs * inputs)))
    )


def flattened_first(adapter_mat):
    adapter_tables, inner_dim, rank_width = adapter_mat.shape
    return jnp.transpose(adapter_mat, (1, 0, 2)).reshape(inner_dim, adapter_tables * rank_width)


def flattened_second(adapter_mat):
    return adapter_mat.reshape(adapter_mat.shape[0] * adapter_mat.shape[1], -1)


def unflat_in(grad_flat, adapter_tables):
    inner_dim = grad_flat.shape[0]
    return jnp.transpose(grad_flat.reshape(inner_dim, adapter_tables, -1), (1, 0, 2))


def matmul(left_mat, right_mat):
    return jnp.dot(left_mat, right_mat, preferred_element_type=jnp.float32)


def matmul_tn(left_mat, right_mat):
    return lax.dot_general(
        left_mat, right_mat, (((0,), (0,)), ((), ())), preferred_element_type=jnp.float32
    )


def matmul_nt(left_mat, right_mat):
    return lax.dot_general(
        left_mat, right_mat, (((1,), (1,)), ((), ())), preferred_element_type=jnp.float32
    )


def piece_labels(starts, positions):
    inside = (positions[None, None, :] >= starts[:, :, None]) & (
        positions[None, None, :] < starts[:, :, None] + PIC
    )
    labels = jnp.arange(1, starts.shape[1] + 1, dtype=jnp.int32)
    return jnp.sum(jnp.where(inside, labels[None, :, None], 0), axis=1)


def visible(query_pos, key_pos, query_labels, key_labels):
    causal = key_pos[None, None, :] <= query_pos[None, :, None]
    shared = (query_labels[:, :, None] == key_labels[:, None, :]) & (query_labels[:, :, None] > 0)
    return causal | shared


def exponents(queries, key_rows, query_pos, key_pos, visible_mask, slopes):
    score_scale = queries.shape[-1] ** (-0.5)
    logits = (
        jnp.einsum("sqhd,skhd->shqk", queries, key_rows, preferred_element_type=jnp.float32)
        * score_scale
    )
    distance = jnp.abs(query_pos[:, None] - key_pos[None, :]).astype(jnp.float32)
    logits = logits - slopes[None, :, None, None] * distance[None, None]
    return jnp.where(visible_mask[:, None], jnp.exp(logits), 0.0)


def block_grads(
    queries, scaled_grad, row_delta, key_rows, value_rows, query_pos, key_pos, visible_mask, slopes
):
    score_scale = queries.shape[-1] ** (-0.5)
    exponent = exponents(queries, key_rows, query_pos, key_pos, visible_mask, slopes)
    products_gv = jnp.einsum(
        "sqhd,skhd->shqk", scaled_grad, value_rows, preferred_element_type=jnp.float32
    )
    grad_logits = (
        exponent * (products_gv - jnp.transpose(row_delta, (0, 2, 1))[..., None])
    ).astype(jnp.bfloat16)
    grad_queries = (
        jnp.einsum("shqk,skhd->sqhd", grad_logits, key_rows, preferred_element_type=jnp.float32)
        * score_scale
    )
    grad_keyrows = (
        jnp.einsum("shqk,sqhd->skhd", grad_logits, queries, preferred_element_type=jnp.float32)
        * score_scale
    )
    grad_valrows = jnp.einsum(
        "shqk,sqhd->skhd",
        exponent.astype(jnp.bfloat16),
        scaled_grad,
        preferred_element_type=jnp.float32,
    )
    return (grad_queries, grad_keyrows, grad_valrows)


def reduce_heads(partials):
    return lax.psum((partials[0], partials[1]), "tp")


def body(
    layer_input,
    output_gradient,
    picture_piece_starts,
    sequence_adapter_index,
    attention_norm_gain,
    attention_norm_bias,
    feedforward_norm_gain,
    feedforward_norm_bias,
    query_key_value_weight,
    attention_output_weight,
    up_projection_weight,
    down_projection_weight,
    adapter_projection_first,
    adapter_projection_second,
    adapter_heads_first,
    adapter_heads_second,
    adapter_up_first,
    adapter_up_second,
    adapter_down_first,
    adapter_down_second,
):
    seq_here, local_len, model_width = layer_input.shape
    tok_rows = seq_here * local_len
    adapter_tables = adapter_projection_first.shape[0]
    rank_width = adapter_projection_first.shape[2]
    head_width = HD
    device_heads = adapter_projection_second.shape[-1] // head_width
    local_width = device_heads * head_width
    columns = jnp.arange(adapter_tables * rank_width, dtype=jnp.int32) // rank_width
    chosen = (sequence_adapter_index[:, None] == columns[None, :]).astype(jnp.float32)
    select = jnp.broadcast_to(
        chosen[:, None, :], (seq_here, local_len, adapter_tables * rank_width)
    ).reshape(tok_rows, adapter_tables * rank_width)
    head_ids = lax.axis_index("tp") * device_heads + jnp.arange(device_heads, dtype=jnp.int32)
    slopes = jnp.exp2(
        -8.0 * (head_ids.astype(jnp.float32) + 1.0) / (device_heads * lax.axis_size("tp"))
    )
    here_pos = lax.axis_index("ctx") * local_len + jnp.arange(local_len, dtype=jnp.int32)
    here_labels = piece_labels(picture_piece_starts, here_pos)
    projection_first_flattened = flattened_first(adapter_projection_first)
    projection_second_flattened = flattened_second(adapter_projection_second)
    heads_first_flattened = flattened_first(adapter_heads_first)
    heads_second_flattened = flattened_second(adapter_heads_second)
    up_first_flattened = flattened_first(adapter_up_first)
    up_second_flattened = flattened_second(adapter_up_second)
    down_first_flattened = flattened_first(adapter_down_first)
    down_second_flattened = flattened_second(adapter_down_second)
    residual = layer_input.reshape(tok_rows, model_width).astype(jnp.float32)
    first_norm, first_back_full = jax.vjp(
        lambda inputs: layer_norm(inputs, attention_norm_gain, attention_norm_bias), residual
    )
    first_act = first_norm.astype(jnp.bfloat16)
    gathered_rows = (
        lax.all_gather(query_key_value_weight, "shard", axis=0, tiled=True),
        lax.all_gather(up_projection_weight, "shard", axis=0, tiled=True),
    )
    qkv_full = gathered_rows[0].reshape(model_width, 3 * local_width)
    up_full = gathered_rows[1]
    gathered_cols = (
        lax.all_gather(attention_output_weight, "shard", axis=1, tiled=True),
        lax.all_gather(down_projection_weight, "shard", axis=1, tiled=True),
    )
    heads_full = gathered_cols[0]
    down_full = gathered_cols[1]
    first_low = (matmul(first_act, projection_first_flattened) * select).astype(jnp.bfloat16)
    projected = (
        matmul(first_act, qkv_full) + matmul(first_low, projection_second_flattened)
    ).astype(jnp.bfloat16)
    queries_flat = projected[:, :local_width].reshape(seq_here, local_len, local_width)
    queries = queries_flat.reshape(seq_here, local_len, device_heads, head_width)
    key_rows = projected[:, local_width : 2 * local_width].reshape(seq_here, local_len, local_width)
    value_rows = projected[:, 2 * local_width :].reshape(seq_here, local_len, local_width)
    pieces = (
        lax.all_gather(key_rows, "ctx", axis=1, tiled=True),
        lax.all_gather(value_rows, "ctx", axis=1, tiled=True),
    )
    piece_len = pieces[0].shape[1]
    key_pos = jnp.arange(piece_len, dtype=jnp.int32)
    key_labels = piece_labels(picture_piece_starts, key_pos)
    visible_mask = visible(here_pos, key_pos, here_labels, key_labels)
    piece_keys = pieces[0].reshape(seq_here, piece_len, device_heads, head_width)
    piece_values = pieces[1].reshape(seq_here, piece_len, device_heads, head_width)
    exponent = exponents(queries, piece_keys, here_pos, key_pos, visible_mask, slopes)
    weighted = jnp.einsum(
        "shqk,skhd->sqhd",
        exponent.astype(jnp.bfloat16),
        piece_values,
        preferred_element_type=jnp.float32,
    )
    weighted, totals = (weighted, jnp.sum(exponent, axis=-1))
    per_total = jnp.transpose(totals, (0, 2, 1))[..., None]
    heads_raw = weighted / per_total
    heads_act = heads_raw.reshape(tok_rows, local_width).astype(jnp.bfloat16)
    heads_part = matmul(heads_act, heads_full)
    heads_low_part = matmul(heads_act, heads_first_flattened)
    attn_total, attn_low_total = reduce_heads((heads_part, heads_low_part))
    heads_low_here = (attn_low_total * select).astype(jnp.bfloat16)
    middle_here = residual + attn_total + matmul(heads_low_here, heads_second_flattened)
    second_norm, second_back = jax.vjp(
        lambda inputs: layer_norm(inputs, feedforward_norm_gain, feedforward_norm_bias), middle_here
    )
    second_act_here = second_norm.astype(jnp.bfloat16)
    up_low_here = (matmul(second_act_here, up_first_flattened) * select).astype(jnp.bfloat16)
    second_act, up_low, heads_low = (second_act_here, up_low_here, heads_low_here)
    hidden = matmul(second_act, up_full) + matmul(up_low, up_second_flattened)
    activated, gelu_back = jax.vjp(gelu_tanh, hidden)
    activated = activated.astype(jnp.bfloat16)
    down_part = matmul(activated, down_full)
    down_low_part = matmul(activated, down_first_flattened)
    ffn_total, ffn_low_total = reduce_heads((down_part, down_low_part))
    down_low_here = (ffn_low_total * select).astype(jnp.bfloat16)
    result_here = (middle_here + ffn_total + matmul(down_low_here, down_second_flattened)).astype(
        jnp.bfloat16
    )
    grad_top_low = output_gradient.reshape(tok_rows, model_width)
    grad_top = grad_top_low.astype(jnp.float32)
    down_back = (matmul_nt(grad_top_low, down_second_flattened) * select).astype(jnp.bfloat16)
    grad_down_in = matmul_tn(activated, down_back)
    grad_activated = matmul_nt(grad_top_low, down_full) + matmul_nt(down_back, down_first_flattened)
    grad_hidden = gelu_back(grad_activated)[0].astype(jnp.bfloat16)
    up_second_gradient = matmul_tn(up_low, grad_hidden)
    ffn_back_part = matmul_nt(grad_hidden, up_full)
    ffn_back_low = matmul_nt(grad_hidden, up_second_flattened)
    back_total, back_low_total = reduce_heads((ffn_back_part, ffn_back_low))
    up_back_here = (back_low_total * select).astype(jnp.bfloat16)
    grad_second = back_total + matmul_nt(up_back_here, up_first_flattened)
    grad_middle_here = grad_top + second_back(grad_second)[0]
    grad_middle_low_here = grad_middle_here.astype(jnp.bfloat16)
    heads_back_here = (matmul_nt(grad_middle_low_here, heads_second_flattened) * select).astype(
        jnp.bfloat16
    )
    result_rows, down_low, grad_middle_low, heads_back, up_back = (
        result_here,
        down_low_here,
        grad_middle_low_here,
        heads_back_here,
        up_back_here,
    )
    layer_out = result_rows.reshape(layer_input.shape)
    down_second_gradient = matmul_tn(down_low, grad_top_low)
    grad_up_in = matmul_tn(second_act, up_back)
    heads_second_gradient = matmul_tn(heads_low, grad_middle_low)
    grad_heads_in = matmul_tn(heads_act, heads_back)
    grad_heads = (
        matmul_nt(grad_middle_low, heads_full) + matmul_nt(heads_back, heads_first_flattened)
    ).astype(jnp.bfloat16)
    grad_heads_wide = grad_heads.reshape(seq_here, local_len, device_heads, head_width).astype(
        jnp.float32
    )
    scaled_grad = (grad_heads_wide / per_total).astype(jnp.bfloat16)
    row_delta = jnp.sum(grad_heads_wide * heads_raw, axis=-1) / per_total[..., 0]
    pieces = (
        lax.all_gather(key_rows, "ctx", axis=1, tiled=True),
        lax.all_gather(value_rows, "ctx", axis=1, tiled=True),
    )
    piece_len = pieces[0].shape[1]
    key_pos = jnp.arange(piece_len, dtype=jnp.int32)
    key_labels = piece_labels(picture_piece_starts, key_pos)
    visible_mask = visible(here_pos, key_pos, here_labels, key_labels)
    piece_keys = pieces[0].reshape(seq_here, piece_len, device_heads, head_width)
    piece_values = pieces[1].reshape(seq_here, piece_len, device_heads, head_width)
    grad_queries, grad_keyrows, grad_valrows = block_grads(
        queries,
        scaled_grad,
        row_delta,
        piece_keys,
        piece_values,
        here_pos,
        key_pos,
        visible_mask,
        slopes,
    )
    grad_keys_all, grad_values_all = (
        lax.psum_scatter(grad_keyrows, "ctx", scatter_dimension=1, tiled=True),
        lax.psum_scatter(grad_valrows, "ctx", scatter_dimension=1, tiled=True),
    )
    grad_projected = jnp.concatenate(
        [
            grad_queries.reshape(tok_rows, local_width),
            grad_keys_all.reshape(tok_rows, local_width),
            grad_values_all.reshape(tok_rows, local_width),
        ],
        axis=1,
    ).astype(jnp.bfloat16)
    projection_second_gradient = matmul_tn(first_low, grad_projected)
    attn_back_part = matmul_nt(grad_projected, qkv_full)
    attn_back_low = matmul_nt(grad_projected, projection_second_flattened)
    first_total, first_low_total = reduce_heads((attn_back_part, attn_back_low))
    qkv_back_here = (first_low_total * select).astype(jnp.bfloat16)
    grad_first = first_total + matmul_nt(qkv_back_here, projection_first_flattened)
    input_here = (grad_middle_here + first_back_full(grad_first)[0]).astype(jnp.bfloat16)
    input_rows, qkv_back = (input_here, qkv_back_here)
    input_grad = input_rows.reshape(layer_input.shape)
    grad_qkv_in = matmul_tn(first_act, qkv_back)
    adapter_terms = (
        unflat_in(grad_qkv_in, adapter_tables),
        projection_second_gradient.reshape(adapter_projection_second.shape),
        unflat_in(grad_heads_in, adapter_tables),
        heads_second_gradient.reshape(adapter_heads_second.shape),
        unflat_in(grad_up_in, adapter_tables),
        up_second_gradient.reshape(adapter_up_second.shape),
        unflat_in(grad_down_in, adapter_tables),
        down_second_gradient.reshape(adapter_down_second.shape),
    )
    summed = lax.psum(
        (
            adapter_terms[0],
            adapter_terms[1],
            adapter_terms[2],
            adapter_terms[3],
            adapter_terms[4],
            adapter_terms[5],
            adapter_terms[6],
            adapter_terms[7],
        ),
        ("shard", "ctx"),
    )
    return (
        layer_out,
        input_grad,
        summed[0],
        summed[1],
        summed[2],
        summed[3],
        summed[4],
        summed[5],
        summed[6],
        summed[7],
    )


def solution(mesh):
    placed = (
        P("shard", "ctx", None),
        P("shard", "ctx", None),
        P("shard", None),
        P("shard"),
        P(),
        P(),
        P(),
        P(),
        P("shard", None, "tp"),
        P("tp", "shard"),
        P("shard", "tp"),
        P("tp", "shard"),
        P(),
        P(None, None, None, "tp"),
        P(None, "tp", None),
        P(),
        P(),
        P(None, None, "tp"),
        P(None, "tp", None),
        P(),
    )
    return jax.shard_map(
        body,
        mesh=mesh,
        in_specs=placed,
        out_specs=(
            P("shard", "ctx", None),
            P("shard", "ctx", None),
            P(),
            P(None, None, None, "tp"),
            P(None, "tp", None),
            P(),
            P(),
            P(None, None, "tp"),
            P(None, "tp", None),
            P(),
        ),
        check_vma=False,
    )
```

profile of v0, /device:TPU:0, one launch (start us, length us, event | category | flops | bytes accessed | tf_op | source)
XLA Modules:
  0.0 1857.9 jit_solution(7738910371380799832)
XLA Ops:
  7.3 4.7 copy.69
  12.6 3.2 convert_reduce_fusion
  23.4 8.2 all-gather.7.cloned.1.call-done
  31.6 10.1 fusion.54
  47.5 2.6 broadcast_multiply_fusion
  53.8 44.1 %all-gather.9.cloned.1.call-done = bf16[4,1024,512]{2,1,0:T(8,128)(2,1)} async-done(((bf16[4,256,512]{2,1,0:T(8,128)(2,1)}), bf16[4,1024,512]{2,1,0:T(8,128)(2,1)}) %all-gather.9.cloned.1.call-update) | async-done | bytes 4194320 | tf_op jit(solution)/shard_map/all_gather | solution.py:190
  97.9 6.3 copy.71
  104.2 48.6 %all-gather.11.cloned.1.call-done = bf16[4,1024,512]{1,2,0:T(8,128)(2,1)} async-done(((bf16[4,256,512]{1,2,0:T(8,128)(2,1)}), bf16[4,1024,512]{1,2,0:T(8,128)(2,1)}) %all-gather.11.cloned.1.call-update) | async-done | bytes 4194320 | tf_op jit(solution)/shard_map/all_gather | solution.py:189
  152.8 12.5 fusion.51
  165.3 10.2 fusion.52
  177.5 7.6 fusion.34
  186.1 3.4 fusion.30
  189.6 14.8 fusion.58
  204.4 294.8 %all-reduce.15.cloned.1.call-done = (f32[1024,2048]{1,0:T(8,128)}, f32[1024,128]{1,0:T(8,128)}) async-done(((f32[1024,2048]{1,0:T(8,128)}, f32[1024,128]{1,0:T(8,128)}), (f32[1024,2048]{1,0:T(8,128)}, f32[1024,128]{1,0:T(8,128)})) %all-reduce.15.cloned.1.call-update) | async-done | bytes 8912912 | tf_op jit(solution)/shard_map/psum | solution.py:112
  500.3 6.3 fusion.53
  514.4 5.2 all-gather.15.cloned.1.call-done
  519.6 12.5 fusion.55
  532.1 5.1 multiply_convert_fusion.1
  537.2 9.4 fusion.3
  548.8 11.2 fusion.59
  560.0 309.0 %all-reduce.13.cloned.1.call-done = (f32[1024,2048]{1,0:T(8,128)}, f32[1024,128]{1,0:T(8,128)}) async-done(((f32[1024,2048]{1,0:T(8,128)}, f32[1024,128]{1,0:T(8,128)}), (f32[1024,2048]{1,0:T(8,128)}, f32[1024,128]{1,0:T(8,128)})) %all-reduce.13.cloned.1.call-update) | async-done | bytes 8912912 | tf_op jit(solution)/shard_map/psum | solution.py:112
  870.1 7.2 multiply_reduce_fusion
  877.3 4.8 fusion.48
  882.2 3.6 fusion.16
  886.8 3.4 fusion.31
  890.2 5.2 fusion.61
  901.5 8.6 multiply_convert_fusion
  910.1 3.2 copy-done.9
  913.3 4.9 multiply_bitcast_fusion
  918.5 10.7 fusion.21
  930.2 4.4 fusion.57
  934.6 14.9 fusion.56
  949.6 2.9 fusion.27
  954.4 49.3 %reduce-scatter.3.cloned.1.call-done = f32[4,256,4,128]{1,3,2,0:T(8,128)} async-done(((f32[4,1024,4,128]{1,3,2,0:T(8,128)}), f32[4,256,4,128]{1,3,2,0:T(8,128)}) %reduce-scatter.3.cloned.1.call-update) | async-done | bytes 2097168 | tf_op jit(solution)/shard_map/reduce_scatter | solution.py:289
  1006.0 86.9 %reduce-scatter.5.cloned.1.call-done = f32[4,256,4,128]{1,3,2,0:T(8,128)} async-done(((f32[4,1024,4,128]{1,3,2,0:T(8,128)}), f32[4,256,4,128]{1,3,2,0:T(8,128)}) %reduce-scatter.5.cloned.1.call-update) | async-done | bytes 2097168 | tf_op jit(solution)/shard_map/reduce_scatter | solution.py:290
  1099.6 3.6 fusion.63
  1103.3 11.8 fusion.62
  1116.7 3.9 fusion.67
  1120.6 4.5 fusion.68
  1126.3 4.2 fusion.66
  1132.3 2.6 fusion.64
  1136.4 575.2 %all-reduce.11.cloned.1.call-done = (f32[1024,2048]{1,0:T(8,128)}, f32[1024,128]{1,0:T(8,128)}, f32[1024,2048]{1,0:T(8,128)}, f32[1024,128]{1,0:T(8,128)}) async-done(((f32[1024,2048]{1,0:T(8,128)}, f32[1024,128]{1,0:T(8,128)}, f32[1024,2048]{1,0:T(8,128)}, f32[1024,128]{1,0:T(8,128)}), (f32[1024,2048]{1,0:T(8,128)}, f32[1024,128]{1,0:T(8,128)}, f32[1024,2048]{1,0:T(8,128)}, ...) | async-done | bytes 17825808 | tf_op jit(solution)/shard_map/psum | solution.py:112
  1713.2 4.0 convolution_bitcast_fusion
  1719.0 8.5 fusion.10
  1728.3 5.8 fusion.47
  1734.2 7.1 add_convert_fusion.1
  1741.4 7.2 add_convert_fusion
  1748.6 88.1 %all-reduce.9.cloned.1.call-done = (f32[8,2048,16]{1,2,0:T(8,128)}, f32[8,16,3,512]{3,2,1,0:T(4,128)}, f32[8,512,16]{1,2,0:T(8,128)}, f32[8,16,2048]{2,1,0:T(8,1...) async-done(((f32[8,2048,16]{1,2,0:T(8,128)}, f32[8,16,3,512]{3,2,1,0:T(4,128)}, ...) | async-done | bytes 7340048 | tf_op jit(solution)/shard_map/psum | solution.py:320
  (223 shorter events, 75.9 us)
Async XLA Ops:
  7.2 524.9 %copy-start = (bf16[8,16,2048]{2,1,0:T(8,128)(2,1)S(1)}, bf16[8,16,2048]{2,1,0:T(8,128)(2,1)}, u32[]{:S(2)}) copy-start(bf16[8,16,2048]{2,1,0:T(8,128)(2,1)} %param.37) | copy-start | bytes 1572868
  7.2 11.1 copy-start.45
  7.2 11.1 copy-start.51
  7.2 24.4 %all-gather.7.cloned.1.call-start = ((), (), s32[]{:S(2)}) async-start(), calls=%async_computation.2 | async-start | bytes 9437184 | tf_op jit(solution)/shard_map/all_gather | solution.py:169
  12.0 85.9 %all-gather.9.cloned.1.call-start = ((), (), s32[]{:S(2)}) async-start(), calls=%async_computation.3 | async-start | bytes 5242880 | tf_op jit(solution)/shard_map/all_gather | solution.py:190
  12.5 29.2 %copy-start.20 = (bf16[16,8,3,512]{3,1,2,0:T(8,128)(2,1)}, bf16[16,8,3,512]{3,1,2,0:T(8,128)(2,1)S(1)}, u32[]{:S(2)}) copy-start(bf16[16,8,3,512]{3,1,2,0:T(8,128)(2,1)S(1)} %copy.93) | copy-start | bytes 1179652
  12.6 856.4 %copy-start.40 = (f32[4,128]{1,0:T(4,128)}, f32[4,128]{1,0:T(4,128)S(1)}, u32[]{:S(2)}) copy-start(f32[4,128]{1,0:T(4,128)S(1)} %compare_convert_fusion) | copy-start | bytes 6148
  12.6 9.5 copy-start.28
  23.4 18.3 copy-start.24
  44.0 108.8 %all-gather.11.cloned.1.call-start = ((), (), s32[]{:S(2)}) async-start(), calls=%async_computation.4 | async-start | bytes 5242880 | tf_op jit(solution)/shard_map/all_gather | solution.py:189
  45.4 132.1 %all-gather.13.cloned.1.call-start = ((), (), s32[]{:S(2)}) async-start(), calls=%async_computation.5 | async-start | bytes 3145728 | tf_op jit(solution)/shard_map/all_gather | solution.py:175
  45.9 143.6 %all-gather.17.cloned.1.call-start = ((), (), s32[]{:S(2)}) async-start(), calls=%async_computation.7 | async-start | bytes 12582912 | tf_op jit(solution)/shard_map/all_gather | solution.py:176
  46.5 452.7 %all-reduce.15.cloned.1.call-start = ((), (), s32[]{:S(2)}) async-start(), calls=%async_computation.13 | async-start | bytes 17825792 | tf_op jit(solution)/shard_map/psum | solution.py:112
  53.8 111.5 %copy-start.16 = (bf16[4,256,4,128]{1,3,2,0:T(8,128)(2,1)}, bf16[4,256,4,128]{1,3,2,0:T(8,128)(2,1)S(1)}, u32[]{:S(2)}) copy-start(bf16[4,256,4,128]{1,3,2,0:T(8,128)(2,1)S(1)} %copy.82) | copy-start | bytes 3145732
  152.8 12.5 copy-start.10
  165.3 10.9 copy-start.38
  176.2 8.9 copy-start.18
  185.1 334.5 %all-gather.15.cloned.1.call-start = ((), (), s32[]{:S(2)}) async-start(), calls=%async_computation.6 | async-start | bytes 12582912 | tf_op jit(solution)/shard_map/all_gather | solution.py:170
  185.9 683.2 %all-reduce.13.cloned.1.call-start = ((), (), s32[]{:S(2)}) async-start(), calls=%async_computation.12 | async-start | bytes 17825792 | tf_op jit(solution)/shard_map/psum | solution.py:112
  189.5 310.8 %copy-start.27 = (bf16[8,16,2048]{2,1,0:T(8,128)(2,1)S(1)}, bf16[8,16,2048]{2,1,0:T(8,128)(2,1)}, u32[]{:S(2)}) copy-start(bf16[8,16,2048]{2,1,0:T(8,128)(2,1)} %param.35) | copy-start | bytes 1572868
  500.3 6.3 copy-start.22
  507.6 5.5 copy-start.26
  514.4 17.7 copy-start.34
  532.1 16.6 slice-start.6
  537.2 11.6 slice-start.7
  560.0 443.7 %reduce-scatter.3.cloned.1.call-start = ((), (), s32[]{:S(2)}) async-start(), calls=%async_computation.8 | async-start | bytes 10485760 | tf_op jit(solution)/shard_map/reduce_scatter | solution.py:289
  901.5 11.8 copy-start.17
  918.2 174.7 %reduce-scatter.5.cloned.1.call-start = ((), (), s32[]{:S(2)}) async-start(), calls=%async_computation.9 | async-start | bytes 10485760 | tf_op jit(solution)/shard_map/reduce_scatter | solution.py:290
  929.1 782.5 %all-reduce.11.cloned.1.call-start = ((), (), s32[]{:S(2)}) async-start(), calls=%async_computation.11 | async-start | bytes 35651584 | tf_op jit(solution)/shard_map/psum | solution.py:112
  930.2 19.4 %slice-start.4 = ((s8[8388608]{0:T(1024)(128)(4,1)}), s8[4194304]{0:T(1024)(128)(4,1)S(1)}, s32[]{:S(2)}) async-start(s8[8388608]{0:T(1024)(128)(4,1)} %bitcast.208), calls=%async_computation.18 | async-start | bytes 8388608
  934.6 14.9 slice-start.5
  934.6 14.9 copy-start.14
  953.2 146.5 %copy-start.21 = (bf16[16,8,3,512]{3,1,2,0:T(8,128)(2,1)S(1)}, bf16[16,8,3,512]{3,1,2,0:T(8,128)(2,1)}, u32[]{:S(2)}) copy-start(bf16[16,8,3,512]{3,1,2,0:T(8,128)(2,1)} %copy-done.20) | copy-start | bytes 1179652
  1115.1 721.6 %all-reduce.9.cloned.1.call-start = ((), (), s32[]{:S(2)}) async-start(), calls=%async_computation.10 | async-start | bytes 15204352 | tf_op jit(solution)/shard_map/psum | solution.py:320
  1120.6 9.9 copy-start.23
  1125.1 7.2 copy-start.25
  1126.3 585.3 %copy-start.42 = (f32[4,128]{1,0:T(4,128)S(1)}, f32[4,128]{1,0:T(4,128)}, u32[]{:S(2)}) copy-start(f32[4,128]{1,0:T(4,128)} %copy-done.40) | copy-start | bytes 6148
  1719.0 15.2 slice-start
  1719.0 9.3 copy-start.4
  1719.0 15.1 slice-start.1
  1728.3 13.0 slice-start.2
  1734.2 7.2 copy-start.7
  1734.2 7.2 slice-start.3
  1734.2 7.1 copy-start.44
  1741.4 109.3 %copy-start.1 = (bf16[8,16,2048]{2,1,0:T(8,128)(2,1)S(1)}, bf16[8,16,2048]{2,1,0:T(8,128)(2,1)}, u32[]{:S(2)}) copy-start(bf16[8,16,2048]{2,1,0:T(8,128)(2,1)} %param.37) | copy-start | bytes 1572868
  1836.7 11.1 copy-start.33
  1836.7 12.0 copy-start.32
  1836.7 13.0 copy-start.31
  (26 other events, 77.7 us)
Sparse Core Ops, SparseCore 0:
  12.1 19.4 all-gather.6
  44.1 53.7 all-gather.8
  100.3 52.4 all-gather.10
  154.2 10.5 all-gather.12
  166.2 21.0 all-gather.16
  190.2 308.9 all-reduce.14
  500.8 18.8 all-gather.14
  560.1 308.9 all-reduce.12
  918.3 85.2 reduce-scatter.2
  1006.5 86.3 reduce-scatter.4
  1115.2 596.3 all-reduce.10
  1719.1 117.4 all-reduce.8
where the time goes:
time: 1870 us; the launch traced here: 1860 us
  waiting for transfers between devices  1510 us (81%)
  matrix products  227 us (12%)
  local copies, waits for them, and re-layouts  58 us (3%)
  other arithmetic  44.6 us (2%)
    psum x3, waiting for transfers between devices, reduce_heads(): return lax.psum((partials[0], partials[1]), 'tp')  1180 us
    psum x1, waiting for transfers between devices, body(): lax.psum((adapter_terms[0], adapter_terms[1], adapter_terms[2], adapter_t...  88.1 us
    reduce_scatter x1, waiting for transfers between devices, body(): lax.psum_scatter(grad_valrows, 'ctx', scatter_dimension=1, tiled=True)  86.9 us
    dot_general x12, matrix products, matmul_nt(): lax.dot_general(left_mat, right_mat, (((1,), (1,)), ((), ())), preferred_...  81.1 us
    dot_general x12, matrix products, matmul(): return jnp.dot(left_mat, right_mat, preferred_element_type=jnp.float32)  72.7 us
    reduce_scatter x1, waiting for transfers between devices, body(): lax.psum_scatter(grad_keyrows, 'ctx', scatter_dimension=1, tiled=True)  49.3 us
    all_gather x1, waiting for transfers between devices, body(): lax.all_gather(key_rows, 'ctx', axis=1, tiled=True)  48.6 us
    all_gather x1, waiting for transfers between devices, body(): lax.all_gather(value_rows, 'ctx', axis=1, tiled=True)  44.1 us
  transfers between devices with their start and end apart: 12, of which 10 were waited for; matrix products, arithmetic and copies ran while one was open for 9% of the time, Pallas kernels for 0%

commit v1 on v0

--- a/solution.py
+++ b/solution.py
@@ -108,8 +108,31 @@
     return (grad_queries, grad_keyrows, grad_valrows)
 
 
-def reduce_heads(partials):
-    return lax.psum((partials[0], partials[1]), "tp")
+def tp_rows(rows_array, tp_count):
+    chunk = rows_array.shape[0] // tp_count
+    return lax.dynamic_slice_in_dim(rows_array, lax.axis_index("tp") * chunk, chunk, axis=0)
+
+
+def scatter_rows(partials):
+    widths = [part.shape[1] for part in partials]
+    joined = lax.psum_scatter(
+        jnp.concatenate(partials, axis=1), "tp", scatter_dimension=0, tiled=True
+    )
+    return split_columns(joined, widths)
+
+
+def gather_rows(rows_here):
+    widths = [part.shape[1] for part in rows_here]
+    joined = lax.all_gather(jnp.concatenate(rows_here, axis=1), "tp", axis=0, tiled=True)
+    return split_columns(joined, widths)
+
+
+def split_columns(joined, widths):
+    parts, offset = [], 0
+    for width in widths:
+        parts.append(joined[:, offset : offset + width])
+        offset += width
+    return tuple(parts)
 
 
 def body(
@@ -136,6 +159,7 @@
 ):
     seq_here, local_len, model_width = layer_input.shape
     tok_rows = seq_here * local_len
+    tp_count = lax.axis_size("tp")
     adapter_tables = adapter_projection_first.shape[0]
     rank_width = adapter_projection_first.shape[2]
     head_width = HD
@@ -146,37 +170,43 @@
     select = jnp.broadcast_to(
         chosen[:, None, :], (seq_here, local_len, adapter_tables * rank_width)
     ).reshape(tok_rows, adapter_tables * rank_width)
+    select_here = tp_rows(select, tp_count)
     head_ids = lax.axis_index("tp") * device_heads + jnp.arange(device_heads, dtype=jnp.int32)
     slopes = jnp.exp2(
-        -8.0 * (head_ids.astype(jnp.float32) + 1.0) / (device_heads * lax.axis_size("tp"))
+        -8.0 * (head_ids.astype(jnp.float32) + 1.0) / (device_heads * tp_count)
     )
     here_pos = lax.axis_index("ctx") * local_len + jnp.arange(local_len, dtype=jnp.int32)
     here_labels = piece_labels(picture_piece_starts, here_pos)
+    heads_full = lax.all_gather(
+        lax.all_gather(attention_output_weight, "tp", axis=0, tiled=True),
+        "shard",
+        axis=1,
+        tiled=True,
+    )
+    heads_first_all = lax.all_gather(adapter_heads_first, "tp", axis=1, tiled=True)
     projection_first_flattened = flattened_first(adapter_projection_first)
     projection_second_flattened = flattened_second(adapter_projection_second)
     heads_first_flattened = flattened_first(adapter_heads_first)
+    heads_first_all_flattened = flattened_first(heads_first_all)
     heads_second_flattened = flattened_second(adapter_heads_second)
     up_first_flattened = flattened_first(adapter_up_first)
     up_second_flattened = flattened_second(adapter_up_second)
     down_first_flattened = flattened_first(adapter_down_first)
     down_second_flattened = flattened_second(adapter_down_second)
     residual = layer_input.reshape(tok_rows, model_width).astype(jnp.float32)
-    first_norm, first_back_full = jax.vjp(
-        lambda inputs: layer_norm(inputs, attention_norm_gain, attention_norm_bias), residual
-    )
+    residual_here = tp_rows(residual, tp_count)
+    first_norm = layer_norm(residual, attention_norm_gain, attention_norm_bias)
     first_act = first_norm.astype(jnp.bfloat16)
+    _, first_back_full = jax.vjp(
+        lambda inputs: layer_norm(inputs, attention_norm_gain, attention_norm_bias), residual_here
+    )
     gathered_rows = (
         lax.all_gather(query_key_value_weight, "shard", axis=0, tiled=True),
         lax.all_gather(up_projection_weight, "shard", axis=0, tiled=True),
     )
     qkv_full = gathered_rows[0].reshape(model_width, 3 * local_width)
     up_full = gathered_rows[1]
-    gathered_cols = (
-        lax.all_gather(attention_output_weight, "shard", axis=1, tiled=True),
-        lax.all_gather(down_projection_weight, "shard", axis=1, tiled=True),
-    )
-    heads_full = gathered_cols[0]
-    down_full = gathered_cols[1]
+    down_full = lax.all_gather(down_projection_weight, "shard", axis=1, tiled=True)
     first_low = (matmul(first_act, projection_first_flattened) * select).astype(jnp.bfloat16)
     projected = (
         matmul(first_act, qkv_full) + matmul(first_low, projection_second_flattened)
@@ -206,29 +236,32 @@
     per_total = jnp.transpose(totals, (0, 2, 1))[..., None]
     heads_raw = weighted / per_total
     heads_act = heads_raw.reshape(tok_rows, local_width).astype(jnp.bfloat16)
-    heads_part = matmul(heads_act, heads_full)
-    heads_low_part = matmul(heads_act, heads_first_flattened)
-    attn_total, attn_low_total = reduce_heads((heads_part, heads_low_part))
-    heads_low_here = (attn_low_total * select).astype(jnp.bfloat16)
-    middle_here = residual + attn_total + matmul(heads_low_here, heads_second_flattened)
+    heads_act_here = lax.all_to_all(heads_act, "tp", 0, 1, tiled=True)
+    attn_here = matmul(heads_act_here, heads_full)
+    heads_low_here = (matmul(heads_act_here, heads_first_all_flattened) * select_here).astype(
+        jnp.bfloat16
+    )
+    middle_here = residual_here + attn_here + matmul(heads_low_here, heads_second_flattened)
     second_norm, second_back = jax.vjp(
         lambda inputs: layer_norm(inputs, feedforward_norm_gain, feedforward_norm_bias), middle_here
     )
     second_act_here = second_norm.astype(jnp.bfloat16)
-    up_low_here = (matmul(second_act_here, up_first_flattened) * select).astype(jnp.bfloat16)
-    second_act, up_low, heads_low = (second_act_here, up_low_here, heads_low_here)
+    (second_act,) = gather_rows((second_act_here,))
+    up_low = (matmul(second_act, up_first_flattened) * select).astype(jnp.bfloat16)
     hidden = matmul(second_act, up_full) + matmul(up_low, up_second_flattened)
     activated, gelu_back = jax.vjp(gelu_tanh, hidden)
     activated = activated.astype(jnp.bfloat16)
     down_part = matmul(activated, down_full)
     down_low_part = matmul(activated, down_first_flattened)
-    ffn_total, ffn_low_total = reduce_heads((down_part, down_low_part))
-    down_low_here = (ffn_low_total * select).astype(jnp.bfloat16)
-    result_here = (middle_here + ffn_total + matmul(down_low_here, down_second_flattened)).astype(
+    ffn_here, ffn_low_here = scatter_rows((down_part, down_low_part))
+    down_low_here = (ffn_low_here * select_here).astype(jnp.bfloat16)
+    result_here = (middle_here + ffn_here + matmul(down_low_here, down_second_flattened)).astype(
         jnp.bfloat16
     )
+    result_rows, down_low = gather_rows((result_here, down_low_here))
+    layer_out = result_rows.reshape(layer_input.shape)
     grad_top_low = output_gradient.reshape(tok_rows, model_width)
-    grad_top = grad_top_low.astype(jnp.float32)
+    grad_top_here = tp_rows(grad_top_low, tp_count).astype(jnp.float32)
     down_back = (matmul_nt(grad_top_low, down_second_flattened) * select).astype(jnp.bfloat16)
     grad_down_in = matmul_tn(activated, down_back)
     grad_activated = matmul_nt(grad_top_low, down_full) + matmul_nt(down_back, down_first_flattened)
@@ -236,44 +269,29 @@
     up_second_gradient = matmul_tn(up_low, grad_hidden)
     ffn_back_part = matmul_nt(grad_hidden, up_full)
     ffn_back_low = matmul_nt(grad_hidden, up_second_flattened)
-    back_total, back_low_total = reduce_heads((ffn_back_part, ffn_back_low))
-    up_back_here = (back_low_total * select).astype(jnp.bfloat16)
-    grad_second = back_total + matmul_nt(up_back_here, up_first_flattened)
-    grad_middle_here = grad_top + second_back(grad_second)[0]
+    back_here, back_low_here = scatter_rows((ffn_back_part, ffn_back_low))
+    up_back_here = (back_low_here * select_here).astype(jnp.bfloat16)
+    grad_second = back_here + matmul_nt(up_back_here, up_first_flattened)
+    grad_middle_here = grad_top_here + second_back(grad_second)[0]
     grad_middle_low_here = grad_middle_here.astype(jnp.bfloat16)
-    heads_back_here = (matmul_nt(grad_middle_low_here, heads_second_flattened) * select).astype(
+    heads_back_here = (matmul_nt(grad_middle_low_here, heads_second_flattened) * select_here).astype(
         jnp.bfloat16
     )
-    result_rows, down_low, grad_middle_low, heads_back, up_back = (
-        result_here,
-        down_low_here,
-        grad_middle_low_here,
-        heads_back_here,
-        up_back_here,
-    )
-    layer_out = result_rows.reshape(layer_input.shape)
+    up_back, heads_back = gather_rows((up_back_here, heads_back_here))
     down_second_gradient = matmul_tn(down_low, grad_top_low)
     grad_up_in = matmul_tn(second_act, up_back)
-    heads_second_gradient = matmul_tn(heads_low, grad_middle_low)
+    heads_second_gradient = matmul_tn(heads_low_here, grad_middle_low_here)
     grad_heads_in = matmul_tn(heads_act, heads_back)
-    grad_heads = (
-        matmul_nt(grad_middle_low, heads_full) + matmul_nt(heads_back, heads_first_flattened)
+    grad_heads_here = (
+        matmul_nt(grad_middle_low_here, heads_full)
+        + matmul_nt(heads_back_here, heads_first_all_flattened)
     ).astype(jnp.bfloat16)
+    grad_heads = lax.all_to_all(grad_heads_here, "tp", 1, 0, tiled=True)
     grad_heads_wide = grad_heads.reshape(seq_here, local_len, device_heads, head_width).astype(
         jnp.float32
     )
     scaled_grad = (grad_heads_wide / per_total).astype(jnp.bfloat16)
     row_delta = jnp.sum(grad_heads_wide * heads_raw, axis=-1) / per_total[..., 0]
-    pieces = (
-        lax.all_gather(key_rows, "ctx", axis=1, tiled=True),
-        lax.all_gather(value_rows, "ctx", axis=1, tiled=True),
-    )
-    piece_len = pieces[0].shape[1]
-    key_pos = jnp.arange(piece_len, dtype=jnp.int32)
-    key_labels = piece_labels(picture_piece_starts, key_pos)
-    visible_mask = visible(here_pos, key_pos, here_labels, key_labels)
-    piece_keys = pieces[0].reshape(seq_here, piece_len, device_heads, head_width)
-    piece_values = pieces[1].reshape(seq_here, piece_len, device_heads, head_width)
     grad_queries, grad_keyrows, grad_valrows = block_grads(
         queries,
         scaled_grad,
@@ -300,36 +318,25 @@
     projection_second_gradient = matmul_tn(first_low, grad_projected)
     attn_back_part = matmul_nt(grad_projected, qkv_full)
     attn_back_low = matmul_nt(grad_projected, projection_second_flattened)
-    first_total, first_low_total = reduce_heads((attn_back_part, attn_back_low))
-    qkv_back_here = (first_low_total * select).astype(jnp.bfloat16)
-    grad_first = first_total + matmul_nt(qkv_back_here, projection_first_flattened)
+    first_here, first_low_here = scatter_rows((attn_back_part, attn_back_low))
+    qkv_back_here = (first_low_here * select_here).astype(jnp.bfloat16)
+    grad_first = first_here + matmul_nt(qkv_back_here, projection_first_flattened)
     input_here = (grad_middle_here + first_back_full(grad_first)[0]).astype(jnp.bfloat16)
-    input_rows, qkv_back = (input_here, qkv_back_here)
+    input_rows, qkv_back = gather_rows((input_here, qkv_back_here))
     input_grad = input_rows.reshape(layer_input.shape)
     grad_qkv_in = matmul_tn(first_act, qkv_back)
+    heads_second_total = lax.psum(heads_second_gradient, "tp")
     adapter_terms = (
         unflat_in(grad_qkv_in, adapter_tables),
         projection_second_gradient.reshape(adapter_projection_second.shape),
         unflat_in(grad_heads_in, adapter_tables),
-        heads_second_gradient.reshape(adapter_heads_second.shape),
+        heads_second_total.reshape(adapter_heads_second.shape),
         unflat_in(grad_up_in, adapter_tables),
         up_second_gradient.reshape(adapter_up_second.shape),
         unflat_in(grad_down_in, adapter_tables),
         down_second_gradient.reshape(adapter_down_second.shape),
     )
-    summed = lax.psum(
-        (
-            adapter_terms[0],
-            adapter_terms[1],
-            adapter_terms[2],
-            adapter_terms[3],
-            adapter_terms[4],
-            adapter_terms[5],
-            adapter_terms[6],
-            adapter_terms[7],
-        ),
-        ("shard", "ctx"),
-    )
+    summed = lax.psum(adapter_terms, ("shard", "ctx"))
     return (
         layer_out,
         input_grad,

time: 1870 us -> 1520 us (0.81)
  waiting for transfers between devices: 1510 us -> 1090 us
  blocking collectives: 0 us -> 81.7 us
  matrix products: 227 us -> 201 us
    psum x4 -> x2, waiting for transfers between devices: 1270 us -> 162 us  [the longest x1 115 us: body(): summed = lax.psum(adapter_terms, ('shard', 'ctx'))]
    reduce_scatter x0 -> x3, waiting for transfers between devices: none -> 434 us  [scatter_rows(): lax.psum_scatter(jnp.concatenate(partials, axis=1), 'tp', scatter_dimensi...]
    all_gather x1 -> x5, waiting for transfers between devices: 0.01 us -> 264 us  [the longest x3 195 us: gather_rows(): lax.all_gather(jnp.concatenate(rows_here, axis=1), 'tp', axis=0, tiled=True)]
    all_gather x0 -> x2, blocking collectives: none -> 51.5 us  [the longest x1 27.4 us: body(): lax.all_gather(adapter_heads_first, 'tp', axis=1, tiled=True)]
    all_to_all x0 -> x1, blocking collectives: none -> 30.1 us  [body(): grad_heads = lax.all_to_all(grad_heads_here, 'tp', 1, 0, tiled=True)]
    dot_general x12, matrix products: 81.1 us -> 59.7 us  [matmul_nt(): lax.dot_general(left_mat, right_mat, (((1,), (1,)), ((), ())), preferred_...]
  transfers between devices with their start and end apart: 12 -> 18, of which waited for: 10 -> 14; matrix products, arithmetic and copies ran while one was open for 9% -> 14% of each run, Pallas kernels for 0% -> 0%
where the time goes in v1:
time: 1520 us; the launch traced here: 1510 us
  waiting for transfers between devices  1090 us (72%)
  matrix products  201 us (13%)
  blocking collectives  81.7 us (5%)
  local copies, waits for them, and re-layouts  66.4 us (4%)
  other arithmetic  54.7 us (4%)
  between operations  15.3 us (1%)
    reduce_scatter x3, waiting for transfers between devices, scatter_rows(): lax.psum_scatter(jnp.concatenate(partials, axis=1), 'tp', scatter_dimensi...  434 us
    all_gather x3, waiting for transfers between devices, gather_rows(): lax.all_gather(jnp.concatenate(rows_here, axis=1), 'tp', axis=0, tiled=True)  195 us
    psum x1, waiting for transfers between devices, body(): summed = lax.psum(adapter_terms, ('shard', 'ctx'))  115 us
    reduce_scatter x1, waiting for transfers between devices, body(): lax.psum_scatter(grad_valrows, 'ctx', scatter_dimension=1, tiled=True)  84.4 us
    all_gather x1, waiting for transfers between devices, body(): lax.all_gather(attention_output_weight, 'tp', axis=0, tiled=True)  69.8 us
    dot_general x12, matrix products, matmul(): return jnp.dot(left_mat, right_mat, preferred_element_type=jnp.float32)  60.3 us
    dot_general x12, matrix products, matmul_nt(): lax.dot_general(left_mat, right_mat, (((1,), (1,)), ((), ())), preferred_...  59.7 us
    all_gather x1, waiting for transfers between devices, body(): lax.all_gather(key_rows, 'ctx', axis=1, tiled=True)  48.4 us
  transfers between devices with their start and end apart: 18, of which 14 were waited for; matrix products, arithmetic and copies ran while one was open for 14% of the time, Pallas kernels for 0%

profile of v1, /device:TPU:0, one launch (start us, length us, event | category | flops | bytes accessed | tf_op | source)
XLA Modules:
  0.0 1514.6 jit_solution(5506899695237392603)
XLA Ops:
  7.2 4.7 copy.75
  13.4 3.2 convert_reduce_fusion
  23.0 8.6 all-gather.11.cloned.1.call-done
  31.6 10.1 fusion.40
  45.4 69.8 %all-gather.17.cloned.1.call-done = bf16[2048,1024]{1,0:T(8,128)(2,1)} async-done(((bf16[512,1024]{1,0:T(8,128)(2,1)}), bf16[2048,1024]{1,0:T(8,128)(2,1)}) %all-gather.17.cloned.1.call-update) | async-done | bytes 4194320 | tf_op jit(solution)/shard_map/all_gather | solution.py:181
  123.6 45.1 %all-gather.13.cloned.1.call-done = bf16[4,1024,512]{2,1,0:T(8,128)(2,1)} async-done(((bf16[4,256,512]{2,1,0:T(8,128)(2,1)}), bf16[4,1024,512]{2,1,0:T(8,128)(2,1)}) %all-gather.13.cloned.1.call-update) | async-done | bytes 4194320 | tf_op jit(solution)/shard_map/all_gather | solution.py:220
  168.7 6.3 copy.77
  175.0 48.4 %all-gather.15.cloned.1.call-done = bf16[4,1024,512]{1,2,0:T(8,128)(2,1)} async-done(((bf16[4,256,512]{1,2,0:T(8,128)(2,1)}), bf16[4,1024,512]{1,2,0:T(8,128)(2,1)}) %all-gather.15.cloned.1.call-update) | async-done | bytes 4194320 | tf_op jit(solution)/shard_map/all_gather | solution.py:219
  223.4 14.3 fusion.37
  237.7 11.8 fusion.38
  249.5 4.6 all-to-all-start
  254.1 8.5 convert.22
  262.6 27.4 %all_gather.41 = bf16[8,2048,16]{1,2,0:T(8,128)(2,1)S(1)} all-gather(bf16[8,512,16]{1,2,0:T(8,128)(2,1)S(1)} %copy-done.44), channel_id=1, replica_groups=mesh['shard'=2,'ctx'=4,'tp'=4] {'tp'}, dimensions={1}, use_global_device_ids=true | all-gather | bytes 655360 | tf_op jit(solution)/shard_map/all_gather | solution.py:186
  290.6 6.4 convolution_add_fusion.6
  299.5 3.6 fusion.23
  303.0 14.9 fusion.44
  318.0 62.4 %all-gather.21.cloned.1.call-done = bf16[1024,2048]{1,0:T(8,128)(2,1)} async-done(((bf16[256,2048]{1,0:T(8,128)(2,1)}), bf16[1024,2048]{1,0:T(8,128)(2,1)}) %all-gather.21.cloned.1.call-update) | async-done | bytes 4194320 | tf_op jit(solution)/shard_map/all_gather | solution.py:126
  380.4 15.4 %fusion.41 = f32[1024,2048]{1,0:T(8,128)} fusion(bf16[1024,2048]{1,0:T(8,128)(2,1)} %all-gather.21.cloned.1.call-done, bf16[2048,2048]{1,0:T(8,128)(2,1)} %all-gather.23.cloned.1.call-done), kind=kOutput, calls=%fused_computation.122 | convolution fusion | flops 8589934592 | bytes 20971520 | tf_op jit(solution)/shard_map/dot_general | solution.py:43
  397.0 6.9 multiply_convert_fusion.1
  404.0 9.8 fusion.3
  415.9 8.9 fusion.45
  424.8 4.2 pad_maximum_fusion.1
  429.2 151.3 %reduce-scatter.8.cloned.1.call-done = f32[256,2176]{1,0:T(8,128)} async-done(((f32[1024,2176]{1,0:T(8,128)}), f32[256,2176]{1,0:T(8,128)}) %reduce-scatter.8.cloned.1.call-update) | async-done | bytes 2228240 | tf_op jit(solution)/shard_map/reduce_scatter | solution.py:118
  594.1 30.1 %all_to_all.29 = bf16[256,4,512]{0,2,1:T(8,128)(2,1)S(1)} all-to-all(bf16[256,4,512]{0,2,1:T(8,128)(2,1)} %bitcast.197), channel_id=1, replica_groups=mesh['shard'=2,'ctx'=4,'tp'=4] {'tp'}, dimensions={1} | all-to-all | bytes 2097152 | tf_op jit(solution)/shard_map/all_to_all | solution.py:289
  627.7 9.2 multiply_convert_fusion
  636.9 3.3 copy-done.2
  640.2 4.9 multiply_bitcast_fusion
  645.1 11.7 fusion.10
  657.1 3.8 fusion.43
  661.0 11.3 fusion.42
  672.3 4.2 pad_maximum_fusion
  676.6 9.0 fusion.19
  690.4 40.2 %reduce-scatter.10.cloned.1.call-done = f32[4,256,4,128]{1,3,2,0:T(8,128)} async-done(((f32[4,1024,4,128]{1,3,2,0:T(8,128)}), f32[4,256,4,128]{1,3,2,0:T(8,128)}) %reduce-scatter.10.cloned.1.call-update) | async-done | bytes 2097168 | tf_op jit(solution)/shard_map/reduce_scatter | solution.py:307
  735.6 84.4 %reduce-scatter.12.cloned.1.call-done = f32[4,256,4,128]{1,3,2,0:T(8,128)} async-done(((f32[4,1024,4,128]{1,3,2,0:T(8,128)}), f32[4,256,4,128]{1,3,2,0:T(8,128)}) %reduce-scatter.12.cloned.1.call-update) | async-done | bytes 2097168 | tf_op jit(solution)/shard_map/reduce_scatter | solution.py:308
  830.1 3.0 fusion.49
  833.2 8.8 fusion.48
  842.0 4.2 pad_maximum_fusion.2
  848.3 126.9 %reduce-scatter.6.cloned.1.call-done = f32[256,2176]{1,0:T(8,128)} async-done(((f32[1024,2176]{1,0:T(8,128)}), f32[256,2176]{1,0:T(8,128)}) %reduce-scatter.6.cloned.1.call-update) | async-done | bytes 2228240 | tf_op jit(solution)/shard_map/reduce_scatter | solution.py:118
  975.2 156.1 %reduce-scatter.14.cloned.1.call-done = f32[256,2176]{1,0:T(8,128)} async-done(((f32[1024,2176]{1,0:T(8,128)}), f32[256,2176]{1,0:T(8,128)}) %reduce-scatter.14.cloned.1.call-update) | async-done | bytes 2228240 | tf_op jit(solution)/shard_map/reduce_scatter | solution.py:118
  1146.0 4.2 fusion.52
  1152.0 24.1 %all_gather.47 = bf16[1024,256]{1,0:T(8,128)(2,1)S(1)} all-gather(bf16[256,256]{1,0:T(8,128)(2,1)S(1)} %pad_maximum_fusion.5), channel_id=1, replica_groups=mesh['shard'=2,'ctx'=4,'tp'=4] {'tp'}, dimensions={0}, use_global_device_ids=true | all-gather | bytes 655360 | tf_op jit(solution)/shard_map/all_gather | solution.py:126
  1178.7 3.9 fusion.26
  1186.7 48.3 %all-gather.29.cloned.1.call-done = bf16[1024,2176]{1,0:T(8,128)(2,1)} async-done(((bf16[256,2176]{1,0:T(8,128)(2,1)}), bf16[1024,2176]{1,0:T(8,128)(2,1)}) %all-gather.29.cloned.1.call-update) | async-done | bytes 4456464 | tf_op jit(solution)/shard_map/all_gather | solution.py:126
  1236.0 84.0 %all-gather.27.cloned.1.call-done = bf16[1024,2176]{1,0:T(8,128)(2,1)} async-done(((bf16[256,2176]{1,0:T(8,128)(2,1)}), bf16[1024,2176]{1,0:T(8,128)(2,1)}) %all-gather.27.cloned.1.call-update) | async-done | bytes 4456464 | tf_op jit(solution)/shard_map/all_gather | solution.py:126
  1321.2 4.0 fusion.54
  1327.0 46.1 %all-reduce.4.cloned.1.call-done = f32[8,16,2048]{2,1,0:T(8,128)} async-done(((f32[8,16,2048]{2,1,0:T(8,128)}), f32[8,16,2048]{2,1,0:T(8,128)}) %all-reduce.4.cloned.1.call-update) | async-done | bytes 1048592 | tf_op jit(solution)/shard_map/psum | solution.py:328
  1373.2 4.9 slice.65
  1380.7 115.5 %all-reduce.6.cloned.1.call-done = (f32[8,2048,16]{1,2,0:T(8,128)}, f32[8,16,3,512]{3,2,1,0:T(4,128)}, f32[8,512,16]{1,2,0:T(8,128)}, f32[8,16,2048]{2,1,0:T(8,1...) async-done(((f32[8,2048,16]{1,2,0:T(8,128)}, f32[8,16,3,512]{3,2,1,0:T(4,128)}, ...) | async-done | bytes 7340048 | tf_op jit(solution)/shard_map/psum | solution.py:339
  (250 shorter events, 106.6 us)
Async XLA Ops:
  7.2 389.8 %copy-start = (bf16[8,16,2048]{2,1,0:T(8,128)(2,1)S(1)}, bf16[8,16,2048]{2,1,0:T(8,128)(2,1)}, u32[]{:S(2)}) copy-start(bf16[8,16,2048]{2,1,0:T(8,128)(2,1)} %param.37) | copy-start | bytes 1572868
  7.2 5.6 copy-start.43
  7.2 24.4 %all-gather.11.cloned.1.call-start = ((), (), s32[]{:S(2)}) async-start(), calls=%async_computation.7 | async-start | bytes 9437184 | tf_op jit(solution)/shard_map/all_gather | solution.py:204
  12.0 103.2 %all-gather.17.cloned.1.call-start = ((), (), s32[]{:S(2)}) async-start(), calls=%async_computation.10 | async-start | bytes 5242880 | tf_op jit(solution)/shard_map/all_gather | solution.py:181
  12.8 155.9 %all-gather.13.cloned.1.call-start = ((), (), s32[]{:S(2)}) async-start(), calls=%async_computation.8 | async-start | bytes 5242880 | tf_op jit(solution)/shard_map/all_gather | solution.py:220
  13.3 28.4 %copy-start.20 = (bf16[16,8,3,512]{3,1,2,0:T(8,128)(2,1)}, bf16[16,8,3,512]{3,1,2,0:T(8,128)(2,1)S(1)}, u32[]{:S(2)}) copy-start(bf16[16,8,3,512]{3,1,2,0:T(8,128)(2,1)S(1)} %copy.105) | copy-start | bytes 1179652
  23.0 18.7 %copy-start.22 = (bf16[1024,128]{1,0:T(8,128)(2,1)}, bf16[1024,128]{1,0:T(8,128)(2,1)S(1)}, u32[]{:S(2)}) copy-start(bf16[1024,128]{1,0:T(8,128)(2,1)S(1)} %fusion.21) | copy-start | bytes 786436
  44.0 179.4 %all-gather.15.cloned.1.call-start = ((), (), s32[]{:S(2)}) async-start(), calls=%async_computation.9 | async-start | bytes 5242880 | tf_op jit(solution)/shard_map/all_gather | solution.py:219
  45.4 245.2 %all-gather.19.cloned.1.call-start = ((), (), s32[]{:S(2)}) async-start(), calls=%async_computation.11 | async-start | bytes 12582912 | tf_op jit(solution)/shard_map/all_gather | solution.py:180
  115.2 187.9 %all-gather.25.cloned.1.call-start = ((), (), s32[]{:S(2)}) async-start(), calls=%async_computation.14 | async-start | bytes 12582912 | tf_op jit(solution)/shard_map/all_gather | solution.py:209
  115.8 202.2 %all-gather.23.cloned.1.call-start = ((), (), s32[]{:S(2)}) async-start(), calls=%async_computation.13 | async-start | bytes 12582912 | tf_op jit(solution)/shard_map/all_gather | solution.py:205
  123.6 99.8 %copy-start.14 = (bf16[4,256,4,128]{1,3,2,0:T(8,128)(2,1)}, bf16[4,256,4,128]{1,3,2,0:T(8,128)(2,1)S(1)}, u32[]{:S(2)}) copy-start(bf16[4,256,4,128]{1,3,2,0:T(8,128)(2,1)S(1)} %copy.88) | copy-start | bytes 3145732
  223.4 14.3 copy-start.4
  249.5 40.5 %all-to-all-start = ((bf16[4,256,512]{1,2,0:T(8,128)(2,1)}), bf16[4,256,512]{1,2,0:T(8,128)(2,1)S(1)}, u32[]{:S(2)}, u32[]{:S(2)}) async-start(bf16[4,256,512]{1,2,0:T(8,128)(2,1)} %bitcast.12), calls=%async_computation | async-start | bytes 2097152 | tf_op jit(solution)/shard_map/all_to_all | solution.py:239
  254.1 126.2 %all-gather.21.cloned.1.call-start = ((), (), s32[]{:S(2)}) async-start(), calls=%async_computation.12 | async-start | bytes 5242880 | tf_op jit(solution)/shard_map/all_gather | solution.py:126
  254.1 8.5 copy-start.44
  290.1 6.9 copy-start.18
  290.6 6.5 copy-start.40
  290.6 6.5 copy-start.29
  299.4 281.1 %reduce-scatter.8.cloned.1.call-start = ((), (), s32[]{:S(2)}) async-start(), calls=%async_computation.17 | async-start | bytes 11141120 | tf_op jit(solution)/shard_map/reduce_scatter | solution.py:118
  380.4 15.4 %copy-start.6 = (bf16[1024,2048]{1,0:T(8,128)(2,1)S(1)}, bf16[1024,2048]{1,0:T(8,128)(2,1)}, u32[]{:S(2)}) copy-start(bf16[1024,2048]{1,0:T(8,128)(2,1)} %all-gather.21.cloned.1.call-done) | copy-start | bytes 12582916
  380.4 15.4 %copy-start.24 = (bf16[8,2048,16]{1,2,0:T(8,128)(2,1)S(1)}, bf16[8,2048,16]{1,2,0:T(8,128)(2,1)}, u32[]{:S(2)}) copy-start(bf16[8,2048,16]{1,2,0:T(8,128)(2,1)} %param.36) | copy-start | bytes 1572868
  397.0 7.0 copy-start.31
  397.0 7.0 copy-start.42
  397.0 18.8 %slice-start.4 = ((s8[8388608]{0:T(1024)(128)(4,1)}), s8[4194304]{0:T(1024)(128)(4,1)S(1)}, s32[]{:S(2)}) async-start(s8[8388608]{0:T(1024)(128)(4,1)} %bitcast.221), calls=%async_computation.28 | async-start | bytes 8388608
  404.0 11.9 slice-start.5
  429.0 152.5 %copy-start.25 = (bf16[8,2048,16]{1,2,0:T(8,128)(2,1)S(1)}, bf16[8,2048,16]{1,2,0:T(8,128)(2,1)}, u32[]{:S(2)}) copy-start(bf16[8,2048,16]{1,2,0:T(8,128)(2,1)} %param.36) | copy-start | bytes 1572868
  429.0 301.6 %reduce-scatter.10.cloned.1.call-start = ((), (), s32[]{:S(2)}) async-start(), calls=%async_computation.18 | async-start | bytes 10485760 | tf_op jit(solution)/shard_map/reduce_scatter | solution.py:307
  581.5 6.5 slice-start
  627.7 12.5 copy-start.15
  645.1 174.9 %reduce-scatter.12.cloned.1.call-start = ((), (), s32[]{:S(2)}) async-start(), calls=%async_computation.19 | async-start | bytes 10485760 | tf_op jit(solution)/shard_map/reduce_scatter | solution.py:308
  656.8 318.3 %reduce-scatter.6.cloned.1.call-start = ((), (), s32[]{:S(2)}) async-start(), calls=%async_computation.15 | async-start | bytes 11141120 | tf_op jit(solution)/shard_map/reduce_scatter | solution.py:118
  676.5 454.7 %reduce-scatter.14.cloned.1.call-start = ((), (), s32[]{:S(2)}) async-start(), calls=%async_computation.20 | async-start | bytes 11141120 | tf_op jit(solution)/shard_map/reduce_scatter | solution.py:118
  735.6 94.5 %copy-start.21 = (bf16[16,8,3,512]{3,1,2,0:T(8,128)(2,1)S(1)}, bf16[16,8,3,512]{3,1,2,0:T(8,128)(2,1)}, u32[]{:S(2)}) copy-start(bf16[16,8,3,512]{3,1,2,0:T(8,128)(2,1)} %copy-done.20) | copy-start | bytes 1179652
  846.2 286.1 %copy-start.27 = (bf16[8,2048,16]{1,2,0:T(8,128)(2,1)S(1)}, bf16[8,2048,16]{1,2,0:T(8,128)(2,1)}, u32[]{:S(2)}) copy-start(bf16[8,2048,16]{1,2,0:T(8,128)(2,1)} %param.32) | copy-start | bytes 1572868
  846.2 286.1 %copy-start.47 = (f32[2048]{0:T(1024)S(1)}, f32[2048]{0:T(1024)}, u32[]{:S(2)}) copy-start(f32[2048]{0:T(1024)} %param.24) | copy-start | bytes 24580
  846.2 388.8 %all-gather.29.cloned.1.call-start = ((), (), s32[]{:S(2)}) async-start(), calls=%async_computation.21 | async-start | bytes 5570560 | tf_op jit(solution)/shard_map/all_gather | solution.py:126
  1140.6 179.3 %all-gather.27.cloned.1.call-start = ((), (), s32[]{:S(2)}) async-start(), calls=%async_computation.16 | async-start | bytes 5570560 | tf_op jit(solution)/shard_map/all_gather | solution.py:126
  1143.9 229.2 %all-reduce.4.cloned.1.call-start = ((), (), s32[]{:S(2)}) async-start(), calls=%async_computation.22 | async-start | bytes 2097152 | tf_op jit(solution)/shard_map/psum | solution.py:328
  1152.0 25.3 %copy-start.17 = (bf16[256,2048]{1,0:T(8,128)(2,1)S(1)}, bf16[256,2048]{1,0:T(8,128)(2,1)}, u32[]{:S(2)}) copy-start(bf16[256,2048]{1,0:T(8,128)(2,1)} %copy-done.16) | copy-start | bytes 3145732
  1152.0 25.3 %copy-start.41 = (bf16[256,128]{1,0:T(8,128)(2,1)S(1)}, bf16[256,128]{1,0:T(8,128)(2,1)}, u32[]{:S(2)}) copy-start(bf16[256,128]{1,0:T(8,128)(2,1)} %copy-done.40) | copy-start | bytes 196612
  1177.3 5.3 copy-start.23
  1178.6 317.5 %all-reduce.6.cloned.1.call-start = ((), (), s32[]{:S(2)}) async-start(), calls=%async_computation.23 | async-start | bytes 15204352 | tf_op jit(solution)/shard_map/psum | solution.py:339
  1373.1 5.0 slice-start.2
  1496.2 6.6 copy-start.37
  1496.2 7.5 copy-start.36
  1496.2 8.5 copy-start.35
  1498.7 7.0 copy-start.34
  (30 other events, 88.7 us)
Sparse Core Ops, SparseCore 0:
  12.1 19.4 all-gather.10
  33.2 81.9 all-gather.16
  117.6 51.0 all-gather.12
  170.9 52.4 all-gather.14
  224.8 19.8 all-gather.18
  246.1 21.0 all-gather.24
  268.7 21.0 all-gather.22
  299.5 80.8 all-gather.20
  429.1 151.3 reduce-scatter.7
  645.2 85.3 reduce-scatter.9
  733.7 86.2 reduce-scatter.11
  822.2 152.8 reduce-scatter.5
  977.5 153.6 reduce-scatter.13
  1140.8 94.1 all-gather.28
  1236.4 83.5 all-gather.26
  1322.8 50.3 all-reduce.3
  1378.3 117.8 all-reduce.5

commit v2 on v1

--- a/solution.py
+++ b/solution.py
@@ -116,9 +116,12 @@
 def scatter_rows(partials):
     widths = [part.shape[1] for part in partials]
     joined = lax.psum_scatter(
-        jnp.concatenate(partials, axis=1), "tp", scatter_dimension=0, tiled=True
-    )
-    return split_columns(joined, widths)
+        jnp.concatenate(partials, axis=1).astype(jnp.bfloat16),
+        "tp",
+        scatter_dimension=0,
+        tiled=True,
+    )
+    return split_columns(joined.astype(jnp.float32), widths)
 
 
 def gather_rows(rows_here):

time: 1520 us -> 1300 us (0.86)
  waiting for transfers between devices: 1090 us -> 874 us
    reduce_scatter x3, waiting for transfers between devices: 434 us -> 217 us  [scatter_rows(): lax.psum_scatter(jnp.concatenate(partials, axis=1).astype(jnp.bfloat16),...]
  transfers between devices with their start and end apart: 18 -> 18, of which waited for: 14 -> 14; matrix products, arithmetic and copies ran while one was open for 14% -> 16% of each run, Pallas kernels for 0% -> 0%
where the time goes in v2:
time: 1300 us; the launch traced here: 1290 us
  waiting for transfers between devices  874 us (67%)
  matrix products  198 us (15%)
  blocking collectives  81 us (6%)
  local copies, waits for them, and re-layouts  65.4 us (5%)
  other arithmetic  55 us (4%)
  between operations  15.4 us (1%)
    reduce_scatter x3, waiting for transfers between devices, scatter_rows(): lax.psum_scatter(jnp.concatenate(partials, axis=1).astype(jnp.bfloat16),...  217 us
    all_gather x3, waiting for transfers between devices, gather_rows(): lax.all_gather(jnp.concatenate(rows_here, axis=1), 'tp', axis=0, tiled=True)  195 us
    psum x1, waiting for transfers between devices, body(): summed = lax.psum(adapter_terms, ('shard', 'ctx'))  115 us
    reduce_scatter x1, waiting for transfers between devices, body(): lax.psum_scatter(grad_valrows, 'ctx', scatter_dimension=1, tiled=True)  84.4 us
    all_gather x1, waiting for transfers between devices, body(): lax.all_gather(attention_output_weight, 'tp', axis=0, tiled=True)  69.8 us
    dot_general x12, matrix products, matmul_nt(): lax.dot_general(left_mat, right_mat, (((1,), (1,)), ((), ())), preferred_...  58.7 us
    dot_general x12, matrix products, matmul(): return jnp.dot(left_mat, right_mat, preferred_element_type=jnp.float32)  57.7 us
    all_gather x1, waiting for transfers between devices, body(): lax.all_gather(key_rows, 'ctx', axis=1, tiled=True)  48.4 us
  transfers between devices with their start and end apart: 18, of which 14 were waited for; matrix products, arithmetic and copies ran while one was open for 16% of the time, Pallas kernels for 0%

profile of v2, /device:TPU:0, one launch (start us, length us, event | category | flops | bytes accessed | tf_op | source)
XLA Modules:
  0.0 1294.6 jit_solution(7161566004308783575)
XLA Ops:
  7.2 4.7 copy.75
  13.4 3.2 convert_reduce_fusion
  23.0 8.6 all-gather.11.cloned.1.call-done
  31.6 10.1 fusion.40
  45.4 69.8 %all-gather.17.cloned.1.call-done = bf16[2048,1024]{1,0:T(8,128)(2,1)} async-done(((bf16[512,1024]{1,0:T(8,128)(2,1)}), bf16[2048,1024]{1,0:T(8,128)(2,1)}) %all-gather.17.cloned.1.call-update) | async-done | bytes 4194320 | tf_op jit(solution)/shard_map/all_gather | solution.py:184
  123.6 45.1 %all-gather.13.cloned.1.call-done = bf16[4,1024,512]{2,1,0:T(8,128)(2,1)} async-done(((bf16[4,256,512]{2,1,0:T(8,128)(2,1)}), bf16[4,1024,512]{2,1,0:T(8,128)(2,1)}) %all-gather.13.cloned.1.call-update) | async-done | bytes 4194320 | tf_op jit(solution)/shard_map/all_gather | solution.py:223
  168.7 6.3 copy.77
  175.0 48.4 %all-gather.15.cloned.1.call-done = bf16[4,1024,512]{1,2,0:T(8,128)(2,1)} async-done(((bf16[4,256,512]{1,2,0:T(8,128)(2,1)}), bf16[4,1024,512]{1,2,0:T(8,128)(2,1)}) %all-gather.15.cloned.1.call-update) | async-done | bytes 4194320 | tf_op jit(solution)/shard_map/all_gather | solution.py:222
  223.4 14.3 %fusion.37 = (f32[4,4,256]{2,1,0:T(4,128)S(1)}, f32[4,4,256,1024]{3,2,1,0:T(8,128)}) fusion(f32[4,256,1024]{2,1,0:T(8,128)} %broadcast_multiply_fusion, bf16[4,256,4,128]{1,3,2,0:T(8,128)(2,1)S(1)} %copy.88, bf16[4,1024,4,128]{1,3,2,0:T(8,128)(2,1)} %bitcast.180, pred[4,256,1024]{2,1,0:T(8,128)(4,1)S(1)} %and_or_fusion), kind=kOutput, calls=%fused_computation.124 | convolution fusion | flops 1090514944 | bytes 27279360 | tf_op jit(solution)/shard_map/sqhd,skhd->shqk/dot_general | solution.py:75
  237.7 11.8 fusion.38
  249.5 4.6 all-to-all-start
  254.1 8.5 convert.52
  262.6 27.4 %all_gather.41 = bf16[8,2048,16]{1,2,0:T(8,128)(2,1)S(1)} all-gather(bf16[8,512,16]{1,2,0:T(8,128)(2,1)S(1)} %copy-done.43), channel_id=1, replica_groups=mesh['shard'=2,'ctx'=4,'tp'=4] {'tp'}, dimensions={1}, use_global_device_ids=true | all-gather | bytes 655360 | tf_op jit(solution)/shard_map/all_gather | solution.py:189
  290.6 6.4 convolution_add_fusion.6
  299.7 3.6 fusion.23
  303.3 14.7 %fusion.42 = f32[1024,2048]{1,0:T(8,128)} fusion(bf16[1024,2048]{1,0:T(8,128)(2,1)} %bitcast.164, bf16[2048,2048]{1,0:T(8,128)(2,1)} %all-gather.25.cloned.1.call-done), kind=kOutput, calls=%fused_computation.129 | convolution fusion | flops 8589934592 | bytes 20971520 | tf_op jit(solution)/shard_map/dot_general | solution.py:53
  318.0 62.4 %all-gather.21.cloned.1.call-done = bf16[1024,2048]{1,0:T(8,128)(2,1)} async-done(((bf16[256,2048]{1,0:T(8,128)(2,1)}), bf16[1024,2048]{1,0:T(8,128)(2,1)}) %all-gather.21.cloned.1.call-update) | async-done | bytes 4194320 | tf_op jit(solution)/shard_map/all_gather | solution.py:129
  380.4 13.5 %fusion.41 = f32[1024,2048]{1,0:T(8,128)S(1)} fusion(bf16[1024,2048]{1,0:T(8,128)(2,1)} %all-gather.21.cloned.1.call-done, bf16[2048,2048]{1,0:T(8,128)(2,1)} %all-gather.23.cloned.1.call-done), kind=kOutput, calls=%fused_computation.128 | convolution fusion | flops 8589934592 | bytes 20971520 | tf_op jit(solution)/shard_map/dot_general | solution.py:43
  395.2 6.2 multiply_convert_fusion.1
  401.4 11.1 fusion.3
  413.8 9.1 convolution_convert_fusion.1
  425.7 79.5 %reduce-scatter.8.cloned.1.call-done = bf16[256,2176]{1,0:T(8,128)(2,1)} async-done(((bf16[1024,2176]{1,0:T(8,128)(2,1)}), bf16[256,2176]{1,0:T(8,128)(2,1)}) %reduce-scatter.8.cloned.1.call-update) | async-done | bytes 1114128 | tf_op jit(solution)/shard_map/reduce_scatter | solution.py:118
  518.1 29.9 %all_to_all.29 = bf16[256,4,512]{0,2,1:T(8,128)(2,1)S(1)} all-to-all(bf16[256,4,512]{0,2,1:T(8,128)(2,1)} %bitcast.197), channel_id=1, replica_groups=mesh['shard'=2,'ctx'=4,'tp'=4] {'tp'}, dimensions={1} | all-to-all | bytes 2097152 | tf_op jit(solution)/shard_map/all_to_all | solution.py:292
  551.4 9.2 multiply_convert_fusion
  560.6 3.2 copy-done.2
  563.9 4.9 multiply_bitcast_fusion
  568.8 11.6 fusion.10
  580.7 3.8 convolution_convert_fusion.5
  584.7 11.3 convolution_convert_fusion.2
  598.7 8.8 fusion.19
  612.2 42.0 %reduce-scatter.10.cloned.1.call-done = f32[4,256,4,128]{1,3,2,0:T(8,128)} async-done(((f32[4,1024,4,128]{1,3,2,0:T(8,128)}), f32[4,256,4,128]{1,3,2,0:T(8,128)}) %reduce-scatter.10.cloned.1.call-update) | async-done | bytes 2097168 | tf_op jit(solution)/shard_map/reduce_scatter | solution.py:310
  654.2 2.7 convert.39
  659.3 84.4 %reduce-scatter.12.cloned.1.call-done = f32[4,256,4,128]{1,3,2,0:T(8,128)} async-done(((f32[4,1024,4,128]{1,3,2,0:T(8,128)}), f32[4,256,4,128]{1,3,2,0:T(8,128)}) %reduce-scatter.12.cloned.1.call-update) | async-done | bytes 2097168 | tf_op jit(solution)/shard_map/reduce_scatter | solution.py:311
  751.1 2.7 bitcast_dynamic-update-slice_fusion
  753.8 3.0 convolution_convert_fusion.3
  756.8 8.8 convolution_convert_fusion
  770.3 56.6 %reduce-scatter.6.cloned.1.call-done = bf16[256,2176]{1,0:T(8,128)(2,1)} async-done(((bf16[1024,2176]{1,0:T(8,128)(2,1)}), bf16[256,2176]{1,0:T(8,128)(2,1)}) %reduce-scatter.6.cloned.1.call-update) | async-done | bytes 1114128 | tf_op jit(solution)/shard_map/reduce_scatter | solution.py:118
  826.9 2.7 convert_element_type.153
  829.6 81.1 %reduce-scatter.14.cloned.1.call-done = bf16[256,2176]{1,0:T(8,128)(2,1)} async-done(((bf16[1024,2176]{1,0:T(8,128)(2,1)}), bf16[256,2176]{1,0:T(8,128)(2,1)}) %reduce-scatter.14.cloned.1.call-update) | async-done | bytes 1114128 | tf_op jit(solution)/shard_map/reduce_scatter | solution.py:118
  926.4 4.3 fusion.46
  932.5 23.7 %all_gather.47 = bf16[1024,256]{1,0:T(8,128)(2,1)S(1)} all-gather(bf16[256,256]{1,0:T(8,128)(2,1)S(1)} %pad_maximum_fusion.5), channel_id=1, replica_groups=mesh['shard'=2,'ctx'=4,'tp'=4] {'tp'}, dimensions={0}, use_global_device_ids=true | all-gather | bytes 655360 | tf_op jit(solution)/shard_map/all_gather | solution.py:129
  958.8 3.9 fusion.26
  966.8 48.3 %all-gather.29.cloned.1.call-done = bf16[1024,2176]{1,0:T(8,128)(2,1)} async-done(((bf16[256,2176]{1,0:T(8,128)(2,1)}), bf16[1024,2176]{1,0:T(8,128)(2,1)}) %all-gather.29.cloned.1.call-update) | async-done | bytes 4456464 | tf_op jit(solution)/shard_map/all_gather | solution.py:129
  1016.0 84.0 %all-gather.27.cloned.1.call-done = bf16[1024,2176]{1,0:T(8,128)(2,1)} async-done(((bf16[256,2176]{1,0:T(8,128)(2,1)}), bf16[1024,2176]{1,0:T(8,128)(2,1)}) %all-gather.27.cloned.1.call-update) | async-done | bytes 4456464 | tf_op jit(solution)/shard_map/all_gather | solution.py:129
  1101.3 4.0 fusion.48
  1107.0 46.1 %all-reduce.4.cloned.1.call-done = f32[8,16,2048]{2,1,0:T(8,128)} async-done(((f32[8,16,2048]{2,1,0:T(8,128)}), f32[8,16,2048]{2,1,0:T(8,128)}) %all-reduce.4.cloned.1.call-update) | async-done | bytes 1048592 | tf_op jit(solution)/shard_map/psum | solution.py:331
  1153.2 4.9 slice.65
  1160.7 115.5 %all-reduce.6.cloned.1.call-done = (f32[8,2048,16]{1,2,0:T(8,128)}, f32[8,16,3,512]{3,2,1,0:T(4,128)}, f32[8,512,16]{1,2,0:T(8,128)}, f32[8,16,2048]{2,1,0:T(8,1...) async-done(((f32[8,2048,16]{1,2,0:T(8,128)}, f32[8,16,3,512]{3,2,1,0:T(4,128)}, ...) | async-done | bytes 7340048 | tf_op jit(solution)/shard_map/psum | solution.py:342
  (253 shorter events, 108.3 us)
Async XLA Ops:
  7.2 388.0 %copy-start = (bf16[8,16,2048]{2,1,0:T(8,128)(2,1)S(1)}, bf16[8,16,2048]{2,1,0:T(8,128)(2,1)}, u32[]{:S(2)}) copy-start(bf16[8,16,2048]{2,1,0:T(8,128)(2,1)} %param.37) | copy-start | bytes 1572868
  7.2 5.6 copy-start.42
  7.2 24.4 %all-gather.11.cloned.1.call-start = ((), (), s32[]{:S(2)}) async-start(), calls=%async_computation.7 | async-start | bytes 9437184 | tf_op jit(solution)/shard_map/all_gather | solution.py:207
  12.0 103.2 %all-gather.17.cloned.1.call-start = ((), (), s32[]{:S(2)}) async-start(), calls=%async_computation.10 | async-start | bytes 5242880 | tf_op jit(solution)/shard_map/all_gather | solution.py:184
  12.8 155.9 %all-gather.13.cloned.1.call-start = ((), (), s32[]{:S(2)}) async-start(), calls=%async_computation.8 | async-start | bytes 5242880 | tf_op jit(solution)/shard_map/all_gather | solution.py:223
  13.3 28.4 %copy-start.29 = (bf16[16,8,3,512]{3,1,2,0:T(8,128)(2,1)}, bf16[16,8,3,512]{3,1,2,0:T(8,128)(2,1)S(1)}, u32[]{:S(2)}) copy-start(bf16[16,8,3,512]{3,1,2,0:T(8,128)(2,1)S(1)} %copy.105) | copy-start | bytes 1179652
  23.0 18.7 %copy-start.20 = (bf16[1024,128]{1,0:T(8,128)(2,1)}, bf16[1024,128]{1,0:T(8,128)(2,1)S(1)}, u32[]{:S(2)}) copy-start(bf16[1024,128]{1,0:T(8,128)(2,1)S(1)} %fusion.21) | copy-start | bytes 786436
  44.0 179.4 %all-gather.15.cloned.1.call-start = ((), (), s32[]{:S(2)}) async-start(), calls=%async_computation.9 | async-start | bytes 5242880 | tf_op jit(solution)/shard_map/all_gather | solution.py:222
  45.4 245.2 %all-gather.19.cloned.1.call-start = ((), (), s32[]{:S(2)}) async-start(), calls=%async_computation.11 | async-start | bytes 12582912 | tf_op jit(solution)/shard_map/all_gather | solution.py:183
  115.2 188.1 %all-gather.25.cloned.1.call-start = ((), (), s32[]{:S(2)}) async-start(), calls=%async_computation.14 | async-start | bytes 12582912 | tf_op jit(solution)/shard_map/all_gather | solution.py:212
  115.8 202.2 %all-gather.23.cloned.1.call-start = ((), (), s32[]{:S(2)}) async-start(), calls=%async_computation.13 | async-start | bytes 12582912 | tf_op jit(solution)/shard_map/all_gather | solution.py:208
  123.6 99.8 %copy-start.10 = (bf16[4,256,4,128]{1,3,2,0:T(8,128)(2,1)}, bf16[4,256,4,128]{1,3,2,0:T(8,128)(2,1)S(1)}, u32[]{:S(2)}) copy-start(bf16[4,256,4,128]{1,3,2,0:T(8,128)(2,1)S(1)} %copy.88) | copy-start | bytes 3145732
  223.4 14.3 %copy-start.4 = (bf16[4,1024,512]{1,2,0:T(8,128)(2,1)S(1)}, bf16[4,1024,512]{1,2,0:T(8,128)(2,1)}, u32[]{:S(2)}) copy-start(bf16[4,1024,512]{1,2,0:T(8,128)(2,1)} %copy.77) | copy-start | bytes 12582916
  249.5 40.5 %all-to-all-start = ((bf16[4,256,512]{1,2,0:T(8,128)(2,1)}), bf16[4,256,512]{1,2,0:T(8,128)(2,1)S(1)}, u32[]{:S(2)}, u32[]{:S(2)}) async-start(bf16[4,256,512]{1,2,0:T(8,128)(2,1)} %bitcast.12), calls=%async_computation | async-start | bytes 2097152 | tf_op jit(solution)/shard_map/all_to_all | solution.py:242
  254.1 126.2 %all-gather.21.cloned.1.call-start = ((), (), s32[]{:S(2)}) async-start(), calls=%async_computation.12 | async-start | bytes 5242880 | tf_op jit(solution)/shard_map/all_gather | solution.py:129
  254.1 8.5 copy-start.43
  290.1 6.9 copy-start.17
  290.6 6.5 copy-start.40
  290.6 6.5 copy-start.27
  299.4 205.8 %reduce-scatter.8.cloned.1.call-start = ((), (), s32[]{:S(2)}) async-start(), calls=%async_computation.17 | async-start | bytes 5570560 | tf_op jit(solution)/shard_map/reduce_scatter | solution.py:118
  380.4 13.5 %copy-start.5 = (bf16[1024,2048]{1,0:T(8,128)(2,1)S(1)}, bf16[1024,2048]{1,0:T(8,128)(2,1)}, u32[]{:S(2)}) copy-start(bf16[1024,2048]{1,0:T(8,128)(2,1)} %all-gather.21.cloned.1.call-done) | copy-start | bytes 12582916
  380.4 13.5 %copy-start.22 = (bf16[8,2048,16]{1,2,0:T(8,128)(2,1)S(1)}, bf16[8,2048,16]{1,2,0:T(8,128)(2,1)}, u32[]{:S(2)}) copy-start(bf16[8,2048,16]{1,2,0:T(8,128)(2,1)} %param.36) | copy-start | bytes 1572868
  395.2 6.3 copy-start.31
  395.2 6.3 copy-start.53
  395.2 18.6 %slice-start.4 = ((s8[8388608]{0:T(1024)(128)(4,1)}), s8[4194304]{0:T(1024)(128)(4,1)S(1)}, s32[]{:S(2)}) async-start(s8[8388608]{0:T(1024)(128)(4,1)} %bitcast.219), calls=%async_computation.28 | async-start | bytes 8388608
  401.4 12.4 slice-start.5
  412.5 10.4 copy-start.19
  425.5 81.1 %copy-start.23 = (bf16[8,2048,16]{1,2,0:T(8,128)(2,1)S(1)}, bf16[8,2048,16]{1,2,0:T(8,128)(2,1)}, u32[]{:S(2)}) copy-start(bf16[8,2048,16]{1,2,0:T(8,128)(2,1)} %param.36) | copy-start | bytes 1572868
  425.5 228.7 %reduce-scatter.10.cloned.1.call-start = ((), (), s32[]{:S(2)}) async-start(), calls=%async_computation.18 | async-start | bytes 10485760 | tf_op jit(solution)/shard_map/reduce_scatter | solution.py:310
  506.6 5.4 slice-start
  551.4 12.4 copy-start.11
  568.7 174.9 %reduce-scatter.12.cloned.1.call-start = ((), (), s32[]{:S(2)}) async-start(), calls=%async_computation.19 | async-start | bytes 10485760 | tf_op jit(solution)/shard_map/reduce_scatter | solution.py:311
  580.5 246.4 %reduce-scatter.6.cloned.1.call-start = ((), (), s32[]{:S(2)}) async-start(), calls=%async_computation.15 | async-start | bytes 5570560 | tf_op jit(solution)/shard_map/reduce_scatter | solution.py:118
  598.6 312.2 %reduce-scatter.14.cloned.1.call-start = ((), (), s32[]{:S(2)}) async-start(), calls=%async_computation.20 | async-start | bytes 5570560 | tf_op jit(solution)/shard_map/reduce_scatter | solution.py:118
  659.3 94.5 %copy-start.30 = (bf16[16,8,3,512]{3,1,2,0:T(8,128)(2,1)S(1)}, bf16[16,8,3,512]{3,1,2,0:T(8,128)(2,1)}, u32[]{:S(2)}) copy-start(bf16[16,8,3,512]{3,1,2,0:T(8,128)(2,1)} %copy-done.29) | copy-start | bytes 1179652
  768.1 145.0 %copy-start.25 = (bf16[8,2048,16]{1,2,0:T(8,128)(2,1)S(1)}, bf16[8,2048,16]{1,2,0:T(8,128)(2,1)}, u32[]{:S(2)}) copy-start(bf16[8,2048,16]{1,2,0:T(8,128)(2,1)} %param.32) | copy-start | bytes 1572868
  768.2 145.0 %copy-start.46 = (f32[2048]{0:T(1024)S(1)}, f32[2048]{0:T(1024)}, u32[]{:S(2)}) copy-start(f32[2048]{0:T(1024)} %param.24) | copy-start | bytes 24580
  768.2 246.9 %all-gather.29.cloned.1.call-start = ((), (), s32[]{:S(2)}) async-start(), calls=%async_computation.21 | async-start | bytes 5570560 | tf_op jit(solution)/shard_map/all_gather | solution.py:129
  921.0 179.0 %all-gather.27.cloned.1.call-start = ((), (), s32[]{:S(2)}) async-start(), calls=%async_computation.16 | async-start | bytes 5570560 | tf_op jit(solution)/shard_map/all_gather | solution.py:129
  924.2 228.9 %all-reduce.4.cloned.1.call-start = ((), (), s32[]{:S(2)}) async-start(), calls=%async_computation.22 | async-start | bytes 2097152 | tf_op jit(solution)/shard_map/psum | solution.py:331
  932.5 24.9 %copy-start.13 = (bf16[256,2048]{1,0:T(8,128)(2,1)S(1)}, bf16[256,2048]{1,0:T(8,128)(2,1)}, u32[]{:S(2)}) copy-start(bf16[256,2048]{1,0:T(8,128)(2,1)} %copy-done.12) | copy-start | bytes 3145732
  932.5 24.9 %copy-start.41 = (bf16[256,128]{1,0:T(8,128)(2,1)S(1)}, bf16[256,128]{1,0:T(8,128)(2,1)}, u32[]{:S(2)}) copy-start(bf16[256,128]{1,0:T(8,128)(2,1)} %copy-done.40) | copy-start | bytes 196612
  957.4 5.3 copy-start.21
  958.7 317.5 %all-reduce.6.cloned.1.call-start = ((), (), s32[]{:S(2)}) async-start(), calls=%async_computation.23 | async-start | bytes 15204352 | tf_op jit(solution)/shard_map/psum | solution.py:342
  1276.2 6.6 copy-start.37
  1276.2 7.5 copy-start.36
  1276.2 8.5 copy-start.35
  1278.7 7.0 copy-start.34
  (30 other events, 92.8 us)
Sparse Core Ops, SparseCore 0:
  12.1 19.4 all-gather.10
  33.2 81.9 all-gather.16
  117.6 51.0 all-gather.12
  170.9 52.4 all-gather.14
  224.8 19.8 all-gather.18
  246.1 21.0 all-gather.24
  268.7 21.0 all-gather.22
  299.5 80.8 all-gather.20
  425.6 79.5 reduce-scatter.7
  568.9 85.3 reduce-scatter.9
  657.3 86.3 reduce-scatter.11
  745.8 81.0 reduce-scatter.5
  829.2 81.5 reduce-scatter.13
  921.1 93.8 all-gather.28
  1016.4 83.5 all-gather.26
  1102.8 50.3 all-reduce.3
  1158.3 117.8 all-reduce.5

commit v3 on v2

--- a/solution.py
+++ b/solution.py
@@ -106,6 +106,24 @@
         preferred_element_type=jnp.float32,
     )
     return (grad_queries, grad_keyrows, grad_valrows)
+
+
+def partner_swaps(block, axis_name, axis_count):
+    received = [block]
+    for offset in range(1, axis_count):
+        pairs = [(index, index ^ offset) for index in range(axis_count)]
+        received.append(lax.ppermute(block, axis_name, pairs))
+    return received
+
+
+def pair_gather(block, axis_name, axis):
+    if lax.axis_size(axis_name) != 2:
+        return lax.all_gather(block, axis_name, axis=axis, tiled=True)
+    other = lax.ppermute(block, axis_name, [(0, 1), (1, 0)])
+    first = lax.axis_index(axis_name) == 0
+    low = jnp.where(first, block, other)
+    high = jnp.where(first, other, block)
+    return jnp.concatenate([low, high], axis=axis)
 
 
 def tp_rows(rows_array, tp_count):
@@ -180,11 +198,8 @@
     )
     here_pos = lax.axis_index("ctx") * local_len + jnp.arange(local_len, dtype=jnp.int32)
     here_labels = piece_labels(picture_piece_starts, here_pos)
-    heads_full = lax.all_gather(
-        lax.all_gather(attention_output_weight, "tp", axis=0, tiled=True),
-        "shard",
-        axis=1,
-        tiled=True,
+    heads_full = pair_gather(
+        lax.all_gather(attention_output_weight, "tp", axis=0, tiled=True), "shard", 1
     )
     heads_first_all = lax.all_gather(adapter_heads_first, "tp", axis=1, tiled=True)
     projection_first_flattened = flattened_first(adapter_projection_first)
@@ -204,12 +219,12 @@
         lambda inputs: layer_norm(inputs, attention_norm_gain, attention_norm_bias), residual_here
     )
     gathered_rows = (
-        lax.all_gather(query_key_value_weight, "shard", axis=0, tiled=True),
-        lax.all_gather(up_projection_weight, "shard", axis=0, tiled=True),
+        pair_gather(query_key_value_weight, "shard", 0),
+        pair_gather(up_projection_weight, "shard", 0),
     )
     qkv_full = gathered_rows[0].reshape(model_width, 3 * local_width)
     up_full = gathered_rows[1]
-    down_full = lax.all_gather(down_projection_weight, "shard", axis=1, tiled=True)
+    down_full = pair_gather(down_projection_weight, "shard", 1)
     first_low = (matmul(first_act, projection_first_flattened) * select).astype(jnp.bfloat16)
     projected = (
         matmul(first_act, qkv_full) + matmul(first_low, projection_second_flattened)
@@ -218,16 +233,25 @@
     queries = queries_flat.reshape(seq_here, local_len, device_heads, head_width)
     key_rows = projected[:, local_width : 2 * local_width].reshape(seq_here, local_len, local_width)
     value_rows = projected[:, 2 * local_width :].reshape(seq_here, local_len, local_width)
-    pieces = (
-        lax.all_gather(key_rows, "ctx", axis=1, tiled=True),
-        lax.all_gather(value_rows, "ctx", axis=1, tiled=True),
-    )
-    piece_len = pieces[0].shape[1]
-    key_pos = jnp.arange(piece_len, dtype=jnp.int32)
+    ctx_count = lax.axis_size("ctx")
+    ctx_here = lax.axis_index("ctx")
+    blocks = partner_swaps(
+        jnp.concatenate([key_rows, value_rows], axis=2), "ctx", ctx_count
+    )
+    pieces = jnp.concatenate(blocks, axis=1)
+    piece_len = pieces.shape[1]
+    key_pos = jnp.concatenate(
+        [
+            (ctx_here ^ offset) * local_len + jnp.arange(local_len, dtype=jnp.int32)
+            for offset in range(ctx_count)
+        ]
+    )
     key_labels = piece_labels(picture_piece_starts, key_pos)
     visible_mask = visible(here_pos, key_pos, here_labels, key_labels)
-    piece_keys = pieces[0].reshape(seq_here, piece_len, device_heads, head_width)
-    piece_values = pieces[1].reshape(seq_here, piece_len, device_heads, head_width)
+    piece_keys = pieces[:, :, :local_width].reshape(seq_here, piece_len, device_heads, head_width)
+    piece_values = pieces[:, :, local_width:].reshape(
+        seq_here, piece_len, device_heads, head_width
+    )
     exponent = exponents(queries, piece_keys, here_pos, key_pos, visible_mask, slopes)
     weighted = jnp.einsum(
         "shqk,skhd->sqhd",
@@ -306,10 +330,19 @@
         visible_mask,
         slopes,
     )
-    grad_keys_all, grad_values_all = (
-        lax.psum_scatter(grad_keyrows, "ctx", scatter_dimension=1, tiled=True),
-        lax.psum_scatter(grad_valrows, "ctx", scatter_dimension=1, tiled=True),
-    )
+    grad_kv = jnp.concatenate(
+        [
+            grad_keyrows.reshape(seq_here, ctx_count, local_len, local_width),
+            grad_valrows.reshape(seq_here, ctx_count, local_len, local_width),
+        ],
+        axis=3,
+    )
+    grad_kv_here = grad_kv[:, 0]
+    for offset in range(1, ctx_count):
+        pairs = [(index, index ^ offset) for index in range(ctx_count)]
+        grad_kv_here = grad_kv_here + lax.ppermute(grad_kv[:, offset], "ctx", pairs)
+    grad_keys_all = grad_kv_here[:, :, :local_width]
+    grad_values_all = grad_kv_here[:, :, local_width:]
     grad_projected = jnp.concatenate(
         [
             grad_queries.reshape(tok_rows, local_width),

time: 1300 us -> 1260 us (0.969)
  waiting for transfers between devices: 874 us -> 769 us
  other arithmetic: 55 us -> 93.7 us
  local copies, waits for them, and re-layouts: 65.4 us -> 100 us
  blocking collectives: 81 us -> 53.7 us
    ppermute x0 -> x10, waiting for transfers between devices: none -> 251 us  [the longest x3 168 us: body(): grad_kv_here = grad_kv_here + lax.ppermute(grad_kv[:, offset], 'ctx', pairs)]
    reduce_scatter x2 -> x0, waiting for transfers between devices: 126 us -> none  [the longest x1 84.4 us: body(): lax.psum_scatter(grad_valrows, 'ctx', scatter_dimension=1, tiled=True)]
    all_gather x6 -> x0, waiting for transfers between devices: 102 us -> none  [the longest x1 48.4 us: body(): lax.all_gather(key_rows, 'ctx', axis=1, tiled=True)]
    all_gather x1, waiting for transfers between devices: 69.8 us -> 0.01 us  [body(): lax.all_gather(attention_output_weight, 'tp', axis=0, tiled=True)]
    reduce_scatter x3, waiting for transfers between devices: 217 us -> 150 us  [scatter_rows(): lax.psum_scatter(jnp.concatenate(partials, axis=1).astype(jnp.bfloat16),...]
    reshape x0 -> x5, local copies, waits for them, and re-layouts: none -> 41.6 us  [the longest x2 20.5 us: body(): grad_valrows.reshape(seq_here, ctx_count, local_len, local_width)]
    all_to_all x1 -> x0, blocking collectives: 29.9 us -> none  [body(): grad_heads = lax.all_to_all(grad_heads_here, 'tp', 1, 0, tiled=True)]
    select_n x0 -> x4, other arithmetic: none -> 15.6 us  [pair_gather(): low = jnp.where(first, block, other)]
  transfers between devices with their start and end apart: 18 -> 21, of which waited for: 14 -> 14; matrix products, arithmetic and copies ran while one was open for 16% -> 22% of each run, Pallas kernels for 0% -> 0%
where the time goes in v3:
time: 1260 us; the launch traced here: 1250 us
  waiting for transfers between devices  769 us (61%)
  matrix products  202 us (16%)
  local copies, waits for them, and re-layouts  100 us (8%)
  other arithmetic  93.7 us (7%)
  blocking collectives  53.7 us (4%)
  starting transfers between devices  18.1 us (1%)
  between operations  15.5 us (1%)
    all_gather x3, waiting for transfers between devices, gather_rows(): lax.all_gather(jnp.concatenate(rows_here, axis=1), 'tp', axis=0, tiled=True)  196 us
    ppermute x3, waiting for transfers between devices, body(): grad_kv_here = grad_kv_here + lax.ppermute(grad_kv[:, offset], 'ctx', pairs)  168 us
    reduce_scatter x3, waiting for transfers between devices, scatter_rows(): lax.psum_scatter(jnp.concatenate(partials, axis=1).astype(jnp.bfloat16),...  150 us
    psum x1, waiting for transfers between devices, body(): summed = lax.psum(adapter_terms, ('shard', 'ctx'))  116 us
    ppermute x3, waiting for transfers between devices, partner_swaps(): received.append(lax.ppermute(block, axis_name, pairs))  82.2 us
    dot_general x12, matrix products, matmul(): return jnp.dot(left_mat, right_mat, preferred_element_type=jnp.float32)  63.3 us
    dot_general x12, matrix products, matmul_nt(): lax.dot_general(left_mat, right_mat, (((1,), (1,)), ((), ())), preferred_...  62.9 us
    psum x1, waiting for transfers between devices, body(): heads_second_total = lax.psum(heads_second_gradient, 'tp')  46.3 us
  transfers between devices with their start and end apart: 21, of which 14 were waited for; matrix products, arithmetic and copies ran while one was open for 22% of the time, Pallas kernels for 0%

profile of v3, /device:TPU:0, one launch (start us, length us, event | category | flops | bytes accessed | tf_op | source)
XLA Modules:
  0.0 1251.7 jit_solution(3907863855423400655)
XLA Ops:
  7.3 4.7 copy.83
  23.8 5.3 broadcast_select_fusion.7
  29.1 6.5 pad_maximum_fusion.4
  35.6 8.9 add_convert_fusion.1
  62.4 37.3 %collective-permute-done.3 = bf16[4,256,1024]{1,2,0:T(8,128)(2,1)} collective-permute-done((bf16[4,256,1024]{1,2,0:T(8,128)(2,1)}, bf16[4,256,1024]{1,2,0:T(8,128)(2,1)}, u32[]{:S(2)}, u32[]{:S(2)}) %collective-permute-start.3) | collective-permute-done | bytes 2097184 | tf_op jit(solution)/shard_map/ppermute | solution.py:115
  99.8 44.5 %collective-permute-done.2 = bf16[4,256,1024]{1,2,0:T(8,128)(2,1)} collective-permute-done((bf16[4,256,1024]{1,2,0:T(8,128)(2,1)}, bf16[4,256,1024]{1,2,0:T(8,128)(2,1)}, u32[]{:S(2)}, u32[]{:S(2)}) %collective-permute-start.2) | collective-permute-done | bytes 2097184 | tf_op jit(solution)/shard_map/ppermute | solution.py:115
  144.6 4.2 pad_maximum_fusion
  152.7 12.6 %fusion.68 = (f32[4,4,256]{2,1,0:T(4,128)S(1)}, f32[4,4,256,1024]{3,2,1,0:T(8,128)}) fusion(f32[4,256,1024]{2,1,0:T(8,128)} %broadcast_multiply_fusion, bf16[4,256,4,128]{1,3,2,0:T(8,128)(2,1)S(1)} %copy.98, bf16[4,1024,4,128]{1,3,2,0:T(8,128)(2,1)} %bitcast.182, pred[4,256,1024]{2,1,0:T(8,128)(4,1)S(1)} %copy-done.29), kind=kOutput, calls=%fused_computation.172 | convolution fusion | flops 1090514944 | bytes 27279360 | tf_op jit(solution)/shard_map/sqhd,skhd->shqk/dot_general | solution.py:75
  165.3 10.5 fusion.69
  175.8 4.9 all-to-all-start
  180.7 6.7 convert.52
  187.4 30.0 %all_gather.19 = bf16[8,2048,16]{1,2,0:T(8,128)(2,1)S(1)} all-gather(bf16[8,512,16]{1,2,0:T(8,128)(2,1)S(1)} %copy-done.63), channel_id=1, replica_groups=mesh['shard'=2,'ctx'=4,'tp'=4] {'tp'}, dimensions={1}, use_global_device_ids=true | all-gather | bytes 655360 | tf_op jit(solution)/shard_map/all_gather | solution.py:204
  222.7 6.8 fusion.70
  236.5 4.9 fusion.74
  241.3 4.2 broadcast_select_fusion.1
  249.7 62.8 %all-gather.7.cloned.1.call-done = bf16[1024,2048]{1,0:T(8,128)(2,1)} async-done(((bf16[256,2048]{1,0:T(8,128)(2,1)}), bf16[1024,2048]{1,0:T(8,128)(2,1)}) %all-gather.7.cloned.1.call-update) | async-done | bytes 4194320 | tf_op jit(solution)/shard_map/all_gather | solution.py:147
  316.1 4.5 fusion.73
  320.6 17.0 %multiply_convert_fusion.1 = (bf16[1024,2048]{1,0:T(8,128)(2,1)}, f32[1024,2048]{1,0:T(8,128)}) fusion(f32[1024,2048]{1,0:T(8,128)} %fusion.73, bf16[1024,2048]{1,0:T(8,128)(2,1)S(1)} %copy-done.7, bf16[1024,2048]{1,0:T(8,128)(2,1)} %get-tuple-element.50, bf16[1024,2048]{1,0:T(8,128)(2,1)} %get-tuple-element.49), kind=kOutput, calls=%fused_computation.24 | convolution fusion | flops 8627683328 | bytes 33554432 | tf_op jit(solution)/shard_map/dot_general | solution.py:43
  337.7 21.5 %fusion.3 = bf16[1024,2048]{1,0:T(8,128)(2,1)} fusion(f32[1024,2048]{1,0:T(8,128)} %get-tuple-element.75, f32[1024,2048]{1,0:T(8,128)} %fusion.74, bf16[1024,2048]{1,0:T(8,128)(2,1)S(1)} %bitcast.181, bf16[2048,1024]{1,0:T(8,128)(2,1)} %get-tuple-element.48, bf16[2048,1024]{1,0:T(8,128)(2,1)} %get-tuple-element.47), kind=kOutput, calls=%fused_computation.15 | convolution fusion | flops 8659140608 | bytes 33554432 | tf_op jit(solution)/shard_map/dot_general | solution.py:53
  362.8 12.0 fusion.28
  377.3 4.3 convolution_convert_fusion.3
  381.7 75.4 %reduce-scatter.6.cloned.1.call-done = bf16[256,2176]{1,0:T(8,128)(2,1)} async-done(((bf16[1024,2176]{1,0:T(8,128)(2,1)}), bf16[256,2176]{1,0:T(8,128)(2,1)}) %reduce-scatter.6.cloned.1.call-update) | async-done | bytes 1114128 | tf_op jit(solution)/shard_map/reduce_scatter | solution.py:136
  469.9 4.2 all-to-all-start.1
  474.3 13.1 %fusion.29 = bf16[1024,2048]{1,0:T(8,128)(2,1)S(1)} fusion(bf16[1024,2048]{1,0:T(8,128)(2,1)} %get-tuple-element.74, bf16[2048,1024]{1,0:T(8,128)(2,1)} %get-tuple-element.48, bf16[2048,1024]{1,0:T(8,128)(2,1)} %get-tuple-element.47), kind=kOutput, calls=%fused_computation.65 | convolution fusion | flops 8608808960 | bytes 16777216 | tf_op jit(solution)/shard_map/dot_general | solution.py:43
  489.9 10.7 all-to-all-done.1
  505.6 9.5 multiply_convert_fusion
  518.3 4.9 multiply_bitcast_fusion
  523.2 10.6 reshape.423
  533.8 9.9 copy.99
  543.7 11.1 fusion.30
  554.8 10.6 reshape.424
  565.4 9.9 copy.100
  575.4 9.3 fusion.21
  588.1 7.3 fusion.42
  599.2 80.2 %collective-permute-done.9 = f32[4,256,1024]{2,1,0:T(8,128)} collective-permute-done((f32[4,256,1024]{2,1,0:T(8,128)}, f32[4,256,1024]{2,1,0:T(8,128)}, u32[]{:S(2)}, u32[]{:S(2)}) %collective-permute-start.9) | collective-permute-done | bytes 4194336 | tf_op jit(solution)/shard_map/ppermute | solution.py:343
  679.4 88.1 %collective-permute-done.8 = f32[4,256,1024]{2,1,0:T(8,128)} collective-permute-done((f32[4,256,1024]{2,1,0:T(8,128)}, f32[4,256,1024]{2,1,0:T(8,128)}, u32[]{:S(2)}, u32[]{:S(2)}) %collective-permute-start.8) | collective-permute-done | bytes 4194336 | tf_op jit(solution)/shard_map/ppermute | solution.py:343
  767.6 6.6 fusion.19
  776.1 9.0 convolution_convert_fusion
  792.5 74.4 %reduce-scatter.8.cloned.1.call-done = bf16[256,2176]{1,0:T(8,128)(2,1)} async-done(((bf16[1024,2176]{1,0:T(8,128)(2,1)}), bf16[256,2176]{1,0:T(8,128)(2,1)}) %reduce-scatter.8.cloned.1.call-update) | async-done | bytes 1114128 | tf_op jit(solution)/shard_map/reduce_scatter | solution.py:136
  882.4 4.3 fusion.77
  888.5 23.7 %all_gather.23 = bf16[1024,256]{1,0:T(8,128)(2,1)S(1)} all-gather(bf16[256,256]{1,0:T(8,128)(2,1)S(1)} %pad_maximum_fusion.35), channel_id=1, replica_groups=mesh['shard'=2,'ctx'=4,'tp'=4] {'tp'}, dimensions={0}, use_global_device_ids=true | all-gather | bytes 655360 | tf_op jit(solution)/shard_map/all_gather | solution.py:147
  914.8 4.1 fusion.49
  923.1 48.0 %all-gather.11.cloned.1.call-done = bf16[1024,2176]{1,0:T(8,128)(2,1)} async-done(((bf16[256,2176]{1,0:T(8,128)(2,1)}), bf16[1024,2176]{1,0:T(8,128)(2,1)}) %all-gather.11.cloned.1.call-update) | async-done | bytes 4456464 | tf_op jit(solution)/shard_map/all_gather | solution.py:147
  972.1 84.7 %all-gather.9.cloned.1.call-done = bf16[1024,2176]{1,0:T(8,128)(2,1)} async-done(((bf16[256,2176]{1,0:T(8,128)(2,1)}), bf16[1024,2176]{1,0:T(8,128)(2,1)}) %all-gather.9.cloned.1.call-update) | async-done | bytes 4456464 | tf_op jit(solution)/shard_map/all_gather | solution.py:147
  1058.1 4.0 fusion.79
  1063.8 46.3 %all-reduce.4.cloned.1.call-done = f32[8,16,2048]{2,1,0:T(8,128)} async-done(((f32[8,16,2048]{2,1,0:T(8,128)}), f32[8,16,2048]{2,1,0:T(8,128)}) %all-reduce.4.cloned.1.call-update) | async-done | bytes 1048592 | tf_op jit(solution)/shard_map/psum | solution.py:364
  1110.1 4.9 slice.101
  1117.7 115.6 %all-reduce.6.cloned.1.call-done = (f32[8,2048,16]{1,2,0:T(8,128)}, f32[8,16,3,512]{3,2,1,0:T(4,128)}, f32[8,512,16]{1,2,0:T(8,128)}, f32[8,16,2048]{2,1,0:T(8,1...) async-done(((f32[8,2048,16]{1,2,0:T(8,128)}, f32[8,16,3,512]{3,2,1,0:T(4,128)}, ...) | async-done | bytes 7340048 | tf_op jit(solution)/shard_map/psum | solution.py:375
  (287 shorter events, 141.8 us)
Async XLA Ops:
  7.2 308.9 %copy-start = (bf16[8,16,2048]{2,1,0:T(8,128)(2,1)S(1)}, bf16[8,16,2048]{2,1,0:T(8,128)(2,1)}, u32[]{:S(2)}) copy-start(bf16[8,16,2048]{2,1,0:T(8,128)(2,1)} %param.37) | copy-start | bytes 1572868
  7.2 145.5 %all-gather.5.cloned.1.call-start = ((), (), s32[]{:S(2)}) async-start(), calls=%async_computation.5 | async-start | bytes 5242880 | tf_op jit(solution)/shard_map/all_gather | solution.py:202
  12.0 10.2 collective-permute-start
  13.0 8.3 copy-start.43
  19.9 15.7 %copy-start.8 = (bf16[4,256,2048]{2,1,0:T(8,128)(2,1)}, bf16[4,256,2048]{2,1,0:T(8,128)(2,1)S(1)}, u32[]{:S(2)}) copy-start(bf16[4,256,2048]{2,1,0:T(8,128)(2,1)S(1)} %add_convert_fusion) | copy-start | bytes 12582916
  46.0 7.5 copy-start.67
  46.0 7.5 copy-start.70
  48.0 8.8 copy-start.17
  49.6 50.1 %collective-permute-start.3 = (bf16[4,256,1024]{1,2,0:T(8,128)(2,1)}, bf16[4,256,1024]{1,2,0:T(8,128)(2,1)}, u32[]{:S(2)}, u32[]{:S(2)}) collective-permute-start(bf16[4,256,1024]{1,2,0:T(8,128)(2,1)} %pad_maximum_fusion.32), channel_id=1, source_target_pairs={{0,12},{4,8},{8,4},{12,0},{1,13},{5,9},{9,5},{13,1},{2,14},{6,10},... | collective-permute-start | bytes 6291464 | tf_op jit(solution)/shard_map/ppermute | solution.py:115
  52.9 91.4 %collective-permute-start.2 = (bf16[4,256,1024]{1,2,0:T(8,128)(2,1)}, bf16[4,256,1024]{1,2,0:T(8,128)(2,1)}, u32[]{:S(2)}, u32[]{:S(2)}) collective-permute-start(bf16[4,256,1024]{1,2,0:T(8,128)(2,1)} %pad_maximum_fusion.32), channel_id=1, source_target_pairs={{0,8},{4,12},{8,0},{12,4},{1,9},{5,13},{9,1},{13,5},{2,10},{6,14},... | collective-permute-start | bytes 6291464 | tf_op jit(solution)/shard_map/ppermute | solution.py:115
  53.5 91.1 %collective-permute-start.1 = (bf16[4,256,1024]{1,2,0:T(8,128)(2,1)}, bf16[4,256,1024]{1,2,0:T(8,128)(2,1)}, u32[]{:S(2)}, u32[]{:S(2)}) collective-permute-start(bf16[4,256,1024]{1,2,0:T(8,128)(2,1)} %pad_maximum_fusion.32), channel_id=1, source_target_pairs={{0,4},{4,0},{8,12},{12,8},{1,5},{5,1},{9,13},{13,9},{2,6},{6,2},{1... | collective-permute-start | bytes 6291464 | tf_op jit(solution)/shard_map/ppermute | solution.py:115
  62.4 90.3 %copy-start.13 = (bf16[4,256,4,128]{1,3,2,0:T(8,128)(2,1)}, bf16[4,256,4,128]{1,3,2,0:T(8,128)(2,1)S(1)}, u32[]{:S(2)}) copy-start(bf16[4,256,4,128]{1,3,2,0:T(8,128)(2,1)S(1)} %copy.98) | copy-start | bytes 3145732
  152.7 65.6 %collective-permute-start.4 = (bf16[2048,1024]{1,0:T(8,128)(2,1)}, bf16[2048,1024]{1,0:T(8,128)(2,1)}, u32[]{:S(2)}, u32[]{:S(2)}) collective-permute-start(bf16[2048,1024]{1,0:T(8,128)(2,1)} %all-gather.5.cloned.1.call-done), channel_id=1, source_target_pairs={{0,16},{16,0},{1,17},{17,1},{2,18},{18,2},{3,19},{19,3},{4,20},{20... | collective-permute-start | bytes 12582920 | tf_op jit(solution)/shard_map/ppermute | solution.py:122
  152.7 12.6 %copy-start.4 = (bf16[4,1024,512]{1,2,0:T(8,128)(2,1)S(1)}, bf16[4,1024,512]{1,2,0:T(8,128)(2,1)}, u32[]{:S(2)}) copy-start(bf16[4,1024,512]{1,2,0:T(8,128)(2,1)} %get-tuple-element.54) | copy-start | bytes 12582916
  165.3 10.5 copy-start.58
  175.8 41.5 %all-to-all-start = ((bf16[4,256,512]{1,2,0:T(8,128)(2,1)}), bf16[4,256,512]{1,2,0:T(8,128)(2,1)S(1)}, u32[]{:S(2)}, u32[]{:S(2)}) async-start(bf16[4,256,512]{1,2,0:T(8,128)(2,1)} %bitcast.12), calls=%async_computation | async-start | bytes 2097152 | tf_op jit(solution)/shard_map/all_to_all | solution.py:266
  180.7 131.8 %all-gather.7.cloned.1.call-start = ((), (), s32[]{:S(2)}) async-start(), calls=%async_computation.6 | async-start | bytes 5242880 | tf_op jit(solution)/shard_map/all_gather | solution.py:147
  180.7 37.2 %copy-start.41 = (bf16[8,16,2048]{2,1,0:T(8,128)(2,1)S(1)}, bf16[8,16,2048]{2,1,0:T(8,128)(2,1)}, u32[]{:S(2)}) copy-start(bf16[8,16,2048]{2,1,0:T(8,128)(2,1)} %param.35) | copy-start | bytes 1572868
  222.7 6.8 copy-start.24
  222.7 7.2 copy-start.64
  222.7 7.2 copy-start.69
  231.3 225.7 %reduce-scatter.6.cloned.1.call-start = ((), (), s32[]{:S(2)}) async-start(), calls=%async_computation.9 | async-start | bytes 5570560 | tf_op jit(solution)/shard_map/reduce_scatter | solution.py:136
  231.6 9.7 collective-permute-start.5
  231.7 13.9 %collective-permute-start.6 = (bf16[2048,1024]{1,0:T(8,128)(2,1)}, bf16[2048,1024]{1,0:T(8,128)(2,1)S(1)}, u32[]{:S(2)}, u32[]{:S(2)}) collective-permute-start(bf16[2048,1024]{1,0:T(8,128)(2,1)} %param.31), channel_id=1, source_target_pairs={{0,16},{16,0},{1,17},{17,1},{2,18},{18,2},{3,19},{19,3},{4,20},{20... | collective-permute-start | bytes 12582920 | tf_op jit(solution)/shard_map/ppermute | solution.py:122
  320.6 17.0 %copy-start.5 = (bf16[4,256,2048]{2,1,0:T(8,128)(2,1)S(1)}, bf16[4,256,2048]{2,1,0:T(8,128)(2,1)}, u32[]{:S(2)}) copy-start(bf16[4,256,2048]{2,1,0:T(8,128)(2,1)} %param.21) | copy-start | bytes 12582916
  377.3 81.1 %copy-start.37 = (bf16[8,2048,16]{1,2,0:T(8,128)(2,1)S(1)}, bf16[8,2048,16]{1,2,0:T(8,128)(2,1)}, u32[]{:S(2)}) copy-start(bf16[8,2048,16]{1,2,0:T(8,128)(2,1)} %param.36) | copy-start | bytes 1572868
  469.9 30.7 %all-to-all-start.1 = ((bf16[256,4,512]{0,2,1:T(8,128)(2,1)}), bf16[256,4,512]{0,2,1:T(8,128)(2,1)}, u32[]{:S(2)}, u32[]{:S(2)}) async-start(bf16[256,4,512]{0,2,1:T(8,128)(2,1)} %bitcast.209), calls=%async_computation.3 | async-start | bytes 2097152 | tf_op jit(solution)/shard_map/all_to_all | solution.py:316
  474.2 13.2 %copy-start.62 = (bf16[1024,128]{1,0:T(8,128)(2,1)S(1)}, bf16[1024,128]{1,0:T(8,128)(2,1)}, u32[]{:S(2)}) copy-start(bf16[1024,128]{1,0:T(8,128)(2,1)} %convolution_convert_fusion.3) | copy-start | bytes 786436
  474.2 315.5 %reduce-scatter.4.cloned.1.call-start = ((), (), s32[]{:S(2)}) async-start(), calls=%async_computation.7 | async-start | bytes 5570560 | tf_op jit(solution)/shard_map/reduce_scatter | solution.py:136
  489.9 12.9 %copy-start.59 = (f32[4,4,256]{2,1,0:T(4,128)S(1)}, f32[4,4,256]{2,1,0:T(4,128)}, u32[]{:S(2)}) copy-start(f32[4,4,256]{2,1,0:T(4,128)} %copy-done.58) | copy-start | bytes 49156
  489.9 377.0 %reduce-scatter.8.cloned.1.call-start = ((), (), s32[]{:S(2)}) async-start(), calls=%async_computation.10 | async-start | bytes 5570560 | tf_op jit(solution)/shard_map/reduce_scatter | solution.py:136
  505.5 12.8 %copy-start.14 = (bf16[4,256,4,128]{1,3,2,0:T(8,128)(2,1)S(1)}, bf16[4,256,4,128]{1,3,2,0:T(8,128)(2,1)}, u32[]{:S(2)}) copy-start(bf16[4,256,4,128]{1,3,2,0:T(8,128)(2,1)} %copy-done.13) | copy-start | bytes 3145732
  575.4 12.8 %copy-start.6 = (bf16[4,1024,512]{1,2,0:T(8,128)(2,1)S(1)}, bf16[4,1024,512]{1,2,0:T(8,128)(2,1)}, u32[]{:S(2)}) copy-start(bf16[4,1024,512]{1,2,0:T(8,128)(2,1)} %get-tuple-element.53) | copy-start | bytes 12582916
  584.6 94.7 %collective-permute-start.9 = (f32[4,256,1024]{2,1,0:T(8,128)}, f32[4,256,1024]{2,1,0:T(8,128)}, u32[]{:S(2)}, u32[]{:S(2)}) collective-permute-start(f32[4,256,1024]{2,1,0:T(8,128)} %get-tuple-element.45), channel_id=1, source_target_pairs={{0,12},{4,8},{8,4},{12,0},{1,13},{5,9},{9,5},{13,1},{2,14},{6,10},... | collective-permute-start | bytes 12582920 | tf_op jit(solution)/shard_map/ppermute | solution.py:343
  587.0 180.4 %collective-permute-start.8 = (f32[4,256,1024]{2,1,0:T(8,128)}, f32[4,256,1024]{2,1,0:T(8,128)}, u32[]{:S(2)}, u32[]{:S(2)}) collective-permute-start(f32[4,256,1024]{2,1,0:T(8,128)} %get-tuple-element.46), channel_id=1, source_target_pairs={{0,8},{4,12},{8,0},{12,4},{1,9},{5,13},{9,1},{13,5},{2,10},{6,14},... | collective-permute-start | bytes 12582920 | tf_op jit(solution)/shard_map/ppermute | solution.py:343
  587.7 179.8 %collective-permute-start.7 = (f32[4,256,1024]{2,1,0:T(8,128)}, f32[4,256,1024]{2,1,0:T(8,128)}, u32[]{:S(2)}, u32[]{:S(2)}) collective-permute-start(f32[4,256,1024]{2,1,0:T(8,128)} %get-tuple-element.44), channel_id=1, source_target_pairs={{0,4},{4,0},{8,12},{12,8},{1,5},{5,1},{9,13},{13,9},{2,6},{6,2},{1... | collective-permute-start | bytes 12582920 | tf_op jit(solution)/shard_map/ppermute | solution.py:343
  599.2 176.9 %copy-start.45 = (bf16[128,8,4,128]{3,1,2,0:T(8,128)(2,1)}, bf16[128,8,4,128]{3,1,2,0:T(8,128)(2,1)S(1)}, u32[]{:S(2)}) copy-start(bf16[128,8,4,128]{3,1,2,0:T(8,128)(2,1)S(1)} %copy.119) | copy-start | bytes 3145732
  787.8 81.5 %copy-start.39 = (bf16[8,2048,16]{1,2,0:T(8,128)(2,1)S(1)}, bf16[8,2048,16]{1,2,0:T(8,128)(2,1)}, u32[]{:S(2)}) copy-start(bf16[8,2048,16]{1,2,0:T(8,128)(2,1)} %param.32) | copy-start | bytes 1572868
  787.8 81.5 %copy-start.66 = (f32[2048]{0:T(1024)S(1)}, f32[2048]{0:T(1024)}, u32[]{:S(2)}) copy-start(f32[2048]{0:T(1024)} %param.24) | copy-start | bytes 24580
  787.8 183.3 %all-gather.11.cloned.1.call-start = ((), (), s32[]{:S(2)}) async-start(), calls=%async_computation.11 | async-start | bytes 5570560 | tf_op jit(solution)/shard_map/all_gather | solution.py:147
  877.0 179.7 %all-gather.9.cloned.1.call-start = ((), (), s32[]{:S(2)}) async-start(), calls=%async_computation.8 | async-start | bytes 5570560 | tf_op jit(solution)/shard_map/all_gather | solution.py:147
  880.2 229.8 %all-reduce.4.cloned.1.call-start = ((), (), s32[]{:S(2)}) async-start(), calls=%async_computation.12 | async-start | bytes 2097152 | tf_op jit(solution)/shard_map/psum | solution.py:364
  888.4 24.9 %copy-start.16 = (bf16[256,2048]{1,0:T(8,128)(2,1)S(1)}, bf16[256,2048]{1,0:T(8,128)(2,1)}, u32[]{:S(2)}) copy-start(bf16[256,2048]{1,0:T(8,128)(2,1)} %copy-done.15) | copy-start | bytes 3145732
  888.5 24.9 %copy-start.57 = (bf16[256,128]{1,0:T(8,128)(2,1)S(1)}, bf16[256,128]{1,0:T(8,128)(2,1)}, u32[]{:S(2)}) copy-start(bf16[256,128]{1,0:T(8,128)(2,1)} %copy-done.56) | copy-start | bytes 196612
  914.7 318.5 %all-reduce.6.cloned.1.call-start = ((), (), s32[]{:S(2)}) async-start(), calls=%async_computation.13 | async-start | bytes 15204352 | tf_op jit(solution)/shard_map/psum | solution.py:375
  1233.3 7.5 copy-start.50
  1233.3 8.5 copy-start.49
  1235.8 7.0 copy-start.48
  (47 other events, 185.5 us)
Sparse Core Ops, SparseCore 0:
  12.6 83.1 all-gather.4
  231.5 81.0 all-gather.6
  377.5 79.5 reduce-scatter.5
  490.0 83.4 reduce-scatter.3
  787.9 78.9 reduce-scatter.7
  877.2 93.8 all-gather.10
  973.2 83.5 all-gather.8
  1059.7 50.3 all-reduce.3
  1115.4 117.8 all-reduce.5

commit v4 on v3

--- a/solution.py
+++ b/solution.py
@@ -156,7 +156,7 @@
     return tuple(parts)
 
 
-def body(
+def layer_body(
     layer_input,
     output_gradient,
     picture_piece_starts,
@@ -198,14 +198,19 @@
     )
     here_pos = lax.axis_index("ctx") * local_len + jnp.arange(local_len, dtype=jnp.int32)
     here_labels = piece_labels(picture_piece_starts, here_pos)
-    heads_full = pair_gather(
-        lax.all_gather(attention_output_weight, "tp", axis=0, tiled=True), "shard", 1
-    )
-    heads_first_all = lax.all_gather(adapter_heads_first, "tp", axis=1, tiled=True)
+    heads_first_local = flattened_first(adapter_heads_first)
+    heads_pair = lax.all_gather(
+        jnp.concatenate([attention_output_weight, heads_first_local], axis=1),
+        "tp",
+        axis=0,
+        tiled=True,
+    )
+    out_cols = attention_output_weight.shape[1]
+    heads_full = pair_gather(heads_pair[:, :out_cols], "shard", 1)
+    heads_first_all_flattened = heads_pair[:, out_cols:]
     projection_first_flattened = flattened_first(adapter_projection_first)
     projection_second_flattened = flattened_second(adapter_projection_second)
     heads_first_flattened = flattened_first(adapter_heads_first)
-    heads_first_all_flattened = flattened_first(heads_first_all)
     heads_second_flattened = flattened_second(adapter_heads_second)
     up_first_flattened = flattened_first(adapter_up_first)
     up_second_flattened = flattened_second(adapter_up_second)
@@ -285,7 +290,7 @@
     result_here = (middle_here + ffn_here + matmul(down_low_here, down_second_flattened)).astype(
         jnp.bfloat16
     )
-    result_rows, down_low = gather_rows((result_here, down_low_here))
+    (result_rows,) = gather_rows((result_here,))
     layer_out = result_rows.reshape(layer_input.shape)
     grad_top_low = output_gradient.reshape(tok_rows, model_width)
     grad_top_here = tp_rows(grad_top_low, tp_count).astype(jnp.float32)
@@ -304,11 +309,35 @@
     heads_back_here = (matmul_nt(grad_middle_low_here, heads_second_flattened) * select_here).astype(
         jnp.bfloat16
     )
-    up_back, heads_back = gather_rows((up_back_here, heads_back_here))
-    down_second_gradient = matmul_tn(down_low, grad_top_low)
-    grad_up_in = matmul_tn(second_act, up_back)
+    down_second_gradient = matmul_tn(down_low_here, tp_rows(grad_top_low, tp_count))
+    grad_up_in = matmul_tn(second_act_here, up_back_here)
     heads_second_gradient = matmul_tn(heads_low_here, grad_middle_low_here)
-    grad_heads_in = matmul_tn(heads_act, heads_back)
+    grad_heads_in_all = matmul_tn(heads_act_here, heads_back_here)
+    hidden_terms = lax.psum(
+        (
+            up_second_gradient.reshape(adapter_up_second.shape),
+            unflat_in(grad_down_in, adapter_tables),
+        ),
+        ("shard", "ctx"),
+    )
+    token_terms = lax.psum(
+        (
+            grad_heads_in_all,
+            unflat_in(grad_up_in, adapter_tables),
+            heads_second_gradient.reshape(adapter_heads_second.shape),
+            down_second_gradient.reshape(adapter_down_second.shape),
+        ),
+        ("shard", "ctx", "tp"),
+    )
+    heads_in_rows = tp_rows(token_terms[0], tp_count)
+    early_terms = (
+        unflat_in(heads_in_rows, adapter_tables),
+        token_terms[1],
+        hidden_terms[0],
+        hidden_terms[1],
+        token_terms[3],
+    )
+    heads_second_total = token_terms[2]
     grad_heads_here = (
         matmul_nt(grad_middle_low_here, heads_full)
         + matmul_nt(heads_back_here, heads_first_all_flattened)
@@ -340,7 +369,9 @@
     grad_kv_here = grad_kv[:, 0]
     for offset in range(1, ctx_count):
         pairs = [(index, index ^ offset) for index in range(ctx_count)]
-        grad_kv_here = grad_kv_here + lax.ppermute(grad_kv[:, offset], "ctx", pairs)
+        grad_kv_here = grad_kv_here + lax.ppermute(
+            grad_kv[:, offset].astype(jnp.bfloat16), "ctx", pairs
+        ).astype(jnp.float32)
     grad_keys_all = grad_kv_here[:, :, :local_width]
     grad_values_all = grad_kv_here[:, :, local_width:]
     grad_projected = jnp.concatenate(
@@ -355,35 +386,34 @@
     attn_back_part = matmul_nt(grad_projected, qkv_full)
     attn_back_low = matmul_nt(grad_projected, projection_second_flattened)
     first_here, first_low_here = scatter_rows((attn_back_part, attn_back_low))
-    qkv_back_here = (first_low_here * select_here).astype(jnp.bfloat16)
+    select_late = lax.optimization_barrier(select_here)
+    qkv_back_here = (first_low_here * select_late).astype(jnp.bfloat16)
     grad_first = first_here + matmul_nt(qkv_back_here, projection_first_flattened)
     input_here = (grad_middle_here + first_back_full(grad_first)[0]).astype(jnp.bfloat16)
     input_rows, qkv_back = gather_rows((input_here, qkv_back_here))
     input_grad = input_rows.reshape(layer_input.shape)
     grad_qkv_in = matmul_tn(first_act, qkv_back)
-    heads_second_total = lax.psum(heads_second_gradient, "tp")
-    adapter_terms = (
-        unflat_in(grad_qkv_in, adapter_tables),
-        projection_second_gradient.reshape(adapter_projection_second.shape),
-        unflat_in(grad_heads_in, adapter_tables),
-        heads_second_total.reshape(adapter_heads_second.shape),
-        unflat_in(grad_up_in, adapter_tables),
-        up_second_gradient.reshape(adapter_up_second.shape),
-        unflat_in(grad_down_in, adapter_tables),
-        down_second_gradient.reshape(adapter_down_second.shape),
-    )
-    summed = lax.psum(adapter_terms, ("shard", "ctx"))
+    early_terms, late_inputs = lax.optimization_barrier(
+        (
+            early_terms,
+            (
+                unflat_in(grad_qkv_in, adapter_tables),
+                projection_second_gradient.reshape(adapter_projection_second.shape),
+            ),
+        )
+    )
+    late_terms = lax.psum(late_inputs, ("shard", "ctx"))
     return (
         layer_out,
         input_grad,
-        summed[0],
-        summed[1],
-        summed[2],
-        summed[3],
-        summed[4],
-        summed[5],
-        summed[6],
-        summed[7],
+        late_terms[0],
+        late_terms[1],
+        early_terms[0],
+        heads_second_total,
+        early_terms[1],
+        early_terms[2],
+        early_terms[3],
+        early_terms[4],
     )
 
 
@@ -411,7 +441,7 @@
         P(),
     )
     return jax.shard_map(
-        body,
+        layer_body,
         mesh=mesh,
         in_specs=placed,
         out_specs=(

time: 1260 us -> 1330 us (1.056)
  waiting for transfers between devices: 769 us -> 866 us
  blocking collectives: 53.7 us -> 30 us
    ppermute x3, waiting for transfers between devices: 168 us -> 77.9 us  [layer_body(): lax.ppermute(grad_kv[:, offset].astype(jnp.bfloat16), 'ctx', pairs)]
    psum x2 -> x3, waiting for transfers between devices: 162 us -> 251 us  [the longest x1 132 us: layer_body(): lax.psum((grad_heads_in_all, unflat_in(grad_up_in, adapter_tables), heads...]
    reduce_scatter x3, waiting for transfers between devices: 150 us -> 212 us  [scatter_rows(): lax.psum_scatter(jnp.concatenate(partials, axis=1).astype(jnp.bfloat16),...]
    all_gather x2 -> x0, blocking collectives: 53.7 us -> none  [the longest x1 30 us: body(): lax.all_gather(adapter_heads_first, 'tp', axis=1, tiled=True)]
    all_to_all x0 -> x1, blocking collectives: none -> 30 us  [layer_body(): grad_heads = lax.all_to_all(grad_heads_here, 'tp', 1, 0, tiled=True)]
    all_gather x3, waiting for transfers between devices: 196 us -> 224 us  [gather_rows(): lax.all_gather(jnp.concatenate(rows_here, axis=1), 'tp', axis=0, tiled=True)]
    reshape x7 -> x8, local copies, waits for them, and re-layouts: 45.8 us -> 44.6 us  [the longest x2 20.5 us: layer_body(): grad_keyrows.reshape(seq_here, ctx_count, local_len, local_width)]
  transfers between devices with their start and end apart: 21 -> 21, of which waited for: 14 -> 15; matrix products, arithmetic and copies ran while one was open for 22% -> 13% of each run, Pallas kernels for 0% -> 0%
where the time goes in v4:
time: 1330 us; the launch traced here: 1320 us
  waiting for transfers between devices  866 us (65%)
  matrix products  200 us (15%)
  local copies, waits for them, and re-layouts  106 us (8%)
  other arithmetic  87.7 us (7%)
  blocking collectives  30 us (2%)
  between operations  15.5 us (1%)
  starting transfers between devices  14 us (1%)
    all_gather x3, waiting for transfers between devices, gather_rows(): lax.all_gather(jnp.concatenate(rows_here, axis=1), 'tp', axis=0, tiled=True)  224 us
    reduce_scatter x3, waiting for transfers between devices, scatter_rows(): lax.psum_scatter(jnp.concatenate(partials, axis=1).astype(jnp.bfloat16),...  212 us
    psum x1, waiting for transfers between devices, layer_body(): lax.psum((grad_heads_in_all, unflat_in(grad_up_in, adapter_tables), heads...  132 us
    ppermute x3, waiting for transfers between devices, partner_swaps(): received.append(lax.ppermute(block, axis_name, pairs))  81.8 us
    ppermute x3, waiting for transfers between devices, layer_body(): lax.ppermute(grad_kv[:, offset].astype(jnp.bfloat16), 'ctx', pairs)  77.9 us
    dot_general x12, matrix products, matmul_nt(): lax.dot_general(left_mat, right_mat, (((1,), (1,)), ((), ())), preferred_...  64.5 us
    dot_general x12, matrix products, matmul(): return jnp.dot(left_mat, right_mat, preferred_element_type=jnp.float32)  63.7 us
    psum x1, waiting for transfers between devices, layer_body(): late_terms = lax.psum(late_inputs, ('shard', 'ctx'))  59.8 us
  transfers between devices with their start and end apart: 21, of which 15 were waited for; matrix products, arithmetic and copies ran while one was open for 13% of the time, Pallas kernels for 0%

profile of v4, /device:TPU:0, one launch (start us, length us, event | category | flops | bytes accessed | tf_op | source)
XLA Modules:
  0.0 1319.3 jit_solution(3034224040208086829)
XLA Ops:
  7.3 4.8 copy.79
  25.2 5.3 broadcast_select_fusion.7
  30.4 6.5 pad_maximum_fusion.5
  36.9 8.9 add_convert_fusion.1
  64.3 37.0 %collective-permute-done.3 = bf16[4,256,1024]{1,2,0:T(8,128)(2,1)} collective-permute-done((bf16[4,256,1024]{1,2,0:T(8,128)(2,1)}, bf16[4,256,1024]{1,2,0:T(8,128)(2,1)}, u32[]{:S(2)}, u32[]{:S(2)}) %collective-permute-start.3) | collective-permute-done | bytes 2097184 | tf_op jit(solution)/shard_map/ppermute | solution.py:115
  101.3 44.5 %collective-permute-done.2 = bf16[4,256,1024]{1,2,0:T(8,128)(2,1)} collective-permute-done((bf16[4,256,1024]{1,2,0:T(8,128)(2,1)}, bf16[4,256,1024]{1,2,0:T(8,128)(2,1)}, u32[]{:S(2)}, u32[]{:S(2)}) %collective-permute-start.2) | collective-permute-done | bytes 2097184 | tf_op jit(solution)/shard_map/ppermute | solution.py:115
  146.2 4.1 pad_maximum_fusion.1
  154.1 4.9 slice.94
  160.4 9.4 fusion.68
  169.7 10.5 fusion.69
  180.3 4.8 all-to-all-start
  185.1 6.7 convert.59
  191.7 19.2 %all-to-all-done = bf16[4,256,512]{1,2,0:T(8,128)(2,1)S(1)} async-done(((bf16[4,256,512]{1,2,0:T(8,128)(2,1)}), bf16[4,256,512]{1,2,0:T(8,128)(2,1)S(1)}, u32[]{:S(2)}, u32[]{:S(2)}) %all-to-all-start) | async-done | bytes 1048608 | tf_op jit(solution)/shard_map/all_to_all | solution.py:271
  217.1 6.8 fusion.70
  230.8 4.7 fusion.74
  235.5 4.1 broadcast_select_fusion.1
  243.5 61.3 %all-gather.7.cloned.1.call-done = bf16[1024,2048]{1,0:T(8,128)(2,1)} async-done(((bf16[256,2048]{1,0:T(8,128)(2,1)}), bf16[1024,2048]{1,0:T(8,128)(2,1)}) %all-gather.7.cloned.1.call-update) | async-done | bytes 4194320 | tf_op jit(solution)/shard_map/all_gather | solution.py:147
  308.3 4.5 fusion.73
  312.9 17.0 %multiply_convert_fusion.1 = (bf16[1024,2048]{1,0:T(8,128)(2,1)}, f32[1024,2048]{1,0:T(8,128)}) fusion(f32[1024,2048]{1,0:T(8,128)} %fusion.73, bf16[1024,2048]{1,0:T(8,128)(2,1)S(1)} %copy-done.23, bf16[1024,2048]{1,0:T(8,128)(2,1)} %get-tuple-element.66, bf16[1024,2048]{1,0:T(8,128)(2,1)} %get-tuple-element.65), kind=kOutput, calls=%fused_computation.22 | convolution fusion | flops 8627683328 | bytes 33554432 | tf_op jit(solution)/shard_map/dot_general | solution.py:43
  329.9 21.3 %fusion.4 = bf16[1024,2048]{1,0:T(8,128)(2,1)} fusion(f32[1024,2048]{1,0:T(8,128)} %get-tuple-element.87, f32[1024,2048]{1,0:T(8,128)} %fusion.74, bf16[1024,2048]{1,0:T(8,128)(2,1)S(1)} %bitcast.180, bf16[2048,1024]{1,0:T(8,128)(2,1)} %get-tuple-element.64, bf16[2048,1024]{1,0:T(8,128)(2,1)} %get-tuple-element.63), kind=kOutput, calls=%fused_computation.13 | convolution fusion | flops 8659140608 | bytes 33554432 | tf_op jit(solution)/shard_map/dot_general | solution.py:53
  354.7 12.2 fusion.24
  374.4 11.7 fusion.25
  388.7 60.6 %reduce-scatter.6.cloned.1.call-done = bf16[256,2176]{1,0:T(8,128)(2,1)} async-done(((bf16[1024,2176]{1,0:T(8,128)(2,1)}), bf16[256,2176]{1,0:T(8,128)(2,1)}) %reduce-scatter.6.cloned.1.call-update) | async-done | bytes 1114128 | tf_op jit(solution)/shard_map/reduce_scatter | solution.py:136
  452.0 81.0 %reduce-scatter.4.cloned.1.call-done = bf16[256,2176]{1,0:T(8,128)(2,1)} async-done(((bf16[1024,2176]{1,0:T(8,128)(2,1)}), bf16[256,2176]{1,0:T(8,128)(2,1)}) %reduce-scatter.4.cloned.1.call-update) | async-done | bytes 1114128 | tf_op jit(solution)/shard_map/reduce_scatter | solution.py:136
  548.5 30.0 %all_to_all.29 = bf16[256,4,512]{0,2,1:T(8,128)(2,1)S(1)} all-to-all(bf16[256,4,512]{0,2,1:T(8,128)(2,1)} %bitcast.194), channel_id=1, replica_groups=mesh['shard'=2,'ctx'=4,'tp'=4] {'tp'}, dimensions={1} | all-to-all | bytes 2097152 | tf_op jit(solution)/shard_map/all_to_all | solution.py:345
  582.0 10.4 fusion.26
  592.4 9.2 multiply_convert_fusion
  604.9 4.9 multiply_bitcast_fusion
  609.8 10.5 reshape.427
  620.3 9.9 copy.95
  630.3 10.5 reshape.428
  640.8 9.9 copy.96
  650.7 6.6 fusion
  664.1 7.3 fusion.38
  675.2 35.2 %collective-permute-done.9 = bf16[4,256,1024]{2,1,0:T(8,128)(2,1)} collective-permute-done((bf16[4,256,1024]{2,1,0:T(8,128)(2,1)}, bf16[4,256,1024]{2,1,0:T(8,128)(2,1)}, u32[]{:S(2)}, u32[]{:S(2)}) %collective-permute-start.9) | collective-permute-done | bytes 2097184 | tf_op jit(solution)/shard_map/ppermute | solution.py:372
  710.4 42.6 %collective-permute-done.8 = bf16[4,256,1024]{2,1,0:T(8,128)(2,1)} collective-permute-done((bf16[4,256,1024]{2,1,0:T(8,128)(2,1)}, bf16[4,256,1024]{2,1,0:T(8,128)(2,1)}, u32[]{:S(2)}, u32[]{:S(2)}) %collective-permute-start.8) | collective-permute-done | bytes 2097184 | tf_op jit(solution)/shard_map/ppermute | solution.py:372
  753.1 4.8 fusion.18
  759.8 9.0 convolution_convert_fusion
  781.6 70.0 %reduce-scatter.8.cloned.1.call-done = bf16[256,2176]{1,0:T(8,128)(2,1)} async-done(((bf16[1024,2176]{1,0:T(8,128)(2,1)}), bf16[256,2176]{1,0:T(8,128)(2,1)}) %reduce-scatter.8.cloned.1.call-update) | async-done | bytes 1114128 | tf_op jit(solution)/shard_map/reduce_scatter | solution.py:136
  861.0 4.0 fusion.77
  870.0 132.5 %all-reduce.7.cloned.1.call-done = (f32[2048,128]{1,0:T(8,128)}, f32[8,2048,16]{1,2,0:T(8,128)}, f32[8,16,2048]{2,1,0:T(8,128)}, f32[8,16,2048]{2,1,0:T(8,128)}) async-done(((f32[2048,128]{1,0:T(8,128)}, f32[8,2048,16]{1,2,0:T(8,128)}, f32[8,16,2048]{2,1,0:T(8,128)}, f32[8,16,2048]{2,1,0:T(8,128)}), (f32[2048,128]{1,0:T(8,128)}, f32[8,2048,16]{1,2,0:T(8,128)}, f32[8,16,2048]{2,1,0:T(8,128)}, ...) | async-done | bytes 4194320 | tf_op jit(solution)/shard_map/psum | solution.py:323
  1008.2 80.7 %all-gather.11.cloned.1.call-done = bf16[1024,2176]{1,0:T(8,128)(2,1)} async-done(((bf16[256,2176]{1,0:T(8,128)(2,1)}), bf16[1024,2176]{1,0:T(8,128)(2,1)}) %all-gather.11.cloned.1.call-update) | async-done | bytes 4456464 | tf_op jit(solution)/shard_map/all_gather | solution.py:147
  1090.1 3.9 convolution_bitcast_fusion
  1093.9 58.6 %all-reduce.11.cloned.1.call-done = (f32[8,16,2048]{2,1,0:T(8,128)}, f32[8,2048,16]{1,2,0:T(8,128)}) async-done(((f32[8,16,2048]{2,1,0:T(8,128)}, f32[8,2048,16]{1,2,0:T(8,128)}), (f32[8,16,2048]{2,1,0:T(8,128)}, f32[8,2048,16]{1,2,0:T(8,128)})) %all-reduce.11.cloned.1.call-update) | async-done | bytes 2097168 | tf_op jit(solution)/shard_map/psum | solution.py:316
  1152.6 81.9 %all-gather.9.cloned.1.call-done = bf16[1024,2048]{1,0:T(8,128)(2,1)} async-done(((bf16[256,2048]{1,0:T(8,128)(2,1)}), bf16[1024,2048]{1,0:T(8,128)(2,1)}) %all-gather.9.cloned.1.call-update) | async-done | bytes 4194320 | tf_op jit(solution)/shard_map/all_gather | solution.py:147
  1234.5 4.8 slice.109
  1239.3 59.8 %all-reduce.9.cloned.1.call-done = (f32[8,2048,16]{1,2,0:T(8,128)}, f32[8,16,3,512]{3,2,1,0:T(4,128)}) async-done(((f32[8,2048,16]{1,2,0:T(8,128)}, f32[8,16,3,512]{3,2,1,0:T(4,128)}), (f32[8,2048,16]{1,2,0:T(8,128)}, f32[8,16,3,512]{3,2,1,0:T(4,128)})) %all-reduce.9.cloned.1.call-update) | async-done | bytes 1835024 | tf_op jit(solution)/shard_map/psum | solution.py:405
  1301.5 4.9 copy.122
  (284 shorter events, 150.1 us)
Async XLA Ops:
  7.2 301.1 %copy-start = (bf16[8,16,2048]{2,1,0:T(8,128)(2,1)S(1)}, bf16[8,16,2048]{2,1,0:T(8,128)(2,1)}, u32[]{:S(2)}) copy-start(bf16[8,16,2048]{2,1,0:T(8,128)(2,1)} %param.37) | copy-start | bytes 1572868
  7.2 146.9 %all-gather.5.cloned.1.call-start = ((), (), s32[]{:S(2)}) async-start(), calls=%async_computation.5 | async-start | bytes 5898240 | tf_op jit(solution)/shard_map/all_gather | solution.py:202
  12.0 11.5 collective-permute-start
  14.3 8.2 copy-start.46
  21.2 15.7 %copy-start.9 = (bf16[4,256,2048]{2,1,0:T(8,128)(2,1)}, bf16[4,256,2048]{2,1,0:T(8,128)(2,1)S(1)}, u32[]{:S(2)}) copy-start(bf16[4,256,2048]{2,1,0:T(8,128)(2,1)S(1)} %add_convert_fusion) | copy-start | bytes 12582916
  47.4 7.7 copy-start.69
  47.4 7.7 copy-start.72
  49.4 9.0 copy-start.19
  51.0 50.3 %collective-permute-start.3 = (bf16[4,256,1024]{1,2,0:T(8,128)(2,1)}, bf16[4,256,1024]{1,2,0:T(8,128)(2,1)}, u32[]{:S(2)}, u32[]{:S(2)}) collective-permute-start(bf16[4,256,1024]{1,2,0:T(8,128)(2,1)} %pad_maximum_fusion.32), channel_id=1, source_target_pairs={{0,12},{4,8},{8,4},{12,0},{1,13},{5,9},{9,5},{13,1},{2,14},{6,10},... | collective-permute-start | bytes 6291464 | tf_op jit(solution)/shard_map/ppermute | solution.py:115
  54.5 91.3 %collective-permute-start.2 = (bf16[4,256,1024]{1,2,0:T(8,128)(2,1)}, bf16[4,256,1024]{1,2,0:T(8,128)(2,1)}, u32[]{:S(2)}, u32[]{:S(2)}) collective-permute-start(bf16[4,256,1024]{1,2,0:T(8,128)(2,1)} %pad_maximum_fusion.32), channel_id=1, source_target_pairs={{0,8},{4,12},{8,0},{12,4},{1,9},{5,13},{9,1},{13,5},{2,10},{6,14},... | collective-permute-start | bytes 6291464 | tf_op jit(solution)/shard_map/ppermute | solution.py:115
  55.0 91.1 %collective-permute-start.1 = (bf16[4,256,1024]{1,2,0:T(8,128)(2,1)}, bf16[4,256,1024]{1,2,0:T(8,128)(2,1)}, u32[]{:S(2)}, u32[]{:S(2)}) collective-permute-start(bf16[4,256,1024]{1,2,0:T(8,128)(2,1)} %pad_maximum_fusion.32), channel_id=1, source_target_pairs={{0,4},{4,0},{8,12},{12,8},{1,5},{5,1},{9,13},{13,9},{2,6},{6,2},{1... | collective-permute-start | bytes 6291464 | tf_op jit(solution)/shard_map/ppermute | solution.py:115
  64.3 94.8 %copy-start.14 = (bf16[4,256,4,128]{1,3,2,0:T(8,128)(2,1)}, bf16[4,256,4,128]{1,3,2,0:T(8,128)(2,1)S(1)}, u32[]{:S(2)}) copy-start(bf16[4,256,4,128]{1,3,2,0:T(8,128)(2,1)S(1)} %copy.94) | copy-start | bytes 3145732
  150.3 8.8 copy-start.33
  159.1 54.2 %collective-permute-start.4 = (bf16[2048,1024]{1,0:T(8,128)(2,1)}, bf16[2048,1024]{1,0:T(8,128)(2,1)}, u32[]{:S(2)}, u32[]{:S(2)}) collective-permute-start(bf16[2048,1024]{1,0:T(8,128)(2,1)} %slice.94), channel_id=1, source_target_pairs={{0,16},{16,0},{1,17},{17,1},{2,18},{18,2},{3,19},{19,3},{4,20},{20... | collective-permute-start | bytes 12582920 | tf_op jit(solution)/shard_map/ppermute | solution.py:122
  160.4 9.4 copy-start.5
  169.7 10.5 copy-start.60
  180.3 30.6 %all-to-all-start = ((bf16[4,256,512]{1,2,0:T(8,128)(2,1)}), bf16[4,256,512]{1,2,0:T(8,128)(2,1)S(1)}, u32[]{:S(2)}, u32[]{:S(2)}) async-start(bf16[4,256,512]{1,2,0:T(8,128)(2,1)} %bitcast.12), calls=%async_computation | async-start | bytes 2097152 | tf_op jit(solution)/shard_map/all_to_all | solution.py:271
  185.1 119.7 %all-gather.7.cloned.1.call-start = ((), (), s32[]{:S(2)}) async-start(), calls=%async_computation.6 | async-start | bytes 5242880 | tf_op jit(solution)/shard_map/all_gather | solution.py:147
  185.1 27.7 %copy-start.44 = (bf16[8,16,2048]{2,1,0:T(8,128)(2,1)S(1)}, bf16[8,16,2048]{2,1,0:T(8,128)(2,1)}, u32[]{:S(2)}) copy-start(bf16[8,16,2048]{2,1,0:T(8,128)(2,1)} %param.35) | copy-start | bytes 1572868
  217.1 6.8 copy-start.28
  217.1 6.8 copy-start.30
  217.1 7.2 copy-start.66
  217.1 7.2 copy-start.71
  225.7 223.5 %reduce-scatter.6.cloned.1.call-start = ((), (), s32[]{:S(2)}) async-start(), calls=%async_computation.9 | async-start | bytes 5570560 | tf_op jit(solution)/shard_map/reduce_scatter | solution.py:136
  225.9 9.5 collective-permute-start.5
  226.0 13.6 %collective-permute-start.6 = (bf16[2048,1024]{1,0:T(8,128)(2,1)}, bf16[2048,1024]{1,0:T(8,128)(2,1)S(1)}, u32[]{:S(2)}, u32[]{:S(2)}) collective-permute-start(bf16[2048,1024]{1,0:T(8,128)(2,1)} %param.31), channel_id=1, source_target_pairs={{0,16},{16,0},{1,17},{17,1},{2,18},{18,2},{3,19},{19,3},{4,20},{20... | collective-permute-start | bytes 12582920 | tf_op jit(solution)/shard_map/ppermute | solution.py:122
  312.9 17.0 %copy-start.12 = (bf16[4,256,2048]{2,1,0:T(8,128)(2,1)S(1)}, bf16[4,256,2048]{2,1,0:T(8,128)(2,1)}, u32[]{:S(2)}) copy-start(bf16[4,256,2048]{2,1,0:T(8,128)(2,1)} %param.21) | copy-start | bytes 12582916
  369.6 163.4 %reduce-scatter.4.cloned.1.call-start = ((), (), s32[]{:S(2)}) async-start(), calls=%async_computation.7 | async-start | bytes 5570560 | tf_op jit(solution)/shard_map/reduce_scatter | solution.py:136
  388.6 147.0 %copy-start.40 = (bf16[8,2048,16]{1,2,0:T(8,128)(2,1)S(1)}, bf16[8,2048,16]{1,2,0:T(8,128)(2,1)}, u32[]{:S(2)}) copy-start(bf16[8,2048,16]{1,2,0:T(8,128)(2,1)} %param.36) | copy-start | bytes 1572868
  388.6 463.1 %reduce-scatter.8.cloned.1.call-start = ((), (), s32[]{:S(2)}) async-start(), calls=%async_computation.10 | async-start | bytes 5570560 | tf_op jit(solution)/shard_map/reduce_scatter | solution.py:136
  546.2 34.2 %copy-start.61 = (f32[4,4,256]{2,1,0:T(4,128)S(1)}, f32[4,4,256]{2,1,0:T(4,128)}, u32[]{:S(2)}) copy-start(f32[4,4,256]{2,1,0:T(4,128)} %copy-done.60) | copy-start | bytes 49156
  592.4 12.5 copy-start.15
  657.3 6.8 copy-start.7
  660.6 49.8 %collective-permute-start.9 = (bf16[4,256,1024]{2,1,0:T(8,128)(2,1)}, bf16[4,256,1024]{2,1,0:T(8,128)(2,1)}, u32[]{:S(2)}, u32[]{:S(2)}) collective-permute-start(bf16[4,256,1024]{2,1,0:T(8,128)(2,1)} %get-tuple-element.61), channel_id=1, source_target_pairs={{0,12},{4,8},{8,4},{12,0},{1,13},{5,9},{9,5},{13,1},{2,14},{6,10},... | collective-permute-start | bytes 6291464 | tf_op jit(solution)/shard_map/ppermute | solution.py:372
  663.0 90.0 %collective-permute-start.8 = (bf16[4,256,1024]{2,1,0:T(8,128)(2,1)}, bf16[4,256,1024]{2,1,0:T(8,128)(2,1)}, u32[]{:S(2)}, u32[]{:S(2)}) collective-permute-start(bf16[4,256,1024]{2,1,0:T(8,128)(2,1)} %get-tuple-element.62), channel_id=1, source_target_pairs={{0,8},{4,12},{8,0},{12,4},{1,9},{5,13},{9,1},{13,5},{2,10},{6,14},... | collective-permute-start | bytes 6291464 | tf_op jit(solution)/shard_map/ppermute | solution.py:372
  663.6 89.5 %collective-permute-start.7 = (bf16[4,256,1024]{2,1,0:T(8,128)(2,1)}, bf16[4,256,1024]{2,1,0:T(8,128)(2,1)}, u32[]{:S(2)}, u32[]{:S(2)}) collective-permute-start(bf16[4,256,1024]{2,1,0:T(8,128)(2,1)} %get-tuple-element.60), channel_id=1, source_target_pairs={{0,4},{4,0},{8,12},{12,8},{1,5},{5,1},{9,13},{13,9},{2,6},{6,2},{1... | collective-permute-start | bytes 6291464 | tf_op jit(solution)/shard_map/ppermute | solution.py:372
  675.2 84.6 %copy-start.50 = (bf16[128,8,4,128]{3,1,2,0:T(8,128)(2,1)}, bf16[128,8,4,128]{3,1,2,0:T(8,128)(2,1)S(1)}, u32[]{:S(2)}) copy-start(bf16[128,8,4,128]{3,1,2,0:T(8,128)(2,1)S(1)} %copy.112) | copy-start | bytes 3145732
  771.4 8.8 copy-start.59
  771.4 231.0 %all-reduce.7.cloned.1.call-start = ((), (), s32[]{:S(2)}) async-start(), calls=%async_computation.12 | async-start | bytes 8388608 | tf_op jit(solution)/shard_map/psum | solution.py:323
  771.5 7.4 copy-start.20
  771.5 8.8 copy-start.18
  781.6 71.5 %copy-start.42 = (bf16[8,2048,16]{1,2,0:T(8,128)(2,1)S(1)}, bf16[8,2048,16]{1,2,0:T(8,128)(2,1)}, u32[]{:S(2)}) copy-start(bf16[8,2048,16]{1,2,0:T(8,128)(2,1)} %param.32) | copy-start | bytes 1572868
  781.6 71.6 %copy-start.68 = (f32[2048]{0:T(1024)S(1)}, f32[2048]{0:T(1024)}, u32[]{:S(2)}) copy-start(f32[2048]{0:T(1024)} %param.24) | copy-start | bytes 24580
  781.6 307.4 %all-gather.11.cloned.1.call-start = ((), (), s32[]{:S(2)}) async-start(), calls=%async_computation.11 | async-start | bytes 5570560 | tf_op jit(solution)/shard_map/all_gather | solution.py:147
  860.9 291.7 %all-reduce.11.cloned.1.call-start = ((), (), s32[]{:S(2)}) async-start(), calls=%async_computation.14 | async-start | bytes 4194304 | tf_op jit(solution)/shard_map/psum | solution.py:316
  866.8 137.4 %copy-start.39 = (bf16[1024,128]{1,0:T(8,128)(2,1)S(1)}, bf16[1024,128]{1,0:T(8,128)(2,1)}, u32[]{:S(2)}) copy-start(bf16[1024,128]{1,0:T(8,128)(2,1)} %copy-done.38) | copy-start | bytes 786436
  866.8 367.7 %all-gather.9.cloned.1.call-start = ((), (), s32[]{:S(2)}) async-start(), calls=%async_computation.8 | async-start | bytes 5242880 | tf_op jit(solution)/shard_map/all_gather | solution.py:147
  869.9 429.2 %all-reduce.9.cloned.1.call-start = ((), (), s32[]{:S(2)}) async-start(), calls=%async_computation.13 | async-start | bytes 4194304 | tf_op jit(solution)/shard_map/psum | solution.py:405
  (47 other events, 168.8 us)
Sparse Core Ops, SparseCore 0:
  13.9 91.7 all-gather.4
  225.8 78.8 all-gather.6
  369.7 79.5 reduce-scatter.5
  451.4 81.5 reduce-scatter.3
  771.5 80.1 reduce-scatter.7
  858.5 143.8 all-reduce.6
  1004.6 84.3 all-gather.10
  1092.2 60.2 all-reduce.10
  1154.7 79.7 all-gather.8
  1238.8 60.3 all-reduce.8

commit v5 on v4

--- a/solution.py
+++ b/solution.py
@@ -124,6 +124,33 @@
     low = jnp.where(first, block, other)
     high = jnp.where(first, other, block)
     return jnp.concatenate([low, high], axis=axis)
+
+
+def butterfly_sum(values, axis_names):
+    leaves, tree = jax.tree.flatten(values)
+    packed = jnp.concatenate([leaf.reshape(-1) for leaf in leaves])
+    for axis_name in axis_names:
+        axis_count = lax.axis_size(axis_name)
+        step = 1
+        while step < axis_count:
+            pairs = [(index, index ^ step) for index in range(axis_count)]
+            packed = packed + lax.ppermute(packed, axis_name, pairs)
+            step *= 2
+    parts, offset = [], 0
+    for leaf in leaves:
+        parts.append(packed[offset : offset + leaf.size].reshape(leaf.shape))
+        offset += leaf.size
+    return jax.tree.unflatten(tree, parts)
+
+
+def partner_gather_rows(rows_here, axis_name):
+    axis_count = lax.axis_size(axis_name)
+    blocks = jnp.stack(partner_swaps(rows_here, axis_name, axis_count))
+    owners = jnp.bitwise_xor(
+        lax.axis_index(axis_name), jnp.arange(axis_count, dtype=jnp.int32)
+    )
+    ordered = jnp.take(blocks, owners, axis=0)
+    return ordered.reshape(axis_count * rows_here.shape[0], *rows_here.shape[1:])
 
 
 def tp_rows(rows_array, tp_count):
@@ -309,35 +336,28 @@
     heads_back_here = (matmul_nt(grad_middle_low_here, heads_second_flattened) * select_here).astype(
         jnp.bfloat16
     )
-    down_second_gradient = matmul_tn(down_low_here, tp_rows(grad_top_low, tp_count))
-    grad_up_in = matmul_tn(second_act_here, up_back_here)
+    low_rows = partner_gather_rows(
+        jnp.concatenate([down_low_here, up_back_here, heads_back_here], axis=1), "tp"
+    )
+    down_low, up_back, heads_back = split_columns(low_rows, [rank_width * adapter_tables] * 3)
+    down_second_gradient = matmul_tn(down_low, grad_top_low)
+    grad_up_in = matmul_tn(second_act, up_back)
+    grad_heads_in = matmul_tn(heads_act, heads_back)
     heads_second_gradient = matmul_tn(heads_low_here, grad_middle_low_here)
-    grad_heads_in_all = matmul_tn(heads_act_here, heads_back_here)
-    hidden_terms = lax.psum(
+    early_terms = butterfly_sum(
         (
+            unflat_in(grad_heads_in, adapter_tables),
+            unflat_in(grad_up_in, adapter_tables),
             up_second_gradient.reshape(adapter_up_second.shape),
             unflat_in(grad_down_in, adapter_tables),
+            down_second_gradient.reshape(adapter_down_second.shape),
+            butterfly_sum(heads_second_gradient, ("tp",)).reshape(
+                adapter_heads_second.shape
+            ),
         ),
         ("shard", "ctx"),
     )
-    token_terms = lax.psum(
-        (
-            grad_heads_in_all,
-            unflat_in(grad_up_in, adapter_tables),
-            heads_second_gradient.reshape(adapter_heads_second.shape),
-            down_second_gradient.reshape(adapter_down_second.shape),
-        ),
-        ("shard", "ctx", "tp"),
-    )
-    heads_in_rows = tp_rows(token_terms[0], tp_count)
-    early_terms = (
-        unflat_in(heads_in_rows, adapter_tables),
-        token_terms[1],
-        hidden_terms[0],
-        hidden_terms[1],
-        token_terms[3],
-    )
-    heads_second_total = token_terms[2]
+    heads_second_total = early_terms[5]
     grad_heads_here = (
         matmul_nt(grad_middle_low_here, heads_full)
         + matmul_nt(heads_back_here, heads_first_all_flattened)
@@ -390,7 +410,8 @@
     qkv_back_here = (first_low_here * select_late).astype(jnp.bfloat16)
     grad_first = first_here + matmul_nt(qkv_back_here, projection_first_flattened)
     input_here = (grad_middle_here + first_back_full(grad_first)[0]).astype(jnp.bfloat16)
-    input_rows, qkv_back = gather_rows((input_here, qkv_back_here))
+    qkv_back = partner_gather_rows(qkv_back_here, "tp")
+    (input_rows,) = gather_rows((input_here,))
     input_grad = input_rows.reshape(layer_input.shape)
     grad_qkv_in = matmul_tn(first_act, qkv_back)
     early_terms, late_inputs = lax.optimization_barrier(
@@ -402,7 +423,7 @@
             ),
         )
     )
-    late_terms = lax.psum(late_inputs, ("shard", "ctx"))
+    late_terms = butterfly_sum(late_inputs, ("shard", "ctx"))
     return (
         layer_out,
         input_grad,

time: 1330 us -> 1230 us (0.925)
  waiting for transfers between devices: 866 us -> 646 us
  local copies, waits for them, and re-layouts: 106 us -> 203 us
  other arithmetic: 87.7 us -> 122 us
  blocking collectives: 30 us -> 0 us
  starting transfers between devices: 14 us -> 35.7 us
    ppermute x0 -> x8, waiting for transfers between devices: none -> 282 us  [butterfly_sum(): packed = packed + lax.ppermute(packed, axis_name, pairs)]
    psum x3 -> x0, waiting for transfers between devices: 251 us -> none  [the longest x1 132 us: layer_body(): lax.psum((grad_heads_in_all, unflat_in(grad_up_in, adapter_tables), heads...]
    all_gather x3, waiting for transfers between devices: 224 us -> 61.6 us  [gather_rows(): lax.all_gather(jnp.concatenate(rows_here, axis=1), 'tp', axis=0, tiled=True)]
    reduce_scatter x3, waiting for transfers between devices: 212 us -> 118 us  [scatter_rows(): lax.psum_scatter(jnp.concatenate(partials, axis=1).astype(jnp.bfloat16),...]
    reshape x0 -> x8, local copies, waits for them, and re-layouts: none -> 35.3 us  [the longest x5 23.2 us: butterfly_sum(): packed = jnp.concatenate([leaf.reshape(-1) for leaf in leaves])]
    all_to_all x1 -> x0, blocking collectives: 30 us -> none  [layer_body(): grad_heads = lax.all_to_all(grad_heads_here, 'tp', 1, 0, tiled=True)]
    add x0 -> x7, other arithmetic: none -> 26.5 us  [butterfly_sum(): packed = packed + lax.ppermute(packed, axis_name, pairs)]
    unnamed x160 -> x178, local copies, waits for them, and re-layouts: 31.6 us -> 58 us
  transfers between devices with their start and end apart: 21 -> 33, of which waited for: 15 -> 17; matrix products, arithmetic and copies ran while one was open for 13% -> 32% of each run, Pallas kernels for 0% -> 0%
where the time goes in v5:
time: 1230 us; the launch traced here: 1220 us
  waiting for transfers between devices  646 us (53%)
  local copies, waits for them, and re-layouts  203 us (17%)
  matrix products  195 us (16%)
  other arithmetic  122 us (10%)
  starting transfers between devices  35.7 us (3%)
  between operations  15.9 us (1%)
    ppermute x8, waiting for transfers between devices, butterfly_sum(): packed = packed + lax.ppermute(packed, axis_name, pairs)  282 us
    reduce_scatter x3, waiting for transfers between devices, scatter_rows(): lax.psum_scatter(jnp.concatenate(partials, axis=1).astype(jnp.bfloat16),...  118 us
    ppermute x9, waiting for transfers between devices, partner_swaps(): received.append(lax.ppermute(block, axis_name, pairs))  91.2 us
    ppermute x3, waiting for transfers between devices, layer_body(): lax.ppermute(grad_kv[:, offset].astype(jnp.bfloat16), 'ctx', pairs)  73.6 us
    dot_general x12, matrix products, matmul(): return jnp.dot(left_mat, right_mat, preferred_element_type=jnp.float32)  62.3 us
    all_gather x3, waiting for transfers between devices, gather_rows(): lax.all_gather(jnp.concatenate(rows_here, axis=1), 'tp', axis=0, tiled=True)  61.6 us
    dot_general x12, matrix products, matmul_nt(): lax.dot_general(left_mat, right_mat, (((1,), (1,)), ((), ())), preferred_...  61.1 us
    unnamed x178, local copies, waits for them, and re-layouts  58 us
  transfers between devices with their start and end apart: 33, of which 17 were waited for; matrix products, arithmetic and copies ran while one was open for 32% of the time, Pallas kernels for 0%

profile of v5, /device:TPU:0, one launch (start us, length us, event | category | flops | bytes accessed | tf_op | source)
XLA Modules:
  0.0 1218.0 jit_solution(16004682394795112338)
XLA Ops:
  25.2 5.3 broadcast_select_fusion.7
  30.4 6.5 pad_maximum_fusion.5
  36.9 8.9 add_convert_fusion.1
  64.0 37.3 %collective-permute-done.3 = bf16[4,256,1024]{1,2,0:T(8,128)(2,1)} collective-permute-done((bf16[4,256,1024]{1,2,0:T(8,128)(2,1)}, bf16[4,256,1024]{1,2,0:T(8,128)(2,1)}, u32[]{:S(2)}, u32[]{:S(2)}) %collective-permute-start.3) | collective-permute-done | bytes 2097184 | tf_op jit(solution)/shard_map/ppermute | solution.py:115
  101.3 44.5 %collective-permute-done.2 = bf16[4,256,1024]{1,2,0:T(8,128)(2,1)} collective-permute-done((bf16[4,256,1024]{1,2,0:T(8,128)(2,1)}, bf16[4,256,1024]{1,2,0:T(8,128)(2,1)}, u32[]{:S(2)}, u32[]{:S(2)}) %collective-permute-start.2) | collective-permute-done | bytes 2097184 | tf_op jit(solution)/shard_map/ppermute | solution.py:115
  154.1 4.9 slice.211
  160.4 9.4 fusion.71
  169.8 10.5 fusion.72
  185.1 6.7 convert.61
  191.8 19.2 %all-to-all-done = bf16[4,256,512]{1,2,0:T(8,128)(2,1)S(1)} async-done(((bf16[4,256,512]{1,2,0:T(8,128)(2,1)}), bf16[4,256,512]{1,2,0:T(8,128)(2,1)S(1)}, u32[]{:S(2)}, u32[]{:S(2)}) %all-to-all-start) | async-done | bytes 1048608 | tf_op jit(solution)/shard_map/all_to_all | solution.py:298
  217.2 6.8 fusion.73
  243.2 61.6 %all-gather.7.cloned.1.call-done = bf16[1024,2048]{1,0:T(8,128)(2,1)} async-done(((bf16[256,2048]{1,0:T(8,128)(2,1)}), bf16[1024,2048]{1,0:T(8,128)(2,1)}) %all-gather.7.cloned.1.call-update) | async-done | bytes 4194320 | tf_op jit(solution)/shard_map/all_gather | solution.py:174
  313.0 16.9 %multiply_convert_fusion.1 = (bf16[1024,2048]{1,0:T(8,128)(2,1)}, f32[1024,2048]{1,0:T(8,128)}) fusion(f32[1024,2048]{1,0:T(8,128)} %fusion.76, bf16[1024,2048]{1,0:T(8,128)(2,1)S(1)} %copy-done.10, bf16[1024,2048]{1,0:T(8,128)(2,1)} %get-tuple-element.58, bf16[1024,2048]{1,0:T(8,128)(2,1)} %get-tuple-element.57), kind=kOutput, calls=%fused_computation.24 | convolution fusion | flops 8627683328 | bytes 33554432 | tf_op jit(solution)/shard_map/dot_general | solution.py:43
  329.9 21.1 %fusion.4 = bf16[1024,2048]{1,0:T(8,128)(2,1)} fusion(f32[1024,2048]{1,0:T(8,128)} %get-tuple-element.86, f32[1024,2048]{1,0:T(8,128)} %fusion.77, bf16[1024,2048]{1,0:T(8,128)(2,1)S(1)} %bitcast.196, bf16[2048,1024]{1,0:T(8,128)(2,1)} %get-tuple-element.56, bf16[2048,1024]{1,0:T(8,128)(2,1)} %get-tuple-element.55), kind=kOutput, calls=%fused_computation.15 | convolution fusion | flops 8659140608 | bytes 33554432 | tf_op jit(solution)/shard_map/dot_general | solution.py:53
  354.6 11.8 fusion.24
  373.7 12.0 fusion.25
  398.8 5.9 copy.114
  404.7 6.5 reshape.538
  411.2 37.3 %reduce-scatter.6.cloned.1.call-done = bf16[256,2176]{1,0:T(8,128)(2,1)} async-done(((bf16[1024,2176]{1,0:T(8,128)(2,1)}), bf16[256,2176]{1,0:T(8,128)(2,1)}) %reduce-scatter.6.cloned.1.call-update) | async-done | bytes 1114128 | tf_op jit(solution)/shard_map/reduce_scatter | solution.py:163
  451.3 81.0 %reduce-scatter.4.cloned.1.call-done = bf16[256,2176]{1,0:T(8,128)(2,1)} async-done(((bf16[1024,2176]{1,0:T(8,128)(2,1)}), bf16[256,2176]{1,0:T(8,128)(2,1)}) %reduce-scatter.4.cloned.1.call-update) | async-done | bytes 1114128 | tf_op jit(solution)/shard_map/reduce_scatter | solution.py:163
  561.3 6.1 collective-permute-done.11
  586.6 5.9 copy.113
  592.5 6.5 reshape.536
  613.5 10.4 fusion.26
  623.9 9.2 multiply_convert_fusion
  636.4 4.9 multiply_bitcast_fusion
  641.3 10.5 reshape.529
  651.9 9.9 copy.107
  661.8 10.5 reshape.530
  672.3 9.9 copy.108
  682.2 6.7 fusion
  695.7 7.3 fusion.38
  710.0 32.0 %collective-permute-done.9 = bf16[4,256,1024]{2,1,0:T(8,128)(2,1)} collective-permute-done((bf16[4,256,1024]{2,1,0:T(8,128)(2,1)}, bf16[4,256,1024]{2,1,0:T(8,128)(2,1)}, u32[]{:S(2)}, u32[]{:S(2)}) %collective-permute-start.9) | collective-permute-done | bytes 2097184 | tf_op jit(solution)/shard_map/ppermute | solution.py:392
  741.9 41.6 %collective-permute-done.8 = bf16[4,256,1024]{2,1,0:T(8,128)(2,1)} collective-permute-done((bf16[4,256,1024]{2,1,0:T(8,128)(2,1)}, bf16[4,256,1024]{2,1,0:T(8,128)(2,1)}, u32[]{:S(2)}, u32[]{:S(2)}) %collective-permute-start.8) | collective-permute-done | bytes 2097184 | tf_op jit(solution)/shard_map/ppermute | solution.py:392
  790.4 6.9 convolution_convert_fusion
  799.8 6.9 add.272
  809.7 117.9 %collective-permute-done.16 = f32[1376256]{0:T(1024)} collective-permute-done((f32[1376256]{0:T(1024)}, f32[1376256]{0:T(1024)}, u32[]{:S(2)}, u32[]{:S(2)}) %collective-permute-start.16) | collective-permute-done | bytes 5505056 | tf_op jit(solution)/shard_map/ppermute | solution.py:137
  927.6 7.1 add.273
  961.6 93.1 %collective-permute-done.17 = f32[1376256]{0:T(1024)} collective-permute-done((f32[1376256]{0:T(1024)}, f32[1376256]{0:T(1024)}, u32[]{:S(2)}, u32[]{:S(2)}) %collective-permute-start.17) | collective-permute-done | bytes 5505056 | tf_op jit(solution)/shard_map/ppermute | solution.py:137
  1062.3 6.0 slice.190
  1070.6 5.9 slice.194
  1081.2 6.0 copy.116
  1087.2 6.5 reshape.541
  1106.0 40.4 %collective-permute-done.22 = f32[458752]{0:T(1024)S(1)} collective-permute-done((f32[458752]{0:T(1024)S(1)}, f32[458752]{0:T(1024)S(1)}, u32[]{:S(2)}, u32[]{:S(2)}) %collective-permute-start.22) | collective-permute-done | bytes 1835040 | tf_op jit(solution)/shard_map/ppermute | solution.py:137
  1150.7 6.0 copy.120
  1156.7 6.0 copy.121
  1162.7 26.6 %collective-permute-done.23 = f32[458752]{0:T(1024)} collective-permute-done((f32[458752]{0:T(1024)}, f32[458752]{0:T(1024)}, u32[]{:S(2)}, u32[]{:S(2)}) %collective-permute-start.23) | collective-permute-done | bytes 1835040 | tf_op jit(solution)/shard_map/ppermute | solution.py:137
  1196.3 6.0 copy.117
  (364 shorter events, 275.6 us)
Async XLA Ops:
  7.2 301.2 %copy-start = (bf16[8,16,2048]{2,1,0:T(8,128)(2,1)S(1)}, bf16[8,16,2048]{2,1,0:T(8,128)(2,1)}, u32[]{:S(2)}) copy-start(bf16[8,16,2048]{2,1,0:T(8,128)(2,1)} %param.37) | copy-start | bytes 1572868
  7.2 146.9 %all-gather.5.cloned.1.call-start = ((), (), s32[]{:S(2)}) async-start(), calls=%async_computation.5 | async-start | bytes 5898240 | tf_op jit(solution)/shard_map/all_gather | solution.py:229
  12.0 11.5 collective-permute-start
  21.2 15.7 %copy-start.11 = (bf16[4,256,2048]{2,1,0:T(8,128)(2,1)}, bf16[4,256,2048]{2,1,0:T(8,128)(2,1)S(1)}, u32[]{:S(2)}) copy-start(bf16[4,256,2048]{2,1,0:T(8,128)(2,1)S(1)} %add_convert_fusion) | copy-start | bytes 12582916
  51.0 50.3 %collective-permute-start.3 = (bf16[4,256,1024]{1,2,0:T(8,128)(2,1)}, bf16[4,256,1024]{1,2,0:T(8,128)(2,1)}, u32[]{:S(2)}, u32[]{:S(2)}) collective-permute-start(bf16[4,256,1024]{1,2,0:T(8,128)(2,1)} %pad_maximum_fusion.32), channel_id=1, source_target_pairs={{0,12},{4,8},{8,4},{12,0},{1,13},{5,9},{9,5},{13,1},{2,14},{6,10},... | collective-permute-start | bytes 6291464 | tf_op jit(solution)/shard_map/ppermute | solution.py:115
  54.5 91.3 %collective-permute-start.2 = (bf16[4,256,1024]{1,2,0:T(8,128)(2,1)}, bf16[4,256,1024]{1,2,0:T(8,128)(2,1)}, u32[]{:S(2)}, u32[]{:S(2)}) collective-permute-start(bf16[4,256,1024]{1,2,0:T(8,128)(2,1)} %pad_maximum_fusion.32), channel_id=1, source_target_pairs={{0,8},{4,12},{8,0},{12,4},{1,9},{5,13},{9,1},{13,5},{2,10},{6,14},... | collective-permute-start | bytes 6291464 | tf_op jit(solution)/shard_map/ppermute | solution.py:115
  55.0 91.1 %collective-permute-start.1 = (bf16[4,256,1024]{1,2,0:T(8,128)(2,1)}, bf16[4,256,1024]{1,2,0:T(8,128)(2,1)}, u32[]{:S(2)}, u32[]{:S(2)}) collective-permute-start(bf16[4,256,1024]{1,2,0:T(8,128)(2,1)} %pad_maximum_fusion.32), channel_id=1, source_target_pairs={{0,4},{4,0},{8,12},{12,8},{1,5},{5,1},{9,13},{13,9},{2,6},{6,2},{1... | collective-permute-start | bytes 6291464 | tf_op jit(solution)/shard_map/ppermute | solution.py:115
  64.0 95.1 %copy-start.15 = (bf16[4,256,4,128]{1,3,2,0:T(8,128)(2,1)}, bf16[4,256,4,128]{1,3,2,0:T(8,128)(2,1)S(1)}, u32[]{:S(2)}) copy-start(bf16[4,256,4,128]{1,3,2,0:T(8,128)(2,1)S(1)} %copy.106) | copy-start | bytes 3145732
  159.1 54.2 %collective-permute-start.4 = (bf16[2048,1024]{1,0:T(8,128)(2,1)}, bf16[2048,1024]{1,0:T(8,128)(2,1)}, u32[]{:S(2)}, u32[]{:S(2)}) collective-permute-start(bf16[2048,1024]{1,0:T(8,128)(2,1)} %slice.211), channel_id=1, source_target_pairs={{0,16},{16,0},{1,17},{17,1},{2,18},{18,2},{3,19},{19,3},{4,20},{20... | collective-permute-start | bytes 12582920 | tf_op jit(solution)/shard_map/ppermute | solution.py:122
  180.3 30.6 %all-to-all-start = ((bf16[4,256,512]{1,2,0:T(8,128)(2,1)}), bf16[4,256,512]{1,2,0:T(8,128)(2,1)S(1)}, u32[]{:S(2)}, u32[]{:S(2)}) async-start(bf16[4,256,512]{1,2,0:T(8,128)(2,1)} %bitcast.12), calls=%async_computation | async-start | bytes 2097152 | tf_op jit(solution)/shard_map/all_to_all | solution.py:298
  185.1 119.7 %all-gather.7.cloned.1.call-start = ((), (), s32[]{:S(2)}) async-start(), calls=%async_computation.6 | async-start | bytes 5242880 | tf_op jit(solution)/shard_map/all_gather | solution.py:174
  185.1 27.8 %copy-start.46 = (bf16[8,16,2048]{2,1,0:T(8,128)(2,1)S(1)}, bf16[8,16,2048]{2,1,0:T(8,128)(2,1)}, u32[]{:S(2)}) copy-start(bf16[8,16,2048]{2,1,0:T(8,128)(2,1)} %param.35) | copy-start | bytes 1572868
  191.8 25.3 %copy-start.44 = (f32[256,128]{1,0:T(8,128)}, f32[256,128]{1,0:T(8,128)S(1)}, u32[]{:S(2)}) copy-start(f32[256,128]{1,0:T(8,128)S(1)} %constant_dynamic-slice_fusion) | copy-start | bytes 393220
  225.8 222.8 %reduce-scatter.6.cloned.1.call-start = ((), (), s32[]{:S(2)}) async-start(), calls=%async_computation.9 | async-start | bytes 5570560 | tf_op jit(solution)/shard_map/reduce_scatter | solution.py:163
  226.2 8.9 collective-permute-start.5
  226.3 13.4 %collective-permute-start.6 = (bf16[2048,1024]{1,0:T(8,128)(2,1)}, bf16[2048,1024]{1,0:T(8,128)(2,1)S(1)}, u32[]{:S(2)}, u32[]{:S(2)}) collective-permute-start(bf16[2048,1024]{1,0:T(8,128)(2,1)} %param.31), channel_id=1, source_target_pairs={{0,16},{16,0},{1,17},{17,1},{2,18},{18,2},{3,19},{19,3},{4,20},{20... | collective-permute-start | bytes 12582920 | tf_op jit(solution)/shard_map/ppermute | solution.py:122
  313.0 16.9 %copy-start.8 = (bf16[4,256,2048]{2,1,0:T(8,128)(2,1)S(1)}, bf16[4,256,2048]{2,1,0:T(8,128)(2,1)}, u32[]{:S(2)}) copy-start(bf16[4,256,2048]{2,1,0:T(8,128)(2,1)} %param.21) | copy-start | bytes 12582916
  368.8 163.4 %reduce-scatter.4.cloned.1.call-start = ((), (), s32[]{:S(2)}) async-start(), calls=%async_computation.7 | async-start | bytes 5570560 | tf_op jit(solution)/shard_map/reduce_scatter | solution.py:163
  411.2 123.7 %copy-start.40 = (bf16[8,2048,16]{1,2,0:T(8,128)(2,1)S(1)}, bf16[8,2048,16]{1,2,0:T(8,128)(2,1)}, u32[]{:S(2)}) copy-start(bf16[8,2048,16]{1,2,0:T(8,128)(2,1)} %param.36) | copy-start | bytes 1572868
  540.6 20.7 %collective-permute-start.12 = (bf16[256,384]{1,0:T(8,128)(2,1)}, bf16[256,384]{1,0:T(8,128)(2,1)S(1)}, u32[]{:S(2)}, u32[]{:S(2)}) collective-permute-start(bf16[256,384]{1,0:T(8,128)(2,1)} %get-tuple-element.74), channel_id=1, source_target_pairs={{0,3},{1,2},{2,1},{3,0},{4,7},{5,6},{6,5},{7,4},{8,11},{9,10},{10,... | collective-permute-start | bytes 589832 | tf_op jit(solution)/shard_map/ppermute | solution.py:115
  543.2 24.2 %collective-permute-start.11 = (bf16[256,384]{1,0:T(8,128)(2,1)}, bf16[256,384]{1,0:T(8,128)(2,1)S(1)}, u32[]{:S(2)}, u32[]{:S(2)}) collective-permute-start(bf16[256,384]{1,0:T(8,128)(2,1)} %get-tuple-element.74), channel_id=1, source_target_pairs={{0,2},{1,3},{2,0},{3,1},{4,6},{5,7},{6,4},{7,5},{8,10},{9,11},{10,... | collective-permute-start | bytes 589832 | tf_op jit(solution)/shard_map/ppermute | solution.py:115
  543.5 23.9 %collective-permute-start.10 = (bf16[256,384]{1,0:T(8,128)(2,1)}, bf16[256,384]{1,0:T(8,128)(2,1)S(1)}, u32[]{:S(2)}, u32[]{:S(2)}) collective-permute-start(bf16[256,384]{1,0:T(8,128)(2,1)} %get-tuple-element.74), channel_id=1, source_target_pairs={{0,1},{1,0},{2,3},{3,2},{4,5},{5,4},{6,7},{7,6},{8,9},{9,8},{10,11... | collective-permute-start | bytes 589832 | tf_op jit(solution)/shard_map/ppermute | solution.py:115
  552.2 56.4 %all-to-all-start.1 = ((bf16[256,4,512]{0,2,1:T(8,128)(2,1)}), bf16[256,4,512]{0,2,1:T(8,128)(2,1)}, u32[]{:S(2)}, u32[]{:S(2)}) async-start(bf16[256,4,512]{0,2,1:T(8,128)(2,1)} %bitcast.218), calls=%async_computation.3 | async-start | bytes 2097152 | tf_op jit(solution)/shard_map/all_to_all | solution.py:365
  556.4 383.8 %reduce-scatter.8.cloned.1.call-start = ((), (), s32[]{:S(2)}) async-start(), calls=%async_computation.10 | async-start | bytes 5570560 | tf_op jit(solution)/shard_map/reduce_scatter | solution.py:163
  559.4 46.6 %collective-permute-start.13 = (f32[262144]{0:T(1024)}, f32[262144]{0:T(1024)}, u32[]{:S(2)}, u32[]{:S(2)}) collective-permute-start(f32[262144]{0:T(1024)} %bitcast.85), channel_id=1, source_target_pairs={{0,1},{1,0},{2,3},{3,2},{4,5},{5,4},{6,7},{7,6},{8,9},{9,8},{10,11... | collective-permute-start | bytes 3145736 | tf_op jit(solution)/shard_map/ppermute | solution.py:137
  608.6 98.3 %collective-permute-start.14 = (f32[262144]{0:T(1024)}, f32[262144]{0:T(1024)}, u32[]{:S(2)}, u32[]{:S(2)}) collective-permute-start(f32[262144]{0:T(1024)} %add.270), channel_id=1, source_target_pairs={{0,2},{1,3},{2,0},{3,1},{4,6},{5,7},{6,4},{7,5},{8,10},{9,11},{10,... | collective-permute-start | bytes 3145736 | tf_op jit(solution)/shard_map/ppermute | solution.py:137
  623.9 12.4 %copy-start.16 = (bf16[4,256,4,128]{1,3,2,0:T(8,128)(2,1)S(1)}, bf16[4,256,4,128]{1,3,2,0:T(8,128)(2,1)}, u32[]{:S(2)}) copy-start(bf16[4,256,4,128]{1,3,2,0:T(8,128)(2,1)} %copy-done.15) | copy-start | bytes 3145732
  692.2 49.7 %collective-permute-start.9 = (bf16[4,256,1024]{2,1,0:T(8,128)(2,1)}, bf16[4,256,1024]{2,1,0:T(8,128)(2,1)}, u32[]{:S(2)}, u32[]{:S(2)}) collective-permute-start(bf16[4,256,1024]{2,1,0:T(8,128)(2,1)} %get-tuple-element.53), channel_id=1, source_target_pairs={{0,12},{4,8},{8,4},{12,0},{1,13},{5,9},{9,5},{13,1},{2,14},{6,10},... | collective-permute-start | bytes 6291464 | tf_op jit(solution)/shard_map/ppermute | solution.py:392
  694.6 88.9 %collective-permute-start.8 = (bf16[4,256,1024]{2,1,0:T(8,128)(2,1)}, bf16[4,256,1024]{2,1,0:T(8,128)(2,1)}, u32[]{:S(2)}, u32[]{:S(2)}) collective-permute-start(bf16[4,256,1024]{2,1,0:T(8,128)(2,1)} %get-tuple-element.54), channel_id=1, source_target_pairs={{0,8},{4,12},{8,0},{12,4},{1,9},{5,13},{9,1},{13,5},{2,10},{6,14},... | collective-permute-start | bytes 6291464 | tf_op jit(solution)/shard_map/ppermute | solution.py:392
  695.2 88.4 %collective-permute-start.7 = (bf16[4,256,1024]{2,1,0:T(8,128)(2,1)}, bf16[4,256,1024]{2,1,0:T(8,128)(2,1)}, u32[]{:S(2)}, u32[]{:S(2)}) collective-permute-start(bf16[4,256,1024]{2,1,0:T(8,128)(2,1)} %get-tuple-element.52), channel_id=1, source_target_pairs={{0,4},{4,0},{8,12},{12,8},{1,5},{5,1},{9,13},{13,9},{2,6},{6,2},{1... | collective-permute-start | bytes 6291464 | tf_op jit(solution)/shard_map/ppermute | solution.py:392
  705.3 85.0 %slice-start = ((s8[6291456]{0:T(1024)(128)(4,1)}), s8[4194304]{0:T(1024)(128)(4,1)S(1)}, s32[]{:S(2)}) async-start(s8[6291456]{0:T(1024)(128)(4,1)} %bitcast.208), calls=%async_computation.12 | async-start | bytes 8388608
  706.9 83.4 %copy-start.51 = (bf16[128,8,4,128]{3,1,2,0:T(8,128)(2,1)}, bf16[128,8,4,128]{3,1,2,0:T(8,128)(2,1)S(1)}, u32[]{:S(2)}) copy-start(bf16[128,8,4,128]{3,1,2,0:T(8,128)(2,1)S(1)} %copy.137) | copy-start | bytes 3145732
  710.0 80.4 %slice-start.1 = ((s8[6291456]{0:T(1024)(128)(4,1)}), s8[2097152]{0:T(1024)(128)(4,1)S(1)}, s32[]{:S(2)}) async-start(s8[6291456]{0:T(1024)(128)(4,1)} %bitcast.208), calls=%async_computation.13 | async-start | bytes 4194304
  710.0 89.9 %collective-permute-start.15 = (f32[1376256]{0:T(1024)}, f32[1376256]{0:T(1024)}, u32[]{:S(2)}, u32[]{:S(2)}) collective-permute-start(f32[1376256]{0:T(1024)} %add_dynamic-update-slice_fusion), channel_id=1, source_target_pairs={{0,16},{16,0},{1,17},{17,1},{2,18},{18,2},{3,19},{19,3},{4,20},{20... | collective-permute-start | bytes 16515080 | tf_op jit(solution)/shard_map/ppermute | solution.py:137
  799.8 349.7 %all-gather.9.cloned.1.call-start = ((), (), s32[]{:S(2)}) async-start(), calls=%async_computation.8 | async-start | bytes 5242880 | tf_op jit(solution)/shard_map/all_gather | solution.py:174
  806.7 120.9 %collective-permute-start.16 = (f32[1376256]{0:T(1024)}, f32[1376256]{0:T(1024)}, u32[]{:S(2)}, u32[]{:S(2)}) collective-permute-start(f32[1376256]{0:T(1024)} %add.272), channel_id=1, source_target_pairs={{0,4},{4,0},{8,12},{12,8},{1,5},{5,1},{9,13},{13,9},{2,6},{6,2},{1... | collective-permute-start | bytes 16515080 | tf_op jit(solution)/shard_map/ppermute | solution.py:137
  809.6 128.4 %copy-start.39 = (bf16[1024,128]{1,0:T(8,128)(2,1)S(1)}, bf16[1024,128]{1,0:T(8,128)(2,1)}, u32[]{:S(2)}) copy-start(bf16[1024,128]{1,0:T(8,128)(2,1)} %copy-done.38) | copy-start | bytes 786436
  809.7 128.4 %copy-start.52 = (bf16[128,8,4,128]{3,1,2,0:T(8,128)(2,1)S(1)}, bf16[128,8,4,128]{3,1,2,0:T(8,128)(2,1)}, u32[]{:S(2)}) copy-start(bf16[128,8,4,128]{3,1,2,0:T(8,128)(2,1)} %copy-done.51) | copy-start | bytes 3145732
  809.7 128.4 %copy-start.54 = (bf16[4,256,512]{2,1,0:T(8,128)(2,1)S(1)}, bf16[4,256,512]{2,1,0:T(8,128)(2,1)}, u32[]{:S(2)}) copy-start(bf16[4,256,512]{2,1,0:T(8,128)(2,1)} %copy-done.53) | copy-start | bytes 3145732
  809.7 353.0 %all-gather.11.cloned.1.call-start = ((), (), s32[]{:S(2)}) async-start(), calls=%async_computation.11 | async-start | bytes 5242880 | tf_op jit(solution)/shard_map/all_gather | solution.py:174
  809.7 128.3 %copy-start.56 = (bf16[4,256,512]{2,1,0:T(8,128)(2,1)S(1)}, bf16[4,256,512]{2,1,0:T(8,128)(2,1)}, u32[]{:S(2)}) copy-start(bf16[4,256,512]{2,1,0:T(8,128)(2,1)} %copy-done.55) | copy-start | bytes 3145732
  934.7 120.0 %collective-permute-start.17 = (f32[1376256]{0:T(1024)}, f32[1376256]{0:T(1024)}, u32[]{:S(2)}, u32[]{:S(2)}) collective-permute-start(f32[1376256]{0:T(1024)} %add.273), channel_id=1, source_target_pairs={{0,8},{4,12},{8,0},{12,4},{1,9},{5,13},{9,1},{13,5},{2,10},{6,14},... | collective-permute-start | bytes 16515080 | tf_op jit(solution)/shard_map/ppermute | solution.py:137
  941.7 12.0 collective-permute-start.20
  941.8 14.9 %collective-permute-start.19 = (bf16[256,128]{1,0:T(8,128)(2,1)S(1)}, bf16[256,128]{1,0:T(8,128)(2,1)S(1)}, u32[]{:S(2)}, u32[]{:S(2)}) collective-permute-start(bf16[256,128]{1,0:T(8,128)(2,1)S(1)} %fusion.51), channel_id=1, source_target_pairs={{0,2},{1,3},{2,0},{3,1},{4,6},{5,7},{6,4},{7,5},{8,10},{9,11},{10,... | collective-permute-start | bytes 196616 | tf_op jit(solution)/shard_map/ppermute | solution.py:115
  944.5 12.2 %collective-permute-start.18 = (bf16[256,128]{1,0:T(8,128)(2,1)S(1)}, bf16[256,128]{1,0:T(8,128)(2,1)S(1)}, u32[]{:S(2)}, u32[]{:S(2)}) collective-permute-start(bf16[256,128]{1,0:T(8,128)(2,1)S(1)} %fusion.51), channel_id=1, source_target_pairs={{0,1},{1,0},{2,3},{3,2},{4,5},{5,4},{6,7},{7,6},{8,9},{9,8},{10,11... | collective-permute-start | bytes 196616 | tf_op jit(solution)/shard_map/ppermute | solution.py:115
  1098.5 4.0 collective-permute-start.21
  1104.2 42.1 %collective-permute-start.22 = (f32[458752]{0:T(1024)S(1)}, f32[458752]{0:T(1024)S(1)}, u32[]{:S(2)}, u32[]{:S(2)}) collective-permute-start(f32[458752]{0:T(1024)S(1)} %add.275), channel_id=1, source_target_pairs={{0,4},{4,0},{8,12},{12,8},{1,5},{5,1},{9,13},{13,9},{2,6},{6,2},{1... | collective-permute-start | bytes 5505032 | tf_op jit(solution)/shard_map/ppermute | solution.py:137
  1147.8 41.5 %collective-permute-start.23 = (f32[458752]{0:T(1024)}, f32[458752]{0:T(1024)}, u32[]{:S(2)}, u32[]{:S(2)}) collective-permute-start(f32[458752]{0:T(1024)} %add.276), channel_id=1, source_target_pairs={{0,8},{4,12},{8,0},{12,4},{1,9},{5,13},{9,1},{13,5},{2,10},{6,14},... | collective-permute-start | bytes 5505032 | tf_op jit(solution)/shard_map/ppermute | solution.py:137
  (64 other events, 326.8 us)
Sparse Core Ops, SparseCore 0:
  13.9 91.7 all-gather.4
  225.9 78.8 all-gather.6
  369.0 79.5 reduce-scatter.5
  450.7 81.5 reduce-scatter.3
  799.9 80.6 reduce-scatter.7
  882.5 86.7 all-gather.8
  971.4 79.1 all-gather.10

commit v6 on v5

--- a/solution.py
+++ b/solution.py
@@ -344,20 +344,19 @@
     grad_up_in = matmul_tn(second_act, up_back)
     grad_heads_in = matmul_tn(heads_act, heads_back)
     heads_second_gradient = matmul_tn(heads_low_here, grad_middle_low_here)
-    early_terms = butterfly_sum(
+    early_terms = lax.psum(
         (
             unflat_in(grad_heads_in, adapter_tables),
             unflat_in(grad_up_in, adapter_tables),
             up_second_gradient.reshape(adapter_up_second.shape),
             unflat_in(grad_down_in, adapter_tables),
             down_second_gradient.reshape(adapter_down_second.shape),
-            butterfly_sum(heads_second_gradient, ("tp",)).reshape(
-                adapter_heads_second.shape
-            ),
         ),
         ("shard", "ctx"),
     )
-    heads_second_total = early_terms[5]
+    heads_second_total = lax.psum(
+        heads_second_gradient.reshape(adapter_heads_second.shape), ("shard", "ctx", "tp")
+    )
     grad_heads_here = (
         matmul_nt(grad_middle_low_here, heads_full)
         + matmul_nt(heads_back_here, heads_first_all_flattened)
@@ -405,25 +404,26 @@
     projection_second_gradient = matmul_tn(first_low, grad_projected)
     attn_back_part = matmul_nt(grad_projected, qkv_full)
     attn_back_low = matmul_nt(grad_projected, projection_second_flattened)
+    low_blocks = jnp.stack(partner_swaps(attn_back_low, "tp", tp_count))
+    low_owners = jnp.bitwise_xor(lax.axis_index("tp"), jnp.arange(tp_count, dtype=jnp.int32))
+    low_total = jnp.sum(jnp.take(low_blocks, low_owners, axis=0), axis=0)
+    select_late = lax.optimization_barrier(select)
+    qkv_back = (low_total * select_late).astype(jnp.bfloat16)
+    grad_qkv_in = matmul_tn(first_act, qkv_back)
+    late_terms = butterfly_sum(
+        (
+            unflat_in(grad_qkv_in, adapter_tables),
+            projection_second_gradient.reshape(adapter_projection_second.shape),
+        ),
+        ("shard", "ctx"),
+    )
     first_here, first_low_here = scatter_rows((attn_back_part, attn_back_low))
-    select_late = lax.optimization_barrier(select_here)
-    qkv_back_here = (first_low_here * select_late).astype(jnp.bfloat16)
+    select_later = lax.optimization_barrier(select_here)
+    qkv_back_here = (first_low_here * select_later).astype(jnp.bfloat16)
     grad_first = first_here + matmul_nt(qkv_back_here, projection_first_flattened)
     input_here = (grad_middle_here + first_back_full(grad_first)[0]).astype(jnp.bfloat16)
-    qkv_back = partner_gather_rows(qkv_back_here, "tp")
     (input_rows,) = gather_rows((input_here,))
     input_grad = input_rows.reshape(layer_input.shape)
-    grad_qkv_in = matmul_tn(first_act, qkv_back)
-    early_terms, late_inputs = lax.optimization_barrier(
-        (
-            early_terms,
-            (
-                unflat_in(grad_qkv_in, adapter_tables),
-                projection_second_gradient.reshape(adapter_projection_second.shape),
-            ),
-        )
-    )
-    late_terms = butterfly_sum(late_inputs, ("shard", "ctx"))
     return (
         layer_out,
         input_grad,

time: 1230 us -> 1330 us (1.081)
  waiting for transfers between devices: 646 us -> 817 us
  local copies, waits for them, and re-layouts: 203 us -> 131 us
  blocking collectives: 0 us -> 30.1 us
  other arithmetic: 122 us -> 102 us
    psum x0 -> x2, waiting for transfers between devices: none -> 222 us  [the longest x1 134 us: layer_body(): lax.psum(heads_second_gradient.reshape(adapter_heads_second.shape), ('sha...]
    ppermute x8 -> x3, waiting for transfers between devices: 282 us -> 73.2 us  [butterfly_sum(): packed = packed + lax.ppermute(packed, axis_name, pairs)]
    ppermute x9, waiting for transfers between devices: 91.2 us -> 211 us  [partner_swaps(): received.append(lax.ppermute(block, axis_name, pairs))]
    all_to_all x0 -> x1, blocking collectives: none -> 30.1 us  [layer_body(): grad_heads = lax.all_to_all(grad_heads_here, 'tp', 1, 0, tiled=True)]
    reduce_scatter x3, waiting for transfers between devices: 118 us -> 142 us  [scatter_rows(): lax.psum_scatter(jnp.concatenate(partials, axis=1).astype(jnp.bfloat16),...]
    slice x11 -> x3, local copies, waits for them, and re-layouts: 26.7 us -> 4.77 us  [butterfly_sum(): parts.append(packed[offset:offset + leaf.size].reshape(leaf.shape))]
    add x7 -> x3, other arithmetic: 26.5 us -> 6.91 us  [butterfly_sum(): packed = packed + lax.ppermute(packed, axis_name, pairs)]
    unnamed x178 -> x191, local copies, waits for them, and re-layouts: 58 us -> 40 us
  transfers between devices with their start and end apart: 33 -> 29, of which waited for: 17 -> 18; matrix products, arithmetic and copies ran while one was open for 32% -> 16% of each run, Pallas kernels for 0% -> 0%
where the time goes in v6:
time: 1330 us; the launch traced here: 1320 us
  waiting for transfers between devices  817 us (61%)
  matrix products  202 us (15%)
  local copies, waits for them, and re-layouts  131 us (10%)
  other arithmetic  102 us (8%)
  blocking collectives  30.1 us (2%)
  starting transfers between devices  26.1 us (2%)
  between operations  15.4 us (1%)
    ppermute x9, waiting for transfers between devices, partner_swaps(): received.append(lax.ppermute(block, axis_name, pairs))  211 us
    reduce_scatter x3, waiting for transfers between devices, scatter_rows(): lax.psum_scatter(jnp.concatenate(partials, axis=1).astype(jnp.bfloat16),...  142 us
    psum x1, waiting for transfers between devices, layer_body(): lax.psum(heads_second_gradient.reshape(adapter_heads_second.shape), ('sha...  134 us
    psum x1, waiting for transfers between devices, layer_body(): lax.psum((unflat_in(grad_heads_in, adapter_tables), unflat_in(grad_up_in,...  88 us
    ppermute x3, waiting for transfers between devices, layer_body(): lax.ppermute(grad_kv[:, offset].astype(jnp.bfloat16), 'ctx', pairs)  77.9 us
    ppermute x3, waiting for transfers between devices, butterfly_sum(): packed = packed + lax.ppermute(packed, axis_name, pairs)  73.2 us
    all_gather x3, waiting for transfers between devices, gather_rows(): lax.all_gather(jnp.concatenate(rows_here, axis=1), 'tp', axis=0, tiled=True)  71.7 us
    dot_general x12, matrix products, matmul_nt(): lax.dot_general(left_mat, right_mat, (((1,), (1,)), ((), ())), preferred_...  67.3 us
  transfers between devices with their start and end apart: 29, of which 18 were waited for; matrix products, arithmetic and copies ran while one was open for 16% of the time, Pallas kernels for 0%

profile of v6, /device:TPU:0, one launch (start us, length us, event | category | flops | bytes accessed | tf_op | source)
XLA Modules:
  0.0 1323.4 jit_solution(10612869074623811178)
XLA Ops:
  7.3 4.8 copy.119
  25.2 5.3 broadcast_select_fusion.7
  30.4 6.5 pad_maximum_fusion.5
  36.9 8.9 add_convert_fusion.1
  64.0 37.3 %collective-permute-done.3 = bf16[4,256,1024]{1,2,0:T(8,128)(2,1)} collective-permute-done((bf16[4,256,1024]{1,2,0:T(8,128)(2,1)}, bf16[4,256,1024]{1,2,0:T(8,128)(2,1)}, u32[]{:S(2)}, u32[]{:S(2)}) %collective-permute-start.3) | collective-permute-done | bytes 2097184 | tf_op jit(solution)/shard_map/ppermute | solution.py:115
  101.4 44.5 %collective-permute-done.2 = bf16[4,256,1024]{1,2,0:T(8,128)(2,1)} collective-permute-done((bf16[4,256,1024]{1,2,0:T(8,128)(2,1)}, bf16[4,256,1024]{1,2,0:T(8,128)(2,1)}, u32[]{:S(2)}, u32[]{:S(2)}) %collective-permute-start.2) | collective-permute-done | bytes 2097184 | tf_op jit(solution)/shard_map/ppermute | solution.py:115
  154.2 4.9 slice.121
  160.4 9.4 fusion.72
  169.8 10.5 fusion.73
  180.3 4.8 all-to-all-start
  185.1 6.7 convert.60
  191.8 19.2 %all-to-all-done = bf16[4,256,512]{1,2,0:T(8,128)(2,1)S(1)} async-done(((bf16[4,256,512]{1,2,0:T(8,128)(2,1)}), bf16[4,256,512]{1,2,0:T(8,128)(2,1)S(1)}, u32[]{:S(2)}, u32[]{:S(2)}) %all-to-all-start) | async-done | bytes 1048608 | tf_op jit(solution)/shard_map/all_to_all | solution.py:298
  217.2 6.8 fusion.74
  243.5 61.3 %all-gather.7.cloned.1.call-done = bf16[1024,2048]{1,0:T(8,128)(2,1)} async-done(((bf16[256,2048]{1,0:T(8,128)(2,1)}), bf16[1024,2048]{1,0:T(8,128)(2,1)}) %all-gather.7.cloned.1.call-update) | async-done | bytes 4194320 | tf_op jit(solution)/shard_map/all_gather | solution.py:174
  313.0 17.0 %multiply_convert_fusion.1 = (bf16[1024,2048]{1,0:T(8,128)(2,1)}, f32[1024,2048]{1,0:T(8,128)}) fusion(f32[1024,2048]{1,0:T(8,128)} %fusion.77, bf16[1024,2048]{1,0:T(8,128)(2,1)S(1)} %copy-done.10, bf16[1024,2048]{1,0:T(8,128)(2,1)} %get-tuple-element.59, bf16[1024,2048]{1,0:T(8,128)(2,1)} %get-tuple-element.58), kind=kOutput, calls=%fused_computation.24 | convolution fusion | flops 8627683328 | bytes 33554432 | tf_op jit(solution)/shard_map/dot_general | solution.py:43
  329.9 21.4 %fusion.4 = bf16[1024,2048]{1,0:T(8,128)(2,1)} fusion(f32[1024,2048]{1,0:T(8,128)} %get-tuple-element.84, f32[1024,2048]{1,0:T(8,128)} %fusion.78, bf16[1024,2048]{1,0:T(8,128)(2,1)S(1)} %bitcast.191, bf16[2048,1024]{1,0:T(8,128)(2,1)} %get-tuple-element.57, bf16[2048,1024]{1,0:T(8,128)(2,1)} %get-tuple-element.56), kind=kOutput, calls=%fused_computation.15 | convolution fusion | flops 8659140608 | bytes 33554432 | tf_op jit(solution)/shard_map/dot_general | solution.py:53
  354.9 12.0 fusion.24
  374.3 11.7 fusion.25
  388.6 60.6 %reduce-scatter.6.cloned.1.call-done = bf16[256,2176]{1,0:T(8,128)(2,1)} async-done(((bf16[1024,2176]{1,0:T(8,128)(2,1)}), bf16[256,2176]{1,0:T(8,128)(2,1)}) %reduce-scatter.6.cloned.1.call-update) | async-done | bytes 1114128 | tf_op jit(solution)/shard_map/reduce_scatter | solution.py:163
  451.9 81.0 %reduce-scatter.4.cloned.1.call-done = bf16[256,2176]{1,0:T(8,128)(2,1)} async-done(((bf16[1024,2176]{1,0:T(8,128)(2,1)}), bf16[256,2176]{1,0:T(8,128)(2,1)}) %reduce-scatter.4.cloned.1.call-update) | async-done | bytes 1114128 | tf_op jit(solution)/shard_map/reduce_scatter | solution.py:163
  549.2 30.1 %all_to_all.29 = bf16[256,4,512]{0,2,1:T(8,128)(2,1)S(1)} all-to-all(bf16[256,4,512]{0,2,1:T(8,128)(2,1)} %bitcast.215), channel_id=1, replica_groups=mesh['shard'=2,'ctx'=4,'tp'=4] {'tp'}, dimensions={1} | all-to-all | bytes 2097152 | tf_op jit(solution)/shard_map/all_to_all | solution.py:364
  582.7 10.4 fusion.26
  593.1 9.2 multiply_convert_fusion
  605.6 4.9 multiply_bitcast_fusion
  610.5 10.5 reshape.462
  621.1 9.9 copy.136
  631.0 10.5 reshape.463
  641.5 9.9 copy.137
  651.4 6.6 fusion
  664.9 7.3 fusion.38
  675.9 35.2 %collective-permute-done.9 = bf16[4,256,1024]{2,1,0:T(8,128)(2,1)} collective-permute-done((bf16[4,256,1024]{2,1,0:T(8,128)(2,1)}, bf16[4,256,1024]{2,1,0:T(8,128)(2,1)}, u32[]{:S(2)}, u32[]{:S(2)}) %collective-permute-start.9) | collective-permute-done | bytes 2097184 | tf_op jit(solution)/shard_map/ppermute | solution.py:391
  711.2 42.6 %collective-permute-done.8 = bf16[4,256,1024]{2,1,0:T(8,128)(2,1)} collective-permute-done((bf16[4,256,1024]{2,1,0:T(8,128)(2,1)}, bf16[4,256,1024]{2,1,0:T(8,128)(2,1)}, u32[]{:S(2)}, u32[]{:S(2)}) %collective-permute-start.8) | collective-permute-done | bytes 2097184 | tf_op jit(solution)/shard_map/ppermute | solution.py:391
  753.8 4.8 fusion.18
  760.9 11.4 convolution_convert_fusion
  772.5 4.8 pad_maximum_fusion.14
  791.5 20.3 %collective-permute-done.12 = f32[1024,128]{0,1:T(8,128)S(1)} collective-permute-done((f32[1024,128]{0,1:T(8,128)}, f32[1024,128]{0,1:T(8,128)S(1)}, u32[]{:S(2)}, u32[]{:S(2)}) %collective-permute-start.12) | collective-permute-done | bytes 524320 | tf_op jit(solution)/shard_map/ppermute | solution.py:115
  811.8 77.0 %collective-permute-done.11 = f32[1024,128]{0,1:T(8,128)S(1)} collective-permute-done((f32[1024,128]{0,1:T(8,128)}, f32[1024,128]{0,1:T(8,128)S(1)}, u32[]{:S(2)}, u32[]{:S(2)}) %collective-permute-start.11) | collective-permute-done | bytes 524320 | tf_op jit(solution)/shard_map/ppermute | solution.py:115
  898.5 4.7 copy.141
  903.2 5.6 reshape.467
  934.9 7.8 collective-permute-done.18
  942.7 24.0 %collective-permute-done.17 = bf16[256,384]{1,0:T(8,128)(2,1)S(1)} collective-permute-done((bf16[256,384]{1,0:T(8,128)(2,1)S(1)}, bf16[256,384]{1,0:T(8,128)(2,1)S(1)}, u32[]{:S(2)}, u32[]{:S(2)}) %collective-permute-start.17) | collective-permute-done | bytes 196640 | tf_op jit(solution)/shard_map/ppermute | solution.py:115
  979.7 33.2 %collective-permute-done.14 = f32[458752]{0:T(1024)} collective-permute-done((f32[458752]{0:T(1024)S(1)}, f32[458752]{0:T(1024)}, u32[]{:S(2)}, u32[]{:S(2)}) %collective-permute-start.14) | collective-permute-done | bytes 1835040 | tf_op jit(solution)/shard_map/ppermute | solution.py:137
  1017.4 39.9 %collective-permute-done.15 = f32[458752]{0:T(1024)S(1)} collective-permute-done((f32[458752]{0:T(1024)}, f32[458752]{0:T(1024)S(1)}, u32[]{:S(2)}, u32[]{:S(2)}) %collective-permute-start.15) | collective-permute-done | bytes 1835040 | tf_op jit(solution)/shard_map/ppermute | solution.py:137
  1063.8 6.0 copy.145
  1071.2 10.4 all-gather.11.cloned.1.call-done
  1081.7 134.3 %all-reduce.4.cloned.1.call-done = f32[8,16,2048]{2,1,0:T(8,128)} async-done(((f32[8,16,2048]{2,1,0:T(8,128)}), f32[8,16,2048]{2,1,0:T(8,128)}) %all-reduce.4.cloned.1.call-update) | async-done | bytes 1048592 | tf_op jit(solution)/shard_map/psum | solution.py:357
  1216.0 88.0 %all-reduce.6.cloned.1.call-done = (f32[8,512,16]{1,2,0:T(8,128)}, f32[8,2048,16]{1,2,0:T(8,128)}, f32[8,16,2048]{2,1,0:T(8,128)}, f32[8,2048,16]{1,2,0:T(8,128)}, f32[8,16,2048]{2,1,0:T(8,128)}) async-done(((f32[8,512,16]{1,2,0:T(8,128)}, f32[8,2048,16]{1,2,0:T(8,128)}, f32[8,16,2048]{2,1,0:T(8,128)}, f32[8,2048,16]{1,2,0:T(8,128)}, f32[8,16,2048]{2,1,0:T(8,128)}), (f32[8,512,16]{1,2,0:T(8,128)}, ...) | async-done | bytes 4456464 | tf_op jit(solution)/shard_map/psum | solution.py:347
  1304.0 4.9 copy.168
  (354 shorter events, 209.4 us)
Async XLA Ops:
  7.2 301.2 %copy-start = (bf16[8,16,2048]{2,1,0:T(8,128)(2,1)S(1)}, bf16[8,16,2048]{2,1,0:T(8,128)(2,1)}, u32[]{:S(2)}) copy-start(bf16[8,16,2048]{2,1,0:T(8,128)(2,1)} %param.37) | copy-start | bytes 1572868
  7.2 146.9 %all-gather.5.cloned.1.call-start = ((), (), s32[]{:S(2)}) async-start(), calls=%async_computation.5 | async-start | bytes 5898240 | tf_op jit(solution)/shard_map/all_gather | solution.py:229
  12.0 11.5 collective-permute-start
  14.3 8.3 copy-start.49
  21.2 15.7 %copy-start.12 = (bf16[4,256,2048]{2,1,0:T(8,128)(2,1)}, bf16[4,256,2048]{2,1,0:T(8,128)(2,1)S(1)}, u32[]{:S(2)}) copy-start(bf16[4,256,2048]{2,1,0:T(8,128)(2,1)S(1)} %add_convert_fusion) | copy-start | bytes 12582916
  47.4 7.7 copy-start.81
  47.4 7.8 copy-start.86
  49.4 9.0 copy-start.20
  51.0 50.3 %collective-permute-start.3 = (bf16[4,256,1024]{1,2,0:T(8,128)(2,1)}, bf16[4,256,1024]{1,2,0:T(8,128)(2,1)}, u32[]{:S(2)}, u32[]{:S(2)}) collective-permute-start(bf16[4,256,1024]{1,2,0:T(8,128)(2,1)} %pad_maximum_fusion.32), channel_id=1, source_target_pairs={{0,12},{4,8},{8,4},{12,0},{1,13},{5,9},{9,5},{13,1},{2,14},{6,10},... | collective-permute-start | bytes 6291464 | tf_op jit(solution)/shard_map/ppermute | solution.py:115
  54.5 91.3 %collective-permute-start.2 = (bf16[4,256,1024]{1,2,0:T(8,128)(2,1)}, bf16[4,256,1024]{1,2,0:T(8,128)(2,1)}, u32[]{:S(2)}, u32[]{:S(2)}) collective-permute-start(bf16[4,256,1024]{1,2,0:T(8,128)(2,1)} %pad_maximum_fusion.32), channel_id=1, source_target_pairs={{0,8},{4,12},{8,0},{12,4},{1,9},{5,13},{9,1},{13,5},{2,10},{6,14},... | collective-permute-start | bytes 6291464 | tf_op jit(solution)/shard_map/ppermute | solution.py:115
  55.1 91.1 %collective-permute-start.1 = (bf16[4,256,1024]{1,2,0:T(8,128)(2,1)}, bf16[4,256,1024]{1,2,0:T(8,128)(2,1)}, u32[]{:S(2)}, u32[]{:S(2)}) collective-permute-start(bf16[4,256,1024]{1,2,0:T(8,128)(2,1)} %pad_maximum_fusion.32), channel_id=1, source_target_pairs={{0,4},{4,0},{8,12},{12,8},{1,5},{5,1},{9,13},{13,9},{2,6},{6,2},{1... | collective-permute-start | bytes 6291464 | tf_op jit(solution)/shard_map/ppermute | solution.py:115
  64.0 95.1 %copy-start.16 = (bf16[4,256,4,128]{1,3,2,0:T(8,128)(2,1)}, bf16[4,256,4,128]{1,3,2,0:T(8,128)(2,1)S(1)}, u32[]{:S(2)}) copy-start(bf16[4,256,4,128]{1,3,2,0:T(8,128)(2,1)S(1)} %copy.135) | copy-start | bytes 3145732
  150.3 8.8 copy-start.33
  159.1 54.2 %collective-permute-start.4 = (bf16[2048,1024]{1,0:T(8,128)(2,1)}, bf16[2048,1024]{1,0:T(8,128)(2,1)}, u32[]{:S(2)}, u32[]{:S(2)}) collective-permute-start(bf16[2048,1024]{1,0:T(8,128)(2,1)} %slice.121), channel_id=1, source_target_pairs={{0,16},{16,0},{1,17},{17,1},{2,18},{18,2},{3,19},{19,3},{4,20},{20... | collective-permute-start | bytes 12582920 | tf_op jit(solution)/shard_map/ppermute | solution.py:122
  160.4 9.4 copy-start.5
  169.8 10.5 copy-start.69
  180.3 30.6 %all-to-all-start = ((bf16[4,256,512]{1,2,0:T(8,128)(2,1)}), bf16[4,256,512]{1,2,0:T(8,128)(2,1)S(1)}, u32[]{:S(2)}, u32[]{:S(2)}) async-start(bf16[4,256,512]{1,2,0:T(8,128)(2,1)} %bitcast.12), calls=%async_computation | async-start | bytes 2097152 | tf_op jit(solution)/shard_map/all_to_all | solution.py:298
  185.1 119.7 %all-gather.7.cloned.1.call-start = ((), (), s32[]{:S(2)}) async-start(), calls=%async_computation.6 | async-start | bytes 5242880 | tf_op jit(solution)/shard_map/all_gather | solution.py:174
  185.1 27.8 %copy-start.44 = (bf16[8,16,2048]{2,1,0:T(8,128)(2,1)S(1)}, bf16[8,16,2048]{2,1,0:T(8,128)(2,1)}, u32[]{:S(2)}) copy-start(bf16[8,16,2048]{2,1,0:T(8,128)(2,1)} %param.35) | copy-start | bytes 1572868
  225.8 223.4 %reduce-scatter.6.cloned.1.call-start = ((), (), s32[]{:S(2)}) async-start(), calls=%async_computation.9 | async-start | bytes 5570560 | tf_op jit(solution)/shard_map/reduce_scatter | solution.py:163
  226.1 9.5 collective-permute-start.5
  226.1 13.6 %collective-permute-start.6 = (bf16[2048,1024]{1,0:T(8,128)(2,1)}, bf16[2048,1024]{1,0:T(8,128)(2,1)S(1)}, u32[]{:S(2)}, u32[]{:S(2)}) collective-permute-start(bf16[2048,1024]{1,0:T(8,128)(2,1)} %param.31), channel_id=1, source_target_pairs={{0,16},{16,0},{1,17},{17,1},{2,18},{18,2},{3,19},{19,3},{4,20},{20... | collective-permute-start | bytes 12582920 | tf_op jit(solution)/shard_map/ppermute | solution.py:122
  313.0 17.0 %copy-start.6 = (bf16[4,256,2048]{2,1,0:T(8,128)(2,1)S(1)}, bf16[4,256,2048]{2,1,0:T(8,128)(2,1)}, u32[]{:S(2)}) copy-start(bf16[4,256,2048]{2,1,0:T(8,128)(2,1)} %param.21) | copy-start | bytes 12582916
  369.5 163.4 %reduce-scatter.4.cloned.1.call-start = ((), (), s32[]{:S(2)}) async-start(), calls=%async_computation.7 | async-start | bytes 5570560 | tf_op jit(solution)/shard_map/reduce_scatter | solution.py:163
  388.6 147.7 %copy-start.43 = (bf16[8,2048,16]{1,2,0:T(8,128)(2,1)S(1)}, bf16[8,2048,16]{1,2,0:T(8,128)(2,1)}, u32[]{:S(2)}) copy-start(bf16[8,2048,16]{1,2,0:T(8,128)(2,1)} %param.36) | copy-start | bytes 1572868
  388.6 520.3 %reduce-scatter.8.cloned.1.call-start = ((), (), s32[]{:S(2)}) async-start(), calls=%async_computation.10 | async-start | bytes 5570560 | tf_op jit(solution)/shard_map/reduce_scatter | solution.py:163
  546.9 34.3 %copy-start.70 = (f32[4,4,256]{2,1,0:T(4,128)S(1)}, f32[4,4,256]{2,1,0:T(4,128)}, u32[]{:S(2)}) copy-start(f32[4,4,256]{2,1,0:T(4,128)} %copy-done.69) | copy-start | bytes 49156
  593.1 12.5 copy-start.17
  661.4 49.8 %collective-permute-start.9 = (bf16[4,256,1024]{2,1,0:T(8,128)(2,1)}, bf16[4,256,1024]{2,1,0:T(8,128)(2,1)}, u32[]{:S(2)}, u32[]{:S(2)}) collective-permute-start(bf16[4,256,1024]{2,1,0:T(8,128)(2,1)} %get-tuple-element.54), channel_id=1, source_target_pairs={{0,12},{4,8},{8,4},{12,0},{1,13},{5,9},{9,5},{13,1},{2,14},{6,10},... | collective-permute-start | bytes 6291464 | tf_op jit(solution)/shard_map/ppermute | solution.py:391
  663.8 90.0 %collective-permute-start.8 = (bf16[4,256,1024]{2,1,0:T(8,128)(2,1)}, bf16[4,256,1024]{2,1,0:T(8,128)(2,1)}, u32[]{:S(2)}, u32[]{:S(2)}) collective-permute-start(bf16[4,256,1024]{2,1,0:T(8,128)(2,1)} %get-tuple-element.55), channel_id=1, source_target_pairs={{0,8},{4,12},{8,0},{12,4},{1,9},{5,13},{9,1},{13,5},{2,10},{6,14},... | collective-permute-start | bytes 6291464 | tf_op jit(solution)/shard_map/ppermute | solution.py:391
  664.3 89.5 %collective-permute-start.7 = (bf16[4,256,1024]{2,1,0:T(8,128)(2,1)}, bf16[4,256,1024]{2,1,0:T(8,128)(2,1)}, u32[]{:S(2)}, u32[]{:S(2)}) collective-permute-start(bf16[4,256,1024]{2,1,0:T(8,128)(2,1)} %get-tuple-element.53), channel_id=1, source_target_pairs={{0,4},{4,0},{8,12},{12,8},{1,5},{5,1},{9,13},{13,9},{2,6},{6,2},{1... | collective-permute-start | bytes 6291464 | tf_op jit(solution)/shard_map/ppermute | solution.py:391
  675.9 85.0 %copy-start.54 = (bf16[128,8,4,128]{3,1,2,0:T(8,128)(2,1)}, bf16[128,8,4,128]{3,1,2,0:T(8,128)(2,1)S(1)}, u32[]{:S(2)}) copy-start(bf16[128,8,4,128]{3,1,2,0:T(8,128)(2,1)S(1)} %copy.158) | copy-start | bytes 3145732
  760.9 11.4 copy-start.48
  777.3 240.1 %all-gather.9.cloned.1.call-start = ((), (), s32[]{:S(2)}) async-start(), calls=%async_computation.8 | async-start | bytes 5242880 | tf_op jit(solution)/shard_map/all_gather | solution.py:174
  778.1 10.1 copy-start.42
  781.3 300.4 %all-gather.11.cloned.1.call-start = ((), (), s32[]{:S(2)}) async-start(), calls=%async_computation.11 | async-start | bytes 5242880 | tf_op jit(solution)/shard_map/all_gather | solution.py:174
  783.7 28.1 %collective-permute-start.12 = (f32[1024,128]{0,1:T(8,128)}, f32[1024,128]{0,1:T(8,128)S(1)}, u32[]{:S(2)}, u32[]{:S(2)}) collective-permute-start(f32[1024,128]{0,1:T(8,128)} %copy-done.48), channel_id=1, source_target_pairs={{0,3},{1,2},{2,1},{3,0},{4,7},{5,6},{6,5},{7,4},{8,11},{9,10},{10,... | collective-permute-start | bytes 1572872 | tf_op jit(solution)/shard_map/ppermute | solution.py:115
  785.4 103.3 %collective-permute-start.11 = (f32[1024,128]{0,1:T(8,128)}, f32[1024,128]{0,1:T(8,128)S(1)}, u32[]{:S(2)}, u32[]{:S(2)}) collective-permute-start(f32[1024,128]{0,1:T(8,128)} %copy-done.48), channel_id=1, source_target_pairs={{0,2},{1,3},{2,0},{3,1},{4,6},{5,7},{6,4},{7,5},{8,10},{9,11},{10,... | collective-permute-start | bytes 1572872 | tf_op jit(solution)/shard_map/ppermute | solution.py:115
  785.4 103.3 %collective-permute-start.10 = (f32[1024,128]{0,1:T(8,128)}, f32[1024,128]{0,1:T(8,128)}, u32[]{:S(2)}, u32[]{:S(2)}) collective-permute-start(f32[1024,128]{0,1:T(8,128)} %copy-done.48), channel_id=1, source_target_pairs={{0,1},{1,0},{2,3},{3,2},{4,5},{5,4},{6,7},{7,6},{8,9},{9,8},{10,11... | collective-permute-start | bytes 1572872 | tf_op jit(solution)/shard_map/ppermute | solution.py:115
  811.8 77.0 %copy-start.73 = (f32[1024,128]{0,1:T(8,128)}, f32[1024,128]{0,1:T(8,128)S(1)}, u32[]{:S(2)}) copy-start(f32[1024,128]{0,1:T(8,128)S(1)} %collective-permute-done.12) | copy-start | bytes 1572868
  918.2 297.8 %all-reduce.4.cloned.1.call-start = ((), (), s32[]{:S(2)}) async-start(), calls=%async_computation.12 | async-start | bytes 2097152 | tf_op jit(solution)/shard_map/psum | solution.py:357
  919.5 48.9 %collective-permute-start.13 = (f32[458752]{0:T(1024)S(1)}, f32[458752]{0:T(1024)}, u32[]{:S(2)}, u32[]{:S(2)}) collective-permute-start(f32[458752]{0:T(1024)S(1)} %constant_dynamic-update-slice_fusion), channel_id=1, source_target_pairs={{0,16},{16,0},{1,17},{17,1},{2,18},{18,2},{3,19},{19,3},{4,20},{20... | collective-permute-start | bytes 5505032 | tf_op jit(solution)/shard_map/ppermute | solution.py:137
  928.9 13.8 %collective-permute-start.18 = (bf16[256,384]{1,0:T(8,128)(2,1)S(1)}, bf16[256,384]{1,0:T(8,128)(2,1)S(1)}, u32[]{:S(2)}, u32[]{:S(2)}) collective-permute-start(bf16[256,384]{1,0:T(8,128)(2,1)S(1)} %get-tuple-element.72), channel_id=1, source_target_pairs={{0,3},{1,2},{2,1},{3,0},{4,7},{5,6},{6,5},{7,4},{8,11},{9,10},{10,... | collective-permute-start | bytes 589832 | tf_op jit(solution)/shard_map/ppermute | solution.py:115
  929.0 37.7 %collective-permute-start.17 = (bf16[256,384]{1,0:T(8,128)(2,1)S(1)}, bf16[256,384]{1,0:T(8,128)(2,1)S(1)}, u32[]{:S(2)}, u32[]{:S(2)}) collective-permute-start(bf16[256,384]{1,0:T(8,128)(2,1)S(1)} %get-tuple-element.72), channel_id=1, source_target_pairs={{0,2},{1,3},{2,0},{3,1},{4,6},{5,7},{6,4},{7,5},{8,10},{9,11},{10,... | collective-permute-start | bytes 589832 | tf_op jit(solution)/shard_map/ppermute | solution.py:115
  929.1 37.7 %collective-permute-start.16 = (bf16[256,384]{1,0:T(8,128)(2,1)S(1)}, bf16[256,384]{1,0:T(8,128)(2,1)S(1)}, u32[]{:S(2)}, u32[]{:S(2)}) collective-permute-start(bf16[256,384]{1,0:T(8,128)(2,1)S(1)} %get-tuple-element.72), channel_id=1, source_target_pairs={{0,1},{1,0},{2,3},{3,2},{4,5},{5,4},{6,7},{7,6},{8,9},{9,8},{10,11... | collective-permute-start | bytes 589832 | tf_op jit(solution)/shard_map/ppermute | solution.py:115
  934.7 369.3 %all-reduce.6.cloned.1.call-start = ((), (), s32[]{:S(2)}) async-start(), calls=%async_computation.13 | async-start | bytes 8912896 | tf_op jit(solution)/shard_map/psum | solution.py:347
  970.7 42.3 %collective-permute-start.14 = (f32[458752]{0:T(1024)S(1)}, f32[458752]{0:T(1024)}, u32[]{:S(2)}, u32[]{:S(2)}) collective-permute-start(f32[458752]{0:T(1024)S(1)} %add.267), channel_id=1, source_target_pairs={{0,4},{4,0},{8,12},{12,8},{1,5},{5,1},{9,13},{13,9},{2,6},{6,2},{1... | collective-permute-start | bytes 5505032 | tf_op jit(solution)/shard_map/ppermute | solution.py:137
  1015.9 41.4 %collective-permute-start.15 = (f32[458752]{0:T(1024)}, f32[458752]{0:T(1024)S(1)}, u32[]{:S(2)}, u32[]{:S(2)}) collective-permute-start(f32[458752]{0:T(1024)} %add.268), channel_id=1, source_target_pairs={{0,8},{4,12},{8,0},{12,4},{1,9},{5,13},{9,1},{13,5},{2,10},{6,14},... | collective-permute-start | bytes 5505032 | tf_op jit(solution)/shard_map/ppermute | solution.py:137
  (69 other events, 276.2 us)
Sparse Core Ops, SparseCore 0:
  13.9 91.7 all-gather.4
  225.9 78.8 all-gather.6
  369.6 79.5 reduce-scatter.5
  451.3 81.5 reduce-scatter.3
  777.4 118.8 reduce-scatter.7
  898.3 101.9 all-gather.8
  1002.4 79.1 all-gather.10
  1086.8 129.0 all-reduce.3
  1221.1 82.8 all-reduce.5

commit v7 on v6

--- a/solution.py
+++ b/solution.py
@@ -151,6 +151,11 @@
     )
     ordered = jnp.take(blocks, owners, axis=0)
     return ordered.reshape(axis_count * rows_here.shape[0], *rows_here.shape[1:])
+
+
+def narrow_psum(values, axis_names):
+    summed = lax.psum(jax.tree.map(lambda value: value.astype(jnp.bfloat16), values), axis_names)
+    return jax.tree.map(lambda value: value.astype(jnp.float32), summed)
 
 
 def tp_rows(rows_array, tp_count):
@@ -344,7 +349,7 @@
     grad_up_in = matmul_tn(second_act, up_back)
     grad_heads_in = matmul_tn(heads_act, heads_back)
     heads_second_gradient = matmul_tn(heads_low_here, grad_middle_low_here)
-    early_terms = lax.psum(
+    early_terms = narrow_psum(
         (
             unflat_in(grad_heads_in, adapter_tables),
             unflat_in(grad_up_in, adapter_tables),
@@ -354,7 +359,7 @@
         ),
         ("shard", "ctx"),
     )
-    heads_second_total = lax.psum(
+    heads_second_total = narrow_psum(
         heads_second_gradient.reshape(adapter_heads_second.shape), ("shard", "ctx", "tp")
     )
     grad_heads_here = (

time: 1330 us -> 1300 us (0.977)
  waiting for transfers between devices: 817 us -> 780 us
    all_gather x3, waiting for transfers between devices: 71.7 us -> 202 us  [gather_rows(): lax.all_gather(jnp.concatenate(rows_here, axis=1), 'tp', axis=0, tiled=True)]
    psum x2, waiting for transfers between devices: 222 us -> 116 us  [narrow_psum(): lax.psum(jax.tree.map(lambda value: value.astype(jnp.bfloat16), values),...]
    ppermute x9, waiting for transfers between devices: 211 us -> 178 us  [partner_swaps(): received.append(lax.ppermute(block, axis_name, pairs))]
    ppermute x3, waiting for transfers between devices: 73.2 us -> 44.5 us  [butterfly_sum(): packed = packed + lax.ppermute(packed, axis_name, pairs)]
    unnamed x191 -> x173, local copies, waits for them, and re-layouts: 40 us -> 33.7 us
  transfers between devices with their start and end apart: 29 -> 29, of which waited for: 18 -> 20; matrix products, arithmetic and copies ran while one was open for 16% -> 17% of each run, Pallas kernels for 0% -> 0%
where the time goes in v7:
time: 1300 us; the launch traced here: 1290 us
  waiting for transfers between devices  780 us (60%)
  matrix products  203 us (16%)
  local copies, waits for them, and re-layouts  126 us (10%)
  other arithmetic  111 us (9%)
  blocking collectives  30.1 us (2%)
  starting transfers between devices  25.9 us (2%)
  between operations  15.4 us (1%)
    all_gather x3, waiting for transfers between devices, gather_rows(): lax.all_gather(jnp.concatenate(rows_here, axis=1), 'tp', axis=0, tiled=True)  202 us
    ppermute x9, waiting for transfers between devices, partner_swaps(): received.append(lax.ppermute(block, axis_name, pairs))  178 us
    reduce_scatter x3, waiting for transfers between devices, scatter_rows(): lax.psum_scatter(jnp.concatenate(partials, axis=1).astype(jnp.bfloat16),...  142 us
    psum x2, waiting for transfers between devices, narrow_psum(): lax.psum(jax.tree.map(lambda value: value.astype(jnp.bfloat16), values),...  116 us
    ppermute x3, waiting for transfers between devices, layer_body(): lax.ppermute(grad_kv[:, offset].astype(jnp.bfloat16), 'ctx', pairs)  77.9 us
    dot_general x12, matrix products, matmul_nt(): lax.dot_general(left_mat, right_mat, (((1,), (1,)), ((), ())), preferred_...  67.3 us
    dot_general x12, matrix products, matmul(): return jnp.dot(left_mat, right_mat, preferred_element_type=jnp.float32)  63.9 us
    ppermute x3, waiting for transfers between devices, butterfly_sum(): packed = packed + lax.ppermute(packed, axis_name, pairs)  44.5 us
  transfers between devices with their start and end apart: 29, of which 20 were waited for; matrix products, arithmetic and copies ran while one was open for 17% of the time, Pallas kernels for 0%

profile of v7, /device:TPU:0, one launch (start us, length us, event | category | flops | bytes accessed | tf_op | source)
XLA Modules:
  0.0 1290.9 jit_solution(9968102797315988165)
XLA Ops:
  7.3 4.8 copy.119
  25.2 5.3 broadcast_select_fusion.7
  30.4 6.5 pad_maximum_fusion.5
  36.9 8.9 add_convert_fusion.1
  64.0 37.3 %collective-permute-done.3 = bf16[4,256,1024]{1,2,0:T(8,128)(2,1)} collective-permute-done((bf16[4,256,1024]{1,2,0:T(8,128)(2,1)}, bf16[4,256,1024]{1,2,0:T(8,128)(2,1)}, u32[]{:S(2)}, u32[]{:S(2)}) %collective-permute-start.3) | collective-permute-done | bytes 2097184 | tf_op jit(solution)/shard_map/ppermute | solution.py:115
  101.3 44.5 %collective-permute-done.2 = bf16[4,256,1024]{1,2,0:T(8,128)(2,1)} collective-permute-done((bf16[4,256,1024]{1,2,0:T(8,128)(2,1)}, bf16[4,256,1024]{1,2,0:T(8,128)(2,1)}, u32[]{:S(2)}, u32[]{:S(2)}) %collective-permute-start.2) | collective-permute-done | bytes 2097184 | tf_op jit(solution)/shard_map/ppermute | solution.py:115
  154.1 4.9 slice.121
  160.3 9.4 fusion.72
  169.7 10.5 fusion.73
  180.3 4.8 all-to-all-start
  185.0 6.7 convert.60
  191.7 19.2 %all-to-all-done = bf16[4,256,512]{1,2,0:T(8,128)(2,1)S(1)} async-done(((bf16[4,256,512]{1,2,0:T(8,128)(2,1)}), bf16[4,256,512]{1,2,0:T(8,128)(2,1)S(1)}, u32[]{:S(2)}, u32[]{:S(2)}) %all-to-all-start) | async-done | bytes 1048608 | tf_op jit(solution)/shard_map/all_to_all | solution.py:303
  217.1 6.8 fusion.74
  230.2 4.8 fusion.78
  243.0 61.8 %all-gather.7.cloned.1.call-done = bf16[1024,2048]{1,0:T(8,128)(2,1)} async-done(((bf16[256,2048]{1,0:T(8,128)(2,1)}), bf16[1024,2048]{1,0:T(8,128)(2,1)}) %all-gather.7.cloned.1.call-update) | async-done | bytes 4194320 | tf_op jit(solution)/shard_map/all_gather | solution.py:179
  312.9 17.0 %multiply_convert_fusion.1 = (bf16[1024,2048]{1,0:T(8,128)(2,1)}, f32[1024,2048]{1,0:T(8,128)}) fusion(f32[1024,2048]{1,0:T(8,128)} %fusion.77, bf16[1024,2048]{1,0:T(8,128)(2,1)S(1)} %copy-done.22, bf16[1024,2048]{1,0:T(8,128)(2,1)} %get-tuple-element.59, bf16[1024,2048]{1,0:T(8,128)(2,1)} %get-tuple-element.58), kind=kOutput, calls=%fused_computation.24 | convolution fusion | flops 8627683328 | bytes 33554432 | tf_op jit(solution)/shard_map/dot_general | solution.py:43
  329.9 21.4 %fusion.4 = bf16[1024,2048]{1,0:T(8,128)(2,1)} fusion(f32[1024,2048]{1,0:T(8,128)} %get-tuple-element.84, f32[1024,2048]{1,0:T(8,128)} %fusion.78, bf16[1024,2048]{1,0:T(8,128)(2,1)S(1)} %bitcast.190, bf16[2048,1024]{1,0:T(8,128)(2,1)} %get-tuple-element.57, bf16[2048,1024]{1,0:T(8,128)(2,1)} %get-tuple-element.56), kind=kOutput, calls=%fused_computation.15 | convolution fusion | flops 8659140608 | bytes 33554432 | tf_op jit(solution)/shard_map/dot_general | solution.py:53
  354.9 12.0 fusion.24
  374.3 11.7 fusion.25
  388.5 60.6 %reduce-scatter.6.cloned.1.call-done = bf16[256,2176]{1,0:T(8,128)(2,1)} async-done(((bf16[1024,2176]{1,0:T(8,128)(2,1)}), bf16[256,2176]{1,0:T(8,128)(2,1)}) %reduce-scatter.6.cloned.1.call-update) | async-done | bytes 1114128 | tf_op jit(solution)/shard_map/reduce_scatter | solution.py:168
  451.9 81.0 %reduce-scatter.4.cloned.1.call-done = bf16[256,2176]{1,0:T(8,128)(2,1)} async-done(((bf16[1024,2176]{1,0:T(8,128)(2,1)}), bf16[256,2176]{1,0:T(8,128)(2,1)}) %reduce-scatter.4.cloned.1.call-update) | async-done | bytes 1114128 | tf_op jit(solution)/shard_map/reduce_scatter | solution.py:168
  549.1 30.1 %all_to_all.29 = bf16[256,4,512]{0,2,1:T(8,128)(2,1)S(1)} all-to-all(bf16[256,4,512]{0,2,1:T(8,128)(2,1)} %bitcast.211), channel_id=1, replica_groups=mesh['shard'=2,'ctx'=4,'tp'=4] {'tp'}, dimensions={1} | all-to-all | bytes 2097152 | tf_op jit(solution)/shard_map/all_to_all | solution.py:369
  582.7 10.4 fusion.26
  593.1 9.2 multiply_convert_fusion
  605.6 4.9 multiply_bitcast_fusion
  610.5 10.5 reshape.458
  621.1 9.9 copy.136
  631.0 10.5 reshape.459
  641.5 9.9 copy.137
  651.4 6.6 fusion
  664.8 7.3 fusion.38
  675.9 35.2 %collective-permute-done.9 = bf16[4,256,1024]{2,1,0:T(8,128)(2,1)} collective-permute-done((bf16[4,256,1024]{2,1,0:T(8,128)(2,1)}, bf16[4,256,1024]{2,1,0:T(8,128)(2,1)}, u32[]{:S(2)}, u32[]{:S(2)}) %collective-permute-start.9) | collective-permute-done | bytes 2097184 | tf_op jit(solution)/shard_map/ppermute | solution.py:396
  711.1 42.6 %collective-permute-done.8 = bf16[4,256,1024]{2,1,0:T(8,128)(2,1)} collective-permute-done((bf16[4,256,1024]{2,1,0:T(8,128)(2,1)}, bf16[4,256,1024]{2,1,0:T(8,128)(2,1)}, u32[]{:S(2)}, u32[]{:S(2)}) %collective-permute-start.8) | collective-permute-done | bytes 2097184 | tf_op jit(solution)/shard_map/ppermute | solution.py:396
  753.7 4.8 fusion.18
  760.8 11.4 convolution_convert_fusion
  794.6 8.4 collective-permute-done.18
  803.0 29.1 %collective-permute-done.17 = bf16[256,384]{1,0:T(8,128)(2,1)S(1)} collective-permute-done((bf16[256,384]{1,0:T(8,128)(2,1)}, bf16[256,384]{1,0:T(8,128)(2,1)S(1)}, u32[]{:S(2)}, u32[]{:S(2)}) %collective-permute-start.17) | collective-permute-done | bytes 196640 | tf_op jit(solution)/shard_map/ppermute | solution.py:115
  860.0 17.1 %collective-permute-done.12 = f32[1024,128]{0,1:T(8,128)} collective-permute-done((f32[1024,128]{0,1:T(8,128)}, f32[1024,128]{0,1:T(8,128)}, u32[]{:S(2)}, u32[]{:S(2)}) %collective-permute-start.12) | collective-permute-done | bytes 524320 | tf_op jit(solution)/shard_map/ppermute | solution.py:115
  877.1 41.7 %collective-permute-done.11 = f32[1024,128]{0,1:T(8,128)} collective-permute-done((f32[1024,128]{0,1:T(8,128)}, f32[1024,128]{0,1:T(8,128)}, u32[]{:S(2)}, u32[]{:S(2)}) %collective-permute-start.11) | collective-permute-done | bytes 524320 | tf_op jit(solution)/shard_map/ppermute | solution.py:115
  927.8 4.9 copy.141
  932.7 5.6 reshape.463
  953.2 40.8 %collective-permute-done.14 = f32[458752]{0:T(1024)S(1)} collective-permute-done((f32[458752]{0:T(1024)S(1)}, f32[458752]{0:T(1024)S(1)}, u32[]{:S(2)}, u32[]{:S(2)}) %collective-permute-start.14) | collective-permute-done | bytes 1835040 | tf_op jit(solution)/shard_map/ppermute | solution.py:137
  995.7 51.7 %all-reduce.4.cloned.1.call-done = bf16[8,16,2048]{2,1,0:T(8,128)(2,1)} async-done(((bf16[8,16,2048]{2,1,0:T(8,128)(2,1)}), bf16[8,16,2048]{2,1,0:T(8,128)(2,1)}) %all-reduce.4.cloned.1.call-update) | async-done | bytes 524304 | tf_op jit(solution)/shard_map/psum | solution.py:157
  1049.5 64.0 %all-reduce.6.cloned.1.call-done = (bf16[8,512,16]{1,2,0:T(8,128)(2,1)}, bf16[8,2048,16]{1,2,0:T(8,128)(2,1)}, bf16[8,16,2048]{2,1,0:T(8,128)(2,1)}, bf16[8,2048,16]{1,2,0:T(8,128)(2,1)}, bf16[8,16,2048]{2,1,0:T(8,128)(2,1)}) async-done(((bf16[8,512,16]{1,2,0:T(8,128)(2,1)}, bf16[8,2048,16]{1,2,0:T(8,128)(2,1)}, bf16[8,16,2048]{2,1,0:T(8,128)(2,1)}, bf16[8,2048,16]{1,2,0:T(8,128)(2,1)}, ...) | async-done | bytes 2228240 | tf_op jit(solution)/shard_map/psum | solution.py:157
  1122.6 73.2 %all-gather.9.cloned.1.call-done = bf16[1024,2048]{1,0:T(8,128)(2,1)} async-done(((bf16[256,2048]{1,0:T(8,128)(2,1)}), bf16[1024,2048]{1,0:T(8,128)(2,1)}) %all-gather.9.cloned.1.call-update) | async-done | bytes 4194320 | tf_op jit(solution)/shard_map/all_gather | solution.py:179
  1202.3 6.5 copy.145
  1210.2 67.0 %all-gather.11.cloned.1.call-done = bf16[1024,2048]{1,0:T(8,128)(2,1)} async-done(((bf16[256,2048]{1,0:T(8,128)(2,1)}), bf16[1024,2048]{1,0:T(8,128)(2,1)}) %all-gather.11.cloned.1.call-update) | async-done | bytes 4194320 | tf_op jit(solution)/shard_map/all_gather | solution.py:179
  1277.2 4.9 copy.168
  (342 shorter events, 217.6 us)
Async XLA Ops:
  7.2 301.1 %copy-start = (bf16[8,16,2048]{2,1,0:T(8,128)(2,1)S(1)}, bf16[8,16,2048]{2,1,0:T(8,128)(2,1)}, u32[]{:S(2)}) copy-start(bf16[8,16,2048]{2,1,0:T(8,128)(2,1)} %param.37) | copy-start | bytes 1572868
  7.2 146.9 %all-gather.5.cloned.1.call-start = ((), (), s32[]{:S(2)}) async-start(), calls=%async_computation.5 | async-start | bytes 5898240 | tf_op jit(solution)/shard_map/all_gather | solution.py:234
  12.0 11.5 collective-permute-start
  14.3 8.2 copy-start.48
  21.2 15.7 %copy-start.11 = (bf16[4,256,2048]{2,1,0:T(8,128)(2,1)}, bf16[4,256,2048]{2,1,0:T(8,128)(2,1)S(1)}, u32[]{:S(2)}) copy-start(bf16[4,256,2048]{2,1,0:T(8,128)(2,1)S(1)} %add_convert_fusion) | copy-start | bytes 12582916
  49.4 9.0 copy-start.19
  51.0 50.3 %collective-permute-start.3 = (bf16[4,256,1024]{1,2,0:T(8,128)(2,1)}, bf16[4,256,1024]{1,2,0:T(8,128)(2,1)}, u32[]{:S(2)}, u32[]{:S(2)}) collective-permute-start(bf16[4,256,1024]{1,2,0:T(8,128)(2,1)} %pad_maximum_fusion.32), channel_id=1, source_target_pairs={{0,12},{4,8},{8,4},{12,0},{1,13},{5,9},{9,5},{13,1},{2,14},{6,10},... | collective-permute-start | bytes 6291464 | tf_op jit(solution)/shard_map/ppermute | solution.py:115
  54.5 91.3 %collective-permute-start.2 = (bf16[4,256,1024]{1,2,0:T(8,128)(2,1)}, bf16[4,256,1024]{1,2,0:T(8,128)(2,1)}, u32[]{:S(2)}, u32[]{:S(2)}) collective-permute-start(bf16[4,256,1024]{1,2,0:T(8,128)(2,1)} %pad_maximum_fusion.32), channel_id=1, source_target_pairs={{0,8},{4,12},{8,0},{12,4},{1,9},{5,13},{9,1},{13,5},{2,10},{6,14},... | collective-permute-start | bytes 6291464 | tf_op jit(solution)/shard_map/ppermute | solution.py:115
  55.0 91.1 %collective-permute-start.1 = (bf16[4,256,1024]{1,2,0:T(8,128)(2,1)}, bf16[4,256,1024]{1,2,0:T(8,128)(2,1)}, u32[]{:S(2)}, u32[]{:S(2)}) collective-permute-start(bf16[4,256,1024]{1,2,0:T(8,128)(2,1)} %pad_maximum_fusion.32), channel_id=1, source_target_pairs={{0,4},{4,0},{8,12},{12,8},{1,5},{5,1},{9,13},{13,9},{2,6},{6,2},{1... | collective-permute-start | bytes 6291464 | tf_op jit(solution)/shard_map/ppermute | solution.py:115
  64.0 95.0 %copy-start.15 = (bf16[4,256,4,128]{1,3,2,0:T(8,128)(2,1)}, bf16[4,256,4,128]{1,3,2,0:T(8,128)(2,1)S(1)}, u32[]{:S(2)}) copy-start(bf16[4,256,4,128]{1,3,2,0:T(8,128)(2,1)S(1)} %copy.135) | copy-start | bytes 3145732
  150.3 8.8 copy-start.31
  159.0 54.2 %collective-permute-start.4 = (bf16[2048,1024]{1,0:T(8,128)(2,1)}, bf16[2048,1024]{1,0:T(8,128)(2,1)}, u32[]{:S(2)}, u32[]{:S(2)}) collective-permute-start(bf16[2048,1024]{1,0:T(8,128)(2,1)} %slice.121), channel_id=1, source_target_pairs={{0,16},{16,0},{1,17},{17,1},{2,18},{18,2},{3,19},{19,3},{4,20},{20... | collective-permute-start | bytes 12582920 | tf_op jit(solution)/shard_map/ppermute | solution.py:122
  160.3 9.4 copy-start.5
  169.7 10.5 copy-start.62
  180.3 30.7 %all-to-all-start = ((bf16[4,256,512]{1,2,0:T(8,128)(2,1)}), bf16[4,256,512]{1,2,0:T(8,128)(2,1)S(1)}, u32[]{:S(2)}, u32[]{:S(2)}) async-start(bf16[4,256,512]{1,2,0:T(8,128)(2,1)} %bitcast.12), calls=%async_computation | async-start | bytes 2097152 | tf_op jit(solution)/shard_map/all_to_all | solution.py:303
  185.0 119.7 %all-gather.7.cloned.1.call-start = ((), (), s32[]{:S(2)}) async-start(), calls=%async_computation.6 | async-start | bytes 5242880 | tf_op jit(solution)/shard_map/all_gather | solution.py:179
  185.0 27.8 %copy-start.41 = (bf16[8,16,2048]{2,1,0:T(8,128)(2,1)S(1)}, bf16[8,16,2048]{2,1,0:T(8,128)(2,1)}, u32[]{:S(2)}) copy-start(bf16[8,16,2048]{2,1,0:T(8,128)(2,1)} %param.35) | copy-start | bytes 1572868
  225.7 223.4 %reduce-scatter.6.cloned.1.call-start = ((), (), s32[]{:S(2)}) async-start(), calls=%async_computation.9 | async-start | bytes 5570560 | tf_op jit(solution)/shard_map/reduce_scatter | solution.py:168
  226.0 9.0 collective-permute-start.5
  226.1 13.4 %collective-permute-start.6 = (bf16[2048,1024]{1,0:T(8,128)(2,1)}, bf16[2048,1024]{1,0:T(8,128)(2,1)S(1)}, u32[]{:S(2)}, u32[]{:S(2)}) collective-permute-start(bf16[2048,1024]{1,0:T(8,128)(2,1)} %param.31), channel_id=1, source_target_pairs={{0,16},{16,0},{1,17},{17,1},{2,18},{18,2},{3,19},{19,3},{4,20},{20... | collective-permute-start | bytes 12582920 | tf_op jit(solution)/shard_map/ppermute | solution.py:122
  312.9 17.0 %copy-start.6 = (bf16[4,256,2048]{2,1,0:T(8,128)(2,1)S(1)}, bf16[4,256,2048]{2,1,0:T(8,128)(2,1)}, u32[]{:S(2)}) copy-start(bf16[4,256,2048]{2,1,0:T(8,128)(2,1)} %param.21) | copy-start | bytes 12582916
  369.5 163.4 %reduce-scatter.4.cloned.1.call-start = ((), (), s32[]{:S(2)}) async-start(), calls=%async_computation.7 | async-start | bytes 5570560 | tf_op jit(solution)/shard_map/reduce_scatter | solution.py:168
  388.5 147.7 %copy-start.40 = (bf16[8,2048,16]{1,2,0:T(8,128)(2,1)S(1)}, bf16[8,2048,16]{1,2,0:T(8,128)(2,1)}, u32[]{:S(2)}) copy-start(bf16[8,2048,16]{1,2,0:T(8,128)(2,1)} %param.36) | copy-start | bytes 1572868
  388.5 549.9 %reduce-scatter.8.cloned.1.call-start = ((), (), s32[]{:S(2)}) async-start(), calls=%async_computation.10 | async-start | bytes 5570560 | tf_op jit(solution)/shard_map/reduce_scatter | solution.py:168
  546.9 34.3 %copy-start.63 = (f32[4,4,256]{2,1,0:T(4,128)S(1)}, f32[4,4,256]{2,1,0:T(4,128)}, u32[]{:S(2)}) copy-start(f32[4,4,256]{2,1,0:T(4,128)} %copy-done.62) | copy-start | bytes 49156
  593.1 12.5 copy-start.16
  661.3 49.8 %collective-permute-start.9 = (bf16[4,256,1024]{2,1,0:T(8,128)(2,1)}, bf16[4,256,1024]{2,1,0:T(8,128)(2,1)}, u32[]{:S(2)}, u32[]{:S(2)}) collective-permute-start(bf16[4,256,1024]{2,1,0:T(8,128)(2,1)} %get-tuple-element.54), channel_id=1, source_target_pairs={{0,12},{4,8},{8,4},{12,0},{1,13},{5,9},{9,5},{13,1},{2,14},{6,10},... | collective-permute-start | bytes 6291464 | tf_op jit(solution)/shard_map/ppermute | solution.py:396
  663.7 90.0 %collective-permute-start.8 = (bf16[4,256,1024]{2,1,0:T(8,128)(2,1)}, bf16[4,256,1024]{2,1,0:T(8,128)(2,1)}, u32[]{:S(2)}, u32[]{:S(2)}) collective-permute-start(bf16[4,256,1024]{2,1,0:T(8,128)(2,1)} %get-tuple-element.55), channel_id=1, source_target_pairs={{0,8},{4,12},{8,0},{12,4},{1,9},{5,13},{9,1},{13,5},{2,10},{6,14},... | collective-permute-start | bytes 6291464 | tf_op jit(solution)/shard_map/ppermute | solution.py:396
  664.3 89.5 %collective-permute-start.7 = (bf16[4,256,1024]{2,1,0:T(8,128)(2,1)}, bf16[4,256,1024]{2,1,0:T(8,128)(2,1)}, u32[]{:S(2)}, u32[]{:S(2)}) collective-permute-start(bf16[4,256,1024]{2,1,0:T(8,128)(2,1)} %get-tuple-element.53), channel_id=1, source_target_pairs={{0,4},{4,0},{8,12},{12,8},{1,5},{5,1},{9,13},{13,9},{2,6},{6,2},{1... | collective-permute-start | bytes 6291464 | tf_op jit(solution)/shard_map/ppermute | solution.py:396
  675.9 84.9 %copy-start.51 = (bf16[128,8,4,128]{3,1,2,0:T(8,128)(2,1)}, bf16[128,8,4,128]{3,1,2,0:T(8,128)(2,1)S(1)}, u32[]{:S(2)}) copy-start(bf16[128,8,4,128]{3,1,2,0:T(8,128)(2,1)S(1)} %copy.158) | copy-start | bytes 3145732
  760.8 11.4 copy-start.45
  777.2 270.2 %all-reduce.4.cloned.1.call-start = ((), (), s32[]{:S(2)}) async-start(), calls=%async_computation.12 | async-start | bytes 1048576 | tf_op jit(solution)/shard_map/psum | solution.py:157
  777.9 8.8 copy-start.47
  789.0 14.0 %collective-permute-start.18 = (bf16[256,384]{1,0:T(8,128)(2,1)}, bf16[256,384]{1,0:T(8,128)(2,1)S(1)}, u32[]{:S(2)}, u32[]{:S(2)}) collective-permute-start(bf16[256,384]{1,0:T(8,128)(2,1)} %get-tuple-element.72), channel_id=1, source_target_pairs={{0,3},{1,2},{2,1},{3,0},{4,7},{5,6},{6,5},{7,4},{8,11},{9,10},{10,... | collective-permute-start | bytes 589832 | tf_op jit(solution)/shard_map/ppermute | solution.py:115
  791.8 40.2 %collective-permute-start.17 = (bf16[256,384]{1,0:T(8,128)(2,1)}, bf16[256,384]{1,0:T(8,128)(2,1)S(1)}, u32[]{:S(2)}, u32[]{:S(2)}) collective-permute-start(bf16[256,384]{1,0:T(8,128)(2,1)} %get-tuple-element.72), channel_id=1, source_target_pairs={{0,2},{1,3},{2,0},{3,1},{4,6},{5,7},{6,4},{7,5},{8,10},{9,11},{10,... | collective-permute-start | bytes 589832 | tf_op jit(solution)/shard_map/ppermute | solution.py:115
  791.8 40.2 %collective-permute-start.16 = (bf16[256,384]{1,0:T(8,128)(2,1)}, bf16[256,384]{1,0:T(8,128)(2,1)}, u32[]{:S(2)}, u32[]{:S(2)}) collective-permute-start(bf16[256,384]{1,0:T(8,128)(2,1)} %get-tuple-element.72), channel_id=1, source_target_pairs={{0,1},{1,0},{2,3},{3,2},{4,5},{5,4},{6,7},{7,6},{8,9},{9,8},{10,11... | collective-permute-start | bytes 589832 | tf_op jit(solution)/shard_map/ppermute | solution.py:115
  794.5 319.0 %all-reduce.6.cloned.1.call-start = ((), (), s32[]{:S(2)}) async-start(), calls=%async_computation.13 | async-start | bytes 4456448 | tf_op jit(solution)/shard_map/psum | solution.py:157
  844.7 8.6 copy-start.55
  847.0 9.6 copy-start.38
  847.0 348.8 %all-gather.9.cloned.1.call-start = ((), (), s32[]{:S(2)}) async-start(), calls=%async_computation.8 | async-start | bytes 5242880 | tf_op jit(solution)/shard_map/all_gather | solution.py:179
  848.9 28.2 %collective-permute-start.12 = (f32[1024,128]{0,1:T(8,128)}, f32[1024,128]{0,1:T(8,128)}, u32[]{:S(2)}, u32[]{:S(2)}) collective-permute-start(f32[1024,128]{0,1:T(8,128)} %copy-done.45), channel_id=1, source_target_pairs={{0,3},{1,2},{2,1},{3,0},{4,7},{5,6},{6,5},{7,4},{8,11},{9,10},{10,... | collective-permute-start | bytes 1572872 | tf_op jit(solution)/shard_map/ppermute | solution.py:115
  849.0 69.9 %collective-permute-start.11 = (f32[1024,128]{0,1:T(8,128)}, f32[1024,128]{0,1:T(8,128)}, u32[]{:S(2)}, u32[]{:S(2)}) collective-permute-start(f32[1024,128]{0,1:T(8,128)} %copy-done.45), channel_id=1, source_target_pairs={{0,2},{1,3},{2,0},{3,1},{4,6},{5,7},{6,4},{7,5},{8,10},{9,11},{10,... | collective-permute-start | bytes 1572872 | tf_op jit(solution)/shard_map/ppermute | solution.py:115
  849.0 69.8 %collective-permute-start.10 = (f32[1024,128]{0,1:T(8,128)}, f32[1024,128]{0,1:T(8,128)}, u32[]{:S(2)}, u32[]{:S(2)}) collective-permute-start(f32[1024,128]{0,1:T(8,128)} %copy-done.45), channel_id=1, source_target_pairs={{0,1},{1,0},{2,3},{3,2},{4,5},{5,4},{6,7},{7,6},{8,9},{9,8},{10,11... | collective-permute-start | bytes 1572872 | tf_op jit(solution)/shard_map/ppermute | solution.py:115
  856.5 420.7 %all-gather.11.cloned.1.call-start = ((), (), s32[]{:S(2)}) async-start(), calls=%async_computation.11 | async-start | bytes 5242880 | tf_op jit(solution)/shard_map/all_gather | solution.py:179
  947.6 3.9 collective-permute-start.13
  951.7 42.3 %collective-permute-start.14 = (f32[458752]{0:T(1024)S(1)}, f32[458752]{0:T(1024)S(1)}, u32[]{:S(2)}, u32[]{:S(2)}) collective-permute-start(f32[458752]{0:T(1024)S(1)} %add.267), channel_id=1, source_target_pairs={{0,4},{4,0},{8,12},{12,8},{1,5},{5,1},{9,13},{13,9},{2,6},{6,2},{1... | collective-permute-start | bytes 5505032 | tf_op jit(solution)/shard_map/ppermute | solution.py:137
  994.2 201.6 %collective-permute-start.15 = (f32[458752]{0:T(1024)S(1)}, f32[458752]{0:T(1024)}, u32[]{:S(2)}, u32[]{:S(2)}) collective-permute-start(f32[458752]{0:T(1024)S(1)} %add.268), channel_id=1, source_target_pairs={{0,8},{4,12},{8,0},{12,4},{1,9},{5,13},{9,1},{13,5},{2,10},{6,14},... | collective-permute-start | bytes 5505032 | tf_op jit(solution)/shard_map/ppermute | solution.py:137
  1113.5 8.0 copy-start.66
  (63 other events, 261.4 us)
Sparse Core Ops, SparseCore 0:
  13.9 91.7 all-gather.4
  225.9 78.8 all-gather.6
  369.6 79.5 reduce-scatter.5
  451.3 81.5 reduce-scatter.3
  777.3 112.7 reduce-scatter.7
  895.2 152.1 all-reduce.3
  1051.2 62.2 all-reduce.5
  1115.7 80.1 all-gather.8
  1198.0 79.2 all-gather.10

commit v8 on v7

--- a/solution.py
+++ b/solution.py
@@ -409,11 +409,13 @@
     projection_second_gradient = matmul_tn(first_low, grad_projected)
     attn_back_part = matmul_nt(grad_projected, qkv_full)
     attn_back_low = matmul_nt(grad_projected, projection_second_flattened)
-    low_blocks = jnp.stack(partner_swaps(attn_back_low, "tp", tp_count))
-    low_owners = jnp.bitwise_xor(lax.axis_index("tp"), jnp.arange(tp_count, dtype=jnp.int32))
-    low_total = jnp.sum(jnp.take(low_blocks, low_owners, axis=0), axis=0)
-    select_late = lax.optimization_barrier(select)
-    qkv_back = (low_total * select_late).astype(jnp.bfloat16)
+
+    first_here, first_low_here = scatter_rows((attn_back_part, attn_back_low))
+    select_later = lax.optimization_barrier(select_here)
+    qkv_back_here = (first_low_here * select_later).astype(jnp.bfloat16)
+    grad_first = first_here + matmul_nt(qkv_back_here, projection_first_flattened)
+    input_here = (grad_middle_here + first_back_full(grad_first)[0]).astype(jnp.bfloat16)
+    qkv_back = partner_gather_rows(qkv_back_here, "tp")
     grad_qkv_in = matmul_tn(first_act, qkv_back)
     late_terms = butterfly_sum(
         (
@@ -422,11 +424,6 @@
         ),
         ("shard", "ctx"),
     )
-    first_here, first_low_here = scatter_rows((attn_back_part, attn_back_low))
-    select_later = lax.optimization_barrier(select_here)
-    qkv_back_here = (first_low_here * select_later).astype(jnp.bfloat16)
-    grad_first = first_here + matmul_nt(qkv_back_here, projection_first_flattened)
-    input_here = (grad_middle_here + first_back_full(grad_first)[0]).astype(jnp.bfloat16)
     (input_rows,) = gather_rows((input_here,))
     input_grad = input_rows.reshape(layer_input.shape)
     return (

time: 1300 us -> 1260 us (0.969)
  waiting for transfers between devices: 780 us -> 746 us
    ppermute x9, waiting for transfers between devices: 178 us -> 117 us  [partner_swaps(): received.append(lax.ppermute(block, axis_name, pairs))]
    reduce_scatter x3, waiting for transfers between devices: 142 us -> 161 us  [scatter_rows(): lax.psum_scatter(jnp.concatenate(partials, axis=1).astype(jnp.bfloat16),...]
    unnamed x173 -> x161, local copies, waits for them, and re-layouts: 33.7 us -> 33 us
  transfers between devices with their start and end apart: 29 -> 29, of which waited for: 20 -> 19; matrix products, arithmetic and copies ran while one was open for 17% -> 17% of each run, Pallas kernels for 0% -> 0%
where the time goes in v8:
time: 1260 us; the launch traced here: 1250 us
  waiting for transfers between devices  746 us (59%)
  matrix products  200 us (16%)
  local copies, waits for them, and re-layouts  123 us (10%)
  other arithmetic  104 us (8%)
  blocking collectives  30.1 us (2%)
  starting transfers between devices  28.6 us (2%)
  between operations  15.3 us (1%)
    all_gather x3, waiting for transfers between devices, gather_rows(): lax.all_gather(jnp.concatenate(rows_here, axis=1), 'tp', axis=0, tiled=True)  202 us
    reduce_scatter x3, waiting for transfers between devices, scatter_rows(): lax.psum_scatter(jnp.concatenate(partials, axis=1).astype(jnp.bfloat16),...  161 us
    psum x2, waiting for transfers between devices, narrow_psum(): lax.psum(jax.tree.map(lambda value: value.astype(jnp.bfloat16), values),...  124 us
    ppermute x9, waiting for transfers between devices, partner_swaps(): received.append(lax.ppermute(block, axis_name, pairs))  117 us
    ppermute x3, waiting for transfers between devices, layer_body(): lax.ppermute(grad_kv[:, offset].astype(jnp.bfloat16), 'ctx', pairs)  77.9 us
    dot_general x12, matrix products, matmul_nt(): lax.dot_general(left_mat, right_mat, (((1,), (1,)), ((), ())), preferred_...  64.7 us
    dot_general x12, matrix products, matmul(): return jnp.dot(left_mat, right_mat, preferred_element_type=jnp.float32)  63.6 us
    ppermute x3, waiting for transfers between devices, butterfly_sum(): packed = packed + lax.ppermute(packed, axis_name, pairs)  45 us
  transfers between devices with their start and end apart: 29, of which 19 were waited for; matrix products, arithmetic and copies ran while one was open for 17% of the time, Pallas kernels for 0%

profile of v8, /device:TPU:0, one launch (start us, length us, event | category | flops | bytes accessed | tf_op | source)
XLA Modules:
  0.0 1246.6 jit_solution(11734615777149870180)
XLA Ops:
  7.3 4.8 copy.86
  25.2 5.3 broadcast_select_fusion.7
  30.4 6.5 pad_maximum_fusion.5
  36.9 8.9 add_convert_fusion.1
  64.0 37.3 %collective-permute-done.3 = bf16[4,256,1024]{1,2,0:T(8,128)(2,1)} collective-permute-done((bf16[4,256,1024]{1,2,0:T(8,128)(2,1)}, bf16[4,256,1024]{1,2,0:T(8,128)(2,1)}, u32[]{:S(2)}, u32[]{:S(2)}) %collective-permute-start.3) | collective-permute-done | bytes 2097184 | tf_op jit(solution)/shard_map/ppermute | solution.py:115
  101.4 44.5 %collective-permute-done.2 = bf16[4,256,1024]{1,2,0:T(8,128)(2,1)} collective-permute-done((bf16[4,256,1024]{1,2,0:T(8,128)(2,1)}, bf16[4,256,1024]{1,2,0:T(8,128)(2,1)}, u32[]{:S(2)}, u32[]{:S(2)}) %collective-permute-start.2) | collective-permute-done | bytes 2097184 | tf_op jit(solution)/shard_map/ppermute | solution.py:115
  154.1 4.9 slice.121
  160.4 9.4 fusion.69
  169.7 10.5 fusion.70
  180.3 4.8 all-to-all-start
  185.1 6.7 convert.61
  191.7 19.2 %all-to-all-done = bf16[4,256,512]{1,2,0:T(8,128)(2,1)S(1)} async-done(((bf16[4,256,512]{1,2,0:T(8,128)(2,1)}), bf16[4,256,512]{1,2,0:T(8,128)(2,1)S(1)}, u32[]{:S(2)}, u32[]{:S(2)}) %all-to-all-start) | async-done | bytes 1048608 | tf_op jit(solution)/shard_map/all_to_all | solution.py:303
  217.1 6.8 fusion.71
  230.2 4.8 fusion.75
  242.9 61.8 %all-gather.7.cloned.1.call-done = bf16[1024,2048]{1,0:T(8,128)(2,1)} async-done(((bf16[256,2048]{1,0:T(8,128)(2,1)}), bf16[1024,2048]{1,0:T(8,128)(2,1)}) %all-gather.7.cloned.1.call-update) | async-done | bytes 4194320 | tf_op jit(solution)/shard_map/all_gather | solution.py:179
  312.9 16.8 %multiply_convert_fusion.1 = (bf16[1024,2048]{1,0:T(8,128)(2,1)}, f32[1024,2048]{1,0:T(8,128)}) fusion(f32[1024,2048]{1,0:T(8,128)} %fusion.74, bf16[1024,2048]{1,0:T(8,128)(2,1)S(1)} %copy-done.22, bf16[1024,2048]{1,0:T(8,128)(2,1)} %get-tuple-element.49, bf16[1024,2048]{1,0:T(8,128)(2,1)} %get-tuple-element.48), kind=kOutput, calls=%fused_computation.24 | convolution fusion | flops 8627683328 | bytes 33554432 | tf_op jit(solution)/shard_map/dot_general | solution.py:43
  329.8 21.3 %fusion.4 = bf16[1024,2048]{1,0:T(8,128)(2,1)} fusion(f32[1024,2048]{1,0:T(8,128)} %get-tuple-element.74, f32[1024,2048]{1,0:T(8,128)} %fusion.75, bf16[1024,2048]{1,0:T(8,128)(2,1)S(1)} %bitcast.192, bf16[2048,1024]{1,0:T(8,128)(2,1)} %get-tuple-element.47, bf16[2048,1024]{1,0:T(8,128)(2,1)} %get-tuple-element.46), kind=kOutput, calls=%fused_computation.15 | convolution fusion | flops 8659140608 | bytes 33554432 | tf_op jit(solution)/shard_map/dot_general | solution.py:53
  354.7 12.0 fusion.24
  374.1 11.7 fusion.25
  388.3 60.6 %reduce-scatter.6.cloned.1.call-done = bf16[256,2176]{1,0:T(8,128)(2,1)} async-done(((bf16[1024,2176]{1,0:T(8,128)(2,1)}), bf16[256,2176]{1,0:T(8,128)(2,1)}) %reduce-scatter.6.cloned.1.call-update) | async-done | bytes 1114128 | tf_op jit(solution)/shard_map/reduce_scatter | solution.py:168
  451.6 81.0 %reduce-scatter.4.cloned.1.call-done = bf16[256,2176]{1,0:T(8,128)(2,1)} async-done(((bf16[1024,2176]{1,0:T(8,128)(2,1)}), bf16[256,2176]{1,0:T(8,128)(2,1)}) %reduce-scatter.4.cloned.1.call-update) | async-done | bytes 1114128 | tf_op jit(solution)/shard_map/reduce_scatter | solution.py:168
  548.2 30.1 %all_to_all.29 = bf16[256,4,512]{0,2,1:T(8,128)(2,1)S(1)} all-to-all(bf16[256,4,512]{0,2,1:T(8,128)(2,1)} %bitcast.212), channel_id=1, replica_groups=mesh['shard'=2,'ctx'=4,'tp'=4] {'tp'}, dimensions={1} | all-to-all | bytes 2097152 | tf_op jit(solution)/shard_map/all_to_all | solution.py:369
  581.8 10.4 fusion.26
  592.2 9.2 multiply_convert_fusion
  604.7 4.9 multiply_bitcast_fusion
  609.7 10.5 reshape.461
  620.2 9.9 copy.103
  630.1 10.5 reshape.462
  640.6 9.9 copy.104
  650.5 6.6 fusion
  664.0 7.3 fusion.38
  675.0 35.2 %collective-permute-done.9 = bf16[4,256,1024]{2,1,0:T(8,128)(2,1)} collective-permute-done((bf16[4,256,1024]{2,1,0:T(8,128)(2,1)}, bf16[4,256,1024]{2,1,0:T(8,128)(2,1)}, u32[]{:S(2)}, u32[]{:S(2)}) %collective-permute-start.9) | collective-permute-done | bytes 2097184 | tf_op jit(solution)/shard_map/ppermute | solution.py:396
  710.2 42.6 %collective-permute-done.8 = bf16[4,256,1024]{2,1,0:T(8,128)(2,1)} collective-permute-done((bf16[4,256,1024]{2,1,0:T(8,128)(2,1)}, bf16[4,256,1024]{2,1,0:T(8,128)(2,1)}, u32[]{:S(2)}, u32[]{:S(2)}) %collective-permute-start.8) | collective-permute-done | bytes 2097184 | tf_op jit(solution)/shard_map/ppermute | solution.py:396
  752.9 4.8 fusion.18
  759.7 9.2 convolution_convert_fusion
  788.5 8.4 collective-permute-done.18
  796.8 26.3 %collective-permute-done.17 = bf16[256,384]{1,0:T(8,128)(2,1)S(1)} collective-permute-done((bf16[256,384]{1,0:T(8,128)(2,1)}, bf16[256,384]{1,0:T(8,128)(2,1)S(1)}, u32[]{:S(2)}, u32[]{:S(2)}) %collective-permute-start.17) | collective-permute-done | bytes 196640 | tf_op jit(solution)/shard_map/ppermute | solution.py:115
  845.2 19.2 %reduce-scatter.8.cloned.1.call-done = bf16[256,2176]{1,0:T(8,128)(2,1)} async-done(((bf16[1024,2176]{1,0:T(8,128)(2,1)}), bf16[256,2176]{1,0:T(8,128)(2,1)}) %reduce-scatter.8.cloned.1.call-update) | async-done | bytes 1114128 | tf_op jit(solution)/shard_map/reduce_scatter | solution.py:168
  884.6 4.9 copy.107
  889.5 5.6 reshape.466
  900.8 41.2 %collective-permute-done.14 = f32[458752]{0:T(1024)S(1)} collective-permute-done((f32[458752]{0:T(1024)S(1)}, f32[458752]{0:T(1024)S(1)}, u32[]{:S(2)}, u32[]{:S(2)}) %collective-permute-start.14) | collective-permute-done | bytes 1835040 | tf_op jit(solution)/shard_map/ppermute | solution.py:137
  943.6 58.9 %all-reduce.4.cloned.1.call-done = bf16[8,16,2048]{2,1,0:T(8,128)(2,1)} async-done(((bf16[8,16,2048]{2,1,0:T(8,128)(2,1)}), bf16[8,16,2048]{2,1,0:T(8,128)(2,1)}) %all-reduce.4.cloned.1.call-update) | async-done | bytes 524304 | tf_op jit(solution)/shard_map/psum | solution.py:157
  1004.7 64.6 %all-reduce.6.cloned.1.call-done = (bf16[8,512,16]{1,2,0:T(8,128)(2,1)}, bf16[8,2048,16]{1,2,0:T(8,128)(2,1)}, bf16[8,16,2048]{2,1,0:T(8,128)(2,1)}, bf16[8,2048,16]{1,2,0:T(8,128)(2,1)}, bf16[8,16,2048]{2,1,0:T(8,128)(2,1)}) async-done(((bf16[8,512,16]{1,2,0:T(8,128)(2,1)}, bf16[8,2048,16]{1,2,0:T(8,128)(2,1)}, bf16[8,16,2048]{2,1,0:T(8,128)(2,1)}, bf16[8,2048,16]{1,2,0:T(8,128)(2,1)}, ...) | async-done | bytes 2228240 | tf_op jit(solution)/shard_map/psum | solution.py:157
  1078.4 73.2 %all-gather.9.cloned.1.call-done = bf16[1024,2048]{1,0:T(8,128)(2,1)} async-done(((bf16[256,2048]{1,0:T(8,128)(2,1)}), bf16[1024,2048]{1,0:T(8,128)(2,1)}) %all-gather.9.cloned.1.call-update) | async-done | bytes 4194320 | tf_op jit(solution)/shard_map/all_gather | solution.py:179
  1153.4 4.7 slice.107
  1158.0 6.5 copy.111
  1166.0 67.0 %all-gather.11.cloned.1.call-done = bf16[1024,2048]{1,0:T(8,128)(2,1)} async-done(((bf16[256,2048]{1,0:T(8,128)(2,1)}), bf16[1024,2048]{1,0:T(8,128)(2,1)}) %all-gather.11.cloned.1.call-update) | async-done | bytes 4194320 | tf_op jit(solution)/shard_map/all_gather | solution.py:179
  1233.0 4.9 copy.135
  (328 shorter events, 205.4 us)
Async XLA Ops:
  7.2 301.2 %copy-start = (bf16[8,16,2048]{2,1,0:T(8,128)(2,1)S(1)}, bf16[8,16,2048]{2,1,0:T(8,128)(2,1)}, u32[]{:S(2)}) copy-start(bf16[8,16,2048]{2,1,0:T(8,128)(2,1)} %param.37) | copy-start | bytes 1572868
  7.2 146.9 %all-gather.5.cloned.1.call-start = ((), (), s32[]{:S(2)}) async-start(), calls=%async_computation.5 | async-start | bytes 5898240 | tf_op jit(solution)/shard_map/all_gather | solution.py:234
  12.0 11.5 collective-permute-start
  14.3 8.3 copy-start.46
  21.2 15.7 %copy-start.11 = (bf16[4,256,2048]{2,1,0:T(8,128)(2,1)}, bf16[4,256,2048]{2,1,0:T(8,128)(2,1)S(1)}, u32[]{:S(2)}) copy-start(bf16[4,256,2048]{2,1,0:T(8,128)(2,1)S(1)} %add_convert_fusion) | copy-start | bytes 12582916
  49.4 9.0 copy-start.19
  51.0 50.3 %collective-permute-start.3 = (bf16[4,256,1024]{1,2,0:T(8,128)(2,1)}, bf16[4,256,1024]{1,2,0:T(8,128)(2,1)}, u32[]{:S(2)}, u32[]{:S(2)}) collective-permute-start(bf16[4,256,1024]{1,2,0:T(8,128)(2,1)} %pad_maximum_fusion.32), channel_id=1, source_target_pairs={{0,12},{4,8},{8,4},{12,0},{1,13},{5,9},{9,5},{13,1},{2,14},{6,10},... | collective-permute-start | bytes 6291464 | tf_op jit(solution)/shard_map/ppermute | solution.py:115
  54.5 91.3 %collective-permute-start.2 = (bf16[4,256,1024]{1,2,0:T(8,128)(2,1)}, bf16[4,256,1024]{1,2,0:T(8,128)(2,1)}, u32[]{:S(2)}, u32[]{:S(2)}) collective-permute-start(bf16[4,256,1024]{1,2,0:T(8,128)(2,1)} %pad_maximum_fusion.32), channel_id=1, source_target_pairs={{0,8},{4,12},{8,0},{12,4},{1,9},{5,13},{9,1},{13,5},{2,10},{6,14},... | collective-permute-start | bytes 6291464 | tf_op jit(solution)/shard_map/ppermute | solution.py:115
  55.1 91.1 %collective-permute-start.1 = (bf16[4,256,1024]{1,2,0:T(8,128)(2,1)}, bf16[4,256,1024]{1,2,0:T(8,128)(2,1)}, u32[]{:S(2)}, u32[]{:S(2)}) collective-permute-start(bf16[4,256,1024]{1,2,0:T(8,128)(2,1)} %pad_maximum_fusion.32), channel_id=1, source_target_pairs={{0,4},{4,0},{8,12},{12,8},{1,5},{5,1},{9,13},{13,9},{2,6},{6,2},{1... | collective-permute-start | bytes 6291464 | tf_op jit(solution)/shard_map/ppermute | solution.py:115
  64.0 95.0 %copy-start.15 = (bf16[4,256,4,128]{1,3,2,0:T(8,128)(2,1)}, bf16[4,256,4,128]{1,3,2,0:T(8,128)(2,1)S(1)}, u32[]{:S(2)}) copy-start(bf16[4,256,4,128]{1,3,2,0:T(8,128)(2,1)S(1)} %copy.102) | copy-start | bytes 3145732
  150.3 8.8 copy-start.31
  159.1 54.2 %collective-permute-start.4 = (bf16[2048,1024]{1,0:T(8,128)(2,1)}, bf16[2048,1024]{1,0:T(8,128)(2,1)}, u32[]{:S(2)}, u32[]{:S(2)}) collective-permute-start(bf16[2048,1024]{1,0:T(8,128)(2,1)} %slice.121), channel_id=1, source_target_pairs={{0,16},{16,0},{1,17},{17,1},{2,18},{18,2},{3,19},{19,3},{4,20},{20... | collective-permute-start | bytes 12582920 | tf_op jit(solution)/shard_map/ppermute | solution.py:122
  160.4 9.4 copy-start.5
  169.7 10.5 copy-start.56
  180.3 30.6 %all-to-all-start = ((bf16[4,256,512]{1,2,0:T(8,128)(2,1)}), bf16[4,256,512]{1,2,0:T(8,128)(2,1)S(1)}, u32[]{:S(2)}, u32[]{:S(2)}) async-start(bf16[4,256,512]{1,2,0:T(8,128)(2,1)} %bitcast.12), calls=%async_computation | async-start | bytes 2097152 | tf_op jit(solution)/shard_map/all_to_all | solution.py:303
  185.1 119.7 %all-gather.7.cloned.1.call-start = ((), (), s32[]{:S(2)}) async-start(), calls=%async_computation.6 | async-start | bytes 5242880 | tf_op jit(solution)/shard_map/all_gather | solution.py:179
  185.1 27.8 %copy-start.42 = (bf16[8,16,2048]{2,1,0:T(8,128)(2,1)S(1)}, bf16[8,16,2048]{2,1,0:T(8,128)(2,1)}, u32[]{:S(2)}) copy-start(bf16[8,16,2048]{2,1,0:T(8,128)(2,1)} %param.35) | copy-start | bytes 1572868
  225.7 223.2 %reduce-scatter.6.cloned.1.call-start = ((), (), s32[]{:S(2)}) async-start(), calls=%async_computation.9 | async-start | bytes 5570560 | tf_op jit(solution)/shard_map/reduce_scatter | solution.py:168
  226.0 9.0 collective-permute-start.5
  226.1 13.4 %collective-permute-start.6 = (bf16[2048,1024]{1,0:T(8,128)(2,1)}, bf16[2048,1024]{1,0:T(8,128)(2,1)S(1)}, u32[]{:S(2)}, u32[]{:S(2)}) collective-permute-start(bf16[2048,1024]{1,0:T(8,128)(2,1)} %param.31), channel_id=1, source_target_pairs={{0,16},{16,0},{1,17},{17,1},{2,18},{18,2},{3,19},{19,3},{4,20},{20... | collective-permute-start | bytes 12582920 | tf_op jit(solution)/shard_map/ppermute | solution.py:122
  312.9 16.8 %copy-start.6 = (bf16[4,256,2048]{2,1,0:T(8,128)(2,1)S(1)}, bf16[4,256,2048]{2,1,0:T(8,128)(2,1)}, u32[]{:S(2)}) copy-start(bf16[4,256,2048]{2,1,0:T(8,128)(2,1)} %param.21) | copy-start | bytes 12582916
  369.2 163.4 %reduce-scatter.4.cloned.1.call-start = ((), (), s32[]{:S(2)}) async-start(), calls=%async_computation.7 | async-start | bytes 5570560 | tf_op jit(solution)/shard_map/reduce_scatter | solution.py:168
  388.2 147.1 %copy-start.38 = (bf16[8,2048,16]{1,2,0:T(8,128)(2,1)S(1)}, bf16[8,2048,16]{1,2,0:T(8,128)(2,1)}, u32[]{:S(2)}) copy-start(bf16[8,2048,16]{1,2,0:T(8,128)(2,1)} %param.36) | copy-start | bytes 1572868
  388.2 476.1 %reduce-scatter.8.cloned.1.call-start = ((), (), s32[]{:S(2)}) async-start(), calls=%async_computation.10 | async-start | bytes 5570560 | tf_op jit(solution)/shard_map/reduce_scatter | solution.py:168
  535.3 246.8 %copy-start.52 = (bf16[256,128]{1,0:T(8,128)(2,1)}, bf16[256,128]{1,0:T(8,128)(2,1)S(1)}, u32[]{:S(2)}) copy-start(bf16[256,128]{1,0:T(8,128)(2,1)S(1)} %get-tuple-element.64) | copy-start | bytes 196612
  546.0 34.3 %copy-start.57 = (f32[4,4,256]{2,1,0:T(4,128)S(1)}, f32[4,4,256]{2,1,0:T(4,128)}, u32[]{:S(2)}) copy-start(f32[4,4,256]{2,1,0:T(4,128)} %copy-done.56) | copy-start | bytes 49156
  592.2 12.5 %copy-start.16 = (bf16[4,256,4,128]{1,3,2,0:T(8,128)(2,1)S(1)}, bf16[4,256,4,128]{1,3,2,0:T(8,128)(2,1)}, u32[]{:S(2)}) copy-start(bf16[4,256,4,128]{1,3,2,0:T(8,128)(2,1)} %copy-done.15) | copy-start | bytes 3145732
  660.5 49.8 %collective-permute-start.9 = (bf16[4,256,1024]{2,1,0:T(8,128)(2,1)}, bf16[4,256,1024]{2,1,0:T(8,128)(2,1)}, u32[]{:S(2)}, u32[]{:S(2)}) collective-permute-start(bf16[4,256,1024]{2,1,0:T(8,128)(2,1)} %get-tuple-element.44), channel_id=1, source_target_pairs={{0,12},{4,8},{8,4},{12,0},{1,13},{5,9},{9,5},{13,1},{2,14},{6,10},... | collective-permute-start | bytes 6291464 | tf_op jit(solution)/shard_map/ppermute | solution.py:396
  662.9 90.0 %collective-permute-start.8 = (bf16[4,256,1024]{2,1,0:T(8,128)(2,1)}, bf16[4,256,1024]{2,1,0:T(8,128)(2,1)}, u32[]{:S(2)}, u32[]{:S(2)}) collective-permute-start(bf16[4,256,1024]{2,1,0:T(8,128)(2,1)} %get-tuple-element.45), channel_id=1, source_target_pairs={{0,8},{4,12},{8,0},{12,4},{1,9},{5,13},{9,1},{13,5},{2,10},{6,14},... | collective-permute-start | bytes 6291464 | tf_op jit(solution)/shard_map/ppermute | solution.py:396
  663.4 89.5 %collective-permute-start.7 = (bf16[4,256,1024]{2,1,0:T(8,128)(2,1)}, bf16[4,256,1024]{2,1,0:T(8,128)(2,1)}, u32[]{:S(2)}, u32[]{:S(2)}) collective-permute-start(bf16[4,256,1024]{2,1,0:T(8,128)(2,1)} %get-tuple-element.43), channel_id=1, source_target_pairs={{0,4},{4,0},{8,12},{12,8},{1,5},{5,1},{9,13},{13,9},{2,6},{6,2},{1... | collective-permute-start | bytes 6291464 | tf_op jit(solution)/shard_map/ppermute | solution.py:396
  675.0 84.6 %copy-start.49 = (bf16[128,8,4,128]{3,1,2,0:T(8,128)(2,1)}, bf16[128,8,4,128]{3,1,2,0:T(8,128)(2,1)S(1)}, u32[]{:S(2)}) copy-start(bf16[128,8,4,128]{3,1,2,0:T(8,128)(2,1)S(1)} %copy.125) | copy-start | bytes 3145732
  771.4 231.2 %all-reduce.4.cloned.1.call-start = ((), (), s32[]{:S(2)}) async-start(), calls=%async_computation.12 | async-start | bytes 1048576 | tf_op jit(solution)/shard_map/psum | solution.py:157
  771.6 9.0 copy-start.45
  782.9 14.0 %collective-permute-start.18 = (bf16[256,384]{1,0:T(8,128)(2,1)}, bf16[256,384]{1,0:T(8,128)(2,1)S(1)}, u32[]{:S(2)}, u32[]{:S(2)}) collective-permute-start(bf16[256,384]{1,0:T(8,128)(2,1)} %get-tuple-element.62), channel_id=1, source_target_pairs={{0,3},{1,2},{2,1},{3,0},{4,7},{5,6},{6,5},{7,4},{8,11},{9,10},{10,... | collective-permute-start | bytes 589832 | tf_op jit(solution)/shard_map/ppermute | solution.py:115
  785.1 38.1 %collective-permute-start.17 = (bf16[256,384]{1,0:T(8,128)(2,1)}, bf16[256,384]{1,0:T(8,128)(2,1)S(1)}, u32[]{:S(2)}, u32[]{:S(2)}) collective-permute-start(bf16[256,384]{1,0:T(8,128)(2,1)} %get-tuple-element.62), channel_id=1, source_target_pairs={{0,2},{1,3},{2,0},{3,1},{4,6},{5,7},{6,4},{7,5},{8,10},{9,11},{10,... | collective-permute-start | bytes 589832 | tf_op jit(solution)/shard_map/ppermute | solution.py:115
  785.1 38.1 %collective-permute-start.16 = (bf16[256,384]{1,0:T(8,128)(2,1)}, bf16[256,384]{1,0:T(8,128)(2,1)S(1)}, u32[]{:S(2)}, u32[]{:S(2)}) collective-permute-start(bf16[256,384]{1,0:T(8,128)(2,1)} %get-tuple-element.62), channel_id=1, source_target_pairs={{0,1},{1,0},{2,3},{3,2},{4,5},{5,4},{6,7},{7,6},{8,9},{9,8},{10,11... | collective-permute-start | bytes 589832 | tf_op jit(solution)/shard_map/ppermute | solution.py:115
  788.4 280.8 %all-reduce.6.cloned.1.call-start = ((), (), s32[]{:S(2)}) async-start(), calls=%async_computation.13 | async-start | bytes 4456448 | tf_op jit(solution)/shard_map/psum | solution.py:157
  837.6 313.9 %all-gather.9.cloned.1.call-start = ((), (), s32[]{:S(2)}) async-start(), calls=%async_computation.8 | async-start | bytes 5242880 | tf_op jit(solution)/shard_map/all_gather | solution.py:179
  840.8 392.2 %all-gather.11.cloned.1.call-start = ((), (), s32[]{:S(2)}) async-start(), calls=%async_computation.11 | async-start | bytes 5242880 | tf_op jit(solution)/shard_map/all_gather | solution.py:179
  845.1 27.9 %copy-start.41 = (bf16[8,2048,16]{1,2,0:T(8,128)(2,1)S(1)}, bf16[8,2048,16]{1,2,0:T(8,128)(2,1)}, u32[]{:S(2)}) copy-start(bf16[8,2048,16]{1,2,0:T(8,128)(2,1)} %param.32) | copy-start | bytes 1572868
  845.1 27.9 %copy-start.67 = (f32[2048]{0:T(1024)S(1)}, f32[2048]{0:T(1024)}, u32[]{:S(2)}) copy-start(f32[2048]{0:T(1024)} %param.24) | copy-start | bytes 24580
  865.7 14.9 %collective-permute-start.12 = (bf16[256,128]{1,0:T(8,128)(2,1)S(1)}, bf16[256,128]{1,0:T(8,128)(2,1)S(1)}, u32[]{:S(2)}, u32[]{:S(2)}) collective-permute-start(bf16[256,128]{1,0:T(8,128)(2,1)S(1)} %fusion.50), channel_id=1, source_target_pairs={{0,3},{1,2},{2,1},{3,0},{4,7},{5,6},{6,5},{7,4},{8,11},{9,10},{10,... | collective-permute-start | bytes 196616 | tf_op jit(solution)/shard_map/ppermute | solution.py:115
  868.4 12.2 collective-permute-start.11
  873.0 7.7 collective-permute-start.10
  895.2 3.9 collective-permute-start.13
  899.3 42.6 %collective-permute-start.14 = (f32[458752]{0:T(1024)S(1)}, f32[458752]{0:T(1024)S(1)}, u32[]{:S(2)}, u32[]{:S(2)}) collective-permute-start(f32[458752]{0:T(1024)S(1)} %add.267), channel_id=1, source_target_pairs={{0,4},{4,0},{8,12},{12,8},{1,5},{5,1},{9,13},{13,9},{2,6},{6,2},{1... | collective-permute-start | bytes 5505032 | tf_op jit(solution)/shard_map/ppermute | solution.py:137
  942.1 209.4 %collective-permute-start.15 = (f32[458752]{0:T(1024)S(1)}, f32[458752]{0:T(1024)}, u32[]{:S(2)}, u32[]{:S(2)}) collective-permute-start(f32[458752]{0:T(1024)S(1)} %add.268), channel_id=1, source_target_pairs={{0,8},{4,12},{8,0},{12,4},{1,9},{5,13},{9,1},{13,5},{2,10},{6,14},... | collective-permute-start | bytes 5505032 | tf_op jit(solution)/shard_map/ppermute | solution.py:137
  1069.2 8.0 copy-start.60
  (57 other events, 234.4 us)
Sparse Core Ops, SparseCore 0:
  13.9 91.7 all-gather.4
  225.8 78.8 all-gather.6
  369.3 79.4 reduce-scatter.5
  451.0 81.5 reduce-scatter.3
  771.5 92.7 reduce-scatter.7
  870.0 132.4 all-reduce.3
  1007.0 62.2 all-reduce.5
  1071.4 80.1 all-gather.8
  1153.7 79.2 all-gather.10

commit v9 on v7

--- a/solution.py
+++ b/solution.py
@@ -134,7 +134,10 @@
         step = 1
         while step < axis_count:
             pairs = [(index, index ^ step) for index in range(axis_count)]
-            packed = packed + lax.ppermute(packed, axis_name, pairs)
+            narrow = packed.astype(jnp.bfloat16)
+            packed = narrow.astype(jnp.float32) + lax.ppermute(narrow, axis_name, pairs).astype(
+                jnp.float32
+            )
             step *= 2
     parts, offset = [], 0
     for leaf in leaves:
@@ -317,13 +320,7 @@
     activated = activated.astype(jnp.bfloat16)
     down_part = matmul(activated, down_full)
     down_low_part = matmul(activated, down_first_flattened)
-    ffn_here, ffn_low_here = scatter_rows((down_part, down_low_part))
-    down_low_here = (ffn_low_here * select_here).astype(jnp.bfloat16)
-    result_here = (middle_here + ffn_here + matmul(down_low_here, down_second_flattened)).astype(
-        jnp.bfloat16
-    )
-    (result_rows,) = gather_rows((result_here,))
-    layer_out = result_rows.reshape(layer_input.shape)
+    (ffn_here,) = scatter_rows((down_part,))
     grad_top_low = output_gradient.reshape(tok_rows, model_width)
     grad_top_here = tp_rows(grad_top_low, tp_count).astype(jnp.float32)
     down_back = (matmul_nt(grad_top_low, down_second_flattened) * select).astype(jnp.bfloat16)
@@ -333,8 +330,16 @@
     up_second_gradient = matmul_tn(up_low, grad_hidden)
     ffn_back_part = matmul_nt(grad_hidden, up_full)
     ffn_back_low = matmul_nt(grad_hidden, up_second_flattened)
-    back_here, back_low_here = scatter_rows((ffn_back_part, ffn_back_low))
+    back_here, back_low_here, ffn_low_here = scatter_rows(
+        (ffn_back_part, ffn_back_low, down_low_part)
+    )
     up_back_here = (back_low_here * select_here).astype(jnp.bfloat16)
+    down_low_here = (ffn_low_here * select_here).astype(jnp.bfloat16)
+    result_here = (middle_here + ffn_here + matmul(down_low_here, down_second_flattened)).astype(
+        jnp.bfloat16
+    )
+    (result_rows,) = gather_rows((result_here,))
+    layer_out = result_rows.reshape(layer_input.shape)
     grad_second = back_here + matmul_nt(up_back_here, up_first_flattened)
     grad_middle_here = grad_top_here + second_back(grad_second)[0]
     grad_middle_low_here = grad_middle_here.astype(jnp.bfloat16)

time: 1300 us -> 1100 us (0.85)
  waiting for transfers between devices: 780 us -> 609 us
  blocking collectives: 30.1 us -> 0 us
    psum x2, waiting for transfers between devices: 116 us -> 37.4 us  [narrow_psum(): lax.psum(jax.tree.map(lambda value: value.astype(jnp.bfloat16), values),...]
    ppermute x9, waiting for transfers between devices: 178 us -> 114 us  [partner_swaps(): received.append(lax.ppermute(block, axis_name, pairs))]
    ppermute x3, waiting for transfers between devices: 44.5 us -> 3.26 us  [butterfly_sum(): lax.ppermute(narrow, axis_name, pairs).astype(jnp.float32)]
    all_to_all x0 -> x1, waiting for transfers between devices: none -> 41.1 us  [layer_body(): grad_heads = lax.all_to_all(grad_heads_here, 'tp', 1, 0, tiled=True)]
    all_to_all x1 -> x0, blocking collectives: 30.1 us -> none  [layer_body(): grad_heads = lax.all_to_all(grad_heads_here, 'tp', 1, 0, tiled=True)]
    all_gather x3, waiting for transfers between devices: 202 us -> 179 us  [gather_rows(): lax.all_gather(jnp.concatenate(rows_here, axis=1), 'tp', axis=0, tiled=True)]
    ppermute x3, waiting for transfers between devices: 77.9 us -> 63.8 us  [layer_body(): lax.ppermute(grad_kv[:, offset].astype(jnp.bfloat16), 'ctx', pairs)]
    unnamed x173 -> x171, local copies, waits for them, and re-layouts: 33.7 us -> 34.6 us
  transfers between devices with their start and end apart: 29 -> 30, of which waited for: 20 -> 16; matrix products, arithmetic and copies ran while one was open for 17% -> 31% of each run, Pallas kernels for 0% -> 0%
where the time goes in v9:
time: 1100 us; the launch traced here: 1090 us
  waiting for transfers between devices  609 us (55%)
  matrix products  202 us (18%)
  local copies, waits for them, and re-layouts  130 us (12%)
  other arithmetic  109 us (10%)
  starting transfers between devices  28.8 us (3%)
  between operations  15.3 us (1%)
    all_gather x3, waiting for transfers between devices, gather_rows(): lax.all_gather(jnp.concatenate(rows_here, axis=1), 'tp', axis=0, tiled=True)  179 us
    reduce_scatter x3, waiting for transfers between devices, scatter_rows(): lax.psum_scatter(jnp.concatenate(partials, axis=1).astype(jnp.bfloat16),...  151 us
    ppermute x9, waiting for transfers between devices, partner_swaps(): received.append(lax.ppermute(block, axis_name, pairs))  114 us
    dot_general x12, matrix products, matmul_nt(): lax.dot_general(left_mat, right_mat, (((1,), (1,)), ((), ())), preferred_...  66.4 us
    ppermute x3, waiting for transfers between devices, layer_body(): lax.ppermute(grad_kv[:, offset].astype(jnp.bfloat16), 'ctx', pairs)  63.8 us
    dot_general x12, matrix products, matmul(): return jnp.dot(left_mat, right_mat, preferred_element_type=jnp.float32)  63.4 us
    all_to_all x1, waiting for transfers between devices, layer_body(): grad_heads = lax.all_to_all(grad_heads_here, 'tp', 1, 0, tiled=True)  41.1 us
    psum x2, waiting for transfers between devices, narrow_psum(): lax.psum(jax.tree.map(lambda value: value.astype(jnp.bfloat16), values),...  37.4 us
  transfers between devices with their start and end apart: 30, of which 16 were waited for; matrix products, arithmetic and copies ran while one was open for 31% of the time, Pallas kernels for 0%

profile of v9, /device:TPU:0, one launch (start us, length us, event | category | flops | bytes accessed | tf_op | source)
XLA Modules:
  0.0 1093.6 jit_solution(12329942876236905962)
XLA Ops:
  7.3 4.8 copy.119
  25.2 5.3 broadcast_select_fusion.7
  30.4 6.5 pad_maximum_fusion.5
  36.9 8.9 add_convert_fusion.1
  64.0 36.3 %collective-permute-done.1 = bf16[4,256,1024]{1,2,0:T(8,128)(2,1)} collective-permute-done((bf16[4,256,1024]{1,2,0:T(8,128)(2,1)}, bf16[4,256,1024]{1,2,0:T(8,128)(2,1)}, u32[]{:S(2)}, u32[]{:S(2)}) %collective-permute-start.1) | collective-permute-done | bytes 2097184 | tf_op jit(solution)/shard_map/ppermute | solution.py:115
  100.3 46.0 %collective-permute-done.2 = bf16[4,256,1024]{1,2,0:T(8,128)(2,1)} collective-permute-done((bf16[4,256,1024]{1,2,0:T(8,128)(2,1)}, bf16[4,256,1024]{1,2,0:T(8,128)(2,1)}, u32[]{:S(2)}, u32[]{:S(2)}) %collective-permute-start.2) | collective-permute-done | bytes 2097184 | tf_op jit(solution)/shard_map/ppermute | solution.py:115
  154.3 4.9 slice.117
  160.6 9.4 fusion.72
  170.0 10.5 fusion.73
  180.5 4.8 all-to-all-start
  185.3 6.6 convert.70
  191.9 18.5 %all-to-all-done = bf16[4,256,512]{1,2,0:T(8,128)(2,1)S(1)} async-done(((bf16[4,256,512]{1,2,0:T(8,128)(2,1)}), bf16[4,256,512]{1,2,0:T(8,128)(2,1)S(1)}, u32[]{:S(2)}, u32[]{:S(2)}) %all-to-all-start) | async-done | bytes 1048608 | tf_op jit(solution)/shard_map/all_to_all | solution.py:306
  216.7 6.8 fusion.74
  229.7 4.8 fusion.78
  242.5 61.8 %all-gather.7.cloned.1.call-done = bf16[1024,2048]{1,0:T(8,128)(2,1)} async-done(((bf16[256,2048]{1,0:T(8,128)(2,1)}), bf16[1024,2048]{1,0:T(8,128)(2,1)}) %all-gather.7.cloned.1.call-update) | async-done | bytes 4194320 | tf_op jit(solution)/shard_map/all_gather | solution.py:182
  307.9 4.5 fusion.77
  312.4 16.9 %multiply_convert_fusion.1 = (bf16[1024,2048]{1,0:T(8,128)(2,1)}, f32[1024,2048]{1,0:T(8,128)}) fusion(f32[1024,2048]{1,0:T(8,128)} %fusion.77, bf16[1024,2048]{1,0:T(8,128)(2,1)S(1)} %copy-done.19, bf16[1024,2048]{1,0:T(8,128)(2,1)} %get-tuple-element.59, bf16[1024,2048]{1,0:T(8,128)(2,1)} %get-tuple-element.58), kind=kOutput, calls=%fused_computation.24 | convolution fusion | flops 8627683328 | bytes 33554432 | tf_op jit(solution)/shard_map/dot_general | solution.py:43
  329.3 21.2 %fusion.4 = bf16[1024,2048]{1,0:T(8,128)(2,1)} fusion(f32[1024,2048]{1,0:T(8,128)} %get-tuple-element.84, f32[1024,2048]{1,0:T(8,128)} %fusion.78, bf16[1024,2048]{1,0:T(8,128)(2,1)S(1)} %bitcast.191, bf16[2048,1024]{1,0:T(8,128)(2,1)} %get-tuple-element.57, bf16[2048,1024]{1,0:T(8,128)(2,1)} %get-tuple-element.56), kind=kOutput, calls=%fused_computation.15 | convolution fusion | flops 8659140608 | bytes 33554432 | tf_op jit(solution)/shard_map/dot_general | solution.py:53
  350.6 13.4 %fusion.24 = bf16[1024,2048]{1,0:T(8,128)(2,1)S(1)} fusion(bf16[1024,2048]{1,0:T(8,128)(2,1)} %fusion.4, bf16[1024,2048]{1,0:T(8,128)(2,1)} %get-tuple-element.59, bf16[1024,2048]{1,0:T(8,128)(2,1)} %get-tuple-element.58), kind=kOutput, calls=%fused_computation.57 | convolution fusion | flops 8608808960 | bytes 16777216 | tf_op jit(solution)/shard_map/dot_general | solution.py:53
  370.2 14.4 %fusion.25 = bf16[1024,2048]{1,0:T(8,128)(2,1)} fusion(bf16[1024,2048]{1,0:T(8,128)(2,1)} %get-tuple-element.83, bf16[2048,1024]{1,0:T(8,128)(2,1)} %get-tuple-element.57, bf16[2048,1024]{1,0:T(8,128)(2,1)} %get-tuple-element.56), kind=kOutput, calls=%fused_computation.58 | convolution fusion | flops 8608808960 | bytes 16777216 | tf_op jit(solution)/shard_map/dot_general | solution.py:43
  384.6 69.5 %reduce-scatter.6.cloned.1.call-done = bf16[256,2304]{1,0:T(8,128)(2,1)} async-done(((bf16[1024,2304]{1,0:T(8,128)(2,1)}), bf16[256,2304]{1,0:T(8,128)(2,1)}) %reduce-scatter.6.cloned.1.call-update) | async-done | bytes 1179664 | tf_op jit(solution)/shard_map/reduce_scatter | solution.py:171
  469.2 4.3 all-to-all-start.1
  490.2 41.1 %all-to-all-done.1 = bf16[256,4,512]{0,2,1:T(8,128)(2,1)} async-done(((bf16[256,4,512]{0,2,1:T(8,128)(2,1)}), bf16[256,4,512]{0,2,1:T(8,128)(2,1)}, u32[]{:S(2)}, u32[]{:S(2)}) %all-to-all-start.1) | async-done | bytes 1048608 | tf_op jit(solution)/shard_map/all_to_all | solution.py:374
  534.0 10.5 fusion.26
  544.5 10.7 reshape.460
  555.2 9.9 copy.137
  567.3 9.2 multiply_convert_fusion
  579.8 4.9 multiply_bitcast_fusion
  584.8 10.5 reshape.459
  595.3 9.9 copy.136
  605.2 6.6 fusion
  631.9 7.3 fusion.39
  642.9 20.7 %collective-permute-done.7 = bf16[4,256,1024]{2,1,0:T(8,128)(2,1)} collective-permute-done((bf16[4,256,1024]{2,1,0:T(8,128)(2,1)}, bf16[4,256,1024]{2,1,0:T(8,128)(2,1)}, u32[]{:S(2)}, u32[]{:S(2)}) %collective-permute-start.7) | collective-permute-done | bytes 2097184 | tf_op jit(solution)/shard_map/ppermute | solution.py:401
  663.6 43.1 %collective-permute-done.8 = bf16[4,256,1024]{2,1,0:T(8,128)(2,1)} collective-permute-done((bf16[4,256,1024]{2,1,0:T(8,128)(2,1)}, bf16[4,256,1024]{2,1,0:T(8,128)(2,1)}, u32[]{:S(2)}, u32[]{:S(2)}) %collective-permute-start.8) | collective-permute-done | bytes 2097184 | tf_op jit(solution)/shard_map/ppermute | solution.py:401
  706.8 5.2 fusion.18
  715.0 4.3 collective-permute-start.12
  724.0 11.8 %collective-permute-done.10 = f32[1024,128]{0,1:T(8,128)} collective-permute-done((f32[1024,128]{0,1:T(8,128)}, f32[1024,128]{0,1:T(8,128)}, u32[]{:S(2)}, u32[]{:S(2)}) %collective-permute-start.10) | collective-permute-done | bytes 524320 | tf_op jit(solution)/shard_map/ppermute | solution.py:115
  735.8 20.1 %collective-permute-done.11 = f32[1024,128]{0,1:T(8,128)} collective-permute-done((f32[1024,128]{0,1:T(8,128)}, f32[1024,128]{0,1:T(8,128)}, u32[]{:S(2)}, u32[]{:S(2)}) %collective-permute-start.11) | collective-permute-done | bytes 524320 | tf_op jit(solution)/shard_map/ppermute | solution.py:115
  773.1 5.9 reshape.464
  787.9 37.4 %all-reduce.6.cloned.1.call-done = (bf16[8,512,16]{1,2,0:T(8,128)(2,1)}, bf16[8,2048,16]{1,2,0:T(8,128)(2,1)}, bf16[8,16,2048]{2,1,0:T(8,128)(2,1)}, bf16[8,2048,16]{1,2,0:T(8,128)(2,1)}, bf16[8,16,2048]{2,1,0:T(8,128)(2,1)}) async-done(((bf16[8,512,16]{1,2,0:T(8,128)(2,1)}, bf16[8,2048,16]{1,2,0:T(8,128)(2,1)}, bf16[8,16,2048]{2,1,0:T(8,128)(2,1)}, bf16[8,2048,16]{1,2,0:T(8,128)(2,1)}, ...) | async-done | bytes 2228240 | tf_op jit(solution)/shard_map/psum | solution.py:160
  835.6 11.3 %convolution_convert_fusion = bf16[1024,2048]{1,0:T(8,128)(2,1)} fusion(bf16[2048,1536]{0,1:T(8,128)(2,1)} %bitcast.206, bf16[1024,512]{1,0:T(8,128)(2,1)S(1)} %bitcast.237, bf16[1024,512]{1,0:T(8,128)(2,1)S(1)} %bitcast.234, bf16[1024,512]{1,0:T(8,128)(2,1)S(1)} %bitcast.231), kind=kOutput, calls=%fused_computation.56 | convolution fusion | flops 6453985280 | bytes 13631488 | tf_op jit(solution)/shard_map/dot_general | solution.py:53
  848.2 4.7 pad_maximum_fusion.13
  858.9 48.7 %all-gather.9.cloned.1.call-done = bf16[1024,2048]{1,0:T(8,128)(2,1)} async-done(((bf16[256,2048]{1,0:T(8,128)(2,1)}), bf16[1024,2048]{1,0:T(8,128)(2,1)}) %all-gather.9.cloned.1.call-update) | async-done | bytes 4194320 | tf_op jit(solution)/shard_map/all_gather | solution.py:182
  907.6 81.9 %reduce-scatter.8.cloned.1.call-done = bf16[256,2176]{1,0:T(8,128)(2,1)} async-done(((bf16[1024,2176]{1,0:T(8,128)(2,1)}), bf16[256,2176]{1,0:T(8,128)(2,1)}) %reduce-scatter.8.cloned.1.call-update) | async-done | bytes 1114128 | tf_op jit(solution)/shard_map/reduce_scatter | solution.py:171
  998.8 4.6 slice.103
  1003.4 6.3 copy.145
  1011.2 68.7 %all-gather.11.cloned.1.call-done = bf16[1024,2048]{1,0:T(8,128)(2,1)} async-done(((bf16[256,2048]{1,0:T(8,128)(2,1)}), bf16[1024,2048]{1,0:T(8,128)(2,1)}) %all-gather.11.cloned.1.call-update) | async-done | bytes 4194320 | tf_op jit(solution)/shard_map/all_gather | solution.py:182
  1079.9 4.9 copy.168
  (339 shorter events, 197.8 us)
Async XLA Ops:
  7.2 300.7 %copy-start = (bf16[8,16,2048]{2,1,0:T(8,128)(2,1)S(1)}, bf16[8,16,2048]{2,1,0:T(8,128)(2,1)}, u32[]{:S(2)}) copy-start(bf16[8,16,2048]{2,1,0:T(8,128)(2,1)} %param.37) | copy-start | bytes 1572868
  7.2 147.1 %all-gather.5.cloned.1.call-start = ((), (), s32[]{:S(2)}) async-start(), calls=%async_computation.5 | async-start | bytes 5898240 | tf_op jit(solution)/shard_map/all_gather | solution.py:237
  12.0 11.5 %collective-permute-start = (bf16[1024,3,512]{0,2,1:T(8,128)(2,1)}, bf16[1024,3,512]{0,2,1:T(8,128)(2,1)}, u32[]{:S(2)}, u32[]{:S(2)}) collective-permute-start(bf16[1024,3,512]{0,2,1:T(8,128)(2,1)} %copy.119), channel_id=1, source_target_pairs={{0,16},{16,0},{1,17},{17,1},{2,18},{18,2},{3,19},{19,3},{4,20},{20... | collective-permute-start | bytes 9437192 | tf_op jit(solution)/shard_map/ppermute | solution.py:122
  21.2 15.7 %copy-start.10 = (bf16[4,256,2048]{2,1,0:T(8,128)(2,1)}, bf16[4,256,2048]{2,1,0:T(8,128)(2,1)S(1)}, u32[]{:S(2)}) copy-start(bf16[4,256,2048]{2,1,0:T(8,128)(2,1)S(1)} %add_convert_fusion) | copy-start | bytes 12582916
  49.4 9.0 copy-start.18
  51.0 49.4 %collective-permute-start.1 = (bf16[4,256,1024]{1,2,0:T(8,128)(2,1)}, bf16[4,256,1024]{1,2,0:T(8,128)(2,1)}, u32[]{:S(2)}, u32[]{:S(2)}) collective-permute-start(bf16[4,256,1024]{1,2,0:T(8,128)(2,1)} %pad_maximum_fusion.31), channel_id=1, source_target_pairs={{0,4},{4,0},{8,12},{12,8},{1,5},{5,1},{9,13},{13,9},{2,6},{6,2},{1... | collective-permute-start | bytes 6291464 | tf_op jit(solution)/shard_map/ppermute | solution.py:115
  53.5 92.8 %collective-permute-start.2 = (bf16[4,256,1024]{1,2,0:T(8,128)(2,1)}, bf16[4,256,1024]{1,2,0:T(8,128)(2,1)}, u32[]{:S(2)}, u32[]{:S(2)}) collective-permute-start(bf16[4,256,1024]{1,2,0:T(8,128)(2,1)} %pad_maximum_fusion.31), channel_id=1, source_target_pairs={{0,8},{4,12},{8,0},{12,4},{1,9},{5,13},{9,1},{13,5},{2,10},{6,14},... | collective-permute-start | bytes 6291464 | tf_op jit(solution)/shard_map/ppermute | solution.py:115
  55.1 91.3 %collective-permute-start.3 = (bf16[4,256,1024]{1,2,0:T(8,128)(2,1)}, bf16[4,256,1024]{1,2,0:T(8,128)(2,1)}, u32[]{:S(2)}, u32[]{:S(2)}) collective-permute-start(bf16[4,256,1024]{1,2,0:T(8,128)(2,1)} %pad_maximum_fusion.31), channel_id=1, source_target_pairs={{0,12},{4,8},{8,4},{12,0},{1,13},{5,9},{9,5},{13,1},{2,14},{6,10},... | collective-permute-start | bytes 6291464 | tf_op jit(solution)/shard_map/ppermute | solution.py:115
  64.0 95.3 %copy-start.14 = (bf16[4,256,4,128]{1,3,2,0:T(8,128)(2,1)}, bf16[4,256,4,128]{1,3,2,0:T(8,128)(2,1)S(1)}, u32[]{:S(2)}) copy-start(bf16[4,256,4,128]{1,3,2,0:T(8,128)(2,1)S(1)} %copy.135) | copy-start | bytes 3145732
  159.3 53.6 %collective-permute-start.4 = (bf16[2048,1024]{1,0:T(8,128)(2,1)}, bf16[2048,1024]{1,0:T(8,128)(2,1)}, u32[]{:S(2)}, u32[]{:S(2)}) collective-permute-start(bf16[2048,1024]{1,0:T(8,128)(2,1)} %slice.117), channel_id=1, source_target_pairs={{0,16},{16,0},{1,17},{17,1},{2,18},{18,2},{3,19},{19,3},{4,20},{20... | collective-permute-start | bytes 12582920 | tf_op jit(solution)/shard_map/ppermute | solution.py:122
  160.6 9.4 copy-start.5
  170.0 10.5 copy-start.61
  180.5 30.0 %all-to-all-start = ((bf16[4,256,512]{1,2,0:T(8,128)(2,1)}), bf16[4,256,512]{1,2,0:T(8,128)(2,1)S(1)}, u32[]{:S(2)}, u32[]{:S(2)}) async-start(bf16[4,256,512]{1,2,0:T(8,128)(2,1)} %bitcast.12), calls=%async_computation | async-start | bytes 2097152 | tf_op jit(solution)/shard_map/all_to_all | solution.py:306
  185.3 119.1 %all-gather.7.cloned.1.call-start = ((), (), s32[]{:S(2)}) async-start(), calls=%async_computation.6 | async-start | bytes 5242880 | tf_op jit(solution)/shard_map/all_gather | solution.py:182
  185.3 27.1 %copy-start.38 = (bf16[8,16,2048]{2,1,0:T(8,128)(2,1)S(1)}, bf16[8,16,2048]{2,1,0:T(8,128)(2,1)}, u32[]{:S(2)}) copy-start(bf16[8,16,2048]{2,1,0:T(8,128)(2,1)} %param.35) | copy-start | bytes 1572868
  191.9 268.6 %copy-start.36 = (f32[256,128]{1,0:T(8,128)}, f32[256,128]{1,0:T(8,128)S(1)}, u32[]{:S(2)}) copy-start(f32[256,128]{1,0:T(8,128)S(1)} %constant_dynamic-slice_fusion) | copy-start | bytes 393220
  225.3 228.8 %reduce-scatter.6.cloned.1.call-start = ((), (), s32[]{:S(2)}) async-start(), calls=%async_computation.8 | async-start | bytes 5898240 | tf_op jit(solution)/shard_map/reduce_scatter | solution.py:171
  225.6 9.0 collective-permute-start.5
  225.6 13.4 %collective-permute-start.6 = (bf16[2048,1024]{1,0:T(8,128)(2,1)}, bf16[2048,1024]{1,0:T(8,128)(2,1)S(1)}, u32[]{:S(2)}, u32[]{:S(2)}) collective-permute-start(bf16[2048,1024]{1,0:T(8,128)(2,1)} %param.31), channel_id=1, source_target_pairs={{0,16},{16,0},{1,17},{17,1},{2,18},{18,2},{3,19},{19,3},{4,20},{20... | collective-permute-start | bytes 12582920 | tf_op jit(solution)/shard_map/ppermute | solution.py:122
  312.4 16.9 %copy-start.6 = (bf16[4,256,2048]{2,1,0:T(8,128)(2,1)S(1)}, bf16[4,256,2048]{2,1,0:T(8,128)(2,1)}, u32[]{:S(2)}) copy-start(bf16[4,256,2048]{2,1,0:T(8,128)(2,1)} %param.21) | copy-start | bytes 12582916
  350.6 13.5 %copy-start.28 = (bf16[1024,2048]{1,0:T(8,128)(2,1)S(1)}, bf16[1024,2048]{1,0:T(8,128)(2,1)}, u32[]{:S(2)}) copy-start(bf16[1024,2048]{1,0:T(8,128)(2,1)} %fusion.4) | copy-start | bytes 12582916
  370.1 412.9 %reduce-scatter.4.cloned.1.call-start = ((), (), s32[]{:S(2)}) async-start(), calls=%async_computation.7 | async-start | bytes 5242880 | tf_op jit(solution)/shard_map/reduce_scatter | solution.py:171
  384.6 71.6 %copy-start.34 = (bf16[8,2048,16]{1,2,0:T(8,128)(2,1)S(1)}, bf16[8,2048,16]{1,2,0:T(8,128)(2,1)}, u32[]{:S(2)}) copy-start(bf16[8,2048,16]{1,2,0:T(8,128)(2,1)} %param.36) | copy-start | bytes 1572868
  469.2 62.1 %all-to-all-start.1 = ((bf16[256,4,512]{0,2,1:T(8,128)(2,1)}), bf16[256,4,512]{0,2,1:T(8,128)(2,1)}, u32[]{:S(2)}, u32[]{:S(2)}) async-start(bf16[256,4,512]{0,2,1:T(8,128)(2,1)} %bitcast.211), calls=%async_computation.3 | async-start | bytes 2097152 | tf_op jit(solution)/shard_map/all_to_all | solution.py:374
  473.5 312.3 %all-reduce.4.cloned.1.call-start = ((), (), s32[]{:S(2)}) async-start(), calls=%async_computation.12 | async-start | bytes 1048576 | tf_op jit(solution)/shard_map/psum | solution.py:160
  483.8 50.2 %copy-start.62 = (f32[4,4,256]{2,1,0:T(4,128)S(1)}, f32[4,4,256]{2,1,0:T(4,128)}, u32[]{:S(2)}) copy-start(f32[4,4,256]{2,1,0:T(4,128)} %copy-done.61) | copy-start | bytes 49156
  484.5 133.0 %collective-permute-start.16 = (bf16[256,384]{1,0:T(8,128)(2,1)}, bf16[256,384]{1,0:T(8,128)(2,1)S(1)}, u32[]{:S(2)}, u32[]{:S(2)}) collective-permute-start(bf16[256,384]{1,0:T(8,128)(2,1)} %get-tuple-element.74), channel_id=1, source_target_pairs={{0,1},{1,0},{2,3},{3,2},{4,5},{5,4},{6,7},{7,6},{8,9},{9,8},{10,11... | collective-permute-start | bytes 589832 | tf_op jit(solution)/shard_map/ppermute | solution.py:115
  486.4 131.7 %collective-permute-start.17 = (bf16[256,384]{1,0:T(8,128)(2,1)}, bf16[256,384]{1,0:T(8,128)(2,1)S(1)}, u32[]{:S(2)}, u32[]{:S(2)}) collective-permute-start(bf16[256,384]{1,0:T(8,128)(2,1)} %get-tuple-element.74), channel_id=1, source_target_pairs={{0,2},{1,3},{2,0},{3,1},{4,6},{5,7},{6,4},{7,5},{8,10},{9,11},{10,... | collective-permute-start | bytes 589832 | tf_op jit(solution)/shard_map/ppermute | solution.py:115
  488.8 129.3 %collective-permute-start.18 = (bf16[256,384]{1,0:T(8,128)(2,1)}, bf16[256,384]{1,0:T(8,128)(2,1)}, u32[]{:S(2)}, u32[]{:S(2)}) collective-permute-start(bf16[256,384]{1,0:T(8,128)(2,1)} %get-tuple-element.74), channel_id=1, source_target_pairs={{0,3},{1,2},{2,1},{3,0},{4,7},{5,6},{6,5},{7,4},{8,11},{9,10},{10,... | collective-permute-start | bytes 589832 | tf_op jit(solution)/shard_map/ppermute | solution.py:115
  490.1 335.2 %all-reduce.6.cloned.1.call-start = ((), (), s32[]{:S(2)}) async-start(), calls=%async_computation.13 | async-start | bytes 4456448 | tf_op jit(solution)/shard_map/psum | solution.py:160
  567.3 12.5 %copy-start.15 = (bf16[4,256,4,128]{1,3,2,0:T(8,128)(2,1)S(1)}, bf16[4,256,4,128]{1,3,2,0:T(8,128)(2,1)}, u32[]{:S(2)}) copy-start(bf16[4,256,4,128]{1,3,2,0:T(8,128)(2,1)} %copy-done.14) | copy-start | bytes 3145732
  614.6 49.0 %collective-permute-start.7 = (bf16[4,256,1024]{2,1,0:T(8,128)(2,1)}, bf16[4,256,1024]{2,1,0:T(8,128)(2,1)}, u32[]{:S(2)}, u32[]{:S(2)}) collective-permute-start(bf16[4,256,1024]{2,1,0:T(8,128)(2,1)} %get-tuple-element.53), channel_id=1, source_target_pairs={{0,4},{4,0},{8,12},{12,8},{1,5},{5,1},{9,13},{13,9},{2,6},{6,2},{1... | collective-permute-start | bytes 6291464 | tf_op jit(solution)/shard_map/ppermute | solution.py:401
  616.1 90.7 %collective-permute-start.8 = (bf16[4,256,1024]{2,1,0:T(8,128)(2,1)}, bf16[4,256,1024]{2,1,0:T(8,128)(2,1)}, u32[]{:S(2)}, u32[]{:S(2)}) collective-permute-start(bf16[4,256,1024]{2,1,0:T(8,128)(2,1)} %get-tuple-element.55), channel_id=1, source_target_pairs={{0,8},{4,12},{8,0},{12,4},{1,9},{5,13},{9,1},{13,5},{2,10},{6,14},... | collective-permute-start | bytes 6291464 | tf_op jit(solution)/shard_map/ppermute | solution.py:401
  617.6 89.2 %collective-permute-start.9 = (bf16[4,256,1024]{2,1,0:T(8,128)(2,1)}, bf16[4,256,1024]{2,1,0:T(8,128)(2,1)}, u32[]{:S(2)}, u32[]{:S(2)}) collective-permute-start(bf16[4,256,1024]{2,1,0:T(8,128)(2,1)} %get-tuple-element.54), channel_id=1, source_target_pairs={{0,12},{4,8},{8,4},{12,0},{1,13},{5,9},{9,5},{13,1},{2,14},{6,10},... | collective-permute-start | bytes 6291464 | tf_op jit(solution)/shard_map/ppermute | solution.py:401
  642.9 69.3 %copy-start.48 = (bf16[128,8,4,128]{3,1,2,0:T(8,128)(2,1)}, bf16[128,8,4,128]{3,1,2,0:T(8,128)(2,1)S(1)}, u32[]{:S(2)}) copy-start(bf16[128,8,4,128]{3,1,2,0:T(8,128)(2,1)S(1)} %copy.158) | copy-start | bytes 3145732
  714.9 20.9 %collective-permute-start.10 = (f32[1024,128]{0,1:T(8,128)}, f32[1024,128]{0,1:T(8,128)}, u32[]{:S(2)}, u32[]{:S(2)}) collective-permute-start(f32[1024,128]{0,1:T(8,128)} %fusion.66), channel_id=1, source_target_pairs={{0,1},{1,0},{2,3},{3,2},{4,5},{5,4},{6,7},{7,6},{8,9},{9,8},{10,11... | collective-permute-start | bytes 1572872 | tf_op jit(solution)/shard_map/ppermute | solution.py:115
  714.9 41.0 %collective-permute-start.11 = (f32[1024,128]{0,1:T(8,128)}, f32[1024,128]{0,1:T(8,128)}, u32[]{:S(2)}, u32[]{:S(2)}) collective-permute-start(f32[1024,128]{0,1:T(8,128)} %fusion.66), channel_id=1, source_target_pairs={{0,2},{1,3},{2,0},{3,1},{4,6},{5,7},{6,4},{7,5},{8,10},{9,11},{10,... | collective-permute-start | bytes 1572872 | tf_op jit(solution)/shard_map/ppermute | solution.py:115
  715.0 40.9 %collective-permute-start.12 = (f32[1024,128]{0,1:T(8,128)}, f32[1024,128]{0,1:T(8,128)}, u32[]{:S(2)}, u32[]{:S(2)}) collective-permute-start(f32[1024,128]{0,1:T(8,128)} %fusion.66), channel_id=1, source_target_pairs={{0,3},{1,2},{2,1},{3,0},{4,7},{5,6},{6,5},{7,4},{8,11},{9,10},{10,... | collective-permute-start | bytes 1572872 | tf_op jit(solution)/shard_map/ppermute | solution.py:115
  720.3 187.3 %all-gather.9.cloned.1.call-start = ((), (), s32[]{:S(2)}) async-start(), calls=%async_computation.9 | async-start | bytes 5242880 | tf_op jit(solution)/shard_map/all_gather | solution.py:182
  773.1 9.9 copy-start.35
  781.1 52.6 %collective-permute-start.13 = (bf16[458752]{0:T(1024)(128)(2,1)S(1)}, bf16[458752]{0:T(1024)(128)(2,1)}, u32[]{:S(2)}, u32[]{:S(2)}) collective-permute-start(bf16[458752]{0:T(1024)(128)(2,1)S(1)} %constant_dynamic-update-slice_fusion), channel_id=1, source_target_pairs={{0,16},{16,0},{1,17},{17,1},{2,18},{18,2},{3,19},{19,3},{4,20},{20... | collective-permute-start | bytes 2752520 | tf_op jit(solution)/shard_map/ppermute | solution.py:138
  785.7 203.8 %reduce-scatter.8.cloned.1.call-start = ((), (), s32[]{:S(2)}) async-start(), calls=%async_computation.10 | async-start | bytes 5570560 | tf_op jit(solution)/shard_map/reduce_scatter | solution.py:171
  835.2 21.2 %collective-permute-start.14 = (bf16[458752]{0:T(1024)(128)(2,1)S(1)}, bf16[458752]{0:T(1024)(128)(2,1)}, u32[]{:S(2)}, u32[]{:S(2)}) collective-permute-start(bf16[458752]{0:T(1024)(128)(2,1)S(1)} %add_convert_fusion.5), channel_id=1, source_target_pairs={{0,4},{4,0},{8,12},{12,8},{1,5},{5,1},{9,13},{13,9},{2,6},{6,2},{1... | collective-permute-start | bytes 2752520 | tf_op jit(solution)/shard_map/ppermute | solution.py:138
  852.9 138.0 %copy-start.37 = (f32[256,128]{1,0:T(8,128)S(1)}, f32[256,128]{1,0:T(8,128)}, u32[]{:S(2)}) copy-start(f32[256,128]{1,0:T(8,128)} %copy-done.36) | copy-start | bytes 393220
  852.9 138.0 %copy-start.41 = (bf16[8,2048,16]{1,2,0:T(8,128)(2,1)S(1)}, bf16[8,2048,16]{1,2,0:T(8,128)(2,1)}, u32[]{:S(2)}) copy-start(bf16[8,2048,16]{1,2,0:T(8,128)(2,1)} %param.32) | copy-start | bytes 1572868
  852.9 138.0 %copy-start.71 = (f32[2048]{0:T(1024)S(1)}, f32[2048]{0:T(1024)}, u32[]{:S(2)}) copy-start(f32[2048]{0:T(1024)} %param.24) | copy-start | bytes 24580
  852.9 227.0 %all-gather.11.cloned.1.call-start = ((), (), s32[]{:S(2)}) async-start(), calls=%async_computation.11 | async-start | bytes 5242880 | tf_op jit(solution)/shard_map/all_gather | solution.py:182
  857.8 140.7 %collective-permute-start.15 = (bf16[458752]{0:T(1024)(128)(2,1)S(1)}, bf16[458752]{0:T(1024)(128)(2,1)S(1)}, u32[]{:S(2)}, u32[]{:S(2)}) collective-permute-start(bf16[458752]{0:T(1024)(128)(2,1)S(1)} %add_convert_fusion.4), channel_id=1, source_target_pairs={{0,8},{4,12},{8,0},{12,4},{1,9},{5,13},{9,1},{13,5},{2,10},{6,14},... | collective-permute-start | bytes 2752520 | tf_op jit(solution)/shard_map/ppermute | solution.py:138
  (63 other events, 295.3 us)
Sparse Core Ops, SparseCore 0:
  13.9 91.7 all-gather.4
  225.4 78.8 all-gather.6
  370.3 83.7 reduce-scatter.5
  456.8 107.5 reduce-scatter.3
  569.5 187.3 all-reduce.3
  761.2 64.1 all-reduce.5
  827.4 80.1 all-gather.8
  909.9 79.5 reduce-scatter.7
  998.6 81.2 all-gather.10

commit v10 on v9

--- a/solution.py
+++ b/solution.py
@@ -354,6 +354,13 @@
     grad_up_in = matmul_tn(second_act, up_back)
     grad_heads_in = matmul_tn(heads_act, heads_back)
     heads_second_gradient = matmul_tn(heads_low_here, grad_middle_low_here)
+    heads_blocks = jnp.stack(
+        partner_swaps(heads_second_gradient.astype(jnp.bfloat16), "tp", tp_count)
+    )
+    heads_owners = jnp.bitwise_xor(lax.axis_index("tp"), jnp.arange(tp_count, dtype=jnp.int32))
+    heads_tp_total = jnp.sum(
+        jnp.take(heads_blocks, heads_owners, axis=0).astype(jnp.float32), axis=0
+    )
     early_terms = narrow_psum(
         (
             unflat_in(grad_heads_in, adapter_tables),
@@ -361,12 +368,11 @@
             up_second_gradient.reshape(adapter_up_second.shape),
             unflat_in(grad_down_in, adapter_tables),
             down_second_gradient.reshape(adapter_down_second.shape),
+            heads_tp_total.reshape(adapter_heads_second.shape),
         ),
         ("shard", "ctx"),
     )
-    heads_second_total = narrow_psum(
-        heads_second_gradient.reshape(adapter_heads_second.shape), ("shard", "ctx", "tp")
-    )
+    heads_second_total = early_terms[5]
     grad_heads_here = (
         matmul_nt(grad_middle_low_here, heads_full)
         + matmul_nt(heads_back_here, heads_first_all_flattened)

time: 1100 us -> 1080 us (0.982)
  waiting for transfers between devices: 609 us -> 551 us
  starting transfers between devices: 28.8 us -> 45.8 us
    all_to_all x1, waiting for transfers between devices: 41.1 us -> 0.01 us  [layer_body(): grad_heads = lax.all_to_all(grad_heads_here, 'tp', 1, 0, tiled=True)]
    psum x2 -> x1, waiting for transfers between devices: 37.4 us -> 2.1 us  [narrow_psum(): lax.psum(jax.tree.map(lambda value: value.astype(jnp.bfloat16), values),...]
    ppermute x9 -> x12, waiting for transfers between devices: 114 us -> 144 us  [partner_swaps(): received.append(lax.ppermute(block, axis_name, pairs))]
    ppermute x3, waiting for transfers between devices: 63.8 us -> 46.8 us  [layer_body(): lax.ppermute(grad_kv[:, offset].astype(jnp.bfloat16), 'ctx', pairs)]
    ppermute x9 -> x12, starting transfers between devices: 12.8 us -> 28.5 us  [partner_swaps(): received.append(lax.ppermute(block, axis_name, pairs))]
    unnamed x171 -> x185, local copies, waits for them, and re-layouts: 34.6 us -> 34.2 us
  transfers between devices with their start and end apart: 30 -> 32, of which waited for: 16 -> 18; matrix products, arithmetic and copies ran while one was open for 31% -> 31% of each run, Pallas kernels for 0% -> 0%
where the time goes in v10:
time: 1080 us; the launch traced here: 1060 us
  waiting for transfers between devices  551 us (51%)
  matrix products  201 us (19%)
  local copies, waits for them, and re-layouts  139 us (13%)
  other arithmetic  112 us (10%)
  starting transfers between devices  45.8 us (4%)
  between operations  15.9 us (1%)
    all_gather x3, waiting for transfers between devices, gather_rows(): lax.all_gather(jnp.concatenate(rows_here, axis=1), 'tp', axis=0, tiled=True)  177 us
    reduce_scatter x3, waiting for transfers between devices, scatter_rows(): lax.psum_scatter(jnp.concatenate(partials, axis=1).astype(jnp.bfloat16),...  158 us
    ppermute x12, waiting for transfers between devices, partner_swaps(): received.append(lax.ppermute(block, axis_name, pairs))  144 us
    dot_general x12, matrix products, matmul_nt(): lax.dot_general(left_mat, right_mat, (((1,), (1,)), ((), ())), preferred_...  66.1 us
    dot_general x12, matrix products, matmul(): return jnp.dot(left_mat, right_mat, preferred_element_type=jnp.float32)  63.5 us
    ppermute x3, waiting for transfers between devices, layer_body(): lax.ppermute(grad_kv[:, offset].astype(jnp.bfloat16), 'ctx', pairs)  46.8 us
    unnamed x185, local copies, waits for them, and re-layouts  34.2 us
    ppermute x12, starting transfers between devices, partner_swaps(): received.append(lax.ppermute(block, axis_name, pairs))  28.5 us
  transfers between devices with their start and end apart: 32, of which 18 were waited for; matrix products, arithmetic and copies ran while one was open for 31% of the time, Pallas kernels for 0%

profile of v10, /device:TPU:0, one launch (start us, length us, event | category | flops | bytes accessed | tf_op | source)
XLA Modules:
  0.0 1064.1 jit_solution(11954946706714499739)
XLA Ops:
  7.3 4.8 copy.119
  25.2 5.3 broadcast_select_fusion.7
  30.4 6.5 pad_maximum_fusion.5
  36.9 8.9 add_convert_fusion.1
  64.1 36.3 %collective-permute-done.1 = bf16[4,256,1024]{1,2,0:T(8,128)(2,1)} collective-permute-done((bf16[4,256,1024]{1,2,0:T(8,128)(2,1)}, bf16[4,256,1024]{1,2,0:T(8,128)(2,1)}, u32[]{:S(2)}, u32[]{:S(2)}) %collective-permute-start.1) | collective-permute-done | bytes 2097184 | tf_op jit(solution)/shard_map/ppermute | solution.py:115
  100.4 46.0 %collective-permute-done.2 = bf16[4,256,1024]{1,2,0:T(8,128)(2,1)} collective-permute-done((bf16[4,256,1024]{1,2,0:T(8,128)(2,1)}, bf16[4,256,1024]{1,2,0:T(8,128)(2,1)}, u32[]{:S(2)}, u32[]{:S(2)}) %collective-permute-start.2) | collective-permute-done | bytes 2097184 | tf_op jit(solution)/shard_map/ppermute | solution.py:115
  154.4 4.9 slice.119
  160.6 9.4 fusion.72
  170.0 10.5 fusion.73
  180.5 4.8 all-to-all-start
  185.3 6.7 convert.72
  192.0 18.5 %all-to-all-done = bf16[4,256,512]{1,2,0:T(8,128)(2,1)S(1)} async-done(((bf16[4,256,512]{1,2,0:T(8,128)(2,1)}), bf16[4,256,512]{1,2,0:T(8,128)(2,1)S(1)}, u32[]{:S(2)}, u32[]{:S(2)}) %all-to-all-start) | async-done | bytes 1048608 | tf_op jit(solution)/shard_map/all_to_all | solution.py:306
  216.7 6.8 fusion.74
  230.0 4.8 fusion.78
  242.8 61.5 %all-gather.7.cloned.1.call-done = bf16[1024,2048]{1,0:T(8,128)(2,1)} async-done(((bf16[256,2048]{1,0:T(8,128)(2,1)}), bf16[1024,2048]{1,0:T(8,128)(2,1)}) %all-gather.7.cloned.1.call-update) | async-done | bytes 4194320 | tf_op jit(solution)/shard_map/all_gather | solution.py:182
  307.9 4.5 fusion.77
  312.5 16.9 %multiply_convert_fusion.1 = (bf16[1024,2048]{1,0:T(8,128)(2,1)}, f32[1024,2048]{1,0:T(8,128)}) fusion(f32[1024,2048]{1,0:T(8,128)} %fusion.77, bf16[1024,2048]{1,0:T(8,128)(2,1)S(1)} %copy-done.19, bf16[1024,2048]{1,0:T(8,128)(2,1)} %get-tuple-element.60, bf16[1024,2048]{1,0:T(8,128)(2,1)} %get-tuple-element.59), kind=kOutput, calls=%fused_computation.25 | convolution fusion | flops 8627683328 | bytes 33554432 | tf_op jit(solution)/shard_map/dot_general | solution.py:43
  329.4 21.1 %fusion.4 = bf16[1024,2048]{1,0:T(8,128)(2,1)} fusion(f32[1024,2048]{1,0:T(8,128)} %get-tuple-element.85, f32[1024,2048]{1,0:T(8,128)} %fusion.78, bf16[1024,2048]{1,0:T(8,128)(2,1)S(1)} %bitcast.195, bf16[2048,1024]{1,0:T(8,128)(2,1)} %get-tuple-element.58, bf16[2048,1024]{1,0:T(8,128)(2,1)} %get-tuple-element.57), kind=kOutput, calls=%fused_computation.16 | convolution fusion | flops 8659140608 | bytes 33554432 | tf_op jit(solution)/shard_map/dot_general | solution.py:53
  350.5 13.7 %fusion.24 = bf16[1024,2048]{1,0:T(8,128)(2,1)S(1)} fusion(bf16[1024,2048]{1,0:T(8,128)(2,1)} %fusion.4, bf16[1024,2048]{1,0:T(8,128)(2,1)} %get-tuple-element.60, bf16[1024,2048]{1,0:T(8,128)(2,1)} %get-tuple-element.59), kind=kOutput, calls=%fused_computation.58 | convolution fusion | flops 8608808960 | bytes 16777216 | tf_op jit(solution)/shard_map/dot_general | solution.py:53
  377.8 76.4 %reduce-scatter.6.cloned.1.call-done = bf16[256,2304]{1,0:T(8,128)(2,1)} async-done(((bf16[1024,2304]{1,0:T(8,128)(2,1)}), bf16[256,2304]{1,0:T(8,128)(2,1)}) %reduce-scatter.6.cloned.1.call-update) | async-done | bytes 1179664 | tf_op jit(solution)/shard_map/reduce_scatter | solution.py:171
  473.6 14.4 %fusion.25 = bf16[1024,2048]{1,0:T(8,128)(2,1)} fusion(bf16[1024,2048]{1,0:T(8,128)(2,1)} %get-tuple-element.84, bf16[2048,1024]{1,0:T(8,128)(2,1)} %get-tuple-element.58, bf16[2048,1024]{1,0:T(8,128)(2,1)} %get-tuple-element.57), kind=kOutput, calls=%fused_computation.59 | convolution fusion | flops 8608808960 | bytes 16777216 | tf_op jit(solution)/shard_map/dot_general | solution.py:43
  502.8 16.2 %collective-permute-done.16 = bf16[256,384]{1,0:T(8,128)(2,1)S(1)} collective-permute-done((bf16[256,384]{1,0:T(8,128)(2,1)S(1)}, bf16[256,384]{1,0:T(8,128)(2,1)S(1)}, u32[]{:S(2)}, u32[]{:S(2)}) %collective-permute-start.16) | collective-permute-done | bytes 196640 | tf_op jit(solution)/shard_map/ppermute | solution.py:115
  519.1 8.8 collective-permute-done.17
  536.7 10.4 fusion.26
  547.1 10.7 %reshape.460 = f32[4,4,256,512]{2,1,3,0:T(4,128)} reshape(f32[4,1024,4,128]{1,3,2,0:T(8,128)} %fusion.26) | data formatting | bytes 16777216 | tf_op jit(solution)/shard_map/reshape | solution.py:400
  557.8 9.9 copy.137
  569.9 9.3 multiply_convert_fusion
  582.5 4.9 multiply_bitcast_fusion
  587.5 10.6 reshape.459
  598.0 9.9 copy.136
  607.9 6.5 fusion
  631.9 7.6 collective-permute-done.21
  645.9 8.6 fusion.39
  658.2 7.9 collective-permute-done.7
  666.1 38.9 %collective-permute-done.8 = bf16[4,256,1024]{2,1,0:T(8,128)(2,1)} collective-permute-done((bf16[4,256,1024]{2,1,0:T(8,128)(2,1)}, bf16[4,256,1024]{2,1,0:T(8,128)(2,1)}, u32[]{:S(2)}, u32[]{:S(2)}) %collective-permute-start.8) | collective-permute-done | bytes 2097184 | tf_op jit(solution)/shard_map/ppermute | solution.py:407
  705.1 5.0 fusion.18
  713.0 13.2 %collective-permute-start.10 = (f32[1024,128]{0,1:T(8,128)}, f32[1024,128]{0,1:T(8,128)}, u32[]{:S(2)}, u32[]{:S(2)}) collective-permute-start(f32[1024,128]{0,1:T(8,128)} %fusion.66), channel_id=1, source_target_pairs={{0,1},{1,0},{2,3},{3,2},{4,5},{5,4},{6,7},{7,6},{8,9},{9,8},{10,11... | collective-permute-start | bytes 1572872 | tf_op jit(solution)/shard_map/ppermute | solution.py:115
  733.7 8.2 collective-permute-done.10
  741.9 21.3 %collective-permute-done.11 = f32[1024,128]{0,1:T(8,128)} collective-permute-done((f32[1024,128]{0,1:T(8,128)}, f32[1024,128]{0,1:T(8,128)}, u32[]{:S(2)}, u32[]{:S(2)}) %collective-permute-start.11) | collective-permute-done | bytes 524320 | tf_op jit(solution)/shard_map/ppermute | solution.py:115
  780.2 5.9 reshape.464
  807.2 11.0 %convolution_convert_fusion = bf16[1024,2048]{1,0:T(8,128)(2,1)} fusion(bf16[2048,1536]{0,1:T(8,128)(2,1)} %bitcast.210, bf16[1024,512]{1,0:T(8,128)(2,1)S(1)} %bitcast.242, bf16[1024,512]{1,0:T(8,128)(2,1)S(1)} %bitcast.239, bf16[1024,512]{1,0:T(8,128)(2,1)S(1)} %bitcast.236), kind=kOutput, calls=%fused_computation.57 | convolution fusion | flops 6453985280 | bytes 13631488 | tf_op jit(solution)/shard_map/dot_general | solution.py:53
  819.4 4.7 pad_maximum_fusion.13
  830.3 47.3 %all-gather.9.cloned.1.call-done = bf16[1024,2048]{1,0:T(8,128)(2,1)} async-done(((bf16[256,2048]{1,0:T(8,128)(2,1)}), bf16[1024,2048]{1,0:T(8,128)(2,1)}) %all-gather.9.cloned.1.call-update) | async-done | bytes 4194320 | tf_op jit(solution)/shard_map/all_gather | solution.py:182
  877.6 81.9 %reduce-scatter.8.cloned.1.call-done = bf16[256,2176]{1,0:T(8,128)(2,1)} async-done(((bf16[1024,2176]{1,0:T(8,128)(2,1)}), bf16[256,2176]{1,0:T(8,128)(2,1)}) %reduce-scatter.8.cloned.1.call-update) | async-done | bytes 1114128 | tf_op jit(solution)/shard_map/reduce_scatter | solution.py:171
  968.8 4.6 slice.103
  973.4 6.3 copy.145
  981.2 68.7 %all-gather.11.cloned.1.call-done = bf16[1024,2048]{1,0:T(8,128)(2,1)} async-done(((bf16[256,2048]{1,0:T(8,128)(2,1)}), bf16[1024,2048]{1,0:T(8,128)(2,1)}) %all-gather.11.cloned.1.call-update) | async-done | bytes 4194320 | tf_op jit(solution)/shard_map/all_gather | solution.py:182
  1049.9 4.9 copy.168
  (359 shorter events, 222.5 us)
Async XLA Ops:
  7.2 300.7 %copy-start = (bf16[8,16,2048]{2,1,0:T(8,128)(2,1)S(1)}, bf16[8,16,2048]{2,1,0:T(8,128)(2,1)}, u32[]{:S(2)}) copy-start(bf16[8,16,2048]{2,1,0:T(8,128)(2,1)} %param.37) | copy-start | bytes 1572868
  7.2 147.1 %all-gather.5.cloned.1.call-start = ((), (), s32[]{:S(2)}) async-start(), calls=%async_computation.5 | async-start | bytes 5898240 | tf_op jit(solution)/shard_map/all_gather | solution.py:237
  12.0 11.5 %collective-permute-start = (bf16[1024,3,512]{0,2,1:T(8,128)(2,1)}, bf16[1024,3,512]{0,2,1:T(8,128)(2,1)}, u32[]{:S(2)}, u32[]{:S(2)}) collective-permute-start(bf16[1024,3,512]{0,2,1:T(8,128)(2,1)} %copy.119), channel_id=1, source_target_pairs={{0,16},{16,0},{1,17},{17,1},{2,18},{18,2},{3,19},{19,3},{4,20},{20... | collective-permute-start | bytes 9437192 | tf_op jit(solution)/shard_map/ppermute | solution.py:122
  21.2 15.7 %copy-start.9 = (bf16[4,256,2048]{2,1,0:T(8,128)(2,1)}, bf16[4,256,2048]{2,1,0:T(8,128)(2,1)S(1)}, u32[]{:S(2)}) copy-start(bf16[4,256,2048]{2,1,0:T(8,128)(2,1)S(1)} %add_convert_fusion) | copy-start | bytes 12582916
  51.0 49.4 %collective-permute-start.1 = (bf16[4,256,1024]{1,2,0:T(8,128)(2,1)}, bf16[4,256,1024]{1,2,0:T(8,128)(2,1)}, u32[]{:S(2)}, u32[]{:S(2)}) collective-permute-start(bf16[4,256,1024]{1,2,0:T(8,128)(2,1)} %pad_maximum_fusion.31), channel_id=1, source_target_pairs={{0,4},{4,0},{8,12},{12,8},{1,5},{5,1},{9,13},{13,9},{2,6},{6,2},{1... | collective-permute-start | bytes 6291464 | tf_op jit(solution)/shard_map/ppermute | solution.py:115
  53.6 92.8 %collective-permute-start.2 = (bf16[4,256,1024]{1,2,0:T(8,128)(2,1)}, bf16[4,256,1024]{1,2,0:T(8,128)(2,1)}, u32[]{:S(2)}, u32[]{:S(2)}) collective-permute-start(bf16[4,256,1024]{1,2,0:T(8,128)(2,1)} %pad_maximum_fusion.31), channel_id=1, source_target_pairs={{0,8},{4,12},{8,0},{12,4},{1,9},{5,13},{9,1},{13,5},{2,10},{6,14},... | collective-permute-start | bytes 6291464 | tf_op jit(solution)/shard_map/ppermute | solution.py:115
  55.1 91.3 %collective-permute-start.3 = (bf16[4,256,1024]{1,2,0:T(8,128)(2,1)}, bf16[4,256,1024]{1,2,0:T(8,128)(2,1)}, u32[]{:S(2)}, u32[]{:S(2)}) collective-permute-start(bf16[4,256,1024]{1,2,0:T(8,128)(2,1)} %pad_maximum_fusion.31), channel_id=1, source_target_pairs={{0,12},{4,8},{8,4},{12,0},{1,13},{5,9},{9,5},{13,1},{2,14},{6,10},... | collective-permute-start | bytes 6291464 | tf_op jit(solution)/shard_map/ppermute | solution.py:115
  64.1 95.2 %copy-start.13 = (bf16[4,256,4,128]{1,3,2,0:T(8,128)(2,1)}, bf16[4,256,4,128]{1,3,2,0:T(8,128)(2,1)S(1)}, u32[]{:S(2)}) copy-start(bf16[4,256,4,128]{1,3,2,0:T(8,128)(2,1)S(1)} %copy.135) | copy-start | bytes 3145732
  159.3 53.6 %collective-permute-start.4 = (bf16[2048,1024]{1,0:T(8,128)(2,1)}, bf16[2048,1024]{1,0:T(8,128)(2,1)}, u32[]{:S(2)}, u32[]{:S(2)}) collective-permute-start(bf16[2048,1024]{1,0:T(8,128)(2,1)} %slice.119), channel_id=1, source_target_pairs={{0,16},{16,0},{1,17},{17,1},{2,18},{18,2},{3,19},{19,3},{4,20},{20... | collective-permute-start | bytes 12582920 | tf_op jit(solution)/shard_map/ppermute | solution.py:122
  180.5 30.0 %all-to-all-start = ((bf16[4,256,512]{1,2,0:T(8,128)(2,1)}), bf16[4,256,512]{1,2,0:T(8,128)(2,1)S(1)}, u32[]{:S(2)}, u32[]{:S(2)}) async-start(bf16[4,256,512]{1,2,0:T(8,128)(2,1)} %bitcast.12), calls=%async_computation | async-start | bytes 2097152 | tf_op jit(solution)/shard_map/all_to_all | solution.py:306
  185.3 119.1 %all-gather.7.cloned.1.call-start = ((), (), s32[]{:S(2)}) async-start(), calls=%async_computation.6 | async-start | bytes 5242880 | tf_op jit(solution)/shard_map/all_gather | solution.py:182
  185.3 27.1 %copy-start.38 = (bf16[8,16,2048]{2,1,0:T(8,128)(2,1)S(1)}, bf16[8,16,2048]{2,1,0:T(8,128)(2,1)}, u32[]{:S(2)}) copy-start(bf16[8,16,2048]{2,1,0:T(8,128)(2,1)} %param.35) | copy-start | bytes 1572868
  192.0 268.7 %copy-start.36 = (f32[256,128]{1,0:T(8,128)}, f32[256,128]{1,0:T(8,128)S(1)}, u32[]{:S(2)}) copy-start(f32[256,128]{1,0:T(8,128)S(1)} %constant_dynamic-slice_fusion) | copy-start | bytes 393220
  225.3 228.9 %reduce-scatter.6.cloned.1.call-start = ((), (), s32[]{:S(2)}) async-start(), calls=%async_computation.8 | async-start | bytes 5898240 | tf_op jit(solution)/shard_map/reduce_scatter | solution.py:171
  225.8 9.0 collective-permute-start.5
  225.9 13.4 %collective-permute-start.6 = (bf16[2048,1024]{1,0:T(8,128)(2,1)}, bf16[2048,1024]{1,0:T(8,128)(2,1)S(1)}, u32[]{:S(2)}, u32[]{:S(2)}) collective-permute-start(bf16[2048,1024]{1,0:T(8,128)(2,1)} %param.31), channel_id=1, source_target_pairs={{0,16},{16,0},{1,17},{17,1},{2,18},{18,2},{3,19},{19,3},{4,20},{20... | collective-permute-start | bytes 12582920 | tf_op jit(solution)/shard_map/ppermute | solution.py:122
  312.5 16.9 %copy-start.6 = (bf16[4,256,2048]{2,1,0:T(8,128)(2,1)S(1)}, bf16[4,256,2048]{2,1,0:T(8,128)(2,1)}, u32[]{:S(2)}) copy-start(bf16[4,256,2048]{2,1,0:T(8,128)(2,1)} %param.21) | copy-start | bytes 12582916
  370.3 86.1 %copy-start.34 = (bf16[8,2048,16]{1,2,0:T(8,128)(2,1)S(1)}, bf16[8,2048,16]{1,2,0:T(8,128)(2,1)}, u32[]{:S(2)}) copy-start(bf16[8,2048,16]{1,2,0:T(8,128)(2,1)} %param.36) | copy-start | bytes 1572868
  469.3 64.6 %all-to-all-start.1 = ((bf16[256,4,512]{0,2,1:T(8,128)(2,1)}), bf16[256,4,512]{0,2,1:T(8,128)(2,1)}, u32[]{:S(2)}, u32[]{:S(2)}) async-start(bf16[256,4,512]{0,2,1:T(8,128)(2,1)} %bitcast.215), calls=%async_computation.3 | async-start | bytes 2097152 | tf_op jit(solution)/shard_map/all_to_all | solution.py:380
  473.6 316.5 %reduce-scatter.4.cloned.1.call-start = ((), (), s32[]{:S(2)}) async-start(), calls=%async_computation.7 | async-start | bytes 5242880 | tf_op jit(solution)/shard_map/reduce_scatter | solution.py:171
  488.1 306.9 %all-reduce.3.cloned.1.call-start = ((), (), s32[]{:S(2)}) async-start(), calls=%async_computation.12 | async-start | bytes 5505024 | tf_op jit(solution)/shard_map/psum | solution.py:160
  492.0 39.7 %copy-start.81 = (pred[1024]{0:T(1024)(128)(4,1)S(1)}, pred[1024]{0:T(1024)(128)(4,1)}, u32[]{:S(2)}) copy-start(pred[1024]{0:T(1024)(128)(4,1)} %broadcast_in_dim.146) | copy-start | bytes 3076
  493.7 25.4 %collective-permute-start.16 = (bf16[256,384]{1,0:T(8,128)(2,1)S(1)}, bf16[256,384]{1,0:T(8,128)(2,1)S(1)}, u32[]{:S(2)}, u32[]{:S(2)}) collective-permute-start(bf16[256,384]{1,0:T(8,128)(2,1)S(1)} %get-tuple-element.75), channel_id=1, source_target_pairs={{0,1},{1,0},{2,3},{3,2},{4,5},{5,4},{6,7},{7,6},{8,9},{9,8},{10,11... | collective-permute-start | bytes 589832 | tf_op jit(solution)/shard_map/ppermute | solution.py:115
  495.7 32.2 %collective-permute-start.17 = (bf16[256,384]{1,0:T(8,128)(2,1)S(1)}, bf16[256,384]{1,0:T(8,128)(2,1)S(1)}, u32[]{:S(2)}, u32[]{:S(2)}) collective-permute-start(bf16[256,384]{1,0:T(8,128)(2,1)S(1)} %get-tuple-element.75), channel_id=1, source_target_pairs={{0,2},{1,3},{2,0},{3,1},{4,6},{5,7},{6,4},{7,5},{8,10},{9,11},{10,... | collective-permute-start | bytes 589832 | tf_op jit(solution)/shard_map/ppermute | solution.py:115
  498.0 29.9 %collective-permute-start.18 = (bf16[256,384]{1,0:T(8,128)(2,1)S(1)}, bf16[256,384]{1,0:T(8,128)(2,1)S(1)}, u32[]{:S(2)}, u32[]{:S(2)}) collective-permute-start(bf16[256,384]{1,0:T(8,128)(2,1)S(1)} %get-tuple-element.75), channel_id=1, source_target_pairs={{0,3},{1,2},{2,1},{3,0},{4,7},{5,6},{6,5},{7,4},{8,11},{9,10},{10,... | collective-permute-start | bytes 589832 | tf_op jit(solution)/shard_map/ppermute | solution.py:115
  498.5 38.2 %copy-start.62 = (f32[4,4,256]{2,1,0:T(4,128)S(1)}, f32[4,4,256]{2,1,0:T(4,128)}, u32[]{:S(2)}) copy-start(f32[4,4,256]{2,1,0:T(4,128)} %copy-done.61) | copy-start | bytes 49156
  498.5 129.8 %collective-permute-start.19 = (bf16[128,2048]{1,0:T(8,128)(2,1)S(1)}, bf16[128,2048]{1,0:T(8,128)(2,1)}, u32[]{:S(2)}, u32[]{:S(2)}) collective-permute-start(bf16[128,2048]{1,0:T(8,128)(2,1)S(1)} %convolution_convert_fusion.5), channel_id=1, source_target_pairs={{0,1},{1,0},{2,3},{3,2},{4,5},{5,4},{6,7},{7,6},{8,9},{9,8},{10,11... | collective-permute-start | bytes 1572872 | tf_op jit(solution)/shard_map/ppermute | solution.py:115
  499.6 132.3 %collective-permute-start.20 = (bf16[128,2048]{1,0:T(8,128)(2,1)S(1)}, bf16[128,2048]{1,0:T(8,128)(2,1)}, u32[]{:S(2)}, u32[]{:S(2)}) collective-permute-start(bf16[128,2048]{1,0:T(8,128)(2,1)S(1)} %convolution_convert_fusion.5), channel_id=1, source_target_pairs={{0,2},{1,3},{2,0},{3,1},{4,6},{5,7},{6,4},{7,5},{8,10},{9,11},{10,... | collective-permute-start | bytes 1572872 | tf_op jit(solution)/shard_map/ppermute | solution.py:115
  617.3 48.8 %collective-permute-start.7 = (bf16[4,256,1024]{2,1,0:T(8,128)(2,1)}, bf16[4,256,1024]{2,1,0:T(8,128)(2,1)}, u32[]{:S(2)}, u32[]{:S(2)}) collective-permute-start(bf16[4,256,1024]{2,1,0:T(8,128)(2,1)} %get-tuple-element.54), channel_id=1, source_target_pairs={{0,4},{4,0},{8,12},{12,8},{1,5},{5,1},{9,13},{13,9},{2,6},{6,2},{1... | collective-permute-start | bytes 6291464 | tf_op jit(solution)/shard_map/ppermute | solution.py:407
  618.7 86.3 %collective-permute-start.8 = (bf16[4,256,1024]{2,1,0:T(8,128)(2,1)}, bf16[4,256,1024]{2,1,0:T(8,128)(2,1)}, u32[]{:S(2)}, u32[]{:S(2)}) collective-permute-start(bf16[4,256,1024]{2,1,0:T(8,128)(2,1)} %get-tuple-element.56), channel_id=1, source_target_pairs={{0,8},{4,12},{8,0},{12,4},{1,9},{5,13},{9,1},{13,5},{2,10},{6,14},... | collective-permute-start | bytes 6291464 | tf_op jit(solution)/shard_map/ppermute | solution.py:407
  620.2 84.8 %collective-permute-start.9 = (bf16[4,256,1024]{2,1,0:T(8,128)(2,1)}, bf16[4,256,1024]{2,1,0:T(8,128)(2,1)}, u32[]{:S(2)}, u32[]{:S(2)}) collective-permute-start(bf16[4,256,1024]{2,1,0:T(8,128)(2,1)} %get-tuple-element.55), channel_id=1, source_target_pairs={{0,12},{4,8},{8,4},{12,0},{1,13},{5,9},{9,5},{13,1},{2,14},{6,10},... | collective-permute-start | bytes 6291464 | tf_op jit(solution)/shard_map/ppermute | solution.py:407
  628.3 11.1 %collective-permute-start.21 = (bf16[128,2048]{1,0:T(8,128)(2,1)S(1)}, bf16[128,2048]{1,0:T(8,128)(2,1)S(1)}, u32[]{:S(2)}, u32[]{:S(2)}) collective-permute-start(bf16[128,2048]{1,0:T(8,128)(2,1)S(1)} %convolution_convert_fusion.5), channel_id=1, source_target_pairs={{0,3},{1,2},{2,1},{3,0},{4,7},{5,6},{6,5},{7,4},{8,11},{9,10},{10,... | collective-permute-start | bytes 1572872 | tf_op jit(solution)/shard_map/ppermute | solution.py:115
  658.2 52.0 %copy-start.48 = (bf16[128,8,4,128]{3,1,2,0:T(8,128)(2,1)}, bf16[128,8,4,128]{3,1,2,0:T(8,128)(2,1)S(1)}, u32[]{:S(2)}) copy-start(bf16[128,8,4,128]{3,1,2,0:T(8,128)(2,1)S(1)} %copy.158) | copy-start | bytes 3145732
  711.0 17.6 %copy-start.18 = (bf16[4,128,2048]{2,1,0:T(8,128)(2,1)S(1)}, bf16[4,128,2048]{2,1,0:T(8,128)(2,1)}, u32[]{:S(2)}) copy-start(bf16[4,128,2048]{2,1,0:T(8,128)(2,1)} %gather_fusion.2) | copy-start | bytes 6291460
  711.0 17.6 %copy-start.84 = (pred[4]{0:T(512)(128)(4,1)S(1)}, pred[4]{0:T(512)(128)(4,1)}, u32[]{:S(2)}) copy-start(pred[4]{0:T(512)(128)(4,1)} %copy-done.83) | copy-start | bytes 16
  713.0 17.1 %copy-start.32 = (bf16[1024,128]{1,0:T(8,128)(2,1)S(1)}, bf16[1024,128]{1,0:T(8,128)(2,1)}, u32[]{:S(2)}) copy-start(bf16[1024,128]{1,0:T(8,128)(2,1)} %copy-done.31) | copy-start | bytes 786436
  713.0 28.9 %collective-permute-start.10 = (f32[1024,128]{0,1:T(8,128)}, f32[1024,128]{0,1:T(8,128)}, u32[]{:S(2)}, u32[]{:S(2)}) collective-permute-start(f32[1024,128]{0,1:T(8,128)} %fusion.66), channel_id=1, source_target_pairs={{0,1},{1,0},{2,3},{3,2},{4,5},{5,4},{6,7},{7,6},{8,9},{9,8},{10,11... | collective-permute-start | bytes 1572872 | tf_op jit(solution)/shard_map/ppermute | solution.py:115
  726.2 37.0 %collective-permute-start.11 = (f32[1024,128]{0,1:T(8,128)}, f32[1024,128]{0,1:T(8,128)}, u32[]{:S(2)}, u32[]{:S(2)}) collective-permute-start(f32[1024,128]{0,1:T(8,128)} %fusion.66), channel_id=1, source_target_pairs={{0,2},{1,3},{2,0},{3,1},{4,6},{5,7},{6,4},{7,5},{8,10},{9,11},{10,... | collective-permute-start | bytes 1572872 | tf_op jit(solution)/shard_map/ppermute | solution.py:115
  726.2 37.0 %collective-permute-start.12 = (f32[1024,128]{0,1:T(8,128)}, f32[1024,128]{0,1:T(8,128)}, u32[]{:S(2)}, u32[]{:S(2)}) collective-permute-start(f32[1024,128]{0,1:T(8,128)} %fusion.66), channel_id=1, source_target_pairs={{0,3},{1,2},{2,1},{3,0},{4,7},{5,6},{6,5},{7,4},{8,11},{9,10},{10,... | collective-permute-start | bytes 1572872 | tf_op jit(solution)/shard_map/ppermute | solution.py:115
  730.0 147.6 %all-gather.9.cloned.1.call-start = ((), (), s32[]{:S(2)}) async-start(), calls=%async_computation.9 | async-start | bytes 5242880 | tf_op jit(solution)/shard_map/all_gather | solution.py:182
  788.2 16.3 %collective-permute-start.13 = (bf16[458752]{0:T(1024)(128)(2,1)S(1)}, bf16[458752]{0:T(1024)(128)(2,1)}, u32[]{:S(2)}, u32[]{:S(2)}) collective-permute-start(bf16[458752]{0:T(1024)(128)(2,1)S(1)} %constant_dynamic-update-slice_fusion), channel_id=1, source_target_pairs={{0,16},{16,0},{1,17},{17,1},{2,18},{18,2},{3,19},{19,3},{4,20},{20... | collective-permute-start | bytes 2752520 | tf_op jit(solution)/shard_map/ppermute | solution.py:138
  792.9 166.6 %reduce-scatter.8.cloned.1.call-start = ((), (), s32[]{:S(2)}) async-start(), calls=%async_computation.10 | async-start | bytes 5570560 | tf_op jit(solution)/shard_map/reduce_scatter | solution.py:171
  806.0 21.4 %collective-permute-start.14 = (bf16[458752]{0:T(1024)(128)(2,1)S(1)}, bf16[458752]{0:T(1024)(128)(2,1)}, u32[]{:S(2)}, u32[]{:S(2)}) collective-permute-start(bf16[458752]{0:T(1024)(128)(2,1)S(1)} %add_convert_fusion.5), channel_id=1, source_target_pairs={{0,4},{4,0},{8,12},{12,8},{1,5},{5,1},{9,13},{13,9},{2,6},{6,2},{1... | collective-permute-start | bytes 2752520 | tf_op jit(solution)/shard_map/ppermute | solution.py:138
  824.1 136.7 %copy-start.37 = (f32[256,128]{1,0:T(8,128)S(1)}, f32[256,128]{1,0:T(8,128)}, u32[]{:S(2)}) copy-start(f32[256,128]{1,0:T(8,128)} %copy-done.36) | copy-start | bytes 393220
  824.1 136.8 %copy-start.41 = (bf16[8,2048,16]{1,2,0:T(8,128)(2,1)S(1)}, bf16[8,2048,16]{1,2,0:T(8,128)(2,1)}, u32[]{:S(2)}) copy-start(bf16[8,2048,16]{1,2,0:T(8,128)(2,1)} %param.32) | copy-start | bytes 1572868
  824.1 136.8 %copy-start.73 = (f32[2048]{0:T(1024)S(1)}, f32[2048]{0:T(1024)}, u32[]{:S(2)}) copy-start(f32[2048]{0:T(1024)} %param.24) | copy-start | bytes 24580
  824.1 225.7 %all-gather.11.cloned.1.call-start = ((), (), s32[]{:S(2)}) async-start(), calls=%async_computation.11 | async-start | bytes 5242880 | tf_op jit(solution)/shard_map/all_gather | solution.py:182
  828.8 139.7 %collective-permute-start.15 = (bf16[458752]{0:T(1024)(128)(2,1)S(1)}, bf16[458752]{0:T(1024)(128)(2,1)S(1)}, u32[]{:S(2)}, u32[]{:S(2)}) collective-permute-start(bf16[458752]{0:T(1024)(128)(2,1)S(1)} %add_convert_fusion.4), channel_id=1, source_target_pairs={{0,8},{4,12},{8,0},{12,4},{1,9},{5,13},{9,1},{13,5},{2,10},{6,14},... | collective-permute-start | bytes 2752520 | tf_op jit(solution)/shard_map/ppermute | solution.py:138
  (72 other events, 369.2 us)
Sparse Core Ops, SparseCore 0:
  13.9 91.7 all-gather.4
  225.5 78.8 all-gather.6
  370.4 83.7 reduce-scatter.5
  488.2 115.4 reduce-scatter.3
  730.1 64.8 all-reduce.2
  797.0 80.5 all-gather.8
  879.9 79.5 reduce-scatter.7
  968.6 81.2 all-gather.10

commit v11 on v7

--- a/solution.py
+++ b/solution.py
@@ -272,17 +272,11 @@
     value_rows = projected[:, 2 * local_width :].reshape(seq_here, local_len, local_width)
     ctx_count = lax.axis_size("ctx")
     ctx_here = lax.axis_index("ctx")
-    blocks = partner_swaps(
-        jnp.concatenate([key_rows, value_rows], axis=2), "ctx", ctx_count
-    )
-    pieces = jnp.concatenate(blocks, axis=1)
+    pieces = lax.all_gather(
+        jnp.concatenate([key_rows, value_rows], axis=2), "ctx", axis=1, tiled=True
+    )
     piece_len = pieces.shape[1]
-    key_pos = jnp.concatenate(
-        [
-            (ctx_here ^ offset) * local_len + jnp.arange(local_len, dtype=jnp.int32)
-            for offset in range(ctx_count)
-        ]
-    )
+    key_pos = jnp.arange(piece_len, dtype=jnp.int32)
     key_labels = piece_labels(picture_piece_starts, key_pos)
     visible_mask = visible(here_pos, key_pos, here_labels, key_labels)
     piece_keys = pieces[:, :, :local_width].reshape(seq_here, piece_len, device_heads, head_width)
@@ -390,11 +384,12 @@
         ],
         axis=3,
     )
-    grad_kv_here = grad_kv[:, 0]
+    grad_kv_here = lax.dynamic_index_in_dim(grad_kv, ctx_here, axis=1, keepdims=False)
     for offset in range(1, ctx_count):
         pairs = [(index, index ^ offset) for index in range(ctx_count)]
+        block = lax.dynamic_index_in_dim(grad_kv, ctx_here ^ offset, axis=1, keepdims=False)
         grad_kv_here = grad_kv_here + lax.ppermute(
-            grad_kv[:, offset].astype(jnp.bfloat16), "ctx", pairs
+            block.astype(jnp.bfloat16), "ctx", pairs
         ).astype(jnp.float32)
     grad_keys_all = grad_kv_here[:, :, :local_width]
     grad_values_all = grad_kv_here[:, :, local_width:]

time: 1300 us -> 1330 us (1.023)
  waiting for transfers between devices: 780 us -> 838 us
  blocking collectives: 30.1 us -> 0 us
    ppermute x9 -> x6, waiting for transfers between devices: 178 us -> 94.7 us  [partner_swaps(): received.append(lax.ppermute(block, axis_name, pairs))]
    all_gather x0 -> x1, waiting for transfers between devices: none -> 77.6 us  [layer_body(): lax.all_gather(jnp.concatenate([key_rows, value_rows], axis=2), 'ctx', ax...]
    all_gather x1, waiting for transfers between devices: 0.01 us -> 45.2 us  [layer_body(): lax.all_gather(jnp.concatenate([attention_output_weight, heads_first_loca...]
    all_to_all x1 -> x0, blocking collectives: 30.1 us -> none  [layer_body(): grad_heads = lax.all_to_all(grad_heads_here, 'tp', 1, 0, tiled=True)]
    all_to_all x0 -> x1, waiting for transfers between devices: none -> 26 us  [layer_body(): grad_heads = lax.all_to_all(grad_heads_here, 'tp', 1, 0, tiled=True)]
    unnamed x173 -> x161, local copies, waits for them, and re-layouts: 33.7 us -> 33.3 us
  transfers between devices with their start and end apart: 29 -> 28, of which waited for: 20 -> 21; matrix products, arithmetic and copies ran while one was open for 17% -> 17% of each run, Pallas kernels for 0% -> 0%
where the time goes in v11:
time: 1330 us; the launch traced here: 1320 us
  waiting for transfers between devices  838 us (63%)
  matrix products  203 us (15%)
  local copies, waits for them, and re-layouts  123 us (9%)
  other arithmetic  115 us (9%)
  starting transfers between devices  26.2 us (2%)
  between operations  15.6 us (1%)
    all_gather x3, waiting for transfers between devices, gather_rows(): lax.all_gather(jnp.concatenate(rows_here, axis=1), 'tp', axis=0, tiled=True)  202 us
    reduce_scatter x3, waiting for transfers between devices, scatter_rows(): lax.psum_scatter(jnp.concatenate(partials, axis=1).astype(jnp.bfloat16),...  142 us
    psum x2, waiting for transfers between devices, narrow_psum(): lax.psum(jax.tree.map(lambda value: value.astype(jnp.bfloat16), values),...  116 us
    ppermute x6, waiting for transfers between devices, partner_swaps(): received.append(lax.ppermute(block, axis_name, pairs))  94.7 us
    all_gather x1, waiting for transfers between devices, layer_body(): lax.all_gather(jnp.concatenate([key_rows, value_rows], axis=2), 'ctx', ax...  77.6 us
    ppermute x3, waiting for transfers between devices, layer_body(): lax.ppermute(block.astype(jnp.bfloat16), 'ctx', pairs).astype(jnp.float32)  77.4 us
    dot_general x12, matrix products, matmul_nt(): lax.dot_general(left_mat, right_mat, (((1,), (1,)), ((), ())), preferred_...  67.3 us
    dot_general x12, matrix products, matmul(): return jnp.dot(left_mat, right_mat, preferred_element_type=jnp.float32)  62.8 us
  transfers between devices with their start and end apart: 28, of which 21 were waited for; matrix products, arithmetic and copies ran while one was open for 17% of the time, Pallas kernels for 0%

profile of v11, /device:TPU:0, one launch (start us, length us, event | category | flops | bytes accessed | tf_op | source)
XLA Modules:
  0.0 1320.8 jit_solution(9093131828759302663)
XLA Ops:
  26.7 5.0 broadcast_select_fusion.7
  31.7 6.5 pad_maximum_fusion.3
  38.2 8.8 add_convert_fusion.1
  57.8 45.2 %all-gather.8.cloned.1.call-done = bf16[2048,1152]{1,0:T(8,128)(2,1)} async-done(((bf16[512,1152]{1,0:T(8,128)(2,1)}), bf16[2048,1152]{1,0:T(8,128)(2,1)}) %all-gather.8.cloned.1.call-update) | async-done | bytes 4718608 | tf_op jit(solution)/shard_map/all_gather | solution.py:234
  103.0 4.7 slice.102
  113.0 77.6 %all-gather.6.cloned.1.call-done = bf16[4,1024,1024]{1,2,0:T(8,128)(2,1)} async-done(((bf16[4,256,1024]{1,2,0:T(8,128)(2,1)}), bf16[4,1024,1024]{1,2,0:T(8,128)(2,1)}) %all-gather.6.cloned.1.call-update) | async-done | bytes 8388624 | tf_op jit(solution)/shard_map/all_gather | solution.py:275
  195.3 9.4 fusion.81
  204.7 10.5 fusion.82
  219.8 6.6 convert.53
  226.5 5.9 broadcast_select_fusion.5
  232.4 13.0 all-to-all-done
  248.1 5.6 fusion.83
  260.0 4.8 fusion.87
  272.9 61.7 %all-gather.10.cloned.1.call-done = bf16[1024,2048]{1,0:T(8,128)(2,1)} async-done(((bf16[256,2048]{1,0:T(8,128)(2,1)}), bf16[1024,2048]{1,0:T(8,128)(2,1)}) %all-gather.10.cloned.1.call-update) | async-done | bytes 4194320 | tf_op jit(solution)/shard_map/all_gather | solution.py:179
  342.8 17.0 %multiply_convert_fusion.1 = (bf16[1024,2048]{1,0:T(8,128)(2,1)}, f32[1024,2048]{1,0:T(8,128)}) fusion(f32[1024,2048]{1,0:T(8,128)} %fusion.86, bf16[1024,2048]{1,0:T(8,128)(2,1)S(1)} %copy-done.20, bf16[1024,2048]{1,0:T(8,128)(2,1)} %get-tuple-element.59, bf16[1024,2048]{1,0:T(8,128)(2,1)} %get-tuple-element.58), kind=kOutput, calls=%fused_computation.27 | convolution fusion | flops 8627683328 | bytes 33554432 | tf_op jit(solution)/shard_map/dot_general | solution.py:43
  359.8 21.3 %fusion.3 = bf16[1024,2048]{1,0:T(8,128)(2,1)} fusion(f32[1024,2048]{1,0:T(8,128)} %get-tuple-element.84, f32[1024,2048]{1,0:T(8,128)} %fusion.87, bf16[1024,2048]{1,0:T(8,128)(2,1)S(1)} %bitcast.190, bf16[2048,1024]{1,0:T(8,128)(2,1)} %get-tuple-element.57, bf16[2048,1024]{1,0:T(8,128)(2,1)} %get-tuple-element.56), kind=kOutput, calls=%fused_computation.19 | convolution fusion | flops 8659140608 | bytes 33554432 | tf_op jit(solution)/shard_map/dot_general | solution.py:53
  384.7 12.0 fusion.29
  404.1 11.7 fusion.30
  418.3 60.7 %reduce-scatter.6.cloned.1.call-done = bf16[256,2176]{1,0:T(8,128)(2,1)} async-done(((bf16[1024,2176]{1,0:T(8,128)(2,1)}), bf16[256,2176]{1,0:T(8,128)(2,1)}) %reduce-scatter.6.cloned.1.call-update) | async-done | bytes 1114128 | tf_op jit(solution)/shard_map/reduce_scatter | solution.py:168
  481.7 81.0 %reduce-scatter.4.cloned.1.call-done = bf16[256,2176]{1,0:T(8,128)(2,1)} async-done(((bf16[1024,2176]{1,0:T(8,128)(2,1)}), bf16[256,2176]{1,0:T(8,128)(2,1)}) %reduce-scatter.4.cloned.1.call-update) | async-done | bytes 1114128 | tf_op jit(solution)/shard_map/reduce_scatter | solution.py:168
  583.5 26.0 %all-to-all-done.1 = bf16[256,4,512]{0,2,1:T(8,128)(2,1)} async-done(((bf16[256,4,512]{0,2,1:T(8,128)(2,1)}), bf16[256,4,512]{0,2,1:T(8,128)(2,1)}, u32[]{:S(2)}, u32[]{:S(2)}) %all-to-all-start.1) | async-done | bytes 1048608 | tf_op jit(solution)/shard_map/all_to_all | solution.py:363
  614.3 10.4 fusion.31
  624.8 9.2 multiply_convert_fusion
  637.3 4.9 multiply_bitcast_fusion
  642.2 10.5 reshape.438
  652.8 9.9 copy.135
  662.7 10.5 reshape.439
  673.2 9.9 copy.136
  683.1 7.6 fusion.42
  694.1 8.6 fusion.46
  706.5 33.9 %collective-permute-done.6 = bf16[4,256,1024]{2,1,0:T(8,128)(2,1)} collective-permute-done((bf16[4,256,1024]{2,1,0:T(8,128)(2,1)}, bf16[4,256,1024]{2,1,0:T(8,128)(2,1)}, u32[]{:S(2)}, u32[]{:S(2)}) %collective-permute-start.6) | collective-permute-done | bytes 2097184 | tf_op jit(solution)/shard_map/ppermute | solution.py:391
  740.4 43.4 %collective-permute-done.5 = bf16[4,256,1024]{2,1,0:T(8,128)(2,1)} collective-permute-done((bf16[4,256,1024]{2,1,0:T(8,128)(2,1)}, bf16[4,256,1024]{2,1,0:T(8,128)(2,1)}, u32[]{:S(2)}, u32[]{:S(2)}) %collective-permute-start.5) | collective-permute-done | bytes 2097184 | tf_op jit(solution)/shard_map/ppermute | solution.py:391
  783.8 5.7 fusion.19
  791.9 11.5 convolution_convert_fusion
  803.5 4.8 pad_maximum_fusion.12
  825.8 8.4 collective-permute-done.15
  834.2 27.6 %collective-permute-done.14 = bf16[256,384]{1,0:T(8,128)(2,1)S(1)} collective-permute-done((bf16[256,384]{1,0:T(8,128)(2,1)}, bf16[256,384]{1,0:T(8,128)(2,1)S(1)}, u32[]{:S(2)}, u32[]{:S(2)}) %collective-permute-start.14) | collective-permute-done | bytes 196640 | tf_op jit(solution)/shard_map/ppermute | solution.py:115
  889.7 17.1 %collective-permute-done.9 = f32[1024,128]{0,1:T(8,128)} collective-permute-done((f32[1024,128]{0,1:T(8,128)}, f32[1024,128]{0,1:T(8,128)}, u32[]{:S(2)}, u32[]{:S(2)}) %collective-permute-start.9) | collective-permute-done | bytes 524320 | tf_op jit(solution)/shard_map/ppermute | solution.py:115
  906.8 41.6 %collective-permute-done.8 = f32[1024,128]{0,1:T(8,128)} collective-permute-done((f32[1024,128]{0,1:T(8,128)}, f32[1024,128]{0,1:T(8,128)}, u32[]{:S(2)}, u32[]{:S(2)}) %collective-permute-start.8) | collective-permute-done | bytes 524320 | tf_op jit(solution)/shard_map/ppermute | solution.py:115
  957.4 4.9 copy.140
  962.2 5.6 reshape.443
  982.8 40.8 %collective-permute-done.11 = f32[458752]{0:T(1024)S(1)} collective-permute-done((f32[458752]{0:T(1024)S(1)}, f32[458752]{0:T(1024)S(1)}, u32[]{:S(2)}, u32[]{:S(2)}) %collective-permute-start.11) | collective-permute-done | bytes 1835040 | tf_op jit(solution)/shard_map/ppermute | solution.py:137
  1025.2 51.9 %all-reduce.4.cloned.1.call-done = bf16[8,16,2048]{2,1,0:T(8,128)(2,1)} async-done(((bf16[8,16,2048]{2,1,0:T(8,128)(2,1)}), bf16[8,16,2048]{2,1,0:T(8,128)(2,1)}) %all-reduce.4.cloned.1.call-update) | async-done | bytes 524304 | tf_op jit(solution)/shard_map/psum | solution.py:157
  1079.3 64.0 %all-reduce.6.cloned.1.call-done = (bf16[8,512,16]{1,2,0:T(8,128)(2,1)}, bf16[8,2048,16]{1,2,0:T(8,128)(2,1)}, bf16[8,16,2048]{2,1,0:T(8,128)(2,1)}, bf16[8,2048,16]{1,2,0:T(8,128)(2,1)}, bf16[8,16,2048]{2,1,0:T(8,128)(2,1)}) async-done(((bf16[8,512,16]{1,2,0:T(8,128)(2,1)}, bf16[8,2048,16]{1,2,0:T(8,128)(2,1)}, bf16[8,16,2048]{2,1,0:T(8,128)(2,1)}, bf16[8,2048,16]{1,2,0:T(8,128)(2,1)}, ...) | async-done | bytes 2228240 | tf_op jit(solution)/shard_map/psum | solution.py:157
  1152.4 73.2 %all-gather.12.cloned.1.call-done = bf16[1024,2048]{1,0:T(8,128)(2,1)} async-done(((bf16[256,2048]{1,0:T(8,128)(2,1)}), bf16[1024,2048]{1,0:T(8,128)(2,1)}) %all-gather.12.cloned.1.call-update) | async-done | bytes 4194320 | tf_op jit(solution)/shard_map/all_gather | solution.py:179
  1232.0 6.5 copy.144
  1240.0 66.8 %all-gather.14.cloned.1.call-done = bf16[1024,2048]{1,0:T(8,128)(2,1)} async-done(((bf16[256,2048]{1,0:T(8,128)(2,1)}), bf16[1024,2048]{1,0:T(8,128)(2,1)}) %all-gather.14.cloned.1.call-update) | async-done | bytes 4194320 | tf_op jit(solution)/shard_map/all_gather | solution.py:179
  1306.8 4.9 copy.167
  (324 shorter events, 216.2 us)
Async XLA Ops:
  7.2 331.0 %copy-start = (bf16[8,16,2048]{2,1,0:T(8,128)(2,1)S(1)}, bf16[8,16,2048]{2,1,0:T(8,128)(2,1)}, u32[]{:S(2)}) copy-start(bf16[8,16,2048]{2,1,0:T(8,128)(2,1)} %param.37) | copy-start | bytes 1572868
  7.2 95.8 %all-gather.8.cloned.1.call-start = ((), (), s32[]{:S(2)}) async-start(), calls=%async_computation.6 | async-start | bytes 5898240 | tf_op jit(solution)/shard_map/all_gather | solution.py:234
  10.7 179.9 %all-gather.6.cloned.1.call-start = ((), (), s32[]{:S(2)}) async-start(), calls=%async_computation.5 | async-start | bytes 10485760 | tf_op jit(solution)/shard_map/all_gather | solution.py:275
  15.5 9.9 collective-permute-start
  16.4 8.0 copy-start.45
  23.1 15.1 %copy-start.10 = (bf16[4,256,2048]{2,1,0:T(8,128)(2,1)}, bf16[4,256,2048]{2,1,0:T(8,128)(2,1)S(1)}, u32[]{:S(2)}) copy-start(bf16[4,256,2048]{2,1,0:T(8,128)(2,1)S(1)} %add_convert_fusion) | copy-start | bytes 12582916
  107.7 118.7 %collective-permute-start.1 = (bf16[2048,1024]{1,0:T(8,128)(2,1)}, bf16[2048,1024]{1,0:T(8,128)(2,1)}, u32[]{:S(2)}, u32[]{:S(2)}) collective-permute-start(bf16[2048,1024]{1,0:T(8,128)(2,1)} %slice.102), channel_id=1, source_target_pairs={{0,16},{16,0},{1,17},{17,1},{2,18},{18,2},{3,19},{19,3},{4,20},{20... | collective-permute-start | bytes 12582920 | tf_op jit(solution)/shard_map/ppermute | solution.py:122
  113.0 81.7 %copy-start.14 = (bf16[4,256,4,128]{1,3,2,0:T(8,128)(2,1)}, bf16[4,256,4,128]{1,3,2,0:T(8,128)(2,1)S(1)}, u32[]{:S(2)}) copy-start(bf16[4,256,4,128]{1,3,2,0:T(8,128)(2,1)S(1)} %copy.134) | copy-start | bytes 3145732
  194.7 10.0 copy-start.8
  194.7 9.9 copy-start.5
  204.7 10.5 copy-start.58
  215.2 30.1 %all-to-all-start = ((bf16[4,256,512]{1,2,0:T(8,128)(2,1)}), bf16[4,256,512]{1,2,0:T(8,128)(2,1)S(1)}, u32[]{:S(2)}, u32[]{:S(2)}) async-start(bf16[4,256,512]{1,2,0:T(8,128)(2,1)} %bitcast.12), calls=%async_computation | async-start | bytes 2097152 | tf_op jit(solution)/shard_map/all_to_all | solution.py:297
  219.8 114.8 %all-gather.10.cloned.1.call-start = ((), (), s32[]{:S(2)}) async-start(), calls=%async_computation.7 | async-start | bytes 5242880 | tf_op jit(solution)/shard_map/all_gather | solution.py:179
  226.4 20.9 %copy-start.38 = (bf16[8,16,2048]{2,1,0:T(8,128)(2,1)S(1)}, bf16[8,16,2048]{2,1,0:T(8,128)(2,1)}, u32[]{:S(2)}) copy-start(bf16[8,16,2048]{2,1,0:T(8,128)(2,1)} %param.35) | copy-start | bytes 1572868
  255.6 223.4 %reduce-scatter.6.cloned.1.call-start = ((), (), s32[]{:S(2)}) async-start(), calls=%async_computation.10 | async-start | bytes 5570560 | tf_op jit(solution)/shard_map/reduce_scatter | solution.py:168
  255.9 9.0 collective-permute-start.2
  255.9 13.4 %collective-permute-start.3 = (bf16[2048,1024]{1,0:T(8,128)(2,1)}, bf16[2048,1024]{1,0:T(8,128)(2,1)S(1)}, u32[]{:S(2)}, u32[]{:S(2)}) collective-permute-start(bf16[2048,1024]{1,0:T(8,128)(2,1)} %param.31), channel_id=1, source_target_pairs={{0,16},{16,0},{1,17},{17,1},{2,18},{18,2},{3,19},{19,3},{4,20},{20... | collective-permute-start | bytes 12582920 | tf_op jit(solution)/shard_map/ppermute | solution.py:122
  342.7 17.0 %copy-start.6 = (bf16[4,256,2048]{2,1,0:T(8,128)(2,1)S(1)}, bf16[4,256,2048]{2,1,0:T(8,128)(2,1)}, u32[]{:S(2)}) copy-start(bf16[4,256,2048]{2,1,0:T(8,128)(2,1)} %param.21) | copy-start | bytes 12582916
  399.3 163.4 %reduce-scatter.4.cloned.1.call-start = ((), (), s32[]{:S(2)}) async-start(), calls=%async_computation.8 | async-start | bytes 5570560 | tf_op jit(solution)/shard_map/reduce_scatter | solution.py:168
  418.3 147.7 %copy-start.37 = (bf16[8,2048,16]{1,2,0:T(8,128)(2,1)S(1)}, bf16[8,2048,16]{1,2,0:T(8,128)(2,1)}, u32[]{:S(2)}) copy-start(bf16[8,2048,16]{1,2,0:T(8,128)(2,1)} %param.36) | copy-start | bytes 1572868
  576.6 35.0 %copy-start.59 = (f32[4,4,256]{2,1,0:T(4,128)S(1)}, f32[4,4,256]{2,1,0:T(4,128)}, u32[]{:S(2)}) copy-start(f32[4,4,256]{2,1,0:T(4,128)} %copy-done.58) | copy-start | bytes 49156
  578.9 30.6 %all-to-all-start.1 = ((bf16[256,4,512]{0,2,1:T(8,128)(2,1)}), bf16[256,4,512]{0,2,1:T(8,128)(2,1)}, u32[]{:S(2)}, u32[]{:S(2)}) async-start(bf16[256,4,512]{0,2,1:T(8,128)(2,1)} %bitcast.211), calls=%async_computation.3 | async-start | bytes 2097152 | tf_op jit(solution)/shard_map/all_to_all | solution.py:363
  583.2 384.8 %reduce-scatter.8.cloned.1.call-start = ((), (), s32[]{:S(2)}) async-start(), calls=%async_computation.11 | async-start | bytes 5570560 | tf_op jit(solution)/shard_map/reduce_scatter | solution.py:168
  624.7 12.6 copy-start.15
  690.6 49.8 %collective-permute-start.6 = (bf16[4,256,1024]{2,1,0:T(8,128)(2,1)}, bf16[4,256,1024]{2,1,0:T(8,128)(2,1)}, u32[]{:S(2)}, u32[]{:S(2)}) collective-permute-start(bf16[4,256,1024]{2,1,0:T(8,128)(2,1)} %get-tuple-element.53), channel_id=1, source_target_pairs={{0,12},{4,8},{8,4},{12,0},{1,13},{5,9},{9,5},{13,1},{2,14},{6,10},... | collective-permute-start | bytes 6291464 | tf_op jit(solution)/shard_map/ppermute | solution.py:391
  693.0 90.7 %collective-permute-start.5 = (bf16[4,256,1024]{2,1,0:T(8,128)(2,1)}, bf16[4,256,1024]{2,1,0:T(8,128)(2,1)}, u32[]{:S(2)}, u32[]{:S(2)}) collective-permute-start(bf16[4,256,1024]{2,1,0:T(8,128)(2,1)} %get-tuple-element.52), channel_id=1, source_target_pairs={{0,8},{4,12},{8,0},{12,4},{1,9},{5,13},{9,1},{13,5},{2,10},{6,14},... | collective-permute-start | bytes 6291464 | tf_op jit(solution)/shard_map/ppermute | solution.py:391
  693.6 90.2 %collective-permute-start.4 = (bf16[4,256,1024]{2,1,0:T(8,128)(2,1)}, bf16[4,256,1024]{2,1,0:T(8,128)(2,1)}, u32[]{:S(2)}, u32[]{:S(2)}) collective-permute-start(bf16[4,256,1024]{2,1,0:T(8,128)(2,1)} %get-tuple-element.51), channel_id=1, source_target_pairs={{0,4},{4,0},{8,12},{12,8},{1,5},{5,1},{9,13},{13,9},{2,6},{6,2},{1... | collective-permute-start | bytes 6291464 | tf_op jit(solution)/shard_map/ppermute | solution.py:391
  706.4 85.4 %copy-start.47 = (bf16[128,8,4,128]{3,1,2,0:T(8,128)(2,1)}, bf16[128,8,4,128]{3,1,2,0:T(8,128)(2,1)S(1)}, u32[]{:S(2)}) copy-start(bf16[128,8,4,128]{3,1,2,0:T(8,128)(2,1)S(1)} %copy.157) | copy-start | bytes 3145732
  791.9 11.5 copy-start.42
  808.3 268.9 %all-reduce.4.cloned.1.call-start = ((), (), s32[]{:S(2)}) async-start(), calls=%async_computation.13 | async-start | bytes 1048576 | tf_op jit(solution)/shard_map/psum | solution.py:157
  809.0 8.8 copy-start.44
  817.8 6.7 copy-start.55
  820.2 14.0 %collective-permute-start.15 = (bf16[256,384]{1,0:T(8,128)(2,1)}, bf16[256,384]{1,0:T(8,128)(2,1)S(1)}, u32[]{:S(2)}, u32[]{:S(2)}) collective-permute-start(bf16[256,384]{1,0:T(8,128)(2,1)} %get-tuple-element.72), channel_id=1, source_target_pairs={{0,3},{1,2},{2,1},{3,0},{4,7},{5,6},{6,5},{7,4},{8,11},{9,10},{10,... | collective-permute-start | bytes 589832 | tf_op jit(solution)/shard_map/ppermute | solution.py:115
  821.3 40.5 %collective-permute-start.14 = (bf16[256,384]{1,0:T(8,128)(2,1)}, bf16[256,384]{1,0:T(8,128)(2,1)S(1)}, u32[]{:S(2)}, u32[]{:S(2)}) collective-permute-start(bf16[256,384]{1,0:T(8,128)(2,1)} %get-tuple-element.72), channel_id=1, source_target_pairs={{0,2},{1,3},{2,0},{3,1},{4,6},{5,7},{6,4},{7,5},{8,10},{9,11},{10,... | collective-permute-start | bytes 589832 | tf_op jit(solution)/shard_map/ppermute | solution.py:115
  821.3 40.5 %collective-permute-start.13 = (bf16[256,384]{1,0:T(8,128)(2,1)}, bf16[256,384]{1,0:T(8,128)(2,1)}, u32[]{:S(2)}, u32[]{:S(2)}) collective-permute-start(bf16[256,384]{1,0:T(8,128)(2,1)} %get-tuple-element.72), channel_id=1, source_target_pairs={{0,1},{1,0},{2,3},{3,2},{4,5},{5,4},{6,7},{7,6},{8,9},{9,8},{10,11... | collective-permute-start | bytes 589832 | tf_op jit(solution)/shard_map/ppermute | solution.py:115
  825.7 317.5 %all-reduce.6.cloned.1.call-start = ((), (), s32[]{:S(2)}) async-start(), calls=%async_computation.14 | async-start | bytes 4456448 | tf_op jit(solution)/shard_map/psum | solution.py:157
  874.5 8.6 copy-start.51
  876.7 9.6 copy-start.35
  876.7 348.8 %all-gather.12.cloned.1.call-start = ((), (), s32[]{:S(2)}) async-start(), calls=%async_computation.9 | async-start | bytes 5242880 | tf_op jit(solution)/shard_map/all_gather | solution.py:179
  878.6 28.2 %collective-permute-start.9 = (f32[1024,128]{0,1:T(8,128)}, f32[1024,128]{0,1:T(8,128)}, u32[]{:S(2)}, u32[]{:S(2)}) collective-permute-start(f32[1024,128]{0,1:T(8,128)} %copy-done.42), channel_id=1, source_target_pairs={{0,3},{1,2},{2,1},{3,0},{4,7},{5,6},{6,5},{7,4},{8,11},{9,10},{10,... | collective-permute-start | bytes 1572872 | tf_op jit(solution)/shard_map/ppermute | solution.py:115
  881.6 66.7 %collective-permute-start.8 = (f32[1024,128]{0,1:T(8,128)}, f32[1024,128]{0,1:T(8,128)}, u32[]{:S(2)}, u32[]{:S(2)}) collective-permute-start(f32[1024,128]{0,1:T(8,128)} %copy-done.42), channel_id=1, source_target_pairs={{0,2},{1,3},{2,0},{3,1},{4,6},{5,7},{6,4},{7,5},{8,10},{9,11},{10,... | collective-permute-start | bytes 1572872 | tf_op jit(solution)/shard_map/ppermute | solution.py:115
  881.6 66.7 %collective-permute-start.7 = (f32[1024,128]{0,1:T(8,128)}, f32[1024,128]{0,1:T(8,128)}, u32[]{:S(2)}, u32[]{:S(2)}) collective-permute-start(f32[1024,128]{0,1:T(8,128)} %copy-done.42), channel_id=1, source_target_pairs={{0,1},{1,0},{2,3},{3,2},{4,5},{5,4},{6,7},{7,6},{8,9},{9,8},{10,11... | collective-permute-start | bytes 1572872 | tf_op jit(solution)/shard_map/ppermute | solution.py:115
  886.2 420.6 %all-gather.14.cloned.1.call-start = ((), (), s32[]{:S(2)}) async-start(), calls=%async_computation.12 | async-start | bytes 5242880 | tf_op jit(solution)/shard_map/all_gather | solution.py:179
  977.2 3.9 collective-permute-start.10
  981.3 42.3 %collective-permute-start.11 = (f32[458752]{0:T(1024)S(1)}, f32[458752]{0:T(1024)S(1)}, u32[]{:S(2)}, u32[]{:S(2)}) collective-permute-start(f32[458752]{0:T(1024)S(1)} %add.258), channel_id=1, source_target_pairs={{0,4},{4,0},{8,12},{12,8},{1,5},{5,1},{9,13},{13,9},{2,6},{6,2},{1... | collective-permute-start | bytes 5505032 | tf_op jit(solution)/shard_map/ppermute | solution.py:137
  1023.8 201.8 %collective-permute-start.12 = (f32[458752]{0:T(1024)S(1)}, f32[458752]{0:T(1024)}, u32[]{:S(2)}, u32[]{:S(2)}) collective-permute-start(f32[458752]{0:T(1024)S(1)} %add.259), channel_id=1, source_target_pairs={{0,8},{4,12},{8,0},{12,4},{1,9},{5,13},{9,1},{13,5},{2,10},{6,14},... | collective-permute-start | bytes 5505032 | tf_op jit(solution)/shard_map/ppermute | solution.py:137
  1143.3 8.0 copy-start.62
  1306.8 7.0 copy-start.1
  (56 other events, 203.3 us)
Sparse Core Ops, SparseCore 0:
  10.8 92.0 all-gather.7
  104.8 85.7 all-gather.5
  255.7 78.8 all-gather.9
  399.4 79.5 reduce-scatter.5
  481.1 81.5 reduce-scatter.3
  808.4 110.7 reduce-scatter.7
  924.4 152.6 all-reduce.3
  1081.0 62.2 all-reduce.5
  1145.4 80.1 all-gather.11
  1227.6 79.2 all-gather.13

commit v12 on v7

--- a/solution.py
+++ b/solution.py
@@ -134,7 +134,10 @@
         step = 1
         while step < axis_count:
             pairs = [(index, index ^ step) for index in range(axis_count)]
-            packed = packed + lax.ppermute(packed, axis_name, pairs)
+            narrow = packed.astype(jnp.bfloat16)
+            packed = narrow.astype(jnp.float32) + lax.ppermute(narrow, axis_name, pairs).astype(
+                jnp.float32
+            )
             step *= 2
     parts, offset = [], 0
     for leaf in leaves:
@@ -359,9 +362,7 @@
         ),
         ("shard", "ctx"),
     )
-    heads_second_total = narrow_psum(
-        heads_second_gradient.reshape(adapter_heads_second.shape), ("shard", "ctx", "tp")
-    )
+    heads_tp_total = narrow_psum(heads_second_gradient.reshape(adapter_heads_second.shape), ("tp",))
     grad_heads_here = (
         matmul_nt(grad_middle_low_here, heads_full)
         + matmul_nt(heads_back_here, heads_first_all_flattened)
@@ -409,9 +410,9 @@
     projection_second_gradient = matmul_tn(first_low, grad_projected)
     attn_back_part = matmul_nt(grad_projected, qkv_full)
     attn_back_low = matmul_nt(grad_projected, projection_second_flattened)
-    low_blocks = jnp.stack(partner_swaps(attn_back_low, "tp", tp_count))
+    low_blocks = jnp.stack(partner_swaps(attn_back_low.astype(jnp.bfloat16), "tp", tp_count))
     low_owners = jnp.bitwise_xor(lax.axis_index("tp"), jnp.arange(tp_count, dtype=jnp.int32))
-    low_total = jnp.sum(jnp.take(low_blocks, low_owners, axis=0), axis=0)
+    low_total = jnp.sum(jnp.take(low_blocks, low_owners, axis=0).astype(jnp.float32), axis=0)
     select_late = lax.optimization_barrier(select)
     qkv_back = (low_total * select_late).astype(jnp.bfloat16)
     grad_qkv_in = matmul_tn(first_act, qkv_back)
@@ -419,9 +420,11 @@
         (
             unflat_in(grad_qkv_in, adapter_tables),
             projection_second_gradient.reshape(adapter_projection_second.shape),
+            heads_tp_total,
         ),
         ("shard", "ctx"),
     )
+    heads_second_total = late_terms[2]
     first_here, first_low_here = scatter_rows((attn_back_part, attn_back_low))
     select_later = lax.optimization_barrier(select_here)
     qkv_back_here = (first_low_here * select_later).astype(jnp.bfloat16)

time: 1300 us -> 1180 us (0.908)
  waiting for transfers between devices: 780 us -> 648 us
    ppermute x9, waiting for transfers between devices: 178 us -> 89.6 us  [partner_swaps(): received.append(lax.ppermute(block, axis_name, pairs))]
    reduce_scatter x3, waiting for transfers between devices: 142 us -> 221 us  [scatter_rows(): lax.psum_scatter(jnp.concatenate(partials, axis=1).astype(jnp.bfloat16),...]
    psum x2, waiting for transfers between devices: 116 us -> 68 us  [narrow_psum(): lax.psum(jax.tree.map(lambda value: value.astype(jnp.bfloat16), values),...]
    ppermute x3, waiting for transfers between devices: 44.5 us -> 0.01 us  [butterfly_sum(): lax.ppermute(narrow, axis_name, pairs).astype(jnp.float32)]
    all_gather x3, waiting for transfers between devices: 202 us -> 185 us  [gather_rows(): lax.all_gather(jnp.concatenate(rows_here, axis=1), 'tp', axis=0, tiled=True)]
    ppermute x3, waiting for transfers between devices: 77.9 us -> 63.8 us  [layer_body(): lax.ppermute(grad_kv[:, offset].astype(jnp.bfloat16), 'ctx', pairs)]
    unnamed x173 -> x185, local copies, waits for them, and re-layouts: 33.7 us -> 35.8 us
  transfers between devices with their start and end apart: 29 -> 29, of which waited for: 20 -> 16; matrix products, arithmetic and copies ran while one was open for 17% -> 20% of each run, Pallas kernels for 0% -> 0%
where the time goes in v12:
time: 1180 us; the launch traced here: 1170 us
  waiting for transfers between devices  648 us (55%)
  matrix products  199 us (17%)
  local copies, waits for them, and re-layouts  133 us (11%)
  other arithmetic  112 us (9%)
  starting transfers between devices  31.3 us (3%)
  blocking collectives  30.1 us (3%)
  between operations  15.2 us (1%)
    reduce_scatter x3, waiting for transfers between devices, scatter_rows(): lax.psum_scatter(jnp.concatenate(partials, axis=1).astype(jnp.bfloat16),...  221 us
    all_gather x3, waiting for transfers between devices, gather_rows(): lax.all_gather(jnp.concatenate(rows_here, axis=1), 'tp', axis=0, tiled=True)  185 us
    ppermute x9, waiting for transfers between devices, partner_swaps(): received.append(lax.ppermute(block, axis_name, pairs))  89.6 us
    psum x2, waiting for transfers between devices, narrow_psum(): lax.psum(jax.tree.map(lambda value: value.astype(jnp.bfloat16), values),...  68 us
    dot_general x12, matrix products, matmul_nt(): lax.dot_general(left_mat, right_mat, (((1,), (1,)), ((), ())), preferred_...  64.6 us
    ppermute x3, waiting for transfers between devices, layer_body(): lax.ppermute(grad_kv[:, offset].astype(jnp.bfloat16), 'ctx', pairs)  63.8 us
    dot_general x12, matrix products, matmul(): return jnp.dot(left_mat, right_mat, preferred_element_type=jnp.float32)  63.7 us
    unnamed x185, local copies, waits for them, and re-layouts  35.8 us
  transfers between devices with their start and end apart: 29, of which 16 were waited for; matrix products, arithmetic and copies ran while one was open for 20% of the time, Pallas kernels for 0%

profile of v12, /device:TPU:0, one launch (start us, length us, event | category | flops | bytes accessed | tf_op | source)
XLA Modules:
  0.0 1168.3 jit_solution(13480395844876726569)
XLA Ops:
  7.3 4.8 copy.86
  25.2 5.3 broadcast_select_fusion.7
  30.4 6.5 pad_maximum_fusion.5
  36.9 8.9 add_convert_fusion.1
  64.0 37.3 %collective-permute-done.3 = bf16[4,256,1024]{1,2,0:T(8,128)(2,1)} collective-permute-done((bf16[4,256,1024]{1,2,0:T(8,128)(2,1)}, bf16[4,256,1024]{1,2,0:T(8,128)(2,1)}, u32[]{:S(2)}, u32[]{:S(2)}) %collective-permute-start.3) | collective-permute-done | bytes 2097184 | tf_op jit(solution)/shard_map/ppermute | solution.py:115
  101.4 44.5 %collective-permute-done.2 = bf16[4,256,1024]{1,2,0:T(8,128)(2,1)} collective-permute-done((bf16[4,256,1024]{1,2,0:T(8,128)(2,1)}, bf16[4,256,1024]{1,2,0:T(8,128)(2,1)}, u32[]{:S(2)}, u32[]{:S(2)}) %collective-permute-start.2) | collective-permute-done | bytes 2097184 | tf_op jit(solution)/shard_map/ppermute | solution.py:115
  146.2 4.1 pad_maximum_fusion.1
  154.2 4.9 slice.136
  160.4 9.4 fusion.73
  169.8 10.5 fusion.74
  180.4 4.8 all-to-all-start
  185.1 6.7 convert.78
  191.8 19.2 %all-to-all-done = bf16[4,256,512]{1,2,0:T(8,128)(2,1)S(1)} async-done(((bf16[4,256,512]{1,2,0:T(8,128)(2,1)}), bf16[4,256,512]{1,2,0:T(8,128)(2,1)S(1)}, u32[]{:S(2)}, u32[]{:S(2)}) %all-to-all-start) | async-done | bytes 1048608 | tf_op jit(solution)/shard_map/all_to_all | solution.py:306
  217.2 6.8 fusion.75
  230.2 4.8 fusion.79
  235.1 4.1 broadcast_select_fusion.1
  243.0 61.8 %all-gather.7.cloned.1.call-done = bf16[1024,2048]{1,0:T(8,128)(2,1)} async-done(((bf16[256,2048]{1,0:T(8,128)(2,1)}), bf16[1024,2048]{1,0:T(8,128)(2,1)}) %all-gather.7.cloned.1.call-update) | async-done | bytes 4194320 | tf_op jit(solution)/shard_map/all_gather | solution.py:182
  308.4 4.5 fusion.78
  313.0 17.0 %multiply_convert_fusion.1 = (bf16[1024,2048]{1,0:T(8,128)(2,1)}, f32[1024,2048]{1,0:T(8,128)}) fusion(f32[1024,2048]{1,0:T(8,128)} %fusion.78, bf16[1024,2048]{1,0:T(8,128)(2,1)S(1)} %copy-done.22, bf16[1024,2048]{1,0:T(8,128)(2,1)} %get-tuple-element.49, bf16[1024,2048]{1,0:T(8,128)(2,1)} %get-tuple-element.48), kind=kOutput, calls=%fused_computation.24 | convolution fusion | flops 8627683328 | bytes 33554432 | tf_op jit(solution)/shard_map/dot_general | solution.py:43
  330.0 21.4 %fusion.4 = bf16[1024,2048]{1,0:T(8,128)(2,1)} fusion(f32[1024,2048]{1,0:T(8,128)} %get-tuple-element.76, f32[1024,2048]{1,0:T(8,128)} %fusion.79, bf16[1024,2048]{1,0:T(8,128)(2,1)S(1)} %bitcast.192, bf16[2048,1024]{1,0:T(8,128)(2,1)} %get-tuple-element.47, bf16[2048,1024]{1,0:T(8,128)(2,1)} %get-tuple-element.46), kind=kOutput, calls=%fused_computation.15 | convolution fusion | flops 8659140608 | bytes 33554432 | tf_op jit(solution)/shard_map/dot_general | solution.py:53
  355.1 12.0 %fusion.24 = bf16[1024,2048]{1,0:T(8,128)(2,1)S(1)} fusion(bf16[1024,2048]{1,0:T(8,128)(2,1)} %fusion.4, bf16[1024,2048]{1,0:T(8,128)(2,1)} %get-tuple-element.49, bf16[1024,2048]{1,0:T(8,128)(2,1)S(1)} %copy-done.32), kind=kOutput, calls=%fused_computation.58 | convolution fusion | flops 8608808960 | bytes 16777216 | tf_op jit(solution)/shard_map/dot_general | solution.py:53
  374.5 11.7 fusion.25
  388.8 60.6 %reduce-scatter.6.cloned.1.call-done = bf16[256,2176]{1,0:T(8,128)(2,1)} async-done(((bf16[1024,2176]{1,0:T(8,128)(2,1)}), bf16[256,2176]{1,0:T(8,128)(2,1)}) %reduce-scatter.6.cloned.1.call-update) | async-done | bytes 1114128 | tf_op jit(solution)/shard_map/reduce_scatter | solution.py:171
  452.1 81.0 %reduce-scatter.4.cloned.1.call-done = bf16[256,2176]{1,0:T(8,128)(2,1)} async-done(((bf16[1024,2176]{1,0:T(8,128)(2,1)}), bf16[256,2176]{1,0:T(8,128)(2,1)}) %reduce-scatter.4.cloned.1.call-update) | async-done | bytes 1114128 | tf_op jit(solution)/shard_map/reduce_scatter | solution.py:171
  549.3 30.1 %all_to_all.29 = bf16[256,4,512]{0,2,1:T(8,128)(2,1)S(1)} all-to-all(bf16[256,4,512]{0,2,1:T(8,128)(2,1)} %bitcast.213), channel_id=1, replica_groups=mesh['shard'=2,'ctx'=4,'tp'=4] {'tp'}, dimensions={1} | all-to-all | bytes 2097152 | tf_op jit(solution)/shard_map/all_to_all | solution.py:370
  582.9 10.4 fusion.26
  593.2 9.2 multiply_convert_fusion
  605.7 4.9 multiply_bitcast_fusion
  610.7 10.5 reshape.472
  621.2 9.9 copy.103
  631.1 10.5 reshape.473
  641.6 9.9 copy.104
  651.6 6.5 fusion
  676.8 8.6 fusion.39
  689.5 21.2 %collective-permute-done.9 = bf16[4,256,1024]{2,1,0:T(8,128)(2,1)} collective-permute-done((bf16[4,256,1024]{2,1,0:T(8,128)(2,1)}, bf16[4,256,1024]{2,1,0:T(8,128)(2,1)}, u32[]{:S(2)}, u32[]{:S(2)}) %collective-permute-start.9) | collective-permute-done | bytes 2097184 | tf_op jit(solution)/shard_map/ppermute | solution.py:397
  710.7 42.6 %collective-permute-done.8 = bf16[4,256,1024]{2,1,0:T(8,128)(2,1)} collective-permute-done((bf16[4,256,1024]{2,1,0:T(8,128)(2,1)}, bf16[4,256,1024]{2,1,0:T(8,128)(2,1)}, u32[]{:S(2)}, u32[]{:S(2)}) %collective-permute-start.8) | collective-permute-done | bytes 2097184 | tf_op jit(solution)/shard_map/ppermute | solution.py:397
  753.4 4.8 fusion.18
  771.3 9.2 collective-permute-start.16
  780.5 4.3 collective-permute-done.11
  797.5 5.1 reshape.477
  832.1 68.0 %all-reduce.6.cloned.1.call-done = (bf16[8,512,16]{1,2,0:T(8,128)(2,1)}, bf16[8,2048,16]{1,2,0:T(8,128)(2,1)}, bf16[8,16,2048]{2,1,0:T(8,128)(2,1)}, bf16[8,2048,16]{1,2,0:T(8,128)(2,1)}, bf16[8,16,2048]{2,1,0:T(8,128)(2,1)}) async-done(((bf16[8,512,16]{1,2,0:T(8,128)(2,1)}, bf16[8,2048,16]{1,2,0:T(8,128)(2,1)}, bf16[8,16,2048]{2,1,0:T(8,128)(2,1)}, bf16[8,2048,16]{1,2,0:T(8,128)(2,1)}, ...) | async-done | bytes 2228240 | tf_op jit(solution)/shard_map/psum | solution.py:160
  912.2 8.9 convolution_convert_fusion
  923.8 58.6 %all-gather.9.cloned.1.call-done = bf16[1024,2048]{1,0:T(8,128)(2,1)} async-done(((bf16[256,2048]{1,0:T(8,128)(2,1)}), bf16[1024,2048]{1,0:T(8,128)(2,1)}) %all-gather.9.cloned.1.call-update) | async-done | bytes 4194320 | tf_op jit(solution)/shard_map/all_gather | solution.py:182
  984.6 79.7 %reduce-scatter.8.cloned.1.call-done = bf16[256,2176]{1,0:T(8,128)(2,1)} async-done(((bf16[1024,2176]{1,0:T(8,128)(2,1)}), bf16[256,2176]{1,0:T(8,128)(2,1)}) %reduce-scatter.8.cloned.1.call-update) | async-done | bytes 1114128 | tf_op jit(solution)/shard_map/reduce_scatter | solution.py:171
  1074.7 6.0 slice.120
  1080.7 6.4 copy.111
  1089.7 64.9 %all-gather.11.cloned.1.call-done = bf16[1024,2048]{1,0:T(8,128)(2,1)} async-done(((bf16[256,2048]{1,0:T(8,128)(2,1)}), bf16[1024,2048]{1,0:T(8,128)(2,1)}) %all-gather.11.cloned.1.call-update) | async-done | bytes 4194320 | tf_op jit(solution)/shard_map/all_gather | solution.py:182
  1154.6 4.9 copy.137
  (353 shorter events, 205.4 us)
Async XLA Ops:
  7.2 301.2 %copy-start = (bf16[8,16,2048]{2,1,0:T(8,128)(2,1)S(1)}, bf16[8,16,2048]{2,1,0:T(8,128)(2,1)}, u32[]{:S(2)}) copy-start(bf16[8,16,2048]{2,1,0:T(8,128)(2,1)} %param.37) | copy-start | bytes 1572868
  7.2 146.9 %all-gather.5.cloned.1.call-start = ((), (), s32[]{:S(2)}) async-start(), calls=%async_computation.5 | async-start | bytes 5898240 | tf_op jit(solution)/shard_map/all_gather | solution.py:237
  12.0 11.5 collective-permute-start
  21.2 15.7 %copy-start.10 = (bf16[4,256,2048]{2,1,0:T(8,128)(2,1)}, bf16[4,256,2048]{2,1,0:T(8,128)(2,1)S(1)}, u32[]{:S(2)}) copy-start(bf16[4,256,2048]{2,1,0:T(8,128)(2,1)S(1)} %add_convert_fusion) | copy-start | bytes 12582916
  49.4 9.0 copy-start.19
  51.0 50.3 %collective-permute-start.3 = (bf16[4,256,1024]{1,2,0:T(8,128)(2,1)}, bf16[4,256,1024]{1,2,0:T(8,128)(2,1)}, u32[]{:S(2)}, u32[]{:S(2)}) collective-permute-start(bf16[4,256,1024]{1,2,0:T(8,128)(2,1)} %pad_maximum_fusion.32), channel_id=1, source_target_pairs={{0,12},{4,8},{8,4},{12,0},{1,13},{5,9},{9,5},{13,1},{2,14},{6,10},... | collective-permute-start | bytes 6291464 | tf_op jit(solution)/shard_map/ppermute | solution.py:115
  54.5 91.3 %collective-permute-start.2 = (bf16[4,256,1024]{1,2,0:T(8,128)(2,1)}, bf16[4,256,1024]{1,2,0:T(8,128)(2,1)}, u32[]{:S(2)}, u32[]{:S(2)}) collective-permute-start(bf16[4,256,1024]{1,2,0:T(8,128)(2,1)} %pad_maximum_fusion.32), channel_id=1, source_target_pairs={{0,8},{4,12},{8,0},{12,4},{1,9},{5,13},{9,1},{13,5},{2,10},{6,14},... | collective-permute-start | bytes 6291464 | tf_op jit(solution)/shard_map/ppermute | solution.py:115
  55.0 91.1 %collective-permute-start.1 = (bf16[4,256,1024]{1,2,0:T(8,128)(2,1)}, bf16[4,256,1024]{1,2,0:T(8,128)(2,1)}, u32[]{:S(2)}, u32[]{:S(2)}) collective-permute-start(bf16[4,256,1024]{1,2,0:T(8,128)(2,1)} %pad_maximum_fusion.32), channel_id=1, source_target_pairs={{0,4},{4,0},{8,12},{12,8},{1,5},{5,1},{9,13},{13,9},{2,6},{6,2},{1... | collective-permute-start | bytes 6291464 | tf_op jit(solution)/shard_map/ppermute | solution.py:115
  64.0 95.1 %copy-start.15 = (bf16[4,256,4,128]{1,3,2,0:T(8,128)(2,1)}, bf16[4,256,4,128]{1,3,2,0:T(8,128)(2,1)S(1)}, u32[]{:S(2)}) copy-start(bf16[4,256,4,128]{1,3,2,0:T(8,128)(2,1)S(1)} %copy.102) | copy-start | bytes 3145732
  159.1 54.2 %collective-permute-start.4 = (bf16[2048,1024]{1,0:T(8,128)(2,1)}, bf16[2048,1024]{1,0:T(8,128)(2,1)}, u32[]{:S(2)}, u32[]{:S(2)}) collective-permute-start(bf16[2048,1024]{1,0:T(8,128)(2,1)} %slice.136), channel_id=1, source_target_pairs={{0,16},{16,0},{1,17},{17,1},{2,18},{18,2},{3,19},{19,3},{4,20},{20... | collective-permute-start | bytes 12582920 | tf_op jit(solution)/shard_map/ppermute | solution.py:122
  160.4 9.4 copy-start.5
  169.8 10.5 copy-start.70
  180.4 30.6 %all-to-all-start = ((bf16[4,256,512]{1,2,0:T(8,128)(2,1)}), bf16[4,256,512]{1,2,0:T(8,128)(2,1)S(1)}, u32[]{:S(2)}, u32[]{:S(2)}) async-start(bf16[4,256,512]{1,2,0:T(8,128)(2,1)} %bitcast.12), calls=%async_computation | async-start | bytes 2097152 | tf_op jit(solution)/shard_map/all_to_all | solution.py:306
  185.1 119.7 %all-gather.7.cloned.1.call-start = ((), (), s32[]{:S(2)}) async-start(), calls=%async_computation.6 | async-start | bytes 5242880 | tf_op jit(solution)/shard_map/all_gather | solution.py:182
  185.1 27.8 %copy-start.43 = (bf16[8,16,2048]{2,1,0:T(8,128)(2,1)S(1)}, bf16[8,16,2048]{2,1,0:T(8,128)(2,1)}, u32[]{:S(2)}) copy-start(bf16[8,16,2048]{2,1,0:T(8,128)(2,1)} %param.35) | copy-start | bytes 1572868
  225.8 223.5 %reduce-scatter.6.cloned.1.call-start = ((), (), s32[]{:S(2)}) async-start(), calls=%async_computation.9 | async-start | bytes 5570560 | tf_op jit(solution)/shard_map/reduce_scatter | solution.py:171
  226.1 9.0 collective-permute-start.5
  226.1 13.4 %collective-permute-start.6 = (bf16[2048,1024]{1,0:T(8,128)(2,1)}, bf16[2048,1024]{1,0:T(8,128)(2,1)S(1)}, u32[]{:S(2)}, u32[]{:S(2)}) collective-permute-start(bf16[2048,1024]{1,0:T(8,128)(2,1)} %param.31), channel_id=1, source_target_pairs={{0,16},{16,0},{1,17},{17,1},{2,18},{18,2},{3,19},{19,3},{4,20},{20... | collective-permute-start | bytes 12582920 | tf_op jit(solution)/shard_map/ppermute | solution.py:122
  313.0 17.0 %copy-start.6 = (bf16[4,256,2048]{2,1,0:T(8,128)(2,1)S(1)}, bf16[4,256,2048]{2,1,0:T(8,128)(2,1)}, u32[]{:S(2)}) copy-start(bf16[4,256,2048]{2,1,0:T(8,128)(2,1)} %param.21) | copy-start | bytes 12582916
  369.7 163.4 %reduce-scatter.4.cloned.1.call-start = ((), (), s32[]{:S(2)}) async-start(), calls=%async_computation.7 | async-start | bytes 5570560 | tf_op jit(solution)/shard_map/reduce_scatter | solution.py:171
  388.7 147.7 %copy-start.41 = (bf16[8,2048,16]{1,2,0:T(8,128)(2,1)S(1)}, bf16[8,2048,16]{1,2,0:T(8,128)(2,1)}, u32[]{:S(2)}) copy-start(bf16[8,2048,16]{1,2,0:T(8,128)(2,1)} %param.36) | copy-start | bytes 1572868
  388.7 416.5 %all-reduce.4.cloned.1.call-start = ((), (), s32[]{:S(2)}) async-start(), calls=%async_computation.12 | async-start | bytes 1048576 | tf_op jit(solution)/shard_map/psum | solution.py:160
  547.0 34.3 %copy-start.71 = (f32[4,4,256]{2,1,0:T(4,128)S(1)}, f32[4,4,256]{2,1,0:T(4,128)}, u32[]{:S(2)}) copy-start(f32[4,4,256]{2,1,0:T(4,128)} %copy-done.70) | copy-start | bytes 49156
  593.2 12.5 %copy-start.16 = (bf16[4,256,4,128]{1,3,2,0:T(8,128)(2,1)S(1)}, bf16[4,256,4,128]{1,3,2,0:T(8,128)(2,1)}, u32[]{:S(2)}) copy-start(bf16[4,256,4,128]{1,3,2,0:T(8,128)(2,1)} %copy-done.15) | copy-start | bytes 3145732
  661.0 49.8 %collective-permute-start.9 = (bf16[4,256,1024]{2,1,0:T(8,128)(2,1)}, bf16[4,256,1024]{2,1,0:T(8,128)(2,1)}, u32[]{:S(2)}, u32[]{:S(2)}) collective-permute-start(bf16[4,256,1024]{2,1,0:T(8,128)(2,1)} %get-tuple-element.44), channel_id=1, source_target_pairs={{0,12},{4,8},{8,4},{12,0},{1,13},{5,9},{9,5},{13,1},{2,14},{6,10},... | collective-permute-start | bytes 6291464 | tf_op jit(solution)/shard_map/ppermute | solution.py:397
  663.4 90.0 %collective-permute-start.8 = (bf16[4,256,1024]{2,1,0:T(8,128)(2,1)}, bf16[4,256,1024]{2,1,0:T(8,128)(2,1)}, u32[]{:S(2)}, u32[]{:S(2)}) collective-permute-start(bf16[4,256,1024]{2,1,0:T(8,128)(2,1)} %get-tuple-element.45), channel_id=1, source_target_pairs={{0,8},{4,12},{8,0},{12,4},{1,9},{5,13},{9,1},{13,5},{2,10},{6,14},... | collective-permute-start | bytes 6291464 | tf_op jit(solution)/shard_map/ppermute | solution.py:397
  663.9 89.5 %collective-permute-start.7 = (bf16[4,256,1024]{2,1,0:T(8,128)(2,1)}, bf16[4,256,1024]{2,1,0:T(8,128)(2,1)}, u32[]{:S(2)}, u32[]{:S(2)}) collective-permute-start(bf16[4,256,1024]{2,1,0:T(8,128)(2,1)} %get-tuple-element.43), channel_id=1, source_target_pairs={{0,4},{4,0},{8,12},{12,8},{1,5},{5,1},{9,13},{13,9},{2,6},{6,2},{1... | collective-permute-start | bytes 6291464 | tf_op jit(solution)/shard_map/ppermute | solution.py:397
  673.8 137.0 %collective-permute-start.18 = (bf16[256,384]{1,0:T(8,128)(2,1)}, bf16[256,384]{1,0:T(8,128)(2,1)}, u32[]{:S(2)}, u32[]{:S(2)}) collective-permute-start(bf16[256,384]{1,0:T(8,128)(2,1)} %get-tuple-element.64), channel_id=1, source_target_pairs={{0,3},{1,2},{2,1},{3,0},{4,7},{5,6},{6,5},{7,4},{8,11},{9,10},{10,... | collective-permute-start | bytes 589832 | tf_op jit(solution)/shard_map/ppermute | solution.py:115
  675.3 135.5 %collective-permute-start.17 = (bf16[256,384]{1,0:T(8,128)(2,1)}, bf16[256,384]{1,0:T(8,128)(2,1)}, u32[]{:S(2)}, u32[]{:S(2)}) collective-permute-start(bf16[256,384]{1,0:T(8,128)(2,1)} %get-tuple-element.64), channel_id=1, source_target_pairs={{0,2},{1,3},{2,0},{3,1},{4,6},{5,7},{6,4},{7,5},{8,10},{9,11},{10,... | collective-permute-start | bytes 589832 | tf_op jit(solution)/shard_map/ppermute | solution.py:115
  676.8 223.3 %all-reduce.6.cloned.1.call-start = ((), (), s32[]{:S(2)}) async-start(), calls=%async_computation.13 | async-start | bytes 4456448 | tf_op jit(solution)/shard_map/psum | solution.py:160
  689.5 75.0 %copy-start.53 = (bf16[128,8,4,128]{3,1,2,0:T(8,128)(2,1)}, bf16[128,8,4,128]{3,1,2,0:T(8,128)(2,1)S(1)}, u32[]{:S(2)}) copy-start(bf16[128,8,4,128]{3,1,2,0:T(8,128)(2,1)S(1)} %copy.126) | copy-start | bytes 3145732
  760.1 24.6 %copy-start.59 = (bf16[1024,128]{1,0:T(8,128)(2,1)}, bf16[1024,128]{1,0:T(8,128)(2,1)S(1)}, u32[]{:S(2)}) copy-start(bf16[1024,128]{1,0:T(8,128)(2,1)S(1)} %convolution_convert_fusion.8) | copy-start | bytes 786436
  760.1 11.2 collective-permute-start.12
  762.4 22.4 %collective-permute-start.11 = (bf16[1024,128]{1,0:T(8,128)(2,1)S(1)}, bf16[1024,128]{1,0:T(8,128)(2,1)}, u32[]{:S(2)}, u32[]{:S(2)}) collective-permute-start(bf16[1024,128]{1,0:T(8,128)(2,1)S(1)} %convolution_convert_fusion.8), channel_id=1, source_target_pairs={{0,2},{1,3},{2,0},{3,1},{4,6},{5,7},{6,4},{7,5},{8,10},{9,11},{10,... | collective-permute-start | bytes 786440 | tf_op jit(solution)/shard_map/ppermute | solution.py:115
  762.4 22.4 %collective-permute-start.10 = (bf16[1024,128]{1,0:T(8,128)(2,1)S(1)}, bf16[1024,128]{1,0:T(8,128)(2,1)}, u32[]{:S(2)}, u32[]{:S(2)}) collective-permute-start(bf16[1024,128]{1,0:T(8,128)(2,1)S(1)} %convolution_convert_fusion.8), channel_id=1, source_target_pairs={{0,1},{1,0},{2,3},{3,2},{4,5},{5,4},{6,7},{7,6},{8,9},{9,8},{10,11... | collective-permute-start | bytes 786440 | tf_op jit(solution)/shard_map/ppermute | solution.py:115
  771.3 39.5 %collective-permute-start.16 = (bf16[256,384]{1,0:T(8,128)(2,1)}, bf16[256,384]{1,0:T(8,128)(2,1)}, u32[]{:S(2)}, u32[]{:S(2)}) collective-permute-start(bf16[256,384]{1,0:T(8,128)(2,1)} %get-tuple-element.64), channel_id=1, source_target_pairs={{0,1},{1,0},{2,3},{3,2},{4,5},{5,4},{6,7},{7,6},{8,9},{9,8},{10,11... | collective-permute-start | bytes 589832 | tf_op jit(solution)/shard_map/ppermute | solution.py:115
  797.5 9.6 copy-start.38
  807.1 13.8 %collective-permute-start.13 = (bf16[720896]{0:T(1024)(128)(2,1)}, bf16[720896]{0:T(1024)(128)(2,1)}, u32[]{:S(2)}, u32[]{:S(2)}) collective-permute-start(bf16[720896]{0:T(1024)(128)(2,1)} %constant_dynamic-update-slice_fusion), channel_id=1, source_target_pairs={{0,16},{16,0},{1,17},{17,1},{2,18},{18,2},{3,19},{19,3},{4,20},{20... | collective-permute-start | bytes 4325384 | tf_op jit(solution)/shard_map/ppermute | solution.py:138
  824.1 85.3 %collective-permute-start.14 = (bf16[720896]{0:T(1024)(128)(2,1)}, bf16[720896]{0:T(1024)(128)(2,1)}, u32[]{:S(2)}, u32[]{:S(2)}) collective-permute-start(bf16[720896]{0:T(1024)(128)(2,1)} %add_convert_fusion.3), channel_id=1, source_target_pairs={{0,4},{4,0},{8,12},{12,8},{1,5},{5,1},{9,13},{13,9},{2,6},{6,2},{1... | collective-permute-start | bytes 4325384 | tf_op jit(solution)/shard_map/ppermute | solution.py:138
  827.2 155.2 %all-gather.9.cloned.1.call-start = ((), (), s32[]{:S(2)}) async-start(), calls=%async_computation.8 | async-start | bytes 5242880 | tf_op jit(solution)/shard_map/all_gather | solution.py:182
  832.0 232.2 %reduce-scatter.8.cloned.1.call-start = ((), (), s32[]{:S(2)}) async-start(), calls=%async_computation.10 | async-start | bytes 5570560 | tf_op jit(solution)/shard_map/reduce_scatter | solution.py:171
  911.6 9.5 copy-start.24
  911.7 9.5 copy-start.60
  911.7 70.7 %collective-permute-start.15 = (bf16[720896]{0:T(1024)(128)(2,1)S(1)}, bf16[720896]{0:T(1024)(128)(2,1)}, u32[]{:S(2)}, u32[]{:S(2)}) collective-permute-start(bf16[720896]{0:T(1024)(128)(2,1)S(1)} %add_convert_fusion.2), channel_id=1, source_target_pairs={{0,8},{4,12},{8,0},{12,4},{1,9},{5,13},{9,1},{13,5},{2,10},{6,14},... | collective-permute-start | bytes 4325384 | tf_op jit(solution)/shard_map/ppermute | solution.py:138
  923.8 230.9 %all-gather.11.cloned.1.call-start = ((), (), s32[]{:S(2)}) async-start(), calls=%async_computation.11 | async-start | bytes 5242880 | tf_op jit(solution)/shard_map/all_gather | solution.py:182
  982.4 83.3 %copy-start.46 = (bf16[8,2048,16]{1,2,0:T(8,128)(2,1)S(1)}, bf16[8,2048,16]{1,2,0:T(8,128)(2,1)}, u32[]{:S(2)}) copy-start(bf16[8,2048,16]{1,2,0:T(8,128)(2,1)} %param.32) | copy-start | bytes 1572868
  982.4 83.3 %copy-start.79 = (f32[2048]{0:T(1024)S(1)}, f32[2048]{0:T(1024)}, u32[]{:S(2)}) copy-start(f32[2048]{0:T(1024)} %param.24) | copy-start | bytes 24580
  984.5 88.7 %copy-start.14 = (f32[720896]{0:T(1024)}, f32[720896]{0:T(1024)S(1)}, u32[]{:S(2)}) copy-start(f32[720896]{0:T(1024)S(1)} %convert_add_fusion) | copy-start | bytes 8650756
  (69 other events, 340.7 us)
Sparse Core Ops, SparseCore 0:
  13.9 91.7 all-gather.4
  225.9 78.8 all-gather.6
  369.8 79.5 reduce-scatter.5
  451.5 81.5 reduce-scatter.3
  676.9 41.0 all-reduce.3
  827.3 72.7 all-reduce.5
  902.2 80.1 all-gather.8
  984.7 79.5 reduce-scatter.7
  1073.4 81.2 all-gather.10

commit v13 on v12

--- a/solution.py
+++ b/solution.py
@@ -362,7 +362,9 @@
         ),
         ("shard", "ctx"),
     )
-    heads_tp_total = narrow_psum(heads_second_gradient.reshape(adapter_heads_second.shape), ("tp",))
+    heads_second_total = narrow_psum(
+        heads_second_gradient.reshape(adapter_heads_second.shape), ("shard", "ctx", "tp")
+    )
     grad_heads_here = (
         matmul_nt(grad_middle_low_here, heads_full)
         + matmul_nt(heads_back_here, heads_first_all_flattened)
@@ -420,11 +422,9 @@
         (
             unflat_in(grad_qkv_in, adapter_tables),
             projection_second_gradient.reshape(adapter_projection_second.shape),
-            heads_tp_total,
         ),
         ("shard", "ctx"),
     )
-    heads_second_total = late_terms[2]
     first_here, first_low_here = scatter_rows((attn_back_part, attn_back_low))
     select_later = lax.optimization_barrier(select_here)
     qkv_back_here = (first_low_here * select_later).astype(jnp.bfloat16)

time: 1180 us -> 1120 us (0.949)
  blocking collectives: 30.1 us -> 0 us
  waiting for transfers between devices: 648 us -> 633 us
    psum x2, waiting for transfers between devices: 68 us -> 0.02 us  [narrow_psum(): lax.psum(jax.tree.map(lambda value: value.astype(jnp.bfloat16), values),...]
    ppermute x9, waiting for transfers between devices: 89.6 us -> 128 us  [partner_swaps(): received.append(lax.ppermute(block, axis_name, pairs))]
    all_to_all x1 -> x0, blocking collectives: 30.1 us -> none  [layer_body(): grad_heads = lax.all_to_all(grad_heads_here, 'tp', 1, 0, tiled=True)]
    ppermute x3, waiting for transfers between devices: 63.8 us -> 80.1 us  [layer_body(): lax.ppermute(grad_kv[:, offset].astype(jnp.bfloat16), 'ctx', pairs)]
    all_gather x3, waiting for transfers between devices: 185 us -> 172 us  [gather_rows(): lax.all_gather(jnp.concatenate(rows_here, axis=1), 'tp', axis=0, tiled=True)]
    unnamed x185 -> x177, local copies, waits for them, and re-layouts: 35.8 us -> 34.7 us
  transfers between devices with their start and end apart: 29 -> 30, of which waited for: 16 -> 18; matrix products, arithmetic and copies ran while one was open for 20% -> 28% of each run, Pallas kernels for 0% -> 0%
where the time goes in v13:
time: 1120 us; the launch traced here: 1110 us
  waiting for transfers between devices  633 us (57%)
  matrix products  198 us (18%)
  local copies, waits for them, and re-layouts  127 us (11%)
  other arithmetic  110 us (10%)
  starting transfers between devices  30.4 us (3%)
  between operations  15.5 us (1%)
    reduce_scatter x3, waiting for transfers between devices, scatter_rows(): lax.psum_scatter(jnp.concatenate(partials, axis=1).astype(jnp.bfloat16),...  224 us
    all_gather x3, waiting for transfers between devices, gather_rows(): lax.all_gather(jnp.concatenate(rows_here, axis=1), 'tp', axis=0, tiled=True)  172 us
    ppermute x9, waiting for transfers between devices, partner_swaps(): received.append(lax.ppermute(block, axis_name, pairs))  128 us
    ppermute x3, waiting for transfers between devices, layer_body(): lax.ppermute(grad_kv[:, offset].astype(jnp.bfloat16), 'ctx', pairs)  80.1 us
    dot_general x12, matrix products, matmul_nt(): lax.dot_general(left_mat, right_mat, (((1,), (1,)), ((), ())), preferred_...  63.9 us
    dot_general x12, matrix products, matmul(): return jnp.dot(left_mat, right_mat, preferred_element_type=jnp.float32)  62.9 us
    unnamed x177, local copies, waits for them, and re-layouts  34.7 us
  transfers between devices with their start and end apart: 30, of which 18 were waited for; matrix products, arithmetic and copies ran while one was open for 28% of the time, Pallas kernels for 0%

profile of v13, /device:TPU:0, one launch (start us, length us, event | category | flops | bytes accessed | tf_op | source)
XLA Modules:
  0.0 1113.0 jit_solution(9663657706377463239)
XLA Ops:
  7.3 4.8 copy.86
  25.2 5.3 broadcast_select_fusion.7
  30.4 6.5 pad_maximum_fusion.5
  36.9 8.9 add_convert_fusion.1
  64.1 37.3 %collective-permute-done.3 = bf16[4,256,1024]{1,2,0:T(8,128)(2,1)} collective-permute-done((bf16[4,256,1024]{1,2,0:T(8,128)(2,1)}, bf16[4,256,1024]{1,2,0:T(8,128)(2,1)}, u32[]{:S(2)}, u32[]{:S(2)}) %collective-permute-start.3) | collective-permute-done | bytes 2097184 | tf_op jit(solution)/shard_map/ppermute | solution.py:115
  101.3 44.5 %collective-permute-done.2 = bf16[4,256,1024]{1,2,0:T(8,128)(2,1)} collective-permute-done((bf16[4,256,1024]{1,2,0:T(8,128)(2,1)}, bf16[4,256,1024]{1,2,0:T(8,128)(2,1)}, u32[]{:S(2)}, u32[]{:S(2)}) %collective-permute-start.2) | collective-permute-done | bytes 2097184 | tf_op jit(solution)/shard_map/ppermute | solution.py:115
  154.1 4.9 slice.121
  160.4 9.4 fusion.71
  169.8 10.5 fusion.72
  180.3 4.8 all-to-all-start
  185.1 6.7 convert.76
  191.8 19.2 %all-to-all-done = bf16[4,256,512]{1,2,0:T(8,128)(2,1)S(1)} async-done(((bf16[4,256,512]{1,2,0:T(8,128)(2,1)}), bf16[4,256,512]{1,2,0:T(8,128)(2,1)S(1)}, u32[]{:S(2)}, u32[]{:S(2)}) %all-to-all-start) | async-done | bytes 1048608 | tf_op jit(solution)/shard_map/all_to_all | solution.py:306
  217.1 6.8 fusion.73
  230.4 4.8 fusion.77
  243.1 61.7 %all-gather.7.cloned.1.call-done = bf16[1024,2048]{1,0:T(8,128)(2,1)} async-done(((bf16[256,2048]{1,0:T(8,128)(2,1)}), bf16[1024,2048]{1,0:T(8,128)(2,1)}) %all-gather.7.cloned.1.call-update) | async-done | bytes 4194320 | tf_op jit(solution)/shard_map/all_gather | solution.py:182
  308.4 4.5 fusion.76
  312.9 16.9 %multiply_convert_fusion.1 = (bf16[1024,2048]{1,0:T(8,128)(2,1)}, f32[1024,2048]{1,0:T(8,128)}) fusion(f32[1024,2048]{1,0:T(8,128)} %fusion.76, bf16[1024,2048]{1,0:T(8,128)(2,1)S(1)} %copy-done.22, bf16[1024,2048]{1,0:T(8,128)(2,1)} %get-tuple-element.49, bf16[1024,2048]{1,0:T(8,128)(2,1)} %get-tuple-element.48), kind=kOutput, calls=%fused_computation.24 | convolution fusion | flops 8627683328 | bytes 33554432 | tf_op jit(solution)/shard_map/dot_general | solution.py:43
  329.8 21.2 %fusion.4 = bf16[1024,2048]{1,0:T(8,128)(2,1)} fusion(f32[1024,2048]{1,0:T(8,128)} %get-tuple-element.74, f32[1024,2048]{1,0:T(8,128)} %fusion.77, bf16[1024,2048]{1,0:T(8,128)(2,1)S(1)} %bitcast.190, bf16[2048,1024]{1,0:T(8,128)(2,1)} %get-tuple-element.47, bf16[2048,1024]{1,0:T(8,128)(2,1)} %get-tuple-element.46), kind=kOutput, calls=%fused_computation.15 | convolution fusion | flops 8659140608 | bytes 33554432 | tf_op jit(solution)/shard_map/dot_general | solution.py:53
  354.6 12.2 %fusion.24 = bf16[1024,2048]{1,0:T(8,128)(2,1)S(1)} fusion(bf16[1024,2048]{1,0:T(8,128)(2,1)} %fusion.4, bf16[1024,2048]{1,0:T(8,128)(2,1)} %get-tuple-element.49, bf16[1024,2048]{1,0:T(8,128)(2,1)S(1)} %copy-done.30), kind=kOutput, calls=%fused_computation.58 | convolution fusion | flops 8608808960 | bytes 16777216 | tf_op jit(solution)/shard_map/dot_general | solution.py:53
  374.3 11.7 %fusion.25 = bf16[1024,2048]{1,0:T(8,128)(2,1)S(1)} fusion(bf16[1024,2048]{1,0:T(8,128)(2,1)} %get-tuple-element.73, bf16[2048,1024]{1,0:T(8,128)(2,1)} %get-tuple-element.47, bf16[2048,1024]{1,0:T(8,128)(2,1)S(1)} %copy-done.29), kind=kOutput, calls=%fused_computation.59 | convolution fusion | flops 8608808960 | bytes 16777216 | tf_op jit(solution)/shard_map/dot_general | solution.py:43
  388.5 60.7 %reduce-scatter.6.cloned.1.call-done = bf16[256,2176]{1,0:T(8,128)(2,1)} async-done(((bf16[1024,2176]{1,0:T(8,128)(2,1)}), bf16[256,2176]{1,0:T(8,128)(2,1)}) %reduce-scatter.6.cloned.1.call-update) | async-done | bytes 1114128 | tf_op jit(solution)/shard_map/reduce_scatter | solution.py:171
  451.9 81.0 %reduce-scatter.4.cloned.1.call-done = bf16[256,2176]{1,0:T(8,128)(2,1)} async-done(((bf16[1024,2176]{1,0:T(8,128)(2,1)}), bf16[256,2176]{1,0:T(8,128)(2,1)}) %reduce-scatter.4.cloned.1.call-update) | async-done | bytes 1114128 | tf_op jit(solution)/shard_map/reduce_scatter | solution.py:171
  549.3 4.3 all-to-all-start.1
  570.4 9.9 collective-permute-done.18
  580.2 18.5 %collective-permute-done.17 = bf16[256,384]{1,0:T(8,128)(2,1)S(1)} collective-permute-done((bf16[256,384]{1,0:T(8,128)(2,1)}, bf16[256,384]{1,0:T(8,128)(2,1)S(1)}, u32[]{:S(2)}, u32[]{:S(2)}) %collective-permute-start.17) | collective-permute-done | bytes 196640 | tf_op jit(solution)/shard_map/ppermute | solution.py:115
  607.4 10.4 fusion.26
  617.8 9.2 multiply_convert_fusion
  630.4 4.9 multiply_bitcast_fusion
  635.3 10.6 reshape.459
  645.9 9.9 copy.103
  655.8 10.6 reshape.460
  666.3 9.9 copy.104
  676.3 6.6 fusion
  698.5 8.6 fusion.39
  711.0 24.8 %collective-permute-done.9 = bf16[4,256,1024]{2,1,0:T(8,128)(2,1)} collective-permute-done((bf16[4,256,1024]{2,1,0:T(8,128)(2,1)}, bf16[4,256,1024]{2,1,0:T(8,128)(2,1)}, u32[]{:S(2)}, u32[]{:S(2)}) %collective-permute-start.9) | collective-permute-done | bytes 2097184 | tf_op jit(solution)/shard_map/ppermute | solution.py:399
  735.8 55.2 %collective-permute-done.8 = bf16[4,256,1024]{2,1,0:T(8,128)(2,1)} collective-permute-done((bf16[4,256,1024]{2,1,0:T(8,128)(2,1)}, bf16[4,256,1024]{2,1,0:T(8,128)(2,1)}, u32[]{:S(2)}, u32[]{:S(2)}) %collective-permute-start.8) | collective-permute-done | bytes 2097184 | tf_op jit(solution)/shard_map/ppermute | solution.py:399
  791.1 5.0 fusion.18
  804.3 5.0 collective-permute-done.12
  809.3 12.1 %collective-permute-done.11 = bf16[1024,128]{1,0:T(8,128)(2,1)} collective-permute-done((bf16[1024,128]{1,0:T(8,128)(2,1)S(1)}, bf16[1024,128]{1,0:T(8,128)(2,1)}, u32[]{:S(2)}, u32[]{:S(2)}) %collective-permute-start.11) | collective-permute-done | bytes 262176 | tf_op jit(solution)/shard_map/ppermute | solution.py:115
  834.3 5.8 reshape.464
  861.0 8.8 convolution_convert_fusion
  872.6 9.9 collective-permute-done.14
  885.3 41.5 %all-gather.9.cloned.1.call-done = bf16[1024,2048]{1,0:T(8,128)(2,1)} async-done(((bf16[256,2048]{1,0:T(8,128)(2,1)}), bf16[1024,2048]{1,0:T(8,128)(2,1)}) %all-gather.9.cloned.1.call-update) | async-done | bytes 4194320 | tf_op jit(solution)/shard_map/all_gather | solution.py:182
  926.9 81.9 %reduce-scatter.8.cloned.1.call-done = bf16[256,2176]{1,0:T(8,128)(2,1)} async-done(((bf16[1024,2176]{1,0:T(8,128)(2,1)}), bf16[256,2176]{1,0:T(8,128)(2,1)}) %reduce-scatter.8.cloned.1.call-update) | async-done | bytes 1114128 | tf_op jit(solution)/shard_map/reduce_scatter | solution.py:171
  1018.1 4.7 slice.107
  1022.7 6.3 copy.111
  1030.5 68.6 %all-gather.11.cloned.1.call-done = bf16[1024,2048]{1,0:T(8,128)(2,1)} async-done(((bf16[256,2048]{1,0:T(8,128)(2,1)}), bf16[1024,2048]{1,0:T(8,128)(2,1)}) %all-gather.11.cloned.1.call-update) | async-done | bytes 4194320 | tf_op jit(solution)/shard_map/all_gather | solution.py:182
  1099.1 4.9 copy.135
  (345 shorter events, 205.4 us)
Async XLA Ops:
  7.2 301.2 %copy-start = (bf16[8,16,2048]{2,1,0:T(8,128)(2,1)S(1)}, bf16[8,16,2048]{2,1,0:T(8,128)(2,1)}, u32[]{:S(2)}) copy-start(bf16[8,16,2048]{2,1,0:T(8,128)(2,1)} %param.37) | copy-start | bytes 1572868
  7.2 146.9 %all-gather.5.cloned.1.call-start = ((), (), s32[]{:S(2)}) async-start(), calls=%async_computation.5 | async-start | bytes 5898240 | tf_op jit(solution)/shard_map/all_gather | solution.py:237
  12.0 11.5 %collective-permute-start = (bf16[1024,3,512]{0,2,1:T(8,128)(2,1)}, bf16[1024,3,512]{0,2,1:T(8,128)(2,1)}, u32[]{:S(2)}, u32[]{:S(2)}) collective-permute-start(bf16[1024,3,512]{0,2,1:T(8,128)(2,1)} %copy.86), channel_id=1, source_target_pairs={{0,16},{16,0},{1,17},{17,1},{2,18},{18,2},{3,19},{19,3},{4,20},{20... | collective-permute-start | bytes 9437192 | tf_op jit(solution)/shard_map/ppermute | solution.py:122
  21.2 15.7 %copy-start.10 = (bf16[4,256,2048]{2,1,0:T(8,128)(2,1)}, bf16[4,256,2048]{2,1,0:T(8,128)(2,1)S(1)}, u32[]{:S(2)}) copy-start(bf16[4,256,2048]{2,1,0:T(8,128)(2,1)S(1)} %add_convert_fusion) | copy-start | bytes 12582916
  51.0 50.3 %collective-permute-start.3 = (bf16[4,256,1024]{1,2,0:T(8,128)(2,1)}, bf16[4,256,1024]{1,2,0:T(8,128)(2,1)}, u32[]{:S(2)}, u32[]{:S(2)}) collective-permute-start(bf16[4,256,1024]{1,2,0:T(8,128)(2,1)} %pad_maximum_fusion.32), channel_id=1, source_target_pairs={{0,12},{4,8},{8,4},{12,0},{1,13},{5,9},{9,5},{13,1},{2,14},{6,10},... | collective-permute-start | bytes 6291464 | tf_op jit(solution)/shard_map/ppermute | solution.py:115
  54.5 91.4 %collective-permute-start.2 = (bf16[4,256,1024]{1,2,0:T(8,128)(2,1)}, bf16[4,256,1024]{1,2,0:T(8,128)(2,1)}, u32[]{:S(2)}, u32[]{:S(2)}) collective-permute-start(bf16[4,256,1024]{1,2,0:T(8,128)(2,1)} %pad_maximum_fusion.32), channel_id=1, source_target_pairs={{0,8},{4,12},{8,0},{12,4},{1,9},{5,13},{9,1},{13,5},{2,10},{6,14},... | collective-permute-start | bytes 6291464 | tf_op jit(solution)/shard_map/ppermute | solution.py:115
  55.0 91.1 %collective-permute-start.1 = (bf16[4,256,1024]{1,2,0:T(8,128)(2,1)}, bf16[4,256,1024]{1,2,0:T(8,128)(2,1)}, u32[]{:S(2)}, u32[]{:S(2)}) collective-permute-start(bf16[4,256,1024]{1,2,0:T(8,128)(2,1)} %pad_maximum_fusion.32), channel_id=1, source_target_pairs={{0,4},{4,0},{8,12},{12,8},{1,5},{5,1},{9,13},{13,9},{2,6},{6,2},{1... | collective-permute-start | bytes 6291464 | tf_op jit(solution)/shard_map/ppermute | solution.py:115
  64.0 95.0 %copy-start.14 = (bf16[4,256,4,128]{1,3,2,0:T(8,128)(2,1)}, bf16[4,256,4,128]{1,3,2,0:T(8,128)(2,1)S(1)}, u32[]{:S(2)}) copy-start(bf16[4,256,4,128]{1,3,2,0:T(8,128)(2,1)S(1)} %copy.102) | copy-start | bytes 3145732
  159.1 54.2 %collective-permute-start.4 = (bf16[2048,1024]{1,0:T(8,128)(2,1)}, bf16[2048,1024]{1,0:T(8,128)(2,1)}, u32[]{:S(2)}, u32[]{:S(2)}) collective-permute-start(bf16[2048,1024]{1,0:T(8,128)(2,1)} %slice.121), channel_id=1, source_target_pairs={{0,16},{16,0},{1,17},{17,1},{2,18},{18,2},{3,19},{19,3},{4,20},{20... | collective-permute-start | bytes 12582920 | tf_op jit(solution)/shard_map/ppermute | solution.py:122
  169.8 10.5 copy-start.66
  180.3 30.6 %all-to-all-start = ((bf16[4,256,512]{1,2,0:T(8,128)(2,1)}), bf16[4,256,512]{1,2,0:T(8,128)(2,1)S(1)}, u32[]{:S(2)}, u32[]{:S(2)}) async-start(bf16[4,256,512]{1,2,0:T(8,128)(2,1)} %bitcast.12), calls=%async_computation | async-start | bytes 2097152 | tf_op jit(solution)/shard_map/all_to_all | solution.py:306
  185.1 119.7 %all-gather.7.cloned.1.call-start = ((), (), s32[]{:S(2)}) async-start(), calls=%async_computation.6 | async-start | bytes 5242880 | tf_op jit(solution)/shard_map/all_gather | solution.py:182
  185.1 27.7 %copy-start.42 = (bf16[8,16,2048]{2,1,0:T(8,128)(2,1)S(1)}, bf16[8,16,2048]{2,1,0:T(8,128)(2,1)}, u32[]{:S(2)}) copy-start(bf16[8,16,2048]{2,1,0:T(8,128)(2,1)} %param.35) | copy-start | bytes 1572868
  191.8 348.9 %copy-start.40 = (f32[256,128]{1,0:T(8,128)}, f32[256,128]{1,0:T(8,128)S(1)}, u32[]{:S(2)}) copy-start(f32[256,128]{1,0:T(8,128)S(1)} %constant_dynamic-slice_fusion) | copy-start | bytes 393220
  225.7 223.4 %reduce-scatter.6.cloned.1.call-start = ((), (), s32[]{:S(2)}) async-start(), calls=%async_computation.9 | async-start | bytes 5570560 | tf_op jit(solution)/shard_map/reduce_scatter | solution.py:171
  226.2 9.0 collective-permute-start.5
  226.3 13.4 %collective-permute-start.6 = (bf16[2048,1024]{1,0:T(8,128)(2,1)}, bf16[2048,1024]{1,0:T(8,128)(2,1)S(1)}, u32[]{:S(2)}, u32[]{:S(2)}) collective-permute-start(bf16[2048,1024]{1,0:T(8,128)(2,1)} %param.31), channel_id=1, source_target_pairs={{0,16},{16,0},{1,17},{17,1},{2,18},{18,2},{3,19},{19,3},{4,20},{20... | collective-permute-start | bytes 12582920 | tf_op jit(solution)/shard_map/ppermute | solution.py:122
  312.9 16.9 %copy-start.6 = (bf16[4,256,2048]{2,1,0:T(8,128)(2,1)S(1)}, bf16[4,256,2048]{2,1,0:T(8,128)(2,1)}, u32[]{:S(2)}) copy-start(bf16[4,256,2048]{2,1,0:T(8,128)(2,1)} %param.21) | copy-start | bytes 12582916
  369.5 163.4 %reduce-scatter.4.cloned.1.call-start = ((), (), s32[]{:S(2)}) async-start(), calls=%async_computation.7 | async-start | bytes 5570560 | tf_op jit(solution)/shard_map/reduce_scatter | solution.py:171
  388.5 147.7 %copy-start.38 = (bf16[8,2048,16]{1,2,0:T(8,128)(2,1)S(1)}, bf16[8,2048,16]{1,2,0:T(8,128)(2,1)}, u32[]{:S(2)}) copy-start(bf16[8,2048,16]{1,2,0:T(8,128)(2,1)} %param.36) | copy-start | bytes 1572868
  549.3 53.2 %all-to-all-start.1 = ((bf16[256,4,512]{0,2,1:T(8,128)(2,1)}), bf16[256,4,512]{0,2,1:T(8,128)(2,1)}, u32[]{:S(2)}, u32[]{:S(2)}) async-start(bf16[256,4,512]{0,2,1:T(8,128)(2,1)} %bitcast.211), calls=%async_computation.3 | async-start | bytes 2097152 | tf_op jit(solution)/shard_map/all_to_all | solution.py:372
  553.6 293.1 %all-reduce.4.cloned.1.call-start = ((), (), s32[]{:S(2)}) async-start(), calls=%async_computation.12 | async-start | bytes 1048576 | tf_op jit(solution)/shard_map/psum | solution.py:160
  564.7 39.9 %copy-start.67 = (f32[4,4,256]{2,1,0:T(4,128)S(1)}, f32[4,4,256]{2,1,0:T(4,128)}, u32[]{:S(2)}) copy-start(f32[4,4,256]{2,1,0:T(4,128)} %copy-done.66) | copy-start | bytes 49156
  564.7 15.5 %collective-permute-start.18 = (bf16[256,384]{1,0:T(8,128)(2,1)}, bf16[256,384]{1,0:T(8,128)(2,1)S(1)}, u32[]{:S(2)}, u32[]{:S(2)}) collective-permute-start(bf16[256,384]{1,0:T(8,128)(2,1)} %get-tuple-element.62), channel_id=1, source_target_pairs={{0,3},{1,2},{2,1},{3,0},{4,7},{5,6},{6,5},{7,4},{8,11},{9,10},{10,... | collective-permute-start | bytes 589832 | tf_op jit(solution)/shard_map/ppermute | solution.py:115
  568.5 30.3 %collective-permute-start.17 = (bf16[256,384]{1,0:T(8,128)(2,1)}, bf16[256,384]{1,0:T(8,128)(2,1)S(1)}, u32[]{:S(2)}, u32[]{:S(2)}) collective-permute-start(bf16[256,384]{1,0:T(8,128)(2,1)} %get-tuple-element.62), channel_id=1, source_target_pairs={{0,2},{1,3},{2,0},{3,1},{4,6},{5,7},{6,4},{7,5},{8,10},{9,11},{10,... | collective-permute-start | bytes 589832 | tf_op jit(solution)/shard_map/ppermute | solution.py:115
  568.5 30.3 %collective-permute-start.16 = (bf16[256,384]{1,0:T(8,128)(2,1)}, bf16[256,384]{1,0:T(8,128)(2,1)S(1)}, u32[]{:S(2)}, u32[]{:S(2)}) collective-permute-start(bf16[256,384]{1,0:T(8,128)(2,1)} %get-tuple-element.62), channel_id=1, source_target_pairs={{0,1},{1,0},{2,3},{3,2},{4,5},{5,4},{6,7},{7,6},{8,9},{9,8},{10,11... | collective-permute-start | bytes 589832 | tf_op jit(solution)/shard_map/ppermute | solution.py:115
  570.3 278.5 %all-reduce.6.cloned.1.call-start = ((), (), s32[]{:S(2)}) async-start(), calls=%async_computation.13 | async-start | bytes 4456448 | tf_op jit(solution)/shard_map/psum | solution.py:160
  617.8 12.6 %copy-start.15 = (bf16[4,256,4,128]{1,3,2,0:T(8,128)(2,1)S(1)}, bf16[4,256,4,128]{1,3,2,0:T(8,128)(2,1)}, u32[]{:S(2)}) copy-start(bf16[4,256,4,128]{1,3,2,0:T(8,128)(2,1)} %copy-done.14) | copy-start | bytes 3145732
  685.8 50.1 %collective-permute-start.9 = (bf16[4,256,1024]{2,1,0:T(8,128)(2,1)}, bf16[4,256,1024]{2,1,0:T(8,128)(2,1)}, u32[]{:S(2)}, u32[]{:S(2)}) collective-permute-start(bf16[4,256,1024]{2,1,0:T(8,128)(2,1)} %get-tuple-element.44), channel_id=1, source_target_pairs={{0,12},{4,8},{8,4},{12,0},{1,13},{5,9},{9,5},{13,1},{2,14},{6,10},... | collective-permute-start | bytes 6291464 | tf_op jit(solution)/shard_map/ppermute | solution.py:399
  688.1 102.9 %collective-permute-start.8 = (bf16[4,256,1024]{2,1,0:T(8,128)(2,1)}, bf16[4,256,1024]{2,1,0:T(8,128)(2,1)}, u32[]{:S(2)}, u32[]{:S(2)}) collective-permute-start(bf16[4,256,1024]{2,1,0:T(8,128)(2,1)} %get-tuple-element.45), channel_id=1, source_target_pairs={{0,8},{4,12},{8,0},{12,4},{1,9},{5,13},{9,1},{13,5},{2,10},{6,14},... | collective-permute-start | bytes 6291464 | tf_op jit(solution)/shard_map/ppermute | solution.py:399
  688.7 102.4 %collective-permute-start.7 = (bf16[4,256,1024]{2,1,0:T(8,128)(2,1)}, bf16[4,256,1024]{2,1,0:T(8,128)(2,1)}, u32[]{:S(2)}, u32[]{:S(2)}) collective-permute-start(bf16[4,256,1024]{2,1,0:T(8,128)(2,1)} %get-tuple-element.43), channel_id=1, source_target_pairs={{0,4},{4,0},{8,12},{12,8},{1,5},{5,1},{9,13},{13,9},{2,6},{6,2},{1... | collective-permute-start | bytes 6291464 | tf_op jit(solution)/shard_map/ppermute | solution.py:399
  698.4 228.4 %all-gather.9.cloned.1.call-start = ((), (), s32[]{:S(2)}) async-start(), calls=%async_computation.8 | async-start | bytes 5242880 | tf_op jit(solution)/shard_map/all_gather | solution.py:182
  711.0 91.5 %copy-start.51 = (bf16[128,8,4,128]{3,1,2,0:T(8,128)(2,1)}, bf16[128,8,4,128]{3,1,2,0:T(8,128)(2,1)S(1)}, u32[]{:S(2)}) copy-start(bf16[128,8,4,128]{3,1,2,0:T(8,128)(2,1)S(1)} %copy.125) | copy-start | bytes 3145732
  798.0 23.5 %copy-start.57 = (bf16[1024,128]{1,0:T(8,128)(2,1)}, bf16[1024,128]{1,0:T(8,128)(2,1)S(1)}, u32[]{:S(2)}) copy-start(bf16[1024,128]{1,0:T(8,128)(2,1)S(1)} %convolution_convert_fusion.8) | copy-start | bytes 786436
  798.0 11.3 %collective-permute-start.12 = (bf16[1024,128]{1,0:T(8,128)(2,1)S(1)}, bf16[1024,128]{1,0:T(8,128)(2,1)}, u32[]{:S(2)}, u32[]{:S(2)}) collective-permute-start(bf16[1024,128]{1,0:T(8,128)(2,1)S(1)} %convolution_convert_fusion.8), channel_id=1, source_target_pairs={{0,3},{1,2},{2,1},{3,0},{4,7},{5,6},{6,5},{7,4},{8,11},{9,10},{10,... | collective-permute-start | bytes 786440 | tf_op jit(solution)/shard_map/ppermute | solution.py:115
  798.8 22.7 %collective-permute-start.11 = (bf16[1024,128]{1,0:T(8,128)(2,1)S(1)}, bf16[1024,128]{1,0:T(8,128)(2,1)}, u32[]{:S(2)}, u32[]{:S(2)}) collective-permute-start(bf16[1024,128]{1,0:T(8,128)(2,1)S(1)} %convolution_convert_fusion.8), channel_id=1, source_target_pairs={{0,2},{1,3},{2,0},{3,1},{4,6},{5,7},{6,4},{7,5},{8,10},{9,11},{10,... | collective-permute-start | bytes 786440 | tf_op jit(solution)/shard_map/ppermute | solution.py:115
  798.8 22.7 %collective-permute-start.10 = (bf16[1024,128]{1,0:T(8,128)(2,1)S(1)}, bf16[1024,128]{1,0:T(8,128)(2,1)}, u32[]{:S(2)}, u32[]{:S(2)}) collective-permute-start(bf16[1024,128]{1,0:T(8,128)(2,1)S(1)} %convolution_convert_fusion.8), channel_id=1, source_target_pairs={{0,1},{1,0},{2,3},{3,2},{4,5},{5,4},{6,7},{7,6},{8,9},{9,8},{10,11... | collective-permute-start | bytes 786440 | tf_op jit(solution)/shard_map/ppermute | solution.py:115
  842.4 15.8 %collective-permute-start.13 = (bf16[458752]{0:T(1024)(128)(2,1)S(1)}, bf16[458752]{0:T(1024)(128)(2,1)}, u32[]{:S(2)}, u32[]{:S(2)}) collective-permute-start(bf16[458752]{0:T(1024)(128)(2,1)S(1)} %constant_dynamic-update-slice_fusion), channel_id=1, source_target_pairs={{0,16},{16,0},{1,17},{17,1},{2,18},{18,2},{3,19},{19,3},{4,20},{20... | collective-permute-start | bytes 2752520 | tf_op jit(solution)/shard_map/ppermute | solution.py:138
  846.6 162.1 %reduce-scatter.8.cloned.1.call-start = ((), (), s32[]{:S(2)}) async-start(), calls=%async_computation.10 | async-start | bytes 5570560 | tf_op jit(solution)/shard_map/reduce_scatter | solution.py:171
  850.5 10.5 copy-start.52
  850.5 10.5 copy-start.54
  850.5 10.5 copy-start.56
  859.6 22.9 %collective-permute-start.14 = (bf16[458752]{0:T(1024)(128)(2,1)S(1)}, bf16[458752]{0:T(1024)(128)(2,1)}, u32[]{:S(2)}, u32[]{:S(2)}) collective-permute-start(bf16[458752]{0:T(1024)(128)(2,1)S(1)} %add_convert_fusion.5), channel_id=1, source_target_pairs={{0,4},{4,0},{8,12},{12,8},{1,5},{5,1},{9,13},{13,9},{2,6},{6,2},{1... | collective-permute-start | bytes 2752520 | tf_op jit(solution)/shard_map/ppermute | solution.py:138
  872.3 137.8 %copy-start.41 = (f32[256,128]{1,0:T(8,128)S(1)}, f32[256,128]{1,0:T(8,128)}, u32[]{:S(2)}) copy-start(f32[256,128]{1,0:T(8,128)} %copy-done.40) | copy-start | bytes 393220
  872.3 137.8 %copy-start.45 = (bf16[8,2048,16]{1,2,0:T(8,128)(2,1)S(1)}, bf16[8,2048,16]{1,2,0:T(8,128)(2,1)}, u32[]{:S(2)}) copy-start(bf16[8,2048,16]{1,2,0:T(8,128)(2,1)} %param.32) | copy-start | bytes 1572868
  872.3 137.8 %copy-start.75 = (f32[2048]{0:T(1024)S(1)}, f32[2048]{0:T(1024)}, u32[]{:S(2)}) copy-start(f32[2048]{0:T(1024)} %param.24) | copy-start | bytes 24580
  872.3 226.8 %all-gather.11.cloned.1.call-start = ((), (), s32[]{:S(2)}) async-start(), calls=%async_computation.11 | async-start | bytes 5242880 | tf_op jit(solution)/shard_map/all_gather | solution.py:182
  883.9 133.8 %collective-permute-start.15 = (bf16[458752]{0:T(1024)(128)(2,1)S(1)}, bf16[458752]{0:T(1024)(128)(2,1)S(1)}, u32[]{:S(2)}, u32[]{:S(2)}) collective-permute-start(bf16[458752]{0:T(1024)(128)(2,1)S(1)} %add_convert_fusion.4), channel_id=1, source_target_pairs={{0,8},{4,12},{8,0},{12,4},{1,9},{5,13},{9,1},{13,5},{2,10},{6,14},... | collective-permute-start | bytes 2752520 | tf_op jit(solution)/shard_map/ppermute | solution.py:138
  (66 other events, 325.1 us)
Sparse Core Ops, SparseCore 0:
  13.9 91.7 all-gather.4
  225.9 78.8 all-gather.6
  369.6 79.5 reduce-scatter.5
  451.3 81.5 reduce-scatter.3
  570.5 169.6 all-reduce.3
  744.4 73.4 all-reduce.5
  846.7 80.0 all-gather.8
  929.2 79.5 reduce-scatter.7
  1017.8 81.2 all-gather.10

commit v14 on v13

--- a/solution.py
+++ b/solution.py
@@ -375,30 +375,35 @@
     )
     scaled_grad = (grad_heads_wide / per_total).astype(jnp.bfloat16)
     row_delta = jnp.sum(grad_heads_wide * heads_raw, axis=-1) / per_total[..., 0]
-    grad_queries, grad_keyrows, grad_valrows = block_grads(
-        queries,
-        scaled_grad,
-        row_delta,
-        piece_keys,
-        piece_values,
-        here_pos,
-        key_pos,
-        visible_mask,
-        slopes,
-    )
-    grad_kv = jnp.concatenate(
-        [
-            grad_keyrows.reshape(seq_here, ctx_count, local_len, local_width),
-            grad_valrows.reshape(seq_here, ctx_count, local_len, local_width),
-        ],
-        axis=3,
-    )
-    grad_kv_here = grad_kv[:, 0]
-    for offset in range(1, ctx_count):
-        pairs = [(index, index ^ offset) for index in range(ctx_count)]
-        grad_kv_here = grad_kv_here + lax.ppermute(
-            grad_kv[:, offset].astype(jnp.bfloat16), "ctx", pairs
-        ).astype(jnp.float32)
+    grad_queries = None
+    grad_kv_here = None
+    for offset in list(range(1, ctx_count)) + [0]:
+        keys_slice = slice(offset * local_len, (offset + 1) * local_len)
+        query_part, key_part, value_part = block_grads(
+            queries,
+            scaled_grad,
+            row_delta,
+            piece_keys[:, keys_slice],
+            piece_values[:, keys_slice],
+            here_pos,
+            key_pos[keys_slice],
+            visible_mask[:, :, keys_slice],
+            slopes,
+        )
+        grad_queries = query_part if grad_queries is None else grad_queries + query_part
+        block_kv = jnp.concatenate(
+            [
+                key_part.reshape(seq_here, local_len, local_width),
+                value_part.reshape(seq_here, local_len, local_width),
+            ],
+            axis=2,
+        )
+        if offset:
+            pairs = [(index, index ^ offset) for index in range(ctx_count)]
+            block_kv = lax.ppermute(block_kv.astype(jnp.bfloat16), "ctx", pairs).astype(
+                jnp.float32
+            )
+        grad_kv_here = block_kv if grad_kv_here is None else grad_kv_here + block_kv
     grad_keys_all = grad_kv_here[:, :, :local_width]
     grad_values_all = grad_kv_here[:, :, local_width:]
     grad_projected = jnp.concatenate(

time: 1120 us -> 1100 us (0.982)
  local copies, waits for them, and re-layouts: 127 us -> 100 us
  waiting for transfers between devices: 633 us -> 609 us
  matrix products: 198 us -> 221 us
    psum x2, waiting for transfers between devices: 0.02 us -> 46.3 us  [narrow_psum(): lax.psum(jax.tree.map(lambda value: value.astype(jnp.bfloat16), values),...]
    ppermute x3, waiting for transfers between devices: 80.1 us -> 40.7 us  [layer_body(): lax.ppermute(block_kv.astype(jnp.bfloat16), 'ctx', pairs)]
    reduce_scatter x3, waiting for transfers between devices: 224 us -> 200 us  [scatter_rows(): lax.psum_scatter(jnp.concatenate(partials, axis=1).astype(jnp.bfloat16),...]
    reshape x4 -> x8, local copies, waits for them, and re-layouts: 41 us -> 19.8 us  [the longest x4 10.1 us: layer_body(): key_part.reshape(seq_here, local_len, local_width)]
    ppermute x9, waiting for transfers between devices: 128 us -> 112 us  [partner_swaps(): received.append(lax.ppermute(block, axis_name, pairs))]
    dot_general x1 -> x5, matrix products: 9.42 us -> 21.7 us  [exponents(): jnp.einsum('sqhd,skhd->shqk', queries, key_rows, preferred_element_type=j...]
    unnamed x177 -> x225, local copies, waits for them, and re-layouts: 34.7 us -> 34.9 us
  transfers between devices with their start and end apart: 30 -> 30, of which waited for: 18 -> 17; matrix products, arithmetic and copies ran while one was open for 28% -> 29% of each run, Pallas kernels for 0% -> 0%
where the time goes in v14:
time: 1100 us; the launch traced here: 1090 us
  waiting for transfers between devices  609 us (55%)
  matrix products  221 us (20%)
  other arithmetic  112 us (10%)
  local copies, waits for them, and re-layouts  100 us (9%)
  starting transfers between devices  28.7 us (3%)
  between operations  15.8 us (1%)
    reduce_scatter x3, waiting for transfers between devices, scatter_rows(): lax.psum_scatter(jnp.concatenate(partials, axis=1).astype(jnp.bfloat16),...  200 us
    all_gather x3, waiting for transfers between devices, gather_rows(): lax.all_gather(jnp.concatenate(rows_here, axis=1), 'tp', axis=0, tiled=True)  177 us
    ppermute x9, waiting for transfers between devices, partner_swaps(): received.append(lax.ppermute(block, axis_name, pairs))  112 us
    dot_general x12, matrix products, matmul_nt(): lax.dot_general(left_mat, right_mat, (((1,), (1,)), ((), ())), preferred_...  66.3 us
    dot_general x12, matrix products, matmul(): return jnp.dot(left_mat, right_mat, preferred_element_type=jnp.float32)  63.4 us
    psum x2, waiting for transfers between devices, narrow_psum(): lax.psum(jax.tree.map(lambda value: value.astype(jnp.bfloat16), values),...  46.3 us
    ppermute x3, waiting for transfers between devices, layer_body(): lax.ppermute(block_kv.astype(jnp.bfloat16), 'ctx', pairs)  40.7 us
    unnamed x225, local copies, waits for them, and re-layouts  34.9 us
  transfers between devices with their start and end apart: 30, of which 17 were waited for; matrix products, arithmetic and copies ran while one was open for 29% of the time, Pallas kernels for 0%

profile of v14, /device:TPU:0, one launch (start us, length us, event | category | flops | bytes accessed | tf_op | source)
XLA Modules:
  0.0 1085.3 jit_solution(2210956386389656238)
XLA Ops:
  7.3 4.8 copy.126
  25.3 5.3 broadcast_select_fusion.7
  30.6 6.5 pad_maximum_fusion.4
  37.0 8.9 add_convert_fusion.1
  63.7 38.0 %collective-permute-done.3 = bf16[4,256,1024]{1,2,0:T(8,128)(2,1)} collective-permute-done((bf16[4,256,1024]{1,2,0:T(8,128)(2,1)}, bf16[4,256,1024]{1,2,0:T(8,128)(2,1)}, u32[]{:S(2)}, u32[]{:S(2)}) %collective-permute-start.3) | collective-permute-done | bytes 2097184 | tf_op jit(solution)/shard_map/ppermute | solution.py:115
  101.7 44.5 %collective-permute-done.2 = bf16[4,256,1024]{1,2,0:T(8,128)(2,1)} collective-permute-done((bf16[4,256,1024]{1,2,0:T(8,128)(2,1)}, bf16[4,256,1024]{1,2,0:T(8,128)(2,1)}, u32[]{:S(2)}, u32[]{:S(2)}) %collective-permute-start.2) | collective-permute-done | bytes 2097184 | tf_op jit(solution)/shard_map/ppermute | solution.py:115
  146.5 4.4 pad_maximum_fusion
  155.4 9.3 fusion
  164.7 4.8 slice.150
  169.6 11.1 %fusion.133 = (bf16[4,256,4,128]{1,3,2,0:T(8,128)(2,1)}, f32[4,256,4,128]{1,3,2,0:T(8,128)}) fusion(f32[4,256,4]{1,2,0:T(4,128)S(1)} %bitcast.284, bf16[4,1024,4,128]{1,3,2,0:T(8,128)(2,1)} %bitcast.240, f32[4,4,256,1024]{3,2,1,0:T(8,128)} %get-tuple-element.77, f32[4,256,1024]{2,1,0:T(8,128)S(1)} %copy-done.5, pred[4,256,1024]{2,1,0:T(8,128)(4,1)S(1)} %and_or_fusion), kind=kOutput, calls=%fused_computation.263 | convolution fusion | flops 1091567616 | bytes 29376512 | tf_op jit(solution)/shard_map/shqk,skhd->sqhd/dot_general | solution.py:296
  180.6 4.8 all-to-all-start
  185.4 6.6 convert.111
  192.1 19.8 %all-to-all-done = bf16[4,256,512]{1,2,0:T(8,128)(2,1)S(1)} async-done(((bf16[4,256,512]{1,2,0:T(8,128)(2,1)}), bf16[4,256,512]{1,2,0:T(8,128)(2,1)S(1)}, u32[]{:S(2)}, u32[]{:S(2)}) %all-to-all-start) | async-done | bytes 1048608 | tf_op jit(solution)/shard_map/all_to_all | solution.py:306
  214.8 3.8 broadcast_select_fusion.5
  218.7 6.5 fusion.134
  232.6 5.8 fusion.138
  238.4 4.1 broadcast_select_fusion.1
  242.9 3.5 broadcast_select_fusion.3
  246.3 61.0 %all-gather.7.cloned.1.call-done = bf16[1024,2048]{1,0:T(8,128)(2,1)} async-done(((bf16[256,2048]{1,0:T(8,128)(2,1)}), bf16[1024,2048]{1,0:T(8,128)(2,1)}) %all-gather.7.cloned.1.call-update) | async-done | bytes 4194320 | tf_op jit(solution)/shard_map/all_gather | solution.py:182
  310.8 4.6 fusion.137
  315.4 16.9 %multiply_convert_fusion = (bf16[1024,2048]{1,0:T(8,128)(2,1)}, f32[1024,2048]{1,0:T(8,128)}) fusion(f32[1024,2048]{1,0:T(8,128)} %fusion.137, bf16[1024,2048]{1,0:T(8,128)(2,1)S(1)} %copy-done.34, bf16[1024,2048]{1,0:T(8,128)(2,1)} %get-tuple-element.46, bf16[1024,2048]{1,0:T(8,128)(2,1)} %get-tuple-element.45), kind=kOutput, calls=%fused_computation.21 | convolution fusion | flops 8627683328 | bytes 33554432 | tf_op jit(solution)/shard_map/dot_general | solution.py:43
  332.3 21.1 %fusion.5 = bf16[1024,2048]{1,0:T(8,128)(2,1)} fusion(f32[1024,2048]{1,0:T(8,128)} %get-tuple-element.83, f32[1024,2048]{1,0:T(8,128)} %fusion.138, bf16[1024,2048]{1,0:T(8,128)(2,1)S(1)} %bitcast.212, bf16[2048,1024]{1,0:T(8,128)(2,1)} %get-tuple-element.44, bf16[2048,1024]{1,0:T(8,128)(2,1)} %get-tuple-element.43), kind=kOutput, calls=%fused_computation.12 | convolution fusion | flops 8659140608 | bytes 33554432 | tf_op jit(solution)/shard_map/dot_general | solution.py:53
  353.4 3.6 convolution_convert_fusion.9
  357.0 12.0 %fusion.22 = bf16[1024,2048]{1,0:T(8,128)(2,1)S(1)} fusion(bf16[1024,2048]{1,0:T(8,128)(2,1)} %fusion.5, bf16[1024,2048]{1,0:T(8,128)(2,1)} %get-tuple-element.46, bf16[1024,2048]{1,0:T(8,128)(2,1)S(1)} %copy-done.42), kind=kOutput, calls=%fused_computation.59 | convolution fusion | flops 8608808960 | bytes 16777216 | tf_op jit(solution)/shard_map/dot_general | solution.py:53
  372.6 3.8 convolution_convert_fusion.10
  376.4 11.7 %fusion.23 = bf16[1024,2048]{1,0:T(8,128)(2,1)S(1)} fusion(bf16[1024,2048]{1,0:T(8,128)(2,1)} %get-tuple-element.82, bf16[2048,1024]{1,0:T(8,128)(2,1)} %get-tuple-element.44, bf16[2048,1024]{1,0:T(8,128)(2,1)S(1)} %copy-done.41), kind=kOutput, calls=%fused_computation.60 | convolution fusion | flops 8608808960 | bytes 16777216 | tf_op jit(solution)/shard_map/dot_general | solution.py:43
  398.3 4.1 fusion.83
  414.5 36.8 %reduce-scatter.6.cloned.1.call-done = bf16[256,2176]{1,0:T(8,128)(2,1)} async-done(((bf16[1024,2176]{1,0:T(8,128)(2,1)}), bf16[256,2176]{1,0:T(8,128)(2,1)}) %reduce-scatter.6.cloned.1.call-update) | async-done | bytes 1114128 | tf_op jit(solution)/shard_map/reduce_scatter | solution.py:171
  454.0 81.0 %reduce-scatter.4.cloned.1.call-done = bf16[256,2176]{1,0:T(8,128)(2,1)} async-done(((bf16[1024,2176]{1,0:T(8,128)(2,1)}), bf16[256,2176]{1,0:T(8,128)(2,1)}) %reduce-scatter.4.cloned.1.call-update) | async-done | bytes 1114128 | tf_op jit(solution)/shard_map/reduce_scatter | solution.py:171
  556.9 3.9 all-to-all-start.1
  563.2 9.0 collective-permute-done.17
  578.4 3.9 convolution_convert_fusion.4
  586.5 3.5 all-to-all-done.1
  646.0 4.4 multiply_convert_fusion.1
  673.9 40.7 %collective-permute-done.8 = bf16[4,256,1024]{2,1,0:T(8,128)(2,1)} collective-permute-done((bf16[4,256,1024]{2,1,0:T(8,128)(2,1)}, bf16[4,256,1024]{2,1,0:T(8,128)(2,1)}, u32[]{:S(2)}, u32[]{:S(2)}) %collective-permute-start.8) | collective-permute-done | bytes 2097184 | tf_op jit(solution)/shard_map/ppermute | solution.py:403
  714.6 5.2 fusion.20
  728.0 5.4 collective-permute-done.12
  733.4 14.9 %collective-permute-done.11 = bf16[1024,128]{1,0:T(8,128)(2,1)S(1)} collective-permute-done((bf16[1024,128]{1,0:T(8,128)(2,1)S(1)}, bf16[1024,128]{1,0:T(8,128)(2,1)S(1)}, u32[]{:S(2)}, u32[]{:S(2)}) %collective-permute-start.11) | collective-permute-done | bytes 262176 | tf_op jit(solution)/shard_map/ppermute | solution.py:115
  755.7 6.0 reshape.645
  770.4 46.3 %all-reduce.6.cloned.1.call-done = (bf16[8,512,16]{1,2,0:T(8,128)(2,1)}, bf16[8,2048,16]{1,2,0:T(8,128)(2,1)}, bf16[8,16,2048]{2,1,0:T(8,128)(2,1)}, bf16[8,2048,16]{1,2,0:T(8,128)(2,1)}, bf16[8,16,2048]{2,1,0:T(8,128)(2,1)}) async-done(((bf16[8,512,16]{1,2,0:T(8,128)(2,1)}, bf16[8,2048,16]{1,2,0:T(8,128)(2,1)}, bf16[8,16,2048]{2,1,0:T(8,128)(2,1)}, bf16[8,2048,16]{1,2,0:T(8,128)(2,1)}, ...) | async-done | bytes 2228240 | tf_op jit(solution)/shard_map/psum | solution.py:160
  828.0 9.1 convolution_convert_fusion
  839.7 9.0 collective-permute-done.14
  851.4 47.7 %all-gather.9.cloned.1.call-done = bf16[1024,2048]{1,0:T(8,128)(2,1)} async-done(((bf16[256,2048]{1,0:T(8,128)(2,1)}), bf16[1024,2048]{1,0:T(8,128)(2,1)}) %all-gather.9.cloned.1.call-update) | async-done | bytes 4194320 | tf_op jit(solution)/shard_map/all_gather | solution.py:182
  899.1 81.9 %reduce-scatter.8.cloned.1.call-done = bf16[256,2176]{1,0:T(8,128)(2,1)} async-done(((bf16[1024,2176]{1,0:T(8,128)(2,1)}), bf16[256,2176]{1,0:T(8,128)(2,1)}) %reduce-scatter.8.cloned.1.call-update) | async-done | bytes 1114128 | tf_op jit(solution)/shard_map/reduce_scatter | solution.py:171
  990.3 4.6 slice.136
  994.9 6.3 copy.178
  1002.7 68.7 %all-gather.11.cloned.1.call-done = bf16[1024,2048]{1,0:T(8,128)(2,1)} async-done(((bf16[256,2048]{1,0:T(8,128)(2,1)}), bf16[1024,2048]{1,0:T(8,128)(2,1)}) %all-gather.11.cloned.1.call-update) | async-done | bytes 4194320 | tf_op jit(solution)/shard_map/all_gather | solution.py:182
  1071.3 4.9 copy.216
  (418 shorter events, 245.3 us)
Async XLA Ops:
  7.2 303.6 %copy-start = (bf16[8,16,2048]{2,1,0:T(8,128)(2,1)S(1)}, bf16[8,16,2048]{2,1,0:T(8,128)(2,1)}, u32[]{:S(2)}) copy-start(bf16[8,16,2048]{2,1,0:T(8,128)(2,1)} %param.37) | copy-start | bytes 1572868
  7.2 157.5 %all-gather.5.cloned.1.call-start = ((), (), s32[]{:S(2)}) async-start(), calls=%async_computation.5 | async-start | bytes 5898240 | tf_op jit(solution)/shard_map/all_gather | solution.py:237
  12.0 11.6 %collective-permute-start = (bf16[1024,3,512]{0,2,1:T(8,128)(2,1)}, bf16[1024,3,512]{0,2,1:T(8,128)(2,1)}, u32[]{:S(2)}, u32[]{:S(2)}) collective-permute-start(bf16[1024,3,512]{0,2,1:T(8,128)(2,1)} %copy.126), channel_id=1, source_target_pairs={{0,16},{16,0},{1,17},{17,1},{2,18},{18,2},{3,19},{19,3},{4,20},{20... | collective-permute-start | bytes 9437192 | tf_op jit(solution)/shard_map/ppermute | solution.py:122
  14.9 40.6 %copy-start.94 = (s32[256]{0:T(256)}, s32[256]{0:T(256)S(1)}, u32[]{:S(2)}) copy-start(s32[256]{0:T(256)S(1)} %get-tuple-element.87) | copy-start | bytes 3076
  14.9 40.6 %copy-start.96 = (s32[256]{0:T(256)}, s32[256]{0:T(256)S(1)}, u32[]{:S(2)}) copy-start(s32[256]{0:T(256)S(1)} %get-tuple-element.88) | copy-start | bytes 3076
  14.9 40.6 %copy-start.98 = (s32[256]{0:T(256)}, s32[256]{0:T(256)S(1)}, u32[]{:S(2)}) copy-start(s32[256]{0:T(256)S(1)} %get-tuple-element.89) | copy-start | bytes 3076
  14.9 41.0 %copy-start.89 = (s32[256]{0:T(256)}, s32[256]{0:T(256)S(1)}, u32[]{:S(2)}) copy-start(s32[256]{0:T(256)S(1)} %get-tuple-element.90) | copy-start | bytes 3076
  21.3 15.7 %copy-start.15 = (bf16[4,256,2048]{2,1,0:T(8,128)(2,1)}, bf16[4,256,2048]{2,1,0:T(8,128)(2,1)S(1)}, u32[]{:S(2)}) copy-start(bf16[4,256,2048]{2,1,0:T(8,128)(2,1)S(1)} %add_convert_fusion) | copy-start | bytes 12582916
  48.0 10.8 copy-start.26
  51.4 50.3 %collective-permute-start.3 = (bf16[4,256,1024]{1,2,0:T(8,128)(2,1)}, bf16[4,256,1024]{1,2,0:T(8,128)(2,1)}, u32[]{:S(2)}, u32[]{:S(2)}) collective-permute-start(bf16[4,256,1024]{1,2,0:T(8,128)(2,1)} %pad_maximum_fusion.31), channel_id=1, source_target_pairs={{0,12},{4,8},{8,4},{12,0},{1,13},{5,9},{9,5},{13,1},{2,14},{6,10},... | collective-permute-start | bytes 6291464 | tf_op jit(solution)/shard_map/ppermute | solution.py:115
  54.9 91.4 %collective-permute-start.2 = (bf16[4,256,1024]{1,2,0:T(8,128)(2,1)}, bf16[4,256,1024]{1,2,0:T(8,128)(2,1)}, u32[]{:S(2)}, u32[]{:S(2)}) collective-permute-start(bf16[4,256,1024]{1,2,0:T(8,128)(2,1)} %pad_maximum_fusion.31), channel_id=1, source_target_pairs={{0,8},{4,12},{8,0},{12,4},{1,9},{5,13},{9,1},{13,5},{2,10},{6,14},... | collective-permute-start | bytes 6291464 | tf_op jit(solution)/shard_map/ppermute | solution.py:115
  55.4 91.1 %collective-permute-start.1 = (bf16[4,256,1024]{1,2,0:T(8,128)(2,1)}, bf16[4,256,1024]{1,2,0:T(8,128)(2,1)}, u32[]{:S(2)}, u32[]{:S(2)}) collective-permute-start(bf16[4,256,1024]{1,2,0:T(8,128)(2,1)} %pad_maximum_fusion.31), channel_id=1, source_target_pairs={{0,4},{4,0},{8,12},{12,8},{1,5},{5,1},{9,13},{13,9},{2,6},{6,2},{1... | collective-permute-start | bytes 6291464 | tf_op jit(solution)/shard_map/ppermute | solution.py:115
  63.7 89.8 %copy-start.2 = (bf16[4,256,4,128]{1,3,2,0:T(8,128)(2,1)}, bf16[4,256,4,128]{1,3,2,0:T(8,128)(2,1)S(1)}, u32[]{:S(2)}) copy-start(bf16[4,256,4,128]{1,3,2,0:T(8,128)(2,1)S(1)} %copy.160) | copy-start | bytes 3145732
  169.5 45.3 %collective-permute-start.4 = (bf16[2048,1024]{1,0:T(8,128)(2,1)}, bf16[2048,1024]{1,0:T(8,128)(2,1)}, u32[]{:S(2)}, u32[]{:S(2)}) collective-permute-start(bf16[2048,1024]{1,0:T(8,128)(2,1)} %slice.150), channel_id=1, source_target_pairs={{0,16},{16,0},{1,17},{17,1},{2,18},{18,2},{3,19},{19,3},{4,20},{20... | collective-permute-start | bytes 12582920 | tf_op jit(solution)/shard_map/ppermute | solution.py:122
  180.6 31.2 %all-to-all-start = ((bf16[4,256,512]{1,2,0:T(8,128)(2,1)}), bf16[4,256,512]{1,2,0:T(8,128)(2,1)S(1)}, u32[]{:S(2)}, u32[]{:S(2)}) async-start(bf16[4,256,512]{1,2,0:T(8,128)(2,1)} %bitcast.232), calls=%async_computation | async-start | bytes 2097152 | tf_op jit(solution)/shard_map/all_to_all | solution.py:306
  185.4 121.9 %all-gather.7.cloned.1.call-start = ((), (), s32[]{:S(2)}) async-start(), calls=%async_computation.6 | async-start | bytes 5242880 | tf_op jit(solution)/shard_map/all_gather | solution.py:182
  192.1 26.6 %copy-start.57 = (f32[256,128]{1,0:T(8,128)}, f32[256,128]{1,0:T(8,128)S(1)}, u32[]{:S(2)}) copy-start(f32[256,128]{1,0:T(8,128)S(1)} %constant_dynamic-slice_fusion) | copy-start | bytes 393220
  228.1 223.2 %reduce-scatter.6.cloned.1.call-start = ((), (), s32[]{:S(2)}) async-start(), calls=%async_computation.9 | async-start | bytes 5570560 | tf_op jit(solution)/shard_map/reduce_scatter | solution.py:171
  228.5 9.9 collective-permute-start.5
  228.6 13.9 %collective-permute-start.6 = (bf16[2048,1024]{1,0:T(8,128)(2,1)}, bf16[2048,1024]{1,0:T(8,128)(2,1)S(1)}, u32[]{:S(2)}, u32[]{:S(2)}) collective-permute-start(bf16[2048,1024]{1,0:T(8,128)(2,1)} %param.31), channel_id=1, source_target_pairs={{0,16},{16,0},{1,17},{17,1},{2,18},{18,2},{3,19},{19,3},{4,20},{20... | collective-permute-start | bytes 12582920 | tf_op jit(solution)/shard_map/ppermute | solution.py:122
  242.5 64.8 %copy-start.53 = (bf16[8,2048,16]{1,2,0:T(8,128)(2,1)S(1)}, bf16[8,2048,16]{1,2,0:T(8,128)(2,1)}, u32[]{:S(2)}) copy-start(bf16[8,2048,16]{1,2,0:T(8,128)(2,1)} %param.36) | copy-start | bytes 1572868
  315.4 16.9 %copy-start.13 = (bf16[4,256,2048]{2,1,0:T(8,128)(2,1)S(1)}, bf16[4,256,2048]{2,1,0:T(8,128)(2,1)}, u32[]{:S(2)}) copy-start(bf16[4,256,2048]{2,1,0:T(8,128)(2,1)} %param.21) | copy-start | bytes 12582916
  371.6 163.4 %reduce-scatter.4.cloned.1.call-start = ((), (), s32[]{:S(2)}) async-start(), calls=%async_computation.7 | async-start | bytes 5570560 | tf_op jit(solution)/shard_map/reduce_scatter | solution.py:171
  414.5 123.3 %copy-start.54 = (bf16[8,2048,16]{1,2,0:T(8,128)(2,1)S(1)}, bf16[8,2048,16]{1,2,0:T(8,128)(2,1)}, u32[]{:S(2)}) copy-start(bf16[8,2048,16]{1,2,0:T(8,128)(2,1)} %param.36) | copy-start | bytes 1572868
  545.3 17.9 %collective-permute-start.18 = (bf16[256,384]{1,0:T(8,128)(2,1)}, bf16[256,384]{1,0:T(8,128)(2,1)S(1)}, u32[]{:S(2)}, u32[]{:S(2)}) collective-permute-start(bf16[256,384]{1,0:T(8,128)(2,1)} %get-tuple-element.63), channel_id=1, source_target_pairs={{0,3},{1,2},{2,1},{3,0},{4,7},{5,6},{6,5},{7,4},{8,11},{9,10},{10,... | collective-permute-start | bytes 589832 | tf_op jit(solution)/shard_map/ppermute | solution.py:115
  547.9 24.3 %collective-permute-start.17 = (bf16[256,384]{1,0:T(8,128)(2,1)}, bf16[256,384]{1,0:T(8,128)(2,1)S(1)}, u32[]{:S(2)}, u32[]{:S(2)}) collective-permute-start(bf16[256,384]{1,0:T(8,128)(2,1)} %get-tuple-element.63), channel_id=1, source_target_pairs={{0,2},{1,3},{2,0},{3,1},{4,6},{5,7},{6,4},{7,5},{8,10},{9,11},{10,... | collective-permute-start | bytes 589832 | tf_op jit(solution)/shard_map/ppermute | solution.py:115
  548.3 24.0 %collective-permute-start.16 = (bf16[256,384]{1,0:T(8,128)(2,1)}, bf16[256,384]{1,0:T(8,128)(2,1)S(1)}, u32[]{:S(2)}, u32[]{:S(2)}) collective-permute-start(bf16[256,384]{1,0:T(8,128)(2,1)} %get-tuple-element.63), channel_id=1, source_target_pairs={{0,1},{1,0},{2,3},{3,2},{4,5},{5,4},{6,7},{7,6},{8,9},{9,8},{10,11... | collective-permute-start | bytes 589832 | tf_op jit(solution)/shard_map/ppermute | solution.py:115
  556.9 33.0 %all-to-all-start.1 = ((bf16[256,4,512]{0,2,1:T(8,128)(2,1)}), bf16[256,4,512]{0,2,1:T(8,128)(2,1)S(1)}, u32[]{:S(2)}, u32[]{:S(2)}) async-start(bf16[256,4,512]{0,2,1:T(8,128)(2,1)} %bitcast.233), calls=%async_computation.3 | async-start | bytes 2097152 | tf_op jit(solution)/shard_map/all_to_all | solution.py:372
  560.8 207.5 %all-reduce.4.cloned.1.call-start = ((), (), s32[]{:S(2)}) async-start(), calls=%async_computation.12 | async-start | bytes 1048576 | tf_op jit(solution)/shard_map/psum | solution.py:160
  563.2 253.6 %all-reduce.6.cloned.1.call-start = ((), (), s32[]{:S(2)}) async-start(), calls=%async_computation.13 | async-start | bytes 4456448 | tf_op jit(solution)/shard_map/psum | solution.py:160
  586.2 312.8 %all-gather.9.cloned.1.call-start = ((), (), s32[]{:S(2)}) async-start(), calls=%async_computation.8 | async-start | bytes 5242880 | tf_op jit(solution)/shard_map/all_gather | solution.py:182
  620.8 53.0 %collective-permute-start.9 = (bf16[4,256,1024]{2,1,0:T(8,128)(2,1)}, bf16[4,256,1024]{2,1,0:T(8,128)(2,1)}, u32[]{:S(2)}, u32[]{:S(2)}) collective-permute-start(bf16[4,256,1024]{2,1,0:T(8,128)(2,1)} %pad_maximum_fusion.34), channel_id=1, source_target_pairs={{0,12},{4,8},{8,4},{12,0},{1,13},{5,9},{9,5},{13,1},{2,14},{6,10},... | collective-permute-start | bytes 6291464 | tf_op jit(solution)/shard_map/ppermute | solution.py:403
  633.9 80.7 %collective-permute-start.8 = (bf16[4,256,1024]{2,1,0:T(8,128)(2,1)}, bf16[4,256,1024]{2,1,0:T(8,128)(2,1)}, u32[]{:S(2)}, u32[]{:S(2)}) collective-permute-start(bf16[4,256,1024]{2,1,0:T(8,128)(2,1)} %pad_maximum_fusion.33), channel_id=1, source_target_pairs={{0,8},{4,12},{8,0},{12,4},{1,9},{5,13},{9,1},{13,5},{2,10},{6,14},... | collective-permute-start | bytes 6291464 | tf_op jit(solution)/shard_map/ppermute | solution.py:403
  645.4 69.2 %collective-permute-start.7 = (bf16[4,256,1024]{2,1,0:T(8,128)(2,1)}, bf16[4,256,1024]{2,1,0:T(8,128)(2,1)}, u32[]{:S(2)}, u32[]{:S(2)}) collective-permute-start(bf16[4,256,1024]{2,1,0:T(8,128)(2,1)} %pad_maximum_fusion.32), channel_id=1, source_target_pairs={{0,4},{4,0},{8,12},{12,8},{1,5},{5,1},{9,13},{13,9},{2,6},{6,2},{1... | collective-permute-start | bytes 6291464 | tf_op jit(solution)/shard_map/ppermute | solution.py:403
  670.0 44.6 %copy-start.33 = (f32[4,256,512]{2,1,0:T(8,128)S(1)}, f32[4,256,512]{2,1,0:T(8,128)}, u32[]{:S(2)}) copy-start(f32[4,256,512]{2,1,0:T(8,128)} %copy.171) | copy-start | bytes 6291460
  673.9 52.3 %copy-start.68 = (bf16[128,8,4,128]{3,1,2,0:T(8,128)(2,1)}, bf16[128,8,4,128]{3,1,2,0:T(8,128)(2,1)S(1)}, u32[]{:S(2)}) copy-start(bf16[128,8,4,128]{3,1,2,0:T(8,128)(2,1)S(1)} %copy.206) | copy-start | bytes 3145732
  721.7 26.6 %copy-start.75 = (bf16[1024,128]{1,0:T(8,128)(2,1)}, bf16[1024,128]{1,0:T(8,128)(2,1)S(1)}, u32[]{:S(2)}) copy-start(bf16[1024,128]{1,0:T(8,128)(2,1)S(1)} %convolution_convert_fusion.8) | copy-start | bytes 786436
  721.7 11.7 %collective-permute-start.12 = (bf16[1024,128]{1,0:T(8,128)(2,1)S(1)}, bf16[1024,128]{1,0:T(8,128)(2,1)S(1)}, u32[]{:S(2)}, u32[]{:S(2)}) collective-permute-start(bf16[1024,128]{1,0:T(8,128)(2,1)S(1)} %convolution_convert_fusion.8), channel_id=1, source_target_pairs={{0,3},{1,2},{2,1},{3,0},{4,7},{5,6},{6,5},{7,4},{8,11},{9,10},{10,... | collective-permute-start | bytes 786440 | tf_op jit(solution)/shard_map/ppermute | solution.py:115
  724.3 24.0 %collective-permute-start.11 = (bf16[1024,128]{1,0:T(8,128)(2,1)S(1)}, bf16[1024,128]{1,0:T(8,128)(2,1)S(1)}, u32[]{:S(2)}, u32[]{:S(2)}) collective-permute-start(bf16[1024,128]{1,0:T(8,128)(2,1)S(1)} %convolution_convert_fusion.8), channel_id=1, source_target_pairs={{0,2},{1,3},{2,0},{3,1},{4,6},{5,7},{6,4},{7,5},{8,10},{9,11},{10,... | collective-permute-start | bytes 786440 | tf_op jit(solution)/shard_map/ppermute | solution.py:115
  724.3 24.0 %collective-permute-start.10 = (bf16[1024,128]{1,0:T(8,128)(2,1)S(1)}, bf16[1024,128]{1,0:T(8,128)(2,1)S(1)}, u32[]{:S(2)}, u32[]{:S(2)}) collective-permute-start(bf16[1024,128]{1,0:T(8,128)(2,1)S(1)} %convolution_convert_fusion.8), channel_id=1, source_target_pairs={{0,1},{1,0},{2,3},{3,2},{4,5},{5,4},{6,7},{7,6},{8,9},{9,8},{10,11... | collective-permute-start | bytes 786440 | tf_op jit(solution)/shard_map/ppermute | solution.py:115
  763.9 62.1 %collective-permute-start.13 = (bf16[458752]{0:T(1024)(128)(2,1)S(1)}, bf16[458752]{0:T(1024)(128)(2,1)}, u32[]{:S(2)}, u32[]{:S(2)}) collective-permute-start(bf16[458752]{0:T(1024)(128)(2,1)S(1)} %constant_dynamic-update-slice_fusion), channel_id=1, source_target_pairs={{0,16},{16,0},{1,17},{17,1},{2,18},{18,2},{3,19},{19,3},{4,20},{20... | collective-permute-start | bytes 2752520 | tf_op jit(solution)/shard_map/ppermute | solution.py:138
  768.2 212.7 %reduce-scatter.8.cloned.1.call-start = ((), (), s32[]{:S(2)}) async-start(), calls=%async_computation.10 | async-start | bytes 5570560 | tf_op jit(solution)/shard_map/reduce_scatter | solution.py:171
  827.5 21.2 %collective-permute-start.14 = (bf16[458752]{0:T(1024)(128)(2,1)S(1)}, bf16[458752]{0:T(1024)(128)(2,1)}, u32[]{:S(2)}, u32[]{:S(2)}) collective-permute-start(bf16[458752]{0:T(1024)(128)(2,1)S(1)} %add_convert_fusion.5), channel_id=1, source_target_pairs={{0,4},{4,0},{8,12},{12,8},{1,5},{5,1},{9,13},{13,9},{2,6},{6,2},{1... | collective-permute-start | bytes 2752520 | tf_op jit(solution)/shard_map/ppermute | solution.py:138
  839.7 142.7 %copy-start.59 = (f32[256,128]{1,0:T(8,128)S(1)}, f32[256,128]{1,0:T(8,128)}, u32[]{:S(2)}) copy-start(f32[256,128]{1,0:T(8,128)} %copy-done.57) | copy-start | bytes 393220
  839.7 142.7 %copy-start.62 = (bf16[8,2048,16]{1,2,0:T(8,128)(2,1)S(1)}, bf16[8,2048,16]{1,2,0:T(8,128)(2,1)}, u32[]{:S(2)}) copy-start(bf16[8,2048,16]{1,2,0:T(8,128)(2,1)} %param.32) | copy-start | bytes 1572868
  839.7 142.7 %copy-start.93 = (f32[2048]{0:T(1024)S(1)}, f32[2048]{0:T(1024)}, u32[]{:S(2)}) copy-start(f32[2048]{0:T(1024)} %param.24) | copy-start | bytes 24580
  839.7 231.6 %all-gather.11.cloned.1.call-start = ((), (), s32[]{:S(2)}) async-start(), calls=%async_computation.11 | async-start | bytes 5242880 | tf_op jit(solution)/shard_map/all_gather | solution.py:182
  850.2 139.8 %collective-permute-start.15 = (bf16[458752]{0:T(1024)(128)(2,1)S(1)}, bf16[458752]{0:T(1024)(128)(2,1)S(1)}, u32[]{:S(2)}, u32[]{:S(2)}) collective-permute-start(bf16[458752]{0:T(1024)(128)(2,1)S(1)} %add_convert_fusion.4), channel_id=1, source_target_pairs={{0,8},{4,12},{8,0},{12,4},{1,9},{5,13},{9,1},{13,5},{2,10},{6,14},... | collective-permute-start | bytes 2752520 | tf_op jit(solution)/shard_map/ppermute | solution.py:138
  (90 other events, 433.3 us)
Sparse Core Ops, SparseCore 0:
  13.9 91.7 all-gather.4
  228.2 79.0 all-gather.6
  371.7 79.5 reduce-scatter.5
  453.4 81.5 reduce-scatter.3
  566.5 182.9 all-reduce.3
  753.2 63.5 all-reduce.5
  818.9 80.1 all-gather.8
  901.4 79.5 reduce-scatter.7
  990.1 81.2 all-gather.10

commit v15 on v14

--- a/solution.py
+++ b/solution.py
@@ -292,14 +292,32 @@
     piece_values = pieces[:, :, local_width:].reshape(
         seq_here, piece_len, device_heads, head_width
     )
-    exponent = exponents(queries, piece_keys, here_pos, key_pos, visible_mask, slopes)
-    weighted = jnp.einsum(
-        "shqk,skhd->sqhd",
-        exponent.astype(jnp.bfloat16),
-        piece_values,
-        preferred_element_type=jnp.float32,
-    )
-    weighted, totals = (weighted, jnp.sum(exponent, axis=-1))
+    weighted, totals = None, None
+    for offset in range(ctx_count):
+        keys_slice = slice(offset * local_len, (offset + 1) * local_len)
+        block_keys = blocks[offset][:, :, :local_width].reshape(
+            seq_here, local_len, device_heads, head_width
+        )
+        block_values = blocks[offset][:, :, local_width:].reshape(
+            seq_here, local_len, device_heads, head_width
+        )
+        block_exponent = exponents(
+            queries,
+            block_keys,
+            here_pos,
+            key_pos[keys_slice],
+            visible_mask[:, :, keys_slice],
+            slopes,
+        )
+        block_weighted = jnp.einsum(
+            "shqk,skhd->sqhd",
+            block_exponent.astype(jnp.bfloat16),
+            block_values,
+            preferred_element_type=jnp.float32,
+        )
+        block_totals = jnp.sum(block_exponent, axis=-1)
+        weighted = block_weighted if weighted is None else weighted + block_weighted
+        totals = block_totals if totals is None else totals + block_totals
     per_total = jnp.transpose(totals, (0, 2, 1))[..., None]
     heads_raw = weighted / per_total
     heads_act = heads_raw.reshape(tok_rows, local_width).astype(jnp.bfloat16)
@@ -377,7 +395,7 @@
     row_delta = jnp.sum(grad_heads_wide * heads_raw, axis=-1) / per_total[..., 0]
     grad_queries = None
     grad_kv_here = None
-    for offset in list(range(1, ctx_count)) + [0]:
+    for offset in list(range(ctx_count - 1, 0, -1)) + [0]:
         keys_slice = slice(offset * local_len, (offset + 1) * local_len)
         query_part, key_part, value_part = block_grads(
             queries,

time: 1100 us -> 1070 us (0.973)
  waiting for transfers between devices: 609 us -> 578 us
  local copies, waits for them, and re-layouts: 100 us -> 117 us
    psum x2, waiting for transfers between devices: 46.3 us -> 19.2 us  [narrow_psum(): lax.psum(jax.tree.map(lambda value: value.astype(jnp.bfloat16), values),...]
    ppermute x9, waiting for transfers between devices: 112 us -> 96.2 us  [partner_swaps(): received.append(lax.ppermute(block, axis_name, pairs))]
    ppermute x3, waiting for transfers between devices: 40.7 us -> 54.7 us  [layer_body(): lax.ppermute(block_kv.astype(jnp.bfloat16), 'ctx', pairs)]
    unnamed x225 -> x281, local copies, waits for them, and re-layouts: 34.9 us -> 39.3 us
    dot_general x5 -> x8, matrix products: 21.7 us -> 22.6 us  [exponents(): jnp.einsum('sqhd,skhd->shqk', queries, key_rows, preferred_element_type=j...]
  transfers between devices with their start and end apart: 30 -> 30, of which waited for: 17 -> 17; matrix products, arithmetic and copies ran while one was open for 29% -> 30% of each run, Pallas kernels for 0% -> 0%
where the time goes in v15:
time: 1070 us; the launch traced here: 1060 us
  waiting for transfers between devices  578 us (54%)
  matrix products  215 us (20%)
  local copies, waits for them, and re-layouts  117 us (11%)
  other arithmetic  109 us (10%)
  starting transfers between devices  29.3 us (3%)
  between operations  16 us (1%)
    reduce_scatter x3, waiting for transfers between devices, scatter_rows(): lax.psum_scatter(jnp.concatenate(partials, axis=1).astype(jnp.bfloat16),...  197 us
    all_gather x3, waiting for transfers between devices, gather_rows(): lax.all_gather(jnp.concatenate(rows_here, axis=1), 'tp', axis=0, tiled=True)  179 us
    ppermute x9, waiting for transfers between devices, partner_swaps(): received.append(lax.ppermute(block, axis_name, pairs))  96.2 us
    dot_general x12, matrix products, matmul_nt(): lax.dot_general(left_mat, right_mat, (((1,), (1,)), ((), ())), preferred_...  65.3 us
    dot_general x12, matrix products, matmul(): return jnp.dot(left_mat, right_mat, preferred_element_type=jnp.float32)  62.7 us
    ppermute x3, waiting for transfers between devices, layer_body(): lax.ppermute(block_kv.astype(jnp.bfloat16), 'ctx', pairs)  54.7 us
    unnamed x281, local copies, waits for them, and re-layouts  39.3 us
    dot_general x8, matrix products, exponents(): jnp.einsum('sqhd,skhd->shqk', queries, key_rows, preferred_element_type=j...  22.6 us
  transfers between devices with their start and end apart: 30, of which 17 were waited for; matrix products, arithmetic and copies ran while one was open for 30% of the time, Pallas kernels for 0%

profile of v15, /device:TPU:0, one launch (start us, length us, event | category | flops | bytes accessed | tf_op | source)
XLA Modules:
  0.0 1064.4 jit_solution(2573390553005369004)
XLA Ops:
  7.3 4.8 copy.184
  27.3 5.0 broadcast_select_fusion.7
  32.3 6.5 pad_maximum_fusion.4
  38.8 8.9 add_convert_fusion.1
  74.1 29.2 %collective-permute-done.3 = bf16[4,256,1024]{1,2,0:T(8,128)(2,1)} collective-permute-done((bf16[4,256,1024]{1,2,0:T(8,128)(2,1)}, bf16[4,256,1024]{1,2,0:T(8,128)(2,1)}, u32[]{:S(2)}, u32[]{:S(2)}) %collective-permute-start.3) | collective-permute-done | bytes 2097184 | tf_op jit(solution)/shard_map/ppermute | solution.py:115
  106.0 41.9 %collective-permute-done.2 = bf16[4,256,1024]{1,2,0:T(8,128)(2,1)} collective-permute-done((bf16[4,256,1024]{1,2,0:T(8,128)(2,1)}, bf16[4,256,1024]{1,2,0:T(8,128)(2,1)}, u32[]{:S(2)}, u32[]{:S(2)}) %collective-permute-start.2) | collective-permute-done | bytes 2097184 | tf_op jit(solution)/shard_map/ppermute | solution.py:115
  160.3 4.9 slice.186
  175.4 5.1 all-to-all-start
  180.9 6.7 convert.111
  187.6 18.8 %all-to-all-done = bf16[4,256,512]{1,2,0:T(8,128)(2,1)S(1)} async-done(((bf16[4,256,512]{1,2,0:T(8,128)(2,1)}), bf16[4,256,512]{1,2,0:T(8,128)(2,1)S(1)}, u32[]{:S(2)}, u32[]{:S(2)}) %all-to-all-start) | async-done | bytes 1048608 | tf_op jit(solution)/shard_map/all_to_all | solution.py:324
  208.3 3.8 broadcast_select_fusion.5
  212.2 6.5 fusion.170
  222.1 3.4 fusion.97
  225.6 5.0 fusion.174
  230.6 4.2 broadcast_select_fusion.1
  235.3 3.6 broadcast_select_fusion.3
  238.9 62.6 %all-gather.7.cloned.1.call-done = bf16[1024,2048]{1,0:T(8,128)(2,1)} async-done(((bf16[256,2048]{1,0:T(8,128)(2,1)}), bf16[1024,2048]{1,0:T(8,128)(2,1)}) %all-gather.7.cloned.1.call-update) | async-done | bytes 4194320 | tf_op jit(solution)/shard_map/all_gather | solution.py:182
  301.5 3.4 fusion.96
  305.0 4.6 fusion.173
  309.6 17.0 %multiply_convert_fusion = (bf16[1024,2048]{1,0:T(8,128)(2,1)}, f32[1024,2048]{1,0:T(8,128)}) fusion(f32[1024,2048]{1,0:T(8,128)} %fusion.173, bf16[1024,2048]{1,0:T(8,128)(2,1)S(1)} %copy-done.47, bf16[1024,2048]{1,0:T(8,128)(2,1)} %get-tuple-element.48, bf16[1024,2048]{1,0:T(8,128)(2,1)} %get-tuple-element.47), kind=kOutput, calls=%fused_computation.17 | convolution fusion | flops 8627683328 | bytes 33554432 | tf_op jit(solution)/shard_map/dot_general | solution.py:43
  326.6 21.1 %fusion.3 = bf16[1024,2048]{1,0:T(8,128)(2,1)} fusion(f32[1024,2048]{1,0:T(8,128)} %get-tuple-element.95, f32[1024,2048]{1,0:T(8,128)} %fusion.174, bf16[1024,2048]{1,0:T(8,128)(2,1)S(1)} %bitcast.229, bf16[2048,1024]{1,0:T(8,128)(2,1)} %get-tuple-element.46, bf16[2048,1024]{1,0:T(8,128)(2,1)} %get-tuple-element.45), kind=kOutput, calls=%fused_computation.9 | convolution fusion | flops 8659140608 | bytes 33554432 | tf_op jit(solution)/shard_map/dot_general | solution.py:53
  347.6 3.6 convolution_convert_fusion.9
  351.2 12.0 %fusion.14 = bf16[1024,2048]{1,0:T(8,128)(2,1)S(1)} fusion(bf16[1024,2048]{1,0:T(8,128)(2,1)} %fusion.3, bf16[1024,2048]{1,0:T(8,128)(2,1)} %get-tuple-element.48, bf16[1024,2048]{1,0:T(8,128)(2,1)S(1)} %copy-done.56), kind=kOutput, calls=%fused_computation.55 | convolution fusion | flops 8608808960 | bytes 16777216 | tf_op jit(solution)/shard_map/dot_general | solution.py:53
  365.9 3.6 convolution_convert_fusion.10
  369.5 12.2 %fusion.15 = bf16[1024,2048]{1,0:T(8,128)(2,1)S(1)} fusion(bf16[1024,2048]{1,0:T(8,128)(2,1)} %get-tuple-element.94, bf16[2048,1024]{1,0:T(8,128)(2,1)} %get-tuple-element.46, bf16[2048,1024]{1,0:T(8,128)(2,1)S(1)} %copy-done.55), kind=kOutput, calls=%fused_computation.56 | convolution fusion | flops 8608808960 | bytes 16777216 | tf_op jit(solution)/shard_map/dot_general | solution.py:43
  389.1 3.9 pad_maximum_fusion.3
  411.3 34.2 %reduce-scatter.6.cloned.1.call-done = bf16[256,2176]{1,0:T(8,128)(2,1)} async-done(((bf16[1024,2176]{1,0:T(8,128)(2,1)}), bf16[256,2176]{1,0:T(8,128)(2,1)}) %reduce-scatter.6.cloned.1.call-update) | async-done | bytes 1114128 | tf_op jit(solution)/shard_map/reduce_scatter | solution.py:171
  448.3 81.0 %reduce-scatter.4.cloned.1.call-done = bf16[256,2176]{1,0:T(8,128)(2,1)} async-done(((bf16[1024,2176]{1,0:T(8,128)(2,1)}), bf16[256,2176]{1,0:T(8,128)(2,1)}) %reduce-scatter.4.cloned.1.call-update) | async-done | bytes 1114128 | tf_op jit(solution)/shard_map/reduce_scatter | solution.py:171
  551.2 3.9 all-to-all-start.1
  557.5 9.0 collective-permute-done.17
  572.6 3.9 convolution_convert_fusion.4
  580.7 3.5 all-to-all-done.1
  644.7 3.5 fusion.36
  651.2 3.7 convolution_multiply_fusion
  670.2 54.7 %collective-permute-done.8 = bf16[4,256,1024]{2,1,0:T(8,128)(2,1)} collective-permute-done((bf16[4,256,1024]{2,1,0:T(8,128)(2,1)}, bf16[4,256,1024]{2,1,0:T(8,128)(2,1)}, u32[]{:S(2)}, u32[]{:S(2)}) %collective-permute-start.8) | collective-permute-done | bytes 2097184 | tf_op jit(solution)/shard_map/ppermute | solution.py:421
  724.9 5.1 fusion.12
  738.4 4.8 collective-permute-done.12
  743.1 11.2 %collective-permute-done.11 = bf16[1024,128]{1,0:T(8,128)(2,1)S(1)} collective-permute-done((bf16[1024,128]{1,0:T(8,128)(2,1)S(1)}, bf16[1024,128]{1,0:T(8,128)(2,1)S(1)}, u32[]{:S(2)}, u32[]{:S(2)}) %collective-permute-start.11) | collective-permute-done | bytes 262176 | tf_op jit(solution)/shard_map/ppermute | solution.py:115
  761.9 6.0 reshape.630
  776.7 19.2 %all-reduce.6.cloned.1.call-done = (bf16[8,512,16]{1,2,0:T(8,128)(2,1)}, bf16[8,2048,16]{1,2,0:T(8,128)(2,1)}, bf16[8,16,2048]{2,1,0:T(8,128)(2,1)}, bf16[8,2048,16]{1,2,0:T(8,128)(2,1)}, bf16[8,16,2048]{2,1,0:T(8,128)(2,1)}) async-done(((bf16[8,512,16]{1,2,0:T(8,128)(2,1)}, bf16[8,2048,16]{1,2,0:T(8,128)(2,1)}, bf16[8,16,2048]{2,1,0:T(8,128)(2,1)}, bf16[8,2048,16]{1,2,0:T(8,128)(2,1)}, ...) | async-done | bytes 2228240 | tf_op jit(solution)/shard_map/psum | solution.py:160
  807.1 8.9 convolution_convert_fusion
  818.9 8.9 collective-permute-done.14
  830.4 47.7 %all-gather.9.cloned.1.call-done = bf16[1024,2048]{1,0:T(8,128)(2,1)} async-done(((bf16[256,2048]{1,0:T(8,128)(2,1)}), bf16[1024,2048]{1,0:T(8,128)(2,1)}) %all-gather.9.cloned.1.call-update) | async-done | bytes 4194320 | tf_op jit(solution)/shard_map/all_gather | solution.py:182
  878.2 81.9 %reduce-scatter.8.cloned.1.call-done = bf16[256,2176]{1,0:T(8,128)(2,1)} async-done(((bf16[1024,2176]{1,0:T(8,128)(2,1)}), bf16[256,2176]{1,0:T(8,128)(2,1)}) %reduce-scatter.8.cloned.1.call-update) | async-done | bytes 1114128 | tf_op jit(solution)/shard_map/reduce_scatter | solution.py:171
  969.4 4.6 slice.164
  974.0 6.3 copy.267
  981.8 68.7 %all-gather.11.cloned.1.call-done = bf16[1024,2048]{1,0:T(8,128)(2,1)} async-done(((bf16[256,2048]{1,0:T(8,128)(2,1)}), bf16[1024,2048]{1,0:T(8,128)(2,1)}) %all-gather.11.cloned.1.call-update) | async-done | bytes 4194320 | tf_op jit(solution)/shard_map/all_gather | solution.py:182
  1050.4 4.9 copy.337
  (484 shorter events, 270.5 us)
Async XLA Ops:
  7.2 297.8 %copy-start = (bf16[8,16,2048]{2,1,0:T(8,128)(2,1)S(1)}, bf16[8,16,2048]{2,1,0:T(8,128)(2,1)}, u32[]{:S(2)}) copy-start(bf16[8,16,2048]{2,1,0:T(8,128)(2,1)} %param.37) | copy-start | bytes 1572868
  7.2 153.0 %all-gather.5.cloned.1.call-start = ((), (), s32[]{:S(2)}) async-start(), calls=%async_computation.5 | async-start | bytes 5898240 | tf_op jit(solution)/shard_map/all_gather | solution.py:237
  12.1 13.5 %collective-permute-start = (bf16[1024,3,512]{0,2,1:T(8,128)(2,1)}, bf16[1024,3,512]{0,2,1:T(8,128)(2,1)}, u32[]{:S(2)}, u32[]{:S(2)}) collective-permute-start(bf16[1024,3,512]{0,2,1:T(8,128)(2,1)} %copy.184), channel_id=1, source_target_pairs={{0,16},{16,0},{1,17},{17,1},{2,18},{18,2},{3,19},{19,3},{4,20},{20... | collective-permute-start | bytes 9437192 | tf_op jit(solution)/shard_map/ppermute | solution.py:122
  23.3 15.5 %copy-start.12 = (bf16[4,256,2048]{2,1,0:T(8,128)(2,1)}, bf16[4,256,2048]{2,1,0:T(8,128)(2,1)S(1)}, u32[]{:S(2)}) copy-start(bf16[4,256,2048]{2,1,0:T(8,128)(2,1)S(1)} %add_convert_fusion) | copy-start | bytes 12582916
  53.2 50.1 %collective-permute-start.3 = (bf16[4,256,1024]{1,2,0:T(8,128)(2,1)}, bf16[4,256,1024]{1,2,0:T(8,128)(2,1)}, u32[]{:S(2)}, u32[]{:S(2)}) collective-permute-start(bf16[4,256,1024]{1,2,0:T(8,128)(2,1)} %pad_maximum_fusion.31), channel_id=1, source_target_pairs={{0,12},{4,8},{8,4},{12,0},{1,13},{5,9},{9,5},{13,1},{2,14},{6,10},... | collective-permute-start | bytes 6291464 | tf_op jit(solution)/shard_map/ppermute | solution.py:115
  57.8 90.1 %collective-permute-start.2 = (bf16[4,256,1024]{1,2,0:T(8,128)(2,1)}, bf16[4,256,1024]{1,2,0:T(8,128)(2,1)}, u32[]{:S(2)}, u32[]{:S(2)}) collective-permute-start(bf16[4,256,1024]{1,2,0:T(8,128)(2,1)} %pad_maximum_fusion.31), channel_id=1, source_target_pairs={{0,8},{4,12},{8,0},{12,4},{1,9},{5,13},{9,1},{13,5},{2,10},{6,14},... | collective-permute-start | bytes 6291464 | tf_op jit(solution)/shard_map/ppermute | solution.py:115
  59.4 12.3 %copy-start.67 = (pred[4,256,256]{1,2,0:T(8,128)(4,1)}, pred[4,256,256]{1,2,0:T(8,128)(4,1)S(1)}, u32[]{:S(2)}) copy-start(pred[4,256,256]{1,2,0:T(8,128)(4,1)S(1)} %get-tuple-element.65) | copy-start | bytes 786436
  59.4 91.1 %collective-permute-start.1 = (bf16[4,256,1024]{1,2,0:T(8,128)(2,1)}, bf16[4,256,1024]{1,2,0:T(8,128)(2,1)}, u32[]{:S(2)}, u32[]{:S(2)}) collective-permute-start(bf16[4,256,1024]{1,2,0:T(8,128)(2,1)} %pad_maximum_fusion.31), channel_id=1, source_target_pairs={{0,4},{4,0},{8,12},{12,8},{1,5},{5,1},{9,13},{13,9},{2,6},{6,2},{1... | collective-permute-start | bytes 6291464 | tf_op jit(solution)/shard_map/ppermute | solution.py:115
  68.8 96.4 %copy-start.2 = (bf16[4,256,4,128]{1,3,2,0:T(8,128)(2,1)}, bf16[4,256,4,128]{1,3,2,0:T(8,128)(2,1)S(1)}, u32[]{:S(2)}) copy-start(bf16[4,256,4,128]{1,3,2,0:T(8,128)(2,1)S(1)} %copy.241) | copy-start | bytes 3145732
  105.9 47.6 %copy-start.34 = (f32[4,256,256]{1,2,0:T(8,128)S(1)}, f32[4,256,256]{1,2,0:T(8,128)}, u32[]{:S(2)}) copy-start(f32[4,256,256]{1,2,0:T(8,128)} %get-tuple-element.78) | copy-start | bytes 3145732
  105.9 47.6 %copy-start.69 = (pred[4,256,256]{1,2,0:T(8,128)(4,1)S(1)}, pred[4,256,256]{1,2,0:T(8,128)(4,1)}, u32[]{:S(2)}) copy-start(pred[4,256,256]{1,2,0:T(8,128)(4,1)} %get-tuple-element.62) | copy-start | bytes 786436
  165.2 43.2 %collective-permute-start.4 = (bf16[2048,1024]{1,0:T(8,128)(2,1)}, bf16[2048,1024]{1,0:T(8,128)(2,1)}, u32[]{:S(2)}, u32[]{:S(2)}) collective-permute-start(bf16[2048,1024]{1,0:T(8,128)(2,1)} %slice.186), channel_id=1, source_target_pairs={{0,16},{16,0},{1,17},{17,1},{2,18},{18,2},{3,19},{19,3},{4,20},{20... | collective-permute-start | bytes 12582920 | tf_op jit(solution)/shard_map/ppermute | solution.py:122
  175.4 31.0 %all-to-all-start = ((bf16[4,256,512]{1,2,0:T(8,128)(2,1)}), bf16[4,256,512]{1,2,0:T(8,128)(2,1)S(1)}, u32[]{:S(2)}, u32[]{:S(2)}) async-start(bf16[4,256,512]{1,2,0:T(8,128)(2,1)} %bitcast.16), calls=%async_computation | async-start | bytes 2097152 | tf_op jit(solution)/shard_map/all_to_all | solution.py:324
  180.4 121.1 %all-gather.7.cloned.1.call-start = ((), (), s32[]{:S(2)}) async-start(), calls=%async_computation.6 | async-start | bytes 5242880 | tf_op jit(solution)/shard_map/all_gather | solution.py:182
  180.9 27.0 %copy-start.84 = (bf16[8,16,2048]{2,1,0:T(8,128)(2,1)S(1)}, bf16[8,16,2048]{2,1,0:T(8,128)(2,1)}, u32[]{:S(2)}) copy-start(bf16[8,16,2048]{2,1,0:T(8,128)(2,1)} %param.35) | copy-start | bytes 1572868
  187.6 24.5 %copy-start.81 = (f32[256,128]{1,0:T(8,128)}, f32[256,128]{1,0:T(8,128)S(1)}, u32[]{:S(2)}) copy-start(f32[256,128]{1,0:T(8,128)S(1)} %constant_dynamic-slice_fusion) | copy-start | bytes 393220
  221.5 224.0 %reduce-scatter.6.cloned.1.call-start = ((), (), s32[]{:S(2)}) async-start(), calls=%async_computation.9 | async-start | bytes 5570560 | tf_op jit(solution)/shard_map/reduce_scatter | solution.py:171
  221.6 9.1 collective-permute-start.5
  221.6 13.4 %collective-permute-start.6 = (bf16[2048,1024]{1,0:T(8,128)(2,1)}, bf16[2048,1024]{1,0:T(8,128)(2,1)S(1)}, u32[]{:S(2)}, u32[]{:S(2)}) collective-permute-start(bf16[2048,1024]{1,0:T(8,128)(2,1)} %param.31), channel_id=1, source_target_pairs={{0,16},{16,0},{1,17},{17,1},{2,18},{18,2},{3,19},{19,3},{4,20},{20... | collective-permute-start | bytes 12582920 | tf_op jit(solution)/shard_map/ppermute | solution.py:122
  234.8 66.7 %copy-start.77 = (bf16[8,2048,16]{1,2,0:T(8,128)(2,1)S(1)}, bf16[8,2048,16]{1,2,0:T(8,128)(2,1)}, u32[]{:S(2)}) copy-start(bf16[8,2048,16]{1,2,0:T(8,128)(2,1)} %param.36) | copy-start | bytes 1572868
  309.6 17.0 %copy-start.10 = (bf16[4,256,2048]{2,1,0:T(8,128)(2,1)S(1)}, bf16[4,256,2048]{2,1,0:T(8,128)(2,1)}, u32[]{:S(2)}) copy-start(bf16[4,256,2048]{2,1,0:T(8,128)(2,1)} %param.21) | copy-start | bytes 12582916
  365.8 163.4 %reduce-scatter.4.cloned.1.call-start = ((), (), s32[]{:S(2)}) async-start(), calls=%async_computation.7 | async-start | bytes 5570560 | tf_op jit(solution)/shard_map/reduce_scatter | solution.py:171
  411.3 120.8 %copy-start.78 = (bf16[8,2048,16]{1,2,0:T(8,128)(2,1)S(1)}, bf16[8,2048,16]{1,2,0:T(8,128)(2,1)}, u32[]{:S(2)}) copy-start(bf16[8,2048,16]{1,2,0:T(8,128)(2,1)} %param.36) | copy-start | bytes 1572868
  538.4 10.5 copy-start.27
  539.6 17.9 %collective-permute-start.18 = (bf16[256,384]{1,0:T(8,128)(2,1)}, bf16[256,384]{1,0:T(8,128)(2,1)S(1)}, u32[]{:S(2)}, u32[]{:S(2)}) collective-permute-start(bf16[256,384]{1,0:T(8,128)(2,1)} %get-tuple-element.69), channel_id=1, source_target_pairs={{0,3},{1,2},{2,1},{3,0},{4,7},{5,6},{6,5},{7,4},{8,11},{9,10},{10,... | collective-permute-start | bytes 589832 | tf_op jit(solution)/shard_map/ppermute | solution.py:115
  542.2 24.3 %collective-permute-start.17 = (bf16[256,384]{1,0:T(8,128)(2,1)}, bf16[256,384]{1,0:T(8,128)(2,1)S(1)}, u32[]{:S(2)}, u32[]{:S(2)}) collective-permute-start(bf16[256,384]{1,0:T(8,128)(2,1)} %get-tuple-element.69), channel_id=1, source_target_pairs={{0,2},{1,3},{2,0},{3,1},{4,6},{5,7},{6,4},{7,5},{8,10},{9,11},{10,... | collective-permute-start | bytes 589832 | tf_op jit(solution)/shard_map/ppermute | solution.py:115
  542.5 24.0 %collective-permute-start.16 = (bf16[256,384]{1,0:T(8,128)(2,1)}, bf16[256,384]{1,0:T(8,128)(2,1)S(1)}, u32[]{:S(2)}, u32[]{:S(2)}) collective-permute-start(bf16[256,384]{1,0:T(8,128)(2,1)} %get-tuple-element.69), channel_id=1, source_target_pairs={{0,1},{1,0},{2,3},{3,2},{4,5},{5,4},{6,7},{7,6},{8,9},{9,8},{10,11... | collective-permute-start | bytes 589832 | tf_op jit(solution)/shard_map/ppermute | solution.py:115
  551.2 33.0 %all-to-all-start.1 = ((bf16[256,4,512]{0,2,1:T(8,128)(2,1)}), bf16[256,4,512]{0,2,1:T(8,128)(2,1)S(1)}, u32[]{:S(2)}, u32[]{:S(2)}) async-start(bf16[256,4,512]{0,2,1:T(8,128)(2,1)} %bitcast.251), calls=%async_computation.3 | async-start | bytes 2097152 | tf_op jit(solution)/shard_map/all_to_all | solution.py:390
  555.0 219.5 %all-reduce.4.cloned.1.call-start = ((), (), s32[]{:S(2)}) async-start(), calls=%async_computation.12 | async-start | bytes 1048576 | tf_op jit(solution)/shard_map/psum | solution.py:160
  557.4 238.4 %all-reduce.6.cloned.1.call-start = ((), (), s32[]{:S(2)}) async-start(), calls=%async_computation.13 | async-start | bytes 4456448 | tf_op jit(solution)/shard_map/psum | solution.py:160
  580.4 297.7 %all-gather.9.cloned.1.call-start = ((), (), s32[]{:S(2)}) async-start(), calls=%async_computation.8 | async-start | bytes 5242880 | tf_op jit(solution)/shard_map/all_gather | solution.py:182
  618.9 51.3 %collective-permute-start.9 = (bf16[4,256,1024]{2,1,0:T(8,128)(2,1)}, bf16[4,256,1024]{2,1,0:T(8,128)(2,1)}, u32[]{:S(2)}, u32[]{:S(2)}) collective-permute-start(bf16[4,256,1024]{2,1,0:T(8,128)(2,1)} %pad_maximum_fusion.34), channel_id=1, source_target_pairs={{0,4},{4,0},{8,12},{12,8},{1,5},{5,1},{9,13},{13,9},{2,6},{6,2},{1... | collective-permute-start | bytes 6291464 | tf_op jit(solution)/shard_map/ppermute | solution.py:421
  631.5 93.4 %collective-permute-start.8 = (bf16[4,256,1024]{2,1,0:T(8,128)(2,1)}, bf16[4,256,1024]{2,1,0:T(8,128)(2,1)}, u32[]{:S(2)}, u32[]{:S(2)}) collective-permute-start(bf16[4,256,1024]{2,1,0:T(8,128)(2,1)} %pad_maximum_fusion.33), channel_id=1, source_target_pairs={{0,8},{4,12},{8,0},{12,4},{1,9},{5,13},{9,1},{13,5},{2,10},{6,14},... | collective-permute-start | bytes 6291464 | tf_op jit(solution)/shard_map/ppermute | solution.py:421
  644.2 80.7 %collective-permute-start.7 = (bf16[4,256,1024]{2,1,0:T(8,128)(2,1)}, bf16[4,256,1024]{2,1,0:T(8,128)(2,1)}, u32[]{:S(2)}, u32[]{:S(2)}) collective-permute-start(bf16[4,256,1024]{2,1,0:T(8,128)(2,1)} %pad_maximum_fusion.32), channel_id=1, source_target_pairs={{0,12},{4,8},{8,4},{12,0},{1,13},{5,9},{9,5},{13,1},{2,14},{6,10},... | collective-permute-start | bytes 6291464 | tf_op jit(solution)/shard_map/ppermute | solution.py:421
  666.0 58.9 %copy-start.46 = (f32[4,256,512]{2,1,0:T(8,128)S(1)}, f32[4,256,512]{2,1,0:T(8,128)}, u32[]{:S(2)}) copy-start(f32[4,256,512]{2,1,0:T(8,128)} %copy.260) | copy-start | bytes 6291460
  670.2 66.3 %copy-start.93 = (bf16[128,8,4,128]{3,1,2,0:T(8,128)(2,1)}, bf16[128,8,4,128]{3,1,2,0:T(8,128)(2,1)S(1)}, u32[]{:S(2)}) copy-start(bf16[128,8,4,128]{3,1,2,0:T(8,128)(2,1)S(1)} %copy.327) | copy-start | bytes 3145732
  732.0 22.3 %copy-start.101 = (bf16[1024,128]{1,0:T(8,128)(2,1)}, bf16[1024,128]{1,0:T(8,128)(2,1)S(1)}, u32[]{:S(2)}) copy-start(bf16[1024,128]{1,0:T(8,128)(2,1)S(1)} %convolution_convert_fusion.8) | copy-start | bytes 786436
  732.0 11.1 %collective-permute-start.12 = (bf16[1024,128]{1,0:T(8,128)(2,1)S(1)}, bf16[1024,128]{1,0:T(8,128)(2,1)S(1)}, u32[]{:S(2)}, u32[]{:S(2)}) collective-permute-start(bf16[1024,128]{1,0:T(8,128)(2,1)S(1)} %convolution_convert_fusion.8), channel_id=1, source_target_pairs={{0,3},{1,2},{2,1},{3,0},{4,7},{5,6},{6,5},{7,4},{8,11},{9,10},{10,... | collective-permute-start | bytes 786440 | tf_op jit(solution)/shard_map/ppermute | solution.py:115
  734.6 19.8 %collective-permute-start.11 = (bf16[1024,128]{1,0:T(8,128)(2,1)S(1)}, bf16[1024,128]{1,0:T(8,128)(2,1)S(1)}, u32[]{:S(2)}, u32[]{:S(2)}) collective-permute-start(bf16[1024,128]{1,0:T(8,128)(2,1)S(1)} %convolution_convert_fusion.8), channel_id=1, source_target_pairs={{0,2},{1,3},{2,0},{3,1},{4,6},{5,7},{6,4},{7,5},{8,10},{9,11},{10,... | collective-permute-start | bytes 786440 | tf_op jit(solution)/shard_map/ppermute | solution.py:115
  734.6 19.8 %collective-permute-start.10 = (bf16[1024,128]{1,0:T(8,128)(2,1)S(1)}, bf16[1024,128]{1,0:T(8,128)(2,1)S(1)}, u32[]{:S(2)}, u32[]{:S(2)}) collective-permute-start(bf16[1024,128]{1,0:T(8,128)(2,1)S(1)} %convolution_convert_fusion.8), channel_id=1, source_target_pairs={{0,1},{1,0},{2,3},{3,2},{4,5},{5,4},{6,7},{7,6},{8,9},{9,8},{10,11... | collective-permute-start | bytes 786440 | tf_op jit(solution)/shard_map/ppermute | solution.py:115
  770.2 35.0 %collective-permute-start.13 = (bf16[458752]{0:T(1024)(128)(2,1)S(1)}, bf16[458752]{0:T(1024)(128)(2,1)}, u32[]{:S(2)}, u32[]{:S(2)}) collective-permute-start(bf16[458752]{0:T(1024)(128)(2,1)S(1)} %constant_dynamic-update-slice_fusion), channel_id=1, source_target_pairs={{0,16},{16,0},{1,17},{17,1},{2,18},{18,2},{3,19},{19,3},{4,20},{20... | collective-permute-start | bytes 2752520 | tf_op jit(solution)/shard_map/ppermute | solution.py:138
  774.5 185.6 %reduce-scatter.8.cloned.1.call-start = ((), (), s32[]{:S(2)}) async-start(), calls=%async_computation.10 | async-start | bytes 5570560 | tf_op jit(solution)/shard_map/reduce_scatter | solution.py:171
  806.6 21.2 %collective-permute-start.14 = (bf16[458752]{0:T(1024)(128)(2,1)S(1)}, bf16[458752]{0:T(1024)(128)(2,1)}, u32[]{:S(2)}, u32[]{:S(2)}) collective-permute-start(bf16[458752]{0:T(1024)(128)(2,1)S(1)} %add_convert_fusion.5), channel_id=1, source_target_pairs={{0,4},{4,0},{8,12},{12,8},{1,5},{5,1},{9,13},{13,9},{2,6},{6,2},{1... | collective-permute-start | bytes 2752520 | tf_op jit(solution)/shard_map/ppermute | solution.py:138
  818.6 142.9 %copy-start.83 = (f32[256,128]{1,0:T(8,128)S(1)}, f32[256,128]{1,0:T(8,128)}, u32[]{:S(2)}) copy-start(f32[256,128]{1,0:T(8,128)} %copy-done.81) | copy-start | bytes 393220
  818.6 142.9 %copy-start.87 = (bf16[8,2048,16]{1,2,0:T(8,128)(2,1)S(1)}, bf16[8,2048,16]{1,2,0:T(8,128)(2,1)}, u32[]{:S(2)}) copy-start(bf16[8,2048,16]{1,2,0:T(8,128)(2,1)} %param.32) | copy-start | bytes 1572868
  818.6 142.9 %copy-start.118 = (f32[2048]{0:T(1024)S(1)}, f32[2048]{0:T(1024)}, u32[]{:S(2)}) copy-start(f32[2048]{0:T(1024)} %param.24) | copy-start | bytes 24580
  818.6 231.8 %all-gather.11.cloned.1.call-start = ((), (), s32[]{:S(2)}) async-start(), calls=%async_computation.11 | async-start | bytes 5242880 | tf_op jit(solution)/shard_map/all_gather | solution.py:182
  829.2 139.8 %collective-permute-start.15 = (bf16[458752]{0:T(1024)(128)(2,1)S(1)}, bf16[458752]{0:T(1024)(128)(2,1)S(1)}, u32[]{:S(2)}, u32[]{:S(2)}) collective-permute-start(bf16[458752]{0:T(1024)(128)(2,1)S(1)} %add_convert_fusion.4), channel_id=1, source_target_pairs={{0,8},{4,12},{8,0},{12,4},{1,9},{5,13},{9,1},{13,5},{2,10},{6,14},... | collective-permute-start | bytes 2752520 | tf_op jit(solution)/shard_map/ppermute | solution.py:138
  (118 other events, 563.7 us)
Sparse Core Ops, SparseCore 0:
  14.0 91.7 all-gather.4
  221.6 79.8 all-gather.6
  366.0 79.5 reduce-scatter.5
  447.7 81.5 reduce-scatter.3
  560.8 170.6 all-reduce.3
  735.2 60.6 all-reduce.5
  798.0 80.1 all-gather.8
  880.5 79.5 reduce-scatter.7
  969.1 81.2 all-gather.10
